TPU v7x, 256 devices: a whole 4x4x8 slice. The times are simulated.
256 devices in a mesh: dp: 4 (over z_lo, core), mp: 64 (over y, z_hi, x).
Axes of the slice: x: 4, y: 4, z: 8 (z_hi: 4, z_lo: 2; z = z_hi * 2 + z_lo), core: 2. Of those that a mesh axis runs over, the one named last changes fastest.
Arguments:
- attn_out: bfloat16 [512, 8192], P('dp', 'mp'), may hold values from -6 to 6
- residual: bfloat16 [512, 8192], P('dp', 'mp'), may hold values from -40 to 40
- output_weight: bfloat16 [8192, 8192], P('mp', 'dp'), may hold values from -0.0625 to 0.0625
- prune_mask: int32 [8192, 128], P('mp'), may hold values 0 or 1
- inverse_factor: float32 [128, 8192], P(None, 'dp'), may hold values from -2 to 2, as said below
- norm_gain: bfloat16 [8192], P('mp'), may hold values from 0.5 to 1.5
- gate_up_weight: bfloat16 [8192, 2, 14336], P('dp', None, 'mp'), may hold values from -0.0625 to 0.0625
Outputs:
- pruned_weight: bfloat16 [8192, 8192], P('mp', 'dp')
- stream: bfloat16 [512, 8192], P('dp', 'mp')
- hessian: float32 [14336, 14336], P('mp', 'dp')
Inputs may be any that keep to these rules, and one draw needn't show every extreme that they name: inverse_factor is zero below its diagonal, and its diagonal lies between 0.5 and 2.
All inputs are finite; a program needn't handle non-finite values. No bound on the sum of `prune_mask` on one device may be relied on, other than what follows from the above.
Results may differ from a plain program's by a relative error of at most 0.012.
Values may be sent and summed in bfloat16 or wider, within the bound.
No kernel may reach another device: no remote copies, remote signals or barrier semaphores. Data moves between devices by JAX's collectives and lax.ppermute only.
A program may use at most 64 MiB of HBM per device.

v0:
```python
import jax
import jax.numpy as jnp
from jax import lax
from jax.experimental import pallas as pl
from jax.experimental.pallas import tpu as pltpu
from jax.sharding import Mesh
from jax.sharding import PartitionSpec as P


DP = ("z_low", "core")
MP = ("y", "z_high", "x")
NT = (((1,), (1,)), ((), ()))
VMEM = pl.BlockSpec(memory_space=pltpu.VMEM)
SMEM = pl.BlockSpec(memory_space=pltpu.SMEM)
LANES = 128
STEPS = (1, 3, 2)


def params(mib):
    return pltpu.CompilerParams(vmem_limit_bytes=mib << 20)


def copy_for_each(x, axis):
    size = lax.axis_size(axis)
    return lax.all_to_all(jnp.broadcast_to(x[None], (size, *x.shape)), axis, 0, 0, tiled=True)


def turned(x):
    pairs = [(d * 4 + y, y * 4 + d) for d in range(4) for y in range(4)]
    return lax.ppermute(x, (*DP, "y"), pairs)


def round_x(x):
    return [x] + [
        lax.ppermute(x, "x", [(k, (k + step) % 4) for k in range(4)]) for step in STEPS
    ]


def over_y_and_x(x):
    half = x.shape[1] // 2
    lower = jnp.stack(round_x(x[:, half:]))
    upper = copy_for_each(x[:, :half], "y")
    upper = round_x(upper)
    lower = copy_for_each(lower, "y")
    return upper, lower


def gathered_z(x):
    x = turned(x)
    return copy_for_each(x, "z_high")


def senders():
    here = lax.axis_index("x")
    return jnp.stack([here] + [(here + 4 - step) % 4 for step in STEPS]).astype(jnp.int32)


def solve_kernel(weight_ref, mask_ref, factor_ref, errors_ref):
    size = factor_ref.shape[0]
    step = 8
    count = size // step
    factor = factor_ref[...]
    row = lax.broadcasted_iota(jnp.int32, (size, size), 0)
    col = lax.broadcasted_iota(jnp.int32, (size, size), 1)
    pivots = jnp.sum(jnp.where(row == col, factor, 0.0), axis=1, keepdims=True)
    kept = mask_ref[...].astype(jnp.float32).T
    cutting = (1.0 - kept) / pivots
    current = weight_ref[...].astype(jnp.float32).T
    turned_factor = factor.T
    cur = [current[b * step : (b + 1) * step] for b in range(count)]
    fac = [turned_factor[b * step : (b + 1) * step] for b in range(count)]
    wide = (step, current.shape[1])
    place = lax.broadcasted_iota(jnp.int32, wide, 0)
    done = []
    for b in range(count):
        block = cur[b]
        cut_block = cutting[b * step : (b + 1) * step]
        fresh = []
        for i in range(step):
            j = b * step + i
            value = jnp.broadcast_to(cut_block[i : i + 1] * block[i : i + 1], wide)
            fresh.append(value)
            if i + 1 < step:
                reach = jnp.broadcast_to(fac[b][:, j : j + 1], wide)
                block = block - jnp.where(place > i, reach, 0.0) * value
        for v in range(b + 1, count):
            total = cur[v]
            for i in range(step):
                j = b * step + i
                total = total - jnp.broadcast_to(fac[v][:, j : j + 1], wide) * fresh[i]
            cur[v] = total
        rows = fresh[0]
        for i in range(1, step):
            rows = jnp.where(place == i, fresh[i], rows)
        done.append(rows)
    errors_ref[...] = jnp.concatenate(done, axis=0).T


def solved_errors(first_weight, mask, factor):
    return pl.pallas_call(
        solve_kernel,
        out_shape=jax.ShapeDtypeStruct(first_weight.shape, jnp.float32),
        in_specs=[VMEM] * 3,
        out_specs=VMEM,
        name="solve",
        compiler_params=params(8),
        cost_estimate=pl.CostEstimate(flops=20_000_000, bytes_accessed=300_000, transcendentals=0),
    )(first_weight, mask, factor)


def columns_at(ref, block):
    return ref[:, pl.ds(pl.multiple_of(block * LANES, LANES), LANES)]


def side_by_side(upper, lower_ref, y):
    high = jnp.concatenate([upper[r][y, z] for r in range(4) for z in range(4)], axis=1)
    low = jnp.concatenate([lower_ref[y, r, z] for r in range(4) for z in range(4)], axis=1)
    return jnp.concatenate([high, low], axis=0)


def project_kernel(from_ref, a0, a1, a2, a3, lower_ref, weight_ref, out_ref):
    upper = (a0, a1, a2, a3)
    weight = jnp.concatenate(
        [columns_at(weight_ref, z * 4 + from_ref[r]) for r in range(4) for z in range(4)], axis=1
    )
    for y in range(4):
        tokens = side_by_side(upper, lower_ref, y)
        out_ref[y] = lax.dot_general(
            tokens, weight, NT, preferred_element_type=jnp.float32
        )[:LANES].astype(out_ref.dtype)


def scale_kernel(from_ref, weight_ref, gain_ref, out_ref):
    for r in range(4):
        for z in range(4):
            gain = gain_ref[r, z, :1].astype(jnp.float32)
            k = r * 4 + z
            out_ref[:, k * LANES : (k + 1) * LANES] = (
                columns_at(weight_ref, z * 4 + from_ref[r]).astype(jnp.float32) * gain
            ).astype(jnp.bfloat16)


def gate_up_kernel(a0, a1, a2, a3, lower_ref, weight_ref, out_ref):
    weight = weight_ref[...]
    units = weight.shape[0]
    ones = jnp.ones((8, LANES), jnp.float32)
    for y in range(4):
        tokens = side_by_side((a0, a1, a2, a3), lower_ref, y)
        part = lax.dot_general(weight, tokens, NT, preferred_element_type=jnp.float32)
        wide = tokens.astype(jnp.float32)
        square = wide * wide
        folded = square[:, :LANES]
        for k in range(1, square.shape[1] // LANES):
            folded = folded + square[:, k * LANES : (k + 1) * LANES]
        total = lax.dot_general(
            ones, folded, NT, precision=lax.Precision.HIGHEST, preferred_element_type=jnp.float32
        )
        high = total.astype(jnp.bfloat16)
        rest = (total - high.astype(jnp.float32)).astype(jnp.bfloat16)
        out_ref[y, :units, :] = part.astype(jnp.bfloat16)
        out_ref[y, units:, :] = jnp.concatenate([high, rest], axis=0)


def hessian_kernel(from_ref, rows_ref, a0, a1, a2, a3, lower_ref, out_ref, right_ref):
    upper = (a0, a1, a2, a3)
    units = rows_ref.shape[1]
    half = units // 2
    for r in range(4):
        base = from_ref[r] * units
        for y in range(4):
            lanes = slice(y * LANES, (y + 1) * LANES)
            right_ref[pl.ds(pl.multiple_of(base, 16), half), lanes] = upper[r][y, 0]
            right_ref[pl.ds(pl.multiple_of(base + half, 16), half), lanes] = lower_ref[y, r, 0]
    left = jnp.concatenate([rows_ref[t] for t in range(4)], axis=1)
    out_ref[...] = (2.0 / 512) * lax.dot_general(
        left, right_ref[...], NT, preferred_element_type=jnp.float32
    )


def body(attn_out, residual, output_weight, prune_mask, inverse_factor, norm_gain, gate_up_weight):
    width_block = prune_mask.shape[1]
    units = gate_up_weight.shape[2]
    kept_mask = prune_mask.astype(jnp.float32)
    is_first = (lax.axis_index("z_low") == 0) & (lax.axis_index("core") == 0)
    order = senders()

    gain_rows = jnp.broadcast_to(norm_gain[None], (16, norm_gain.shape[0]))
    upper, lower = over_y_and_x(gathered_z(jnp.concatenate([attn_out, gain_rows], axis=0)))
    flat_weight = gate_up_weight.transpose(1, 2, 0).reshape(2 * units, -1)

    solved = solved_errors(
        output_weight[:, :width_block], prune_mask, inverse_factor[:, :width_block]
    )
    errors = lax.all_gather(solved, DP)[0]
    weight_cols = output_weight.astype(jnp.float32)
    updated = weight_cols - jnp.dot(
        errors, inverse_factor, precision=lax.Precision.HIGHEST, preferred_element_type=jnp.float32
    )
    leading = jnp.where(is_first, updated[:, :width_block] * kept_mask, updated[:, :width_block])
    pruned_weight = lax.dynamic_update_slice_in_dim(updated, leading, 0, 1).astype(jnp.bfloat16)

    parts = pl.pallas_call(
        project_kernel,
        out_shape=jax.ShapeDtypeStruct((4, 128, 128), jnp.bfloat16),
        in_specs=[SMEM] + [VMEM] * 6,
        out_specs=VMEM,
        name="project",
        compiler_params=params(10),
        cost_estimate=pl.CostEstimate(flops=268_000_000, bytes_accessed=2_700_000, transcendentals=0),
    )(order, *upper, lower, pruned_weight)
    parts = lax.all_to_all(parts, DP, 0, 0, tiled=True)
    projected = jnp.sum(parts.astype(jnp.float32), axis=0)
    stream = (residual.astype(jnp.float32) + projected).astype(jnp.bfloat16)

    gains = lower[0, :, :, -16:]
    scaled_weight = pl.pallas_call(
        scale_kernel,
        out_shape=jax.ShapeDtypeStruct(flat_weight.shape, jnp.bfloat16),
        in_specs=[SMEM] + [VMEM] * 2,
        out_specs=VMEM,
        name="scale",
        compiler_params=params(16),
        cost_estimate=pl.CostEstimate(flops=2_000_000, bytes_accessed=3_700_000, transcendentals=0),
    )(order, flat_weight, gains)
    upper, lower = over_y_and_x(gathered_z(stream))
    parts = pl.pallas_call(
        gate_up_kernel,
        out_shape=jax.ShapeDtypeStruct((4, 2 * units + 16, 128), jnp.bfloat16),
        in_specs=[VMEM] * 6,
        out_specs=VMEM,
        name="gate_up",
        compiler_params=params(14),
        cost_estimate=pl.CostEstimate(flops=940_000_000, bytes_accessed=4_300_000, transcendentals=0),
    )(*upper, lower, scaled_weight)
    parts = lax.all_to_all(parts, DP, 0, 0, tiled=True)
    sums = jnp.sum(parts.astype(jnp.float32), axis=0)
    square = sums[2 * units : 2 * units + 1] + sums[2 * units + 8 : 2 * units + 9]
    inverse = lax.rsqrt(square / 8192 + 1e-05)
    gate_part = sums[:units] * inverse
    up_part = sums[units : 2 * units] * inverse
    hidden = (jax.nn.silu(gate_part) * up_part).astype(jnp.bfloat16)

    upper, lower = over_y_and_x(gathered_z(hidden))
    hidden_rows = lax.all_gather(hidden, DP)
    piece = pl.BlockSpec((4, 1, units // 2, 128), lambda z: (0, z, 0, 0))
    hessian = pl.pallas_call(
        hessian_kernel,
        grid=(4,),
        out_shape=jax.ShapeDtypeStruct((units, 16 * units), jnp.float32),
        in_specs=[
            SMEM,
            pl.BlockSpec((4, units, 128), lambda z: (0, 0, 0)),
            *[piece] * 4,
            pl.BlockSpec((4, 4, 1, units // 2, 128), lambda z: (0, 0, z, 0, 0)),
        ],
        out_specs=pl.BlockSpec((units, 4 * units), lambda z: (0, z)),
        scratch_shapes=[pltpu.VMEM((4 * units, 4 * LANES), jnp.bfloat16)],
        name="hessian",
        compiler_params=params(14),
        cost_estimate=pl.CostEstimate(flops=822_000_000, bytes_accessed=7_100_000, transcendentals=0),
    )(order, hidden_rows, *upper, lower)
    return (pruned_weight, stream, hessian)


def solution(mesh):
    split = Mesh(mesh.devices.reshape(2, 2, 4, 4, 4), (*DP, *MP))
    return jax.shard_map(
        body,
        mesh=split,
        in_specs=(
            P(DP, MP),
            P(DP, MP),
            P(MP, DP),
            P(MP, None),
            P(None, DP),
            P(MP),
            P(DP, None, MP),
        ),
        out_specs=(P(MP, DP), P(DP, MP), P(MP, DP)),
        check_vma=False,
    )
```

profile of v0, /device:TPU:1, one launch (start us, length us, event | category | flops | bytes accessed | tf_op | source)
XLA Modules:
  0.0 217.9 jit_solution(9413405866704249865)
XLA Ops:
  2.0 4.6 %collective-permute-start = (bf16[144,128]{1,0:T(8,128)(2,1)S(1)}, bf16[144,128]{1,0:T(8,128)(2,1)S(1)}, u32[]{:S(2)}, u32[]{:S(2)}) collective-permute-start(bf16[144,128]{1,0:T(8,128)(2,1)S(1)} %pad_maximum_fusion.3), channel_id=1, source_target_pairs={{0,0},{16,64},{32,128},{48,192},{64,16},{80,80},{96,144},{112,208}... | collective-permute-start | bytes 110600 | tf_op jit(solution)/shard_map/ppermute | solution.py:30
  6.6 1.6 collective-permute-done
  8.3 15.6 %all_to_all.55 = bf16[4,144,128]{2,1,0:T(8,128)(2,1)S(1)} all-to-all(bf16[4,144,128]{2,1,0:T(8,128)(2,1)S(1)} %broadcast_in_dim.21), channel_id=1, replica_groups=mesh['z_low'=2,'core'=2,'y'=4,'z_high'=4,'x'=4] {'z_high'}, dimensions={0} | all-to-all | bytes 294912 | tf_op jit(solution)/shard_map/all_to_all | solution.py:25
  24.7 5.9 %all-to-all-start.1 = ((bf16[4,4,72,128]{3,2,1,0:T(8,128)(2,1)}), bf16[4,4,72,128]{3,2,1,0:T(8,128)(2,1)S(1)}, u32[]{:S(2)}, u32[]{:S(2)}) async-start(bf16[4,4,72,128]{3,2,1,0:T(8,128)(2,1)} %broadcast_in_dim.22), calls=%async_computation.1 | async-start | bytes 589824 | tf_op jit(solution)/shard_map/all_to_all | solution.py:25
  30.6 2.5 %collective-permute-start.5 = (bf16[4,72,128]{2,1,0:T(8,128)(2,1)S(1)}, bf16[4,72,128]{2,1,0:T(8,128)(2,1)S(1)}, u32[]{:S(2)}, u32[]{:S(2)}) collective-permute-start(bf16[4,72,128]{2,1,0:T(8,128)(2,1)S(1)} %get-tuple-element.7), channel_id=1, source_target_pairs={{0,3},{1,0},{2,1},{3,2},{4,7},{5,4},{6,5},{7,6},{8,11},{9,8},{10,9... | collective-permute-start | bytes 221192 | tf_op jit(solution)/shard_map/ppermute | solution.py:35
  33.1 1.7 collective-permute-start.6
  34.8 3.5 %collective-permute-done.4 = bf16[4,72,128]{2,1,0:T(8,128)(2,1)S(1)} collective-permute-done((bf16[4,72,128]{2,1,0:T(8,128)(2,1)S(1)}, bf16[4,72,128]{2,1,0:T(8,128)(2,1)S(1)}, u32[]{:S(2)}, u32[]{:S(2)}) %collective-permute-start.4) | collective-permute-done | bytes 73760 | tf_op jit(solution)/shard_map/ppermute | solution.py:35
  38.4 1.2 broadcast_in_dim.23
  39.6 4.2 %all-to-all-start.2 = ((bf16[4,4,4,72,128]{4,3,2,1,0:T(8,128)(2,1)}), bf16[4,4,4,72,128]{4,3,2,1,0:T(8,128)(2,1)S(1)}, u32[]{:S(2)}, u32[]{:S(2)}) async-start(bf16[4,4,4,72,128]{4,3,2,1,0:T(8,128)(2,1)} %broadcast_in_dim.23), calls=%async_computation.2 | async-start | bytes 2359296 | tf_op jit(solution)/shard_map/all_to_all | solution.py:25
  43.9 2.2 solve.1
  46.1 11.2 %all-gather = f32[512,128]{1,0:T(8,128)S(1)} all-gather(f32[128,128]{1,0:T(8,128)S(1)} %solve.1), channel_id=2, replica_groups=mesh['z_low'=2,'core'=2,'y'=4,'z_high'=4,'x'=4] {'z_low','core'}, dimensions={0}, use_global_device_ids=true | all-gather | bytes 327680 | tf_op jit(solution)/shard_map/all_gather | solution.py:194
  57.2 1.0 convolution_subtract_fusion
  58.2 1.6 collective-permute-start.3
  59.8 1.0 collective-permute-start.2
  61.6 6.7 %collective-permute-done.3.a3 = bf16[4,4,72,128]{3,2,1,0:T(8,128)(2,1)S(1)} collective-permute-done((bf16[4,4,72,128]{3,2,1,0:T(8,128)(2,1)S(1)}, bf16[4,4,72,128]{3,2,1,0:T(8,128)(2,1)S(1)}, u32[]{:S(2)}, u32[]{:S(2)}) %collective-permute-start.3) | collective-permute-done | bytes 294944 | tf_op jit(solution)/shard_map/ppermute | solution.py:35
  68.3 6.4 %collective-permute-done.2.a2 = bf16[4,4,72,128]{3,2,1,0:T(8,128)(2,1)S(1)} collective-permute-done((bf16[4,4,72,128]{3,2,1,0:T(8,128)(2,1)S(1)}, bf16[4,4,72,128]{3,2,1,0:T(8,128)(2,1)S(1)}, u32[]{:S(2)}, u32[]{:S(2)}) %collective-permute-start.2) | collective-permute-done | bytes 294944 | tf_op jit(solution)/shard_map/ppermute | solution.py:35
  75.1 1.3 project.1
  76.4 6.6 %all_to_all.56 = bf16[4,128,128]{2,1,0:T(8,128)(2,1)S(1)} all-to-all(bf16[4,128,128]{2,1,0:T(8,128)(2,1)S(1)} %project.1), channel_id=1, replica_groups=mesh['z_low'=2,'core'=2,'y'=4,'z_high'=4,'x'=4] {'z_low','core'}, dimensions={0} | all-to-all | bytes 262144 | tf_op jit(solution)/shard_map/all_to_all | solution.py:211
  83.0 4.6 %collective-permute-start.7 = (bf16[128,128]{1,0:T(8,128)(2,1)S(1)}, bf16[128,128]{1,0:T(8,128)(2,1)S(1)}, u32[]{:S(2)}, u32[]{:S(2)}) collective-permute-start(bf16[128,128]{1,0:T(8,128)(2,1)S(1)} %add_convert_fusion), channel_id=1, source_target_pairs={{0,0},{16,64},{32,128},{48,192},{64,16},{80,80},{96,144},{112,208}... | collective-permute-start | bytes 98312 | tf_op jit(solution)/shard_map/ppermute | solution.py:30
  87.6 1.6 collective-permute-done.7
  89.2 9.6 %all_to_all.57 = bf16[4,128,128]{2,1,0:T(8,128)(2,1)S(1)} all-to-all(bf16[4,128,128]{2,1,0:T(8,128)(2,1)S(1)} %broadcast_in_dim.24), channel_id=1, replica_groups=mesh['z_low'=2,'core'=2,'y'=4,'z_high'=4,'x'=4] {'z_high'}, dimensions={0} | all-to-all | bytes 262144 | tf_op jit(solution)/shard_map/all_to_all | solution.py:25
  99.6 5.6 %all-to-all-start.5 = ((bf16[4,4,64,128]{3,2,1,0:T(8,128)(2,1)}), bf16[4,4,64,128]{3,2,1,0:T(8,128)(2,1)S(1)}, u32[]{:S(2)}, u32[]{:S(2)}) async-start(bf16[4,4,64,128]{3,2,1,0:T(8,128)(2,1)} %broadcast_in_dim.25), calls=%async_computation.5 | async-start | bytes 524288 | tf_op jit(solution)/shard_map/all_to_all | solution.py:25
  105.2 2.2 collective-permute-start.12
  107.3 1.2 collective-permute-start.13
  108.7 3.7 %collective-permute-done.11 = bf16[4,64,128]{2,1,0:T(8,128)(2,1)S(1)} collective-permute-done((bf16[4,64,128]{2,1,0:T(8,128)(2,1)S(1)}, bf16[4,64,128]{2,1,0:T(8,128)(2,1)S(1)}, u32[]{:S(2)}, u32[]{:S(2)}) %collective-permute-start.11) | collective-permute-done | bytes 65568 | tf_op jit(solution)/shard_map/ppermute | solution.py:35
  112.4 1.2 broadcast_in_dim.26
  113.7 4.2 %all-to-all-start.6 = ((bf16[4,4,4,64,128]{4,3,2,1,0:T(8,128)(2,1)}), bf16[4,4,4,64,128]{4,3,2,1,0:T(8,128)(2,1)S(1)}, u32[]{:S(2)}, u32[]{:S(2)}) async-start(bf16[4,4,4,64,128]{4,3,2,1,0:T(8,128)(2,1)} %broadcast_in_dim.26), calls=%async_computation.6 | async-start | bytes 2097152 | tf_op jit(solution)/shard_map/all_to_all | solution.py:25
  117.9 1.1 collective-permute-start.10
  119.0 1.3 collective-permute-start.9
  120.8 1.5 copy-done.1
  122.3 1.1 scale.1.weight_ref
  123.4 1.3 collective-permute-done.10.a3
  124.7 3.0 %collective-permute-done.9.a2 = bf16[4,4,64,128]{3,2,1,0:T(8,128)(2,1)S(1)} collective-permute-done((bf16[4,4,64,128]{3,2,1,0:T(8,128)(2,1)S(1)}, bf16[4,4,64,128]{3,2,1,0:T(8,128)(2,1)S(1)}, u32[]{:S(2)}, u32[]{:S(2)}) %collective-permute-start.9) | collective-permute-done | bytes 262176 | tf_op jit(solution)/shard_map/ppermute | solution.py:35
  131.0 2.5 %gate_up.1 = bf16[4,464,128]{2,1,0:T(8,128)(2,1)S(1)} custom-call(bf16[4,4,64,128]{3,2,1,0:T(8,128)(2,1)S(1)} %all-to-all-done.5.a0, bf16[4,4,64,128]{3,2,1,0:T(8,128)(2,1)S(1)} %copy-done.7, bf16[4,4,64,128]{3,2,1,0:T(8,128)(2,1)S(1)} %copy-done.5, bf16[4,4,64,128]{3,2,1,0:T(8,128)(2,1)S(1)} %collective-permute-done.10.a3, ...), custom_call_target="tpu_custom_call" | custom-call | flops 940000000 | bytes 4300000 | tf_op jit(solution)/shard_map/gate_up/pallas_call | solution.py:226
  133.5 16.7 %all_to_all.58 = bf16[4,464,128]{2,1,0:T(8,128)(2,1)S(1)} all-to-all(bf16[4,464,128]{2,1,0:T(8,128)(2,1)S(1)} %gate_up.1), channel_id=1, replica_groups=mesh['z_low'=2,'core'=2,'y'=4,'z_high'=4,'x'=4] {'z_low','core'}, dimensions={0} | all-to-all | bytes 950272 | tf_op jit(solution)/shard_map/all_to_all | solution.py:235
  150.3 4.4 %collective-permute-start.14 = (bf16[224,128]{1,0:T(8,128)(2,1)S(1)}, bf16[224,128]{1,0:T(8,128)(2,1)S(1)}, u32[]{:S(2)}, u32[]{:S(2)}) collective-permute-start(bf16[224,128]{1,0:T(8,128)(2,1)S(1)} %fusion.1), channel_id=1, source_target_pairs={{0,0},{16,64},{32,128},{48,192},{64,16},{80,80},{96,144},{112,208}... | collective-permute-start | bytes 172040 | tf_op jit(solution)/shard_map/ppermute | solution.py:30
  154.7 1.8 collective-permute-done.14
  156.6 10.5 %all_to_all.59 = bf16[4,224,128]{2,1,0:T(8,128)(2,1)S(1)} all-to-all(bf16[4,224,128]{2,1,0:T(8,128)(2,1)S(1)} %broadcast_in_dim.27), channel_id=1, replica_groups=mesh['z_low'=2,'core'=2,'y'=4,'z_high'=4,'x'=4] {'z_high'}, dimensions={0} | all-to-all | bytes 458752 | tf_op jit(solution)/shard_map/all_to_all | solution.py:25
  167.9 7.0 %all-to-all-start.9 = ((bf16[4,4,112,128]{3,2,1,0:T(8,128)(2,1)}), bf16[4,4,112,128]{3,2,1,0:T(8,128)(2,1)S(1)}, u32[]{:S(2)}, u32[]{:S(2)}) async-start(bf16[4,4,112,128]{3,2,1,0:T(8,128)(2,1)} %broadcast_in_dim.28), calls=%async_computation.9 | async-start | bytes 917504 | tf_op jit(solution)/shard_map/all_to_all | solution.py:25
  175.0 2.1 collective-permute-start.19
  177.0 1.2 collective-permute-start.20
  178.8 4.6 %collective-permute-done.18 = bf16[4,112,128]{2,1,0:T(8,128)(2,1)S(1)} collective-permute-done((bf16[4,112,128]{2,1,0:T(8,128)(2,1)S(1)}, bf16[4,112,128]{2,1,0:T(8,128)(2,1)S(1)}, u32[]{:S(2)}, u32[]{:S(2)}) %collective-permute-start.18) | collective-permute-done | bytes 114720 | tf_op jit(solution)/shard_map/ppermute | solution.py:35
  183.5 1.6 broadcast_in_dim.29
  185.1 3.9 %all-to-all-start.10 = ((bf16[4,4,4,112,128]{4,3,2,1,0:T(8,128)(2,1)}), bf16[4,4,4,112,128]{4,3,2,1,0:T(8,128)(2,1)S(1)}, u32[]{:S(2)}, u32[]{:S(2)}) async-start(bf16[4,4,4,112,128]{4,3,2,1,0:T(8,128)(2,1)} %broadcast_in_dim.29), calls=%async_computation.10 | async-start | bytes 3670016 | tf_op jit(solution)/shard_map/all_to_all | solution.py:25
  189.4 2.2 %collective-permute-start.16 = (bf16[4,4,112,128]{3,2,1,0:T(8,128)(2,1)S(1)}, bf16[4,4,112,128]{3,2,1,0:T(8,128)(2,1)S(1)}, u32[]{:S(2)}, u32[]{:S(2)}) collective-permute-start(bf16[4,4,112,128]{3,2,1,0:T(8,128)(2,1)S(1)} %all-to-all-done.9.a0), channel_id=1, source_target_pairs={{0,3},{1,0},{2,1},{3,2},{4,7},{5,4},{6,5},{7,6},{8,11},{9,8},{10,9... | collective-permute-start | bytes 1376264 | tf_op jit(solution)/shard_map/ppermute | solution.py:35
  192.2 10.1 %all-gather.1 = bf16[896,128]{1,0:T(8,128)(2,1)S(1)} all-gather(bf16[224,128]{1,0:T(8,128)(2,1)S(1)} %fusion.1), channel_id=3, replica_groups=mesh['z_low'=2,'core'=2,'y'=4,'z_high'=4,'x'=4] {'z_low','core'}, dimensions={0}, use_global_device_ids=true | all-gather | bytes 286720 | tf_op jit(solution)/shard_map/all_gather | solution.py:244
  202.3 9.1 %collective-permute-done.16.a2 = bf16[4,4,112,128]{3,2,1,0:T(8,128)(2,1)S(1)} collective-permute-done((bf16[4,4,112,128]{3,2,1,0:T(8,128)(2,1)S(1)}, bf16[4,4,112,128]{3,2,1,0:T(8,128)(2,1)S(1)}, u32[]{:S(2)}, u32[]{:S(2)}) %collective-permute-start.16) | collective-permute-done | bytes 458784 | tf_op jit(solution)/shard_map/ppermute | solution.py:35
  213.5 4.4 %hessian.1 = f32[224,3584]{1,0:T(8,128)} custom-call(s32[4]{0:T(128)S(1)} %pad_add_fusion.from_ref, bf16[4,224,128]{2,1,0:T(8,128)(2,1)S(1)} %bitcast.29, bf16[4,4,112,128]{3,2,1,0:T(8,128)(2,1)S(1)} %all-to-all-done.9.a0, bf16[4,4,112,128]{3,2,1,0:T(8,128)(2,1)S(1)} %copy-done.3, bf16[4,4,112,128]{3,2,1,0:T(8,128)(2,1)S(1)} %collective-permute-done.16.a2, ...), custom_call_target="tpu_custom_call" | custom-call | flops 822000000 | bytes 7100000 | tf_op jit(solution)/shard_map/hessian/pallas_call | solution.py:246
  (73 shorter events, 13.1 us)
Async XLA Ops:
  2.0 6.2 %collective-permute-start = (bf16[144,128]{1,0:T(8,128)(2,1)S(1)}, bf16[144,128]{1,0:T(8,128)(2,1)S(1)}, u32[]{:S(2)}, u32[]{:S(2)}) collective-permute-start(bf16[144,128]{1,0:T(8,128)(2,1)S(1)} %pad_maximum_fusion.3), channel_id=1, source_target_pairs={{0,0},{16,64},{32,128},{48,192},{64,16},{80,80},{96,144},{112,208}... | collective-permute-start | bytes 110600 | tf_op jit(solution)/shard_map/ppermute | solution.py:30
  24.7 13.7 %all-to-all-start.1 = ((bf16[4,4,72,128]{3,2,1,0:T(8,128)(2,1)}), bf16[4,4,72,128]{3,2,1,0:T(8,128)(2,1)S(1)}, u32[]{:S(2)}, u32[]{:S(2)}) async-start(bf16[4,4,72,128]{3,2,1,0:T(8,128)(2,1)} %broadcast_in_dim.22), calls=%async_computation.1 | async-start | bytes 589824 | tf_op jit(solution)/shard_map/all_to_all | solution.py:25
  30.6 4.2 %collective-permute-start.5 = (bf16[4,72,128]{2,1,0:T(8,128)(2,1)S(1)}, bf16[4,72,128]{2,1,0:T(8,128)(2,1)S(1)}, u32[]{:S(2)}, u32[]{:S(2)}) collective-permute-start(bf16[4,72,128]{2,1,0:T(8,128)(2,1)S(1)} %get-tuple-element.7), channel_id=1, source_target_pairs={{0,3},{1,0},{2,1},{3,2},{4,7},{5,4},{6,5},{7,6},{8,11},{9,8},{10,9... | collective-permute-start | bytes 221192 | tf_op jit(solution)/shard_map/ppermute | solution.py:35
  33.1 5.2 %collective-permute-start.4 = (bf16[4,72,128]{2,1,0:T(8,128)(2,1)S(1)}, bf16[4,72,128]{2,1,0:T(8,128)(2,1)S(1)}, u32[]{:S(2)}, u32[]{:S(2)}) collective-permute-start(bf16[4,72,128]{2,1,0:T(8,128)(2,1)S(1)} %get-tuple-element.7), channel_id=1, source_target_pairs={{0,1},{1,2},{2,3},{3,0},{4,5},{5,6},{6,7},{7,4},{8,9},{9,10},{10,1... | collective-permute-start | bytes 221192 | tf_op jit(solution)/shard_map/ppermute | solution.py:35
  33.1 5.2 %collective-permute-start.6 = (bf16[4,72,128]{2,1,0:T(8,128)(2,1)S(1)}, bf16[4,72,128]{2,1,0:T(8,128)(2,1)S(1)}, u32[]{:S(2)}, u32[]{:S(2)}) collective-permute-start(bf16[4,72,128]{2,1,0:T(8,128)(2,1)S(1)} %get-tuple-element.7), channel_id=1, source_target_pairs={{0,2},{1,3},{2,0},{3,1},{4,6},{5,7},{6,4},{7,5},{8,10},{9,11},{10,... | collective-permute-start | bytes 221192 | tf_op jit(solution)/shard_map/ppermute | solution.py:35
  38.4 5.5 %copy-start.10 = (bf16[128,2048]{1,0:T(8,128)(2,1)S(1)}, bf16[128,2048]{1,0:T(8,128)(2,1)}, u32[]{:S(2)}) copy-start(bf16[128,2048]{1,0:T(8,128)(2,1)} %param.9) | copy-start | bytes 1572868
  38.4 5.5 %copy-start.9 = (f32[128,2048]{1,0:T(8,128)S(1)}, f32[128,2048]{1,0:T(8,128)}, u32[]{:S(2)}) copy-start(f32[128,2048]{1,0:T(8,128)} %param.11) | copy-start | bytes 3145732
  38.4 5.5 %copy-start.8 = (s32[128,128]{1,0:T(8,128)S(1)}, s32[128,128]{1,0:T(8,128)}, u32[]{:S(2)}) copy-start(s32[128,128]{1,0:T(8,128)} %mask_ref.1) | copy-start | bytes 196612
  39.6 35.5 %all-to-all-start.2 = ((bf16[4,4,4,72,128]{4,3,2,1,0:T(8,128)(2,1)}), bf16[4,4,4,72,128]{4,3,2,1,0:T(8,128)(2,1)S(1)}, u32[]{:S(2)}, u32[]{:S(2)}) async-start(bf16[4,4,4,72,128]{4,3,2,1,0:T(8,128)(2,1)} %broadcast_in_dim.23), calls=%async_computation.2 | async-start | bytes 2359296 | tf_op jit(solution)/shard_map/all_to_all | solution.py:25
  58.2 10.0 %collective-permute-start.3 = (bf16[4,4,72,128]{3,2,1,0:T(8,128)(2,1)S(1)}, bf16[4,4,72,128]{3,2,1,0:T(8,128)(2,1)S(1)}, u32[]{:S(2)}, u32[]{:S(2)}) collective-permute-start(bf16[4,4,72,128]{3,2,1,0:T(8,128)(2,1)S(1)} %all-to-all-done.1.a0), channel_id=1, source_target_pairs={{0,2},{1,3},{2,0},{3,1},{4,6},{5,7},{6,4},{7,5},{8,10},{9,11},{10,... | collective-permute-start | bytes 884744 | tf_op jit(solution)/shard_map/ppermute | solution.py:35
  59.8 14.8 %collective-permute-start.2 = (bf16[4,4,72,128]{3,2,1,0:T(8,128)(2,1)S(1)}, bf16[4,4,72,128]{3,2,1,0:T(8,128)(2,1)S(1)}, u32[]{:S(2)}, u32[]{:S(2)}) collective-permute-start(bf16[4,4,72,128]{3,2,1,0:T(8,128)(2,1)S(1)} %all-to-all-done.1.a0), channel_id=1, source_target_pairs={{0,3},{1,0},{2,1},{3,2},{4,7},{5,4},{6,5},{7,6},{8,11},{9,8},{10,9... | collective-permute-start | bytes 884744 | tf_op jit(solution)/shard_map/ppermute | solution.py:35
  60.9 14.2 %collective-permute-start.1 = (bf16[4,4,72,128]{3,2,1,0:T(8,128)(2,1)S(1)}, bf16[4,4,72,128]{3,2,1,0:T(8,128)(2,1)S(1)}, u32[]{:S(2)}, u32[]{:S(2)}) collective-permute-start(bf16[4,4,72,128]{3,2,1,0:T(8,128)(2,1)S(1)} %all-to-all-done.1.a0), channel_id=1, source_target_pairs={{0,1},{1,2},{2,3},{3,0},{4,5},{5,6},{6,7},{7,4},{8,9},{9,10},{10,1... | collective-permute-start | bytes 884744 | tf_op jit(solution)/shard_map/ppermute | solution.py:35
  61.5 27.8 %copy-start = (bf16[128,2048]{1,0:T(8,128)(2,1)}, bf16[128,2048]{1,0:T(8,128)(2,1)S(1)}, u32[]{:S(2)}) copy-start(bf16[128,2048]{1,0:T(8,128)(2,1)S(1)} %convert_element_type.26.weight_ref) | copy-start | bytes 1572868
  61.5 21.5 %copy-start.11 = (bf16[128,128]{1,0:T(8,128)(2,1)S(1)}, bf16[128,128]{1,0:T(8,128)(2,1)}, u32[]{:S(2)}) copy-start(bf16[128,128]{1,0:T(8,128)(2,1)} %param.8) | copy-start | bytes 98308
  83.0 30.7 %copy-start.12 = (bf16[128,128]{1,0:T(8,128)(2,1)}, bf16[128,128]{1,0:T(8,128)(2,1)S(1)}, u32[]{:S(2)}) copy-start(bf16[128,128]{1,0:T(8,128)(2,1)S(1)} %add_convert_fusion) | copy-start | bytes 98308
  83.0 6.2 %collective-permute-start.7 = (bf16[128,128]{1,0:T(8,128)(2,1)S(1)}, bf16[128,128]{1,0:T(8,128)(2,1)S(1)}, u32[]{:S(2)}, u32[]{:S(2)}) collective-permute-start(bf16[128,128]{1,0:T(8,128)(2,1)S(1)} %add_convert_fusion), channel_id=1, source_target_pairs={{0,0},{16,64},{32,128},{48,192},{64,16},{80,80},{96,144},{112,208}... | collective-permute-start | bytes 98312 | tf_op jit(solution)/shard_map/ppermute | solution.py:30
  99.6 12.8 %all-to-all-start.5 = ((bf16[4,4,64,128]{3,2,1,0:T(8,128)(2,1)}), bf16[4,4,64,128]{3,2,1,0:T(8,128)(2,1)S(1)}, u32[]{:S(2)}, u32[]{:S(2)}) async-start(bf16[4,4,64,128]{3,2,1,0:T(8,128)(2,1)} %broadcast_in_dim.25), calls=%async_computation.5 | async-start | bytes 524288 | tf_op jit(solution)/shard_map/all_to_all | solution.py:25
  105.2 3.5 %collective-permute-start.12 = (bf16[4,64,128]{2,1,0:T(8,128)(2,1)S(1)}, bf16[4,64,128]{2,1,0:T(8,128)(2,1)S(1)}, u32[]{:S(2)}, u32[]{:S(2)}) collective-permute-start(bf16[4,64,128]{2,1,0:T(8,128)(2,1)S(1)} %get-tuple-element.10), channel_id=1, source_target_pairs={{0,3},{1,0},{2,1},{3,2},{4,7},{5,4},{6,5},{7,6},{8,11},{9,8},{10,9... | collective-permute-start | bytes 196616 | tf_op jit(solution)/shard_map/ppermute | solution.py:35
  107.3 5.0 %collective-permute-start.11 = (bf16[4,64,128]{2,1,0:T(8,128)(2,1)S(1)}, bf16[4,64,128]{2,1,0:T(8,128)(2,1)S(1)}, u32[]{:S(2)}, u32[]{:S(2)}) collective-permute-start(bf16[4,64,128]{2,1,0:T(8,128)(2,1)S(1)} %get-tuple-element.10), channel_id=1, source_target_pairs={{0,1},{1,2},{2,3},{3,0},{4,5},{5,6},{6,7},{7,4},{8,9},{9,10},{10,1... | collective-permute-start | bytes 196616 | tf_op jit(solution)/shard_map/ppermute | solution.py:35
  107.3 5.0 %collective-permute-start.13 = (bf16[4,64,128]{2,1,0:T(8,128)(2,1)S(1)}, bf16[4,64,128]{2,1,0:T(8,128)(2,1)S(1)}, u32[]{:S(2)}, u32[]{:S(2)}) collective-permute-start(bf16[4,64,128]{2,1,0:T(8,128)(2,1)S(1)} %get-tuple-element.10), channel_id=1, source_target_pairs={{0,2},{1,3},{2,0},{3,1},{4,6},{5,7},{6,4},{7,5},{8,10},{9,11},{10,... | collective-permute-start | bytes 196616 | tf_op jit(solution)/shard_map/ppermute | solution.py:35
  113.7 15.5 %all-to-all-start.6 = ((bf16[4,4,4,64,128]{4,3,2,1,0:T(8,128)(2,1)}), bf16[4,4,4,64,128]{4,3,2,1,0:T(8,128)(2,1)S(1)}, u32[]{:S(2)}, u32[]{:S(2)}) async-start(bf16[4,4,4,64,128]{4,3,2,1,0:T(8,128)(2,1)} %broadcast_in_dim.26), calls=%async_computation.6 | async-start | bytes 2097152 | tf_op jit(solution)/shard_map/all_to_all | solution.py:25
  117.9 6.8 %collective-permute-start.10 = (bf16[4,4,64,128]{3,2,1,0:T(8,128)(2,1)S(1)}, bf16[4,4,64,128]{3,2,1,0:T(8,128)(2,1)S(1)}, u32[]{:S(2)}, u32[]{:S(2)}) collective-permute-start(bf16[4,4,64,128]{3,2,1,0:T(8,128)(2,1)S(1)} %all-to-all-done.5.a0), channel_id=1, source_target_pairs={{0,2},{1,3},{2,0},{3,1},{4,6},{5,7},{6,4},{7,5},{8,10},{9,11},{10,... | collective-permute-start | bytes 786440 | tf_op jit(solution)/shard_map/ppermute | solution.py:35
  119.0 8.8 %collective-permute-start.9 = (bf16[4,4,64,128]{3,2,1,0:T(8,128)(2,1)S(1)}, bf16[4,4,64,128]{3,2,1,0:T(8,128)(2,1)S(1)}, u32[]{:S(2)}, u32[]{:S(2)}) collective-permute-start(bf16[4,4,64,128]{3,2,1,0:T(8,128)(2,1)S(1)} %all-to-all-done.5.a0), channel_id=1, source_target_pairs={{0,3},{1,0},{2,1},{3,2},{4,7},{5,4},{6,5},{7,6},{8,11},{9,8},{10,9... | collective-permute-start | bytes 786440 | tf_op jit(solution)/shard_map/ppermute | solution.py:35
  120.3 8.2 %collective-permute-start.8 = (bf16[4,4,64,128]{3,2,1,0:T(8,128)(2,1)S(1)}, bf16[4,4,64,128]{3,2,1,0:T(8,128)(2,1)S(1)}, u32[]{:S(2)}, u32[]{:S(2)}) collective-permute-start(bf16[4,4,64,128]{3,2,1,0:T(8,128)(2,1)S(1)} %all-to-all-done.5.a0), channel_id=1, source_target_pairs={{0,1},{1,2},{2,3},{3,0},{4,5},{5,6},{6,7},{7,4},{8,9},{9,10},{10,1... | collective-permute-start | bytes 786440 | tf_op jit(solution)/shard_map/ppermute | solution.py:35
  120.8 1.5 copy-start.1
  127.7 0.7 copy-start.4
  128.4 0.7 copy-start.6
  129.1 1.0 copy-start.5
  130.1 0.9 copy-start.7
  150.3 6.2 %collective-permute-start.14 = (bf16[224,128]{1,0:T(8,128)(2,1)S(1)}, bf16[224,128]{1,0:T(8,128)(2,1)S(1)}, u32[]{:S(2)}, u32[]{:S(2)}) collective-permute-start(bf16[224,128]{1,0:T(8,128)(2,1)S(1)} %fusion.1), channel_id=1, source_target_pairs={{0,0},{16,64},{32,128},{48,192},{64,16},{80,80},{96,144},{112,208}... | collective-permute-start | bytes 172040 | tf_op jit(solution)/shard_map/ppermute | solution.py:30
  167.9 15.5 %all-to-all-start.9 = ((bf16[4,4,112,128]{3,2,1,0:T(8,128)(2,1)}), bf16[4,4,112,128]{3,2,1,0:T(8,128)(2,1)S(1)}, u32[]{:S(2)}, u32[]{:S(2)}) async-start(bf16[4,4,112,128]{3,2,1,0:T(8,128)(2,1)} %broadcast_in_dim.28), calls=%async_computation.9 | async-start | bytes 917504 | tf_op jit(solution)/shard_map/all_to_all | solution.py:25
  175.0 3.9 %collective-permute-start.19 = (bf16[4,112,128]{2,1,0:T(8,128)(2,1)S(1)}, bf16[4,112,128]{2,1,0:T(8,128)(2,1)S(1)}, u32[]{:S(2)}, u32[]{:S(2)}) collective-permute-start(bf16[4,112,128]{2,1,0:T(8,128)(2,1)S(1)} %get-tuple-element.4), channel_id=1, source_target_pairs={{0,3},{1,0},{2,1},{3,2},{4,7},{5,4},{6,5},{7,6},{8,11},{9,8},{10,9... | collective-permute-start | bytes 344072 | tf_op jit(solution)/shard_map/ppermute | solution.py:35
  177.0 6.4 %collective-permute-start.18 = (bf16[4,112,128]{2,1,0:T(8,128)(2,1)S(1)}, bf16[4,112,128]{2,1,0:T(8,128)(2,1)S(1)}, u32[]{:S(2)}, u32[]{:S(2)}) collective-permute-start(bf16[4,112,128]{2,1,0:T(8,128)(2,1)S(1)} %get-tuple-element.4), channel_id=1, source_target_pairs={{0,1},{1,2},{2,3},{3,0},{4,5},{5,6},{6,7},{7,4},{8,9},{9,10},{10,1... | collective-permute-start | bytes 344072 | tf_op jit(solution)/shard_map/ppermute | solution.py:35
  177.0 6.4 %collective-permute-start.20 = (bf16[4,112,128]{2,1,0:T(8,128)(2,1)S(1)}, bf16[4,112,128]{2,1,0:T(8,128)(2,1)S(1)}, u32[]{:S(2)}, u32[]{:S(2)}) collective-permute-start(bf16[4,112,128]{2,1,0:T(8,128)(2,1)S(1)} %get-tuple-element.4), channel_id=1, source_target_pairs={{0,2},{1,3},{2,0},{3,1},{4,6},{5,7},{6,4},{7,5},{8,10},{9,11},{10,... | collective-permute-start | bytes 344072 | tf_op jit(solution)/shard_map/ppermute | solution.py:35
  185.1 27.4 %all-to-all-start.10 = ((bf16[4,4,4,112,128]{4,3,2,1,0:T(8,128)(2,1)}), bf16[4,4,4,112,128]{4,3,2,1,0:T(8,128)(2,1)S(1)}, u32[]{:S(2)}, u32[]{:S(2)}) async-start(bf16[4,4,4,112,128]{4,3,2,1,0:T(8,128)(2,1)} %broadcast_in_dim.29), calls=%async_computation.10 | async-start | bytes 3670016 | tf_op jit(solution)/shard_map/all_to_all | solution.py:25
  189.0 13.3 %collective-permute-start.17 = (bf16[4,4,112,128]{3,2,1,0:T(8,128)(2,1)S(1)}, bf16[4,4,112,128]{3,2,1,0:T(8,128)(2,1)S(1)}, u32[]{:S(2)}, u32[]{:S(2)}) collective-permute-start(bf16[4,4,112,128]{3,2,1,0:T(8,128)(2,1)S(1)} %all-to-all-done.9.a0), channel_id=1, source_target_pairs={{0,2},{1,3},{2,0},{3,1},{4,6},{5,7},{6,4},{7,5},{8,10},{9,11},{10,... | collective-permute-start | bytes 1376264 | tf_op jit(solution)/shard_map/ppermute | solution.py:35
  189.4 22.0 %collective-permute-start.16 = (bf16[4,4,112,128]{3,2,1,0:T(8,128)(2,1)S(1)}, bf16[4,4,112,128]{3,2,1,0:T(8,128)(2,1)S(1)}, u32[]{:S(2)}, u32[]{:S(2)}) collective-permute-start(bf16[4,4,112,128]{3,2,1,0:T(8,128)(2,1)S(1)} %all-to-all-done.9.a0), channel_id=1, source_target_pairs={{0,3},{1,0},{2,1},{3,2},{4,7},{5,4},{6,5},{7,6},{8,11},{9,8},{10,9... | collective-permute-start | bytes 1376264 | tf_op jit(solution)/shard_map/ppermute | solution.py:35
  191.6 20.1 %collective-permute-start.15 = (bf16[4,4,112,128]{3,2,1,0:T(8,128)(2,1)S(1)}, bf16[4,4,112,128]{3,2,1,0:T(8,128)(2,1)S(1)}, u32[]{:S(2)}, u32[]{:S(2)}) collective-permute-start(bf16[4,4,112,128]{3,2,1,0:T(8,128)(2,1)S(1)} %all-to-all-done.9.a0), channel_id=1, source_target_pairs={{0,1},{1,2},{2,3},{3,0},{4,5},{5,6},{6,7},{7,4},{8,9},{9,10},{10,1... | collective-permute-start | bytes 1376264 | tf_op jit(solution)/shard_map/ppermute | solution.py:35
  211.7 0.8 copy-start.2
  212.5 1.0 copy-start.3
where the time goes:
time: 219 us; the launch traced here: 218 us
  blocking collectives  80.2 us (37%)
  starting transfers between devices  64.5 us (29%)
  waiting for transfers between devices  44.8 us (20%)
  local copies, waits for them, and re-layouts  13.8 us (6%)
  Pallas kernels  11.4 us (5%)
    ppermute x18, waiting for transfers between devices, round_x(): lax.ppermute(x, 'x', [(k, (k + step) % 4) for k in range(4)])  39.8 us
    all_to_all x3, blocking collectives, copy_for_each(): lax.all_to_all(jnp.broadcast_to(x[None], (size, *x.shape)), axis, 0, 0, t...  35.7 us
    all_to_all x6, starting transfers between devices, copy_for_each(): lax.all_to_all(jnp.broadcast_to(x[None], (size, *x.shape)), axis, 0, 0, t...  30.9 us
    all_to_all x2, blocking collectives, body(): parts = lax.all_to_all(parts, DP, 0, 0, tiled=True)  23.2 us
    ppermute x18, starting transfers between devices, round_x(): lax.ppermute(x, 'x', [(k, (k + step) % 4) for k in range(4)])  20 us
    ppermute x3, starting transfers between devices, turned(): return lax.ppermute(x, (*DP, 'y'), pairs)  13.5 us
    all_gather x1, blocking collectives, body(): errors = lax.all_gather(solved, DP)[0]  11.2 us
    all_gather x1, blocking collectives, body(): hidden_rows = lax.all_gather(hidden, DP)  10.1 us
  transfers between devices with their start and end apart: 27, of which 15 were waited for; matrix products, arithmetic and copies ran while one was open for 1% of the time, Pallas kernels for 1%

commit v1 on v0

--- a/solution.py
+++ b/solution.py
@@ -36,8 +36,7 @@
     ]
 
 
-def over_y_and_x(x):
-    half = x.shape[1] // 2
+def over_y_and_x(x, half):
     lower = jnp.stack(round_x(x[:, half:]))
     upper = copy_for_each(x[:, :half], "y")
     upper = round_x(upper)
@@ -45,8 +44,7 @@
     return upper, lower
 
 
-def gathered_z(x):
-    x = turned(x)
+def over_z(x):
     return copy_for_each(x, "z_high")
 
 
@@ -112,53 +110,70 @@
     return ref[:, pl.ds(pl.multiple_of(block * LANES, LANES), LANES)]
 
 
-def side_by_side(upper, lower_ref, y):
-    high = jnp.concatenate([upper[r][y, z] for r in range(4) for z in range(4)], axis=1)
-    low = jnp.concatenate([lower_ref[y, r, z] for r in range(4) for z in range(4)], axis=1)
-    return jnp.concatenate([high, low], axis=0)
-
-
-def project_kernel(from_ref, a0, a1, a2, a3, lower_ref, weight_ref, out_ref):
+def ordered_columns(ref, from_ref):
+    return jnp.concatenate(
+        [columns_at(ref, z * 4 + from_ref[r]) for r in range(4) for z in range(4)], axis=1
+    )
+
+
+def project_kernel(from_ref, core_ref, *refs):
+    mine, other, weight_ref, out_ref = refs[:4], refs[4:8], refs[8], refs[9]
+    weight = ordered_columns(weight_ref, from_ref)
+    for low in range(2):
+        for source, core in ((mine, core_ref[0]), (other, 1 - core_ref[0])):
+            tokens = jnp.concatenate(
+                [source[r][z * 2 + low] for r in range(4) for z in range(4)], axis=1
+            )
+            out_ref[low * 2 + core] = lax.dot_general(
+                tokens, weight, NT, preferred_element_type=jnp.float32
+            ).astype(out_ref.dtype)
+
+
+def stream_kernel(parts_ref, residual_ref, stream_ref, block_ref):
+    rows = stream_ref.shape[0]
+    total = residual_ref[:rows].astype(jnp.float32)
+    for k in range(4):
+        total = total + parts_ref[k].astype(jnp.float32)
+    stream = total.astype(jnp.bfloat16)
+    stream_ref[...] = stream
+    wide = stream.astype(jnp.float32)
+    gain = residual_ref[rows : rows + 16].astype(jnp.float32)[:1]
+    square = lax.dot_general(
+        jnp.ones((8, LANES), jnp.float32),
+        wide * wide,
+        NT,
+        precision=lax.Precision.HIGHEST,
+        preferred_element_type=jnp.float32,
+    )
+    high = square.astype(jnp.bfloat16).astype(jnp.float32)
+    first = lax.broadcasted_iota(jnp.int32, square.shape, 0) == 0
+    pair = jnp.where(first, high, square - high)
+    block_ref[...] = jnp.concatenate([wide * gain, pair], axis=0).astype(jnp.bfloat16)
+
+
+def gate_up_kernel(from_ref, a0, a1, a2, a3, lower_ref, weight_ref, out_ref):
     upper = (a0, a1, a2, a3)
-    weight = jnp.concatenate(
-        [columns_at(weight_ref, z * 4 + from_ref[r]) for r in range(4) for z in range(4)], axis=1
-    )
+    half = a0.shape[2]
+    weight = ordered_columns(weight_ref, from_ref)
+    units = weight.shape[0]
+    places = [(r, z) for r in range(4) for z in range(4)]
     for y in range(4):
-        tokens = side_by_side(upper, lower_ref, y)
-        out_ref[y] = lax.dot_general(
-            tokens, weight, NT, preferred_element_type=jnp.float32
-        )[:LANES].astype(out_ref.dtype)
-
-
-def scale_kernel(from_ref, weight_ref, gain_ref, out_ref):
-    for r in range(4):
-        for z in range(4):
-            gain = gain_ref[r, z, :1].astype(jnp.float32)
-            k = r * 4 + z
-            out_ref[:, k * LANES : (k + 1) * LANES] = (
-                columns_at(weight_ref, z * 4 + from_ref[r]).astype(jnp.float32) * gain
-            ).astype(jnp.bfloat16)
-
-
-def gate_up_kernel(a0, a1, a2, a3, lower_ref, weight_ref, out_ref):
-    weight = weight_ref[...]
-    units = weight.shape[0]
-    ones = jnp.ones((8, LANES), jnp.float32)
-    for y in range(4):
-        tokens = side_by_side((a0, a1, a2, a3), lower_ref, y)
-        part = lax.dot_general(weight, tokens, NT, preferred_element_type=jnp.float32)
-        wide = tokens.astype(jnp.float32)
-        square = wide * wide
-        folded = square[:, :LANES]
-        for k in range(1, square.shape[1] // LANES):
-            folded = folded + square[:, k * LANES : (k + 1) * LANES]
-        total = lax.dot_general(
-            ones, folded, NT, precision=lax.Precision.HIGHEST, preferred_element_type=jnp.float32
+        high = jnp.concatenate([upper[r][y, z] for r, z in places], axis=1)
+        low = jnp.concatenate([lower_ref[y, r, z, :half] for r, z in places], axis=1)
+        part = lax.dot_general(
+            weight,
+            jnp.concatenate([high, low], axis=0),
+            NT,
+            preferred_element_type=jnp.float32,
         )
-        high = total.astype(jnp.bfloat16)
-        rest = (total - high.astype(jnp.float32)).astype(jnp.bfloat16)
+        square = jnp.zeros((8, LANES), jnp.float32)
+        for r, z in places:
+            square = square + lower_ref[y, r, z, half:].astype(jnp.float32)
+        total = jnp.broadcast_to(square[0:1] + square[1:2], square.shape)
+        big = total.astype(jnp.bfloat16)
+        rest = (total - big.astype(jnp.float32)).astype(jnp.bfloat16)
         out_ref[y, :units, :] = part.astype(jnp.bfloat16)
-        out_ref[y, units:, :] = jnp.concatenate([high, rest], axis=0)
+        out_ref[y, units:, :] = jnp.concatenate([big, rest], axis=0)
 
 
 def hessian_kernel(from_ref, rows_ref, a0, a1, a2, a3, lower_ref, out_ref, right_ref):
@@ -183,10 +198,13 @@
     kept_mask = prune_mask.astype(jnp.float32)
     is_first = (lax.axis_index("z_low") == 0) & (lax.axis_index("core") == 0)
     order = senders()
-
+    core = lax.axis_index("core").astype(jnp.int32)[None]
+
+    mine = copy_for_each(attn_out, ("z_high", "z_low"))
+    mine = round_x(mine)
+    other = [lax.ppermute(block, "core", [(0, 1), (1, 0)]) for block in mine]
     gain_rows = jnp.broadcast_to(norm_gain[None], (16, norm_gain.shape[0]))
-    upper, lower = over_y_and_x(gathered_z(jnp.concatenate([attn_out, gain_rows], axis=0)))
-    flat_weight = gate_up_weight.transpose(1, 2, 0).reshape(2 * units, -1)
+    residual_turned = turned(jnp.concatenate([residual, gain_rows], axis=0))
 
     solved = solved_errors(
         output_weight[:, :width_block], prune_mask, inverse_factor[:, :width_block]
@@ -194,44 +212,52 @@
     errors = lax.all_gather(solved, DP)[0]
     weight_cols = output_weight.astype(jnp.float32)
     updated = weight_cols - jnp.dot(
-        errors, inverse_factor, precision=lax.Precision.HIGHEST, preferred_element_type=jnp.float32
+        errors,
+        inverse_factor,
+        precision=lax.Precision.HIGHEST,
+        preferred_element_type=jnp.float32,
     )
     leading = jnp.where(is_first, updated[:, :width_block] * kept_mask, updated[:, :width_block])
-    pruned_weight = lax.dynamic_update_slice_in_dim(updated, leading, 0, 1).astype(jnp.bfloat16)
+    pruned_weight = lax.dynamic_update_slice_in_dim(updated, leading, 0, 1).astype(
+        jnp.bfloat16
+    )
+    weight_turned = turned(pruned_weight)
 
     parts = pl.pallas_call(
         project_kernel,
         out_shape=jax.ShapeDtypeStruct((4, 128, 128), jnp.bfloat16),
-        in_specs=[SMEM] + [VMEM] * 6,
+        in_specs=[SMEM] * 2 + [VMEM] * 9,
         out_specs=VMEM,
         name="project",
         compiler_params=params(10),
         cost_estimate=pl.CostEstimate(flops=268_000_000, bytes_accessed=2_700_000, transcendentals=0),
-    )(order, *upper, lower, pruned_weight)
-    parts = lax.all_to_all(parts, DP, 0, 0, tiled=True)
-    projected = jnp.sum(parts.astype(jnp.float32), axis=0)
-    stream = (residual.astype(jnp.float32) + projected).astype(jnp.bfloat16)
-
-    gains = lower[0, :, :, -16:]
-    scaled_weight = pl.pallas_call(
-        scale_kernel,
-        out_shape=jax.ShapeDtypeStruct(flat_weight.shape, jnp.bfloat16),
-        in_specs=[SMEM] + [VMEM] * 2,
-        out_specs=VMEM,
-        name="scale",
-        compiler_params=params(16),
-        cost_estimate=pl.CostEstimate(flops=2_000_000, bytes_accessed=3_700_000, transcendentals=0),
-    )(order, flat_weight, gains)
-    upper, lower = over_y_and_x(gathered_z(stream))
+    )(order, core, *mine, *other, weight_turned)
+    parts = lax.all_to_all(parts, "y", 0, 0, tiled=True)
+    stream_turned, block = pl.pallas_call(
+        stream_kernel,
+        out_shape=(
+            jax.ShapeDtypeStruct((128, 128), jnp.bfloat16),
+            jax.ShapeDtypeStruct((136, 128), jnp.bfloat16),
+        ),
+        in_specs=[VMEM] * 2,
+        out_specs=[VMEM] * 2,
+        name="stream",
+        compiler_params=params(4),
+        cost_estimate=pl.CostEstimate(flops=300_000, bytes_accessed=250_000, transcendentals=0),
+    )(parts, residual_turned)
+    stream = turned(stream_turned)
+
+    flat_weight = gate_up_weight.transpose(1, 2, 0).reshape(2 * units, -1)
+    upper, lower = over_y_and_x(over_z(block), 64)
     parts = pl.pallas_call(
         gate_up_kernel,
         out_shape=jax.ShapeDtypeStruct((4, 2 * units + 16, 128), jnp.bfloat16),
-        in_specs=[VMEM] * 6,
+        in_specs=[SMEM] + [VMEM] * 6,
         out_specs=VMEM,
         name="gate_up",
         compiler_params=params(14),
         cost_estimate=pl.CostEstimate(flops=940_000_000, bytes_accessed=4_300_000, transcendentals=0),
-    )(*upper, lower, scaled_weight)
+    )(order, *upper, lower, flat_weight)
     parts = lax.all_to_all(parts, DP, 0, 0, tiled=True)
     sums = jnp.sum(parts.astype(jnp.float32), axis=0)
     square = sums[2 * units : 2 * units + 1] + sums[2 * units + 8 : 2 * units + 9]
@@ -240,7 +266,8 @@
     up_part = sums[units : 2 * units] * inverse
     hidden = (jax.nn.silu(gate_part) * up_part).astype(jnp.bfloat16)
 
-    upper, lower = over_y_and_x(gathered_z(hidden))
+    hidden_turned = turned(hidden)
+    upper, lower = over_y_and_x(over_z(hidden_turned), units // 2)
     hidden_rows = lax.all_gather(hidden, DP)
     piece = pl.BlockSpec((4, 1, units // 2, 128), lambda z: (0, z, 0, 0))
     hessian = pl.pallas_call(

time: 219 us -> 198 us (0.904)
  blocking collectives: 80.2 us -> 53.2 us
  starting transfers between devices: 64.5 us -> 75.2 us
  waiting for transfers between devices: 44.8 us -> 39 us
    ppermute x18 -> x15, waiting for transfers between devices: 39.8 us -> 21.8 us  [round_x(): lax.ppermute(x, 'x', [(k, (k + step) % 4) for k in range(4)])]
    all_to_all x3 -> x2, blocking collectives: 35.7 us -> 24 us  [copy_for_each(): lax.all_to_all(jnp.broadcast_to(x[None], (size, *x.shape)), axis, 0, 0, t...]
    ppermute x3 -> x4, waiting for transfers between devices: 5.06 us -> 16.4 us  [turned(): return lax.ppermute(x, (*DP, 'y'), pairs)]
    ppermute x3 -> x4, starting transfers between devices: 13.5 us -> 21.1 us  [turned(): return lax.ppermute(x, (*DP, 'y'), pairs)]
    all_to_all x0 -> x1, starting transfers between devices: none -> 7.21 us  [body(): parts = lax.all_to_all(parts, 'y', 0, 0, tiled=True)]
    all_to_all x2 -> x1, blocking collectives: 23.2 us -> 17.6 us  [body(): parts = lax.all_to_all(parts, DP, 0, 0, tiled=True)]
    all_gather x1, blocking collectives: 10.1 us -> 4.52 us  [body(): hidden_rows = lax.all_gather(hidden, DP)]
    ppermute x18 -> x15, starting transfers between devices: 20 us -> 15.7 us  [round_x(): lax.ppermute(x, 'x', [(k, (k + step) % 4) for k in range(4)])]
  transfers between devices with their start and end apart: 27 -> 29, of which waited for: 15 -> 15; matrix products, arithmetic and copies ran while one was open for 1% -> 2% of each run, Pallas kernels for 1% -> 1%
where the time goes in v1:
time: 198 us; the launch traced here: 197 us
  starting transfers between devices  75.2 us (38%)
  blocking collectives  53.2 us (27%)
  waiting for transfers between devices  39 us (20%)
  local copies, waits for them, and re-layouts  15 us (8%)
  Pallas kernels  11.3 us (6%)
  matrix products  2.22 us (1%)
    all_to_all x5, starting transfers between devices, copy_for_each(): lax.all_to_all(jnp.broadcast_to(x[None], (size, *x.shape)), axis, 0, 0, t...  29 us
    all_to_all x2, blocking collectives, copy_for_each(): lax.all_to_all(jnp.broadcast_to(x[None], (size, *x.shape)), axis, 0, 0, t...  24 us
    ppermute x15, waiting for transfers between devices, round_x(): lax.ppermute(x, 'x', [(k, (k + step) % 4) for k in range(4)])  21.8 us
    ppermute x4, starting transfers between devices, turned(): return lax.ppermute(x, (*DP, 'y'), pairs)  21.1 us
    all_to_all x1, blocking collectives, body(): parts = lax.all_to_all(parts, DP, 0, 0, tiled=True)  17.6 us
    ppermute x4, waiting for transfers between devices, turned(): return lax.ppermute(x, (*DP, 'y'), pairs)  16.4 us
    ppermute x15, starting transfers between devices, round_x(): lax.ppermute(x, 'x', [(k, (k + step) % 4) for k in range(4)])  15.7 us
    unnamed x31, local copies, waits for them, and re-layouts  7.36 us
  transfers between devices with their start and end apart: 29, of which 15 were waited for; matrix products, arithmetic and copies ran while one was open for 2% of the time, Pallas kernels for 1%

profile of v1, /device:TPU:1, one launch (start us, length us, event | category | flops | bytes accessed | tf_op | source)
XLA Modules:
  0.0 197.2 jit_solution(12442811349919241074)
XLA Ops:
  0.6 1.6 broadcast_in_dim.19
  2.2 9.0 %all-to-all-start = ((bf16[8,128,128]{2,1,0:T(8,128)(2,1)}), bf16[8,128,128]{2,1,0:T(8,128)(2,1)S(1)}, u32[]{:S(2)}, u32[]{:S(2)}) async-start(bf16[8,128,128]{2,1,0:T(8,128)(2,1)} %broadcast_in_dim.19), calls=%async_computation | async-start | bytes 524288 | tf_op jit(solution)/shard_map/all_to_all | solution.py:25
  13.7 2.2 %solve.1 = f32[128,128]{1,0:T(8,128)S(1)} custom-call(bf16[128,128]{1,0:T(8,128)(2,1)S(1)} %slice.37.weight_ref, s32[128,128]{1,0:T(8,128)S(1)} %copy-done.7, f32[128,128]{1,0:T(8,128)S(1)} %slice.38.factor_ref), custom_call_target="tpu_custom_call" | custom-call | flops 20000000 | bytes 300000 | tf_op jit(solution)/shard_map/solve/pallas_call | solution.py:98
  15.9 7.0 %all-gather = f32[512,128]{1,0:T(8,128)S(1)} all-gather(f32[128,128]{1,0:T(8,128)S(1)} %solve.1), channel_id=2, replica_groups=mesh['z_low'=2,'core'=2,'y'=4,'z_high'=4,'x'=4] {'z_low','core'}, dimensions={0}, use_global_device_ids=true | all-gather | bytes 327680 | tf_op jit(solution)/shard_map/all_gather | solution.py:212
  22.9 2.2 %convolution_subtract_fusion = f32[128,2048]{1,0:T(8,128)S(1)} fusion(f32[128,2048]{1,0:T(8,128)} %param.11, bf16[128,2048]{1,0:T(8,128)(2,1)S(1)} %copy-done.11, f32[512,128]{1,0:T(8,128)S(1)} %all-gather), kind=kOutput, calls=%fused_computation | convolution fusion | flops 403177472 | bytes 2686976 | tf_op jit(solution)/shard_map/dot_general | solution.py:214
  25.3 2.8 %collective-permute-start.2 = (bf16[8,128,128]{2,1,0:T(8,128)(2,1)S(1)}, bf16[8,128,128]{2,1,0:T(8,128)(2,1)S(1)}, u32[]{:S(2)}, u32[]{:S(2)}) collective-permute-start(bf16[8,128,128]{2,1,0:T(8,128)(2,1)S(1)} %all-to-all-done.refs_0_), channel_id=1, source_target_pairs={{0,2},{1,3},{2,0},{3,1},{4,6},{5,7},{6,4},{7,5},{8,10},{9,11},{10,... | collective-permute-start | bytes 786440 | tf_op jit(solution)/shard_map/ppermute | solution.py:35
  28.1 3.5 %collective-permute-start.7 = (bf16[128,2048]{1,0:T(8,128)(2,1)S(1)}, bf16[128,2048]{1,0:T(8,128)(2,1)S(1)}, u32[]{:S(2)}, u32[]{:S(2)}) collective-permute-start(bf16[128,2048]{1,0:T(8,128)(2,1)S(1)} %convert_element_type.17), channel_id=1, source_target_pairs={{0,0},{16,64},{32,128},{48,192},{64,16},{80,80},{96,144},{112,208}... | collective-permute-start | bytes 1572872 | tf_op jit(solution)/shard_map/ppermute | solution.py:30
  31.7 0.9 collective-permute-start.1
  33.2 1.4 collective-permute-done.2.refs_3_
  34.6 1.1 collective-permute-start.6
  35.7 4.6 %collective-permute-done.1.refs_2_ = bf16[8,128,128]{2,1,0:T(8,128)(2,1)S(1)} collective-permute-done((bf16[8,128,128]{2,1,0:T(8,128)(2,1)S(1)}, bf16[8,128,128]{2,1,0:T(8,128)(2,1)S(1)}, u32[]{:S(2)}, u32[]{:S(2)}) %collective-permute-start.1) | collective-permute-done | bytes 262176 | tf_op jit(solution)/shard_map/ppermute | solution.py:35
  40.4 1.0 collective-permute-start.5
  42.9 1.9 project.1
  44.8 7.2 %all-to-all-start.1 = ((bf16[4,128,128]{2,1,0:T(8,128)(2,1)}), bf16[4,128,128]{2,1,0:T(8,128)(2,1)S(1)}, u32[]{:S(2)}, u32[]{:S(2)}) async-start(bf16[4,128,128]{2,1,0:T(8,128)(2,1)} %project.1), calls=%async_computation.1 | async-start | bytes 262144 | tf_op jit(solution)/shard_map/all_to_all | solution.py:235
  52.1 4.8 %collective-permute-start.8 = (bf16[144,128]{1,0:T(8,128)(2,1)S(1)}, bf16[144,128]{1,0:T(8,128)(2,1)S(1)}, u32[]{:S(2)}, u32[]{:S(2)}) collective-permute-start(bf16[144,128]{1,0:T(8,128)(2,1)S(1)} %pad_maximum_fusion.2), channel_id=1, source_target_pairs={{0,0},{16,64},{32,128},{48,192},{64,16},{80,80},{96,144},{112,208}... | collective-permute-start | bytes 110600 | tf_op jit(solution)/shard_map/ppermute | solution.py:30
  56.9 1.9 collective-permute-done.8.residual_ref
  59.1 13.5 %all_to_all.45 = bf16[4,136,128]{2,1,0:T(8,128)(2,1)S(1)} all-to-all(bf16[4,136,128]{2,1,0:T(8,128)(2,1)S(1)} %broadcast_in_dim.21), channel_id=1, replica_groups=mesh['z_low'=2,'core'=2,'y'=4,'z_high'=4,'x'=4] {'z_high'}, dimensions={0} | all-to-all | bytes 278528 | tf_op jit(solution)/shard_map/all_to_all | solution.py:25
  73.3 4.7 %all-to-all-start.3 = ((bf16[4,4,64,128]{3,2,1,0:T(8,128)(2,1)}), bf16[4,4,64,128]{3,2,1,0:T(8,128)(2,1)S(1)}, u32[]{:S(2)}, u32[]{:S(2)}) async-start(bf16[4,4,64,128]{3,2,1,0:T(8,128)(2,1)} %broadcast_in_dim.22), calls=%async_computation.3 | async-start | bytes 524288 | tf_op jit(solution)/shard_map/all_to_all | solution.py:25
  78.0 0.9 collective-permute-start.14
  80.2 1.1 collective-permute-done.14
  81.3 2.1 %collective-permute-done.13 = bf16[4,72,128]{2,1,0:T(8,128)(2,1)S(1)} collective-permute-done((bf16[4,72,128]{2,1,0:T(8,128)(2,1)S(1)}, bf16[4,72,128]{2,1,0:T(8,128)(2,1)S(1)}, u32[]{:S(2)}, u32[]{:S(2)}) %collective-permute-start.13) | collective-permute-done | bytes 73760 | tf_op jit(solution)/shard_map/ppermute | solution.py:35
  83.4 0.9 collective-permute-done.15
  84.4 1.2 broadcast_in_dim.23
  85.5 4.2 %all-to-all-start.4 = ((bf16[4,4,4,72,128]{4,3,2,1,0:T(8,128)(2,1)}), bf16[4,4,4,72,128]{4,3,2,1,0:T(8,128)(2,1)S(1)}, u32[]{:S(2)}, u32[]{:S(2)}) async-start(bf16[4,4,4,72,128]{4,3,2,1,0:T(8,128)(2,1)} %broadcast_in_dim.23), calls=%async_computation.4 | async-start | bytes 2359296 | tf_op jit(solution)/shard_map/all_to_all | solution.py:25
  89.8 1.1 collective-permute-start.12
  90.8 1.6 collective-permute-start.11
  92.5 4.0 %collective-permute-done.12.a3 = bf16[4,4,64,128]{3,2,1,0:T(8,128)(2,1)S(1)} collective-permute-done((bf16[4,4,64,128]{3,2,1,0:T(8,128)(2,1)S(1)}, bf16[4,4,64,128]{3,2,1,0:T(8,128)(2,1)S(1)}, u32[]{:S(2)}, u32[]{:S(2)}) %collective-permute-start.12) | collective-permute-done | bytes 262176 | tf_op jit(solution)/shard_map/ppermute | solution.py:35
  96.5 2.5 %collective-permute-done.11.a2 = bf16[4,4,64,128]{3,2,1,0:T(8,128)(2,1)S(1)} collective-permute-done((bf16[4,4,64,128]{3,2,1,0:T(8,128)(2,1)S(1)}, bf16[4,4,64,128]{3,2,1,0:T(8,128)(2,1)S(1)}, u32[]{:S(2)}, u32[]{:S(2)}) %collective-permute-start.11) | collective-permute-done | bytes 262176 | tf_op jit(solution)/shard_map/ppermute | solution.py:35
  100.4 0.9 copy-done.4
  101.4 0.9 copy-done.6
  102.3 2.6 %gate_up.1 = bf16[4,464,128]{2,1,0:T(8,128)(2,1)S(1)} custom-call(s32[4]{0:T(128)S(1)} %pad_add_fusion.from_ref, bf16[4,4,64,128]{3,2,1,0:T(8,128)(2,1)S(1)} %all-to-all-done.3.a0, bf16[4,4,64,128]{3,2,1,0:T(8,128)(2,1)S(1)} %copy-done.6, bf16[4,4,64,128]{3,2,1,0:T(8,128)(2,1)S(1)} %copy-done.4, bf16[4,4,64,128]{3,2,1,0:T(8,128)(2,1)S(1)} %collective-permute-done.12.a3, ...), custom_call_target="tpu_custom_call" | custom-call | flops 940000000 | bytes 4300000 | tf_op jit(solution)/shard_map/gate_up/pallas_call | solution.py:252
  104.9 17.6 %all_to_all.46 = bf16[4,464,128]{2,1,0:T(8,128)(2,1)S(1)} all-to-all(bf16[4,464,128]{2,1,0:T(8,128)(2,1)S(1)} %gate_up.1), channel_id=1, replica_groups=mesh['z_low'=2,'core'=2,'y'=4,'z_high'=4,'x'=4] {'z_low','core'}, dimensions={0} | all-to-all | bytes 950272 | tf_op jit(solution)/shard_map/all_to_all | solution.py:261
  122.7 4.4 %collective-permute-start.16 = (bf16[224,128]{1,0:T(8,128)(2,1)S(1)}, bf16[224,128]{1,0:T(8,128)(2,1)S(1)}, u32[]{:S(2)}, u32[]{:S(2)}) collective-permute-start(bf16[224,128]{1,0:T(8,128)(2,1)S(1)} %fusion.1), channel_id=1, source_target_pairs={{0,0},{16,64},{32,128},{48,192},{64,16},{80,80},{96,144},{112,208}... | collective-permute-start | bytes 172040 | tf_op jit(solution)/shard_map/ppermute | solution.py:30
  127.1 1.8 collective-permute-done.16
  128.9 10.5 %all_to_all.47 = bf16[4,224,128]{2,1,0:T(8,128)(2,1)S(1)} all-to-all(bf16[4,224,128]{2,1,0:T(8,128)(2,1)S(1)} %broadcast_in_dim.24), channel_id=1, replica_groups=mesh['z_low'=2,'core'=2,'y'=4,'z_high'=4,'x'=4] {'z_high'}, dimensions={0} | all-to-all | bytes 458752 | tf_op jit(solution)/shard_map/all_to_all | solution.py:25
  140.3 7.0 %all-to-all-start.7 = ((bf16[4,4,112,128]{3,2,1,0:T(8,128)(2,1)}), bf16[4,4,112,128]{3,2,1,0:T(8,128)(2,1)S(1)}, u32[]{:S(2)}, u32[]{:S(2)}) async-start(bf16[4,4,112,128]{3,2,1,0:T(8,128)(2,1)} %broadcast_in_dim.25), calls=%async_computation.7 | async-start | bytes 917504 | tf_op jit(solution)/shard_map/all_to_all | solution.py:25
  147.3 2.4 %collective-permute-start.21 = (bf16[4,112,128]{2,1,0:T(8,128)(2,1)S(1)}, bf16[4,112,128]{2,1,0:T(8,128)(2,1)S(1)}, u32[]{:S(2)}, u32[]{:S(2)}) collective-permute-start(bf16[4,112,128]{2,1,0:T(8,128)(2,1)S(1)} %get-tuple-element.8), channel_id=1, source_target_pairs={{0,3},{1,0},{2,1},{3,2},{4,7},{5,4},{6,5},{7,6},{8,11},{9,8},{10,9... | collective-permute-start | bytes 344072 | tf_op jit(solution)/shard_map/ppermute | solution.py:35
  149.7 1.2 collective-permute-start.22
  151.5 4.6 %collective-permute-done.20 = bf16[4,112,128]{2,1,0:T(8,128)(2,1)S(1)} collective-permute-done((bf16[4,112,128]{2,1,0:T(8,128)(2,1)S(1)}, bf16[4,112,128]{2,1,0:T(8,128)(2,1)S(1)}, u32[]{:S(2)}, u32[]{:S(2)}) %collective-permute-start.20) | collective-permute-done | bytes 114720 | tf_op jit(solution)/shard_map/ppermute | solution.py:35
  156.2 1.6 broadcast_in_dim.26
  157.7 4.1 %all-to-all-start.8 = ((bf16[4,4,4,112,128]{4,3,2,1,0:T(8,128)(2,1)}), bf16[4,4,4,112,128]{4,3,2,1,0:T(8,128)(2,1)S(1)}, u32[]{:S(2)}, u32[]{:S(2)}) async-start(bf16[4,4,4,112,128]{4,3,2,1,0:T(8,128)(2,1)} %broadcast_in_dim.26), calls=%async_computation.8 | async-start | bytes 3670016 | tf_op jit(solution)/shard_map/all_to_all | solution.py:25
  162.1 2.3 %collective-permute-start.18 = (bf16[4,4,112,128]{3,2,1,0:T(8,128)(2,1)S(1)}, bf16[4,4,112,128]{3,2,1,0:T(8,128)(2,1)S(1)}, u32[]{:S(2)}, u32[]{:S(2)}) collective-permute-start(bf16[4,4,112,128]{3,2,1,0:T(8,128)(2,1)S(1)} %all-to-all-done.7.a0), channel_id=1, source_target_pairs={{0,3},{1,0},{2,1},{3,2},{4,7},{5,4},{6,5},{7,6},{8,11},{9,8},{10,9... | collective-permute-start | bytes 1376264 | tf_op jit(solution)/shard_map/ppermute | solution.py:35
  164.7 8.4 %collective-permute-start.9 = (bf16[128,128]{1,0:T(8,128)(2,1)S(1)}, bf16[128,128]{1,0:T(8,128)(2,1)}, u32[]{:S(2)}, u32[]{:S(2)}) collective-permute-start(bf16[128,128]{1,0:T(8,128)(2,1)S(1)} %copy-done.10), channel_id=1, source_target_pairs={{0,0},{16,64},{32,128},{48,192},{64,16},{80,80},{96,144},{112,208}... | collective-permute-start | bytes 98312 | tf_op jit(solution)/shard_map/ppermute | solution.py:30
  173.1 12.0 %collective-permute-done.9 = bf16[128,128]{1,0:T(8,128)(2,1)} collective-permute-done((bf16[128,128]{1,0:T(8,128)(2,1)S(1)}, bf16[128,128]{1,0:T(8,128)(2,1)}, u32[]{:S(2)}, u32[]{:S(2)}) %collective-permute-start.9) | collective-permute-done | bytes 32800 | tf_op jit(solution)/shard_map/ppermute | solution.py:30
  185.1 4.5 %all-gather.1 = bf16[896,128]{1,0:T(8,128)(2,1)S(1)} all-gather(bf16[224,128]{1,0:T(8,128)(2,1)S(1)} %fusion.1), channel_id=3, replica_groups=mesh['z_low'=2,'core'=2,'y'=4,'z_high'=4,'x'=4] {'z_low','core'}, dimensions={0}, use_global_device_ids=true | all-gather | bytes 286720 | tf_op jit(solution)/shard_map/all_gather | solution.py:271
  190.4 1.0 copy-done.2
  191.4 4.4 %hessian.1 = f32[224,3584]{1,0:T(8,128)} custom-call(s32[4]{0:T(128)S(1)} %pad_add_fusion.from_ref, bf16[4,224,128]{2,1,0:T(8,128)(2,1)S(1)} %bitcast.23, bf16[4,4,112,128]{3,2,1,0:T(8,128)(2,1)S(1)} %all-to-all-done.7.a0, bf16[4,4,112,128]{3,2,1,0:T(8,128)(2,1)S(1)} %copy-done.2, bf16[4,4,112,128]{3,2,1,0:T(8,128)(2,1)S(1)} %collective-permute-done.18.a2, ...), custom_call_target="tpu_custom_call" | custom-call | flops 822000000 | bytes 7100000 | tf_op jit(solution)/shard_map/hessian/pallas_call | solution.py:273
  195.8 1.4 copy.12
  (74 shorter events, 11.6 us)
Async XLA Ops:
  0.6 22.3 %copy-start.11 = (bf16[128,2048]{1,0:T(8,128)(2,1)S(1)}, bf16[128,2048]{1,0:T(8,128)(2,1)}, u32[]{:S(2)}) copy-start(bf16[128,2048]{1,0:T(8,128)(2,1)} %param.9) | copy-start | bytes 1572868
  2.2 23.1 %all-to-all-start = ((bf16[8,128,128]{2,1,0:T(8,128)(2,1)}), bf16[8,128,128]{2,1,0:T(8,128)(2,1)S(1)}, u32[]{:S(2)}, u32[]{:S(2)}) async-start(bf16[8,128,128]{2,1,0:T(8,128)(2,1)} %broadcast_in_dim.19), calls=%async_computation | async-start | bytes 524288 | tf_op jit(solution)/shard_map/all_to_all | solution.py:25
  11.2 14.0 %copy-start.8 = (s32[128,128]{1,0:T(8,128)S(1)}, s32[128,128]{1,0:T(8,128)}, u32[]{:S(2)}) copy-start(s32[128,128]{1,0:T(8,128)} %mask_ref.1) | copy-start | bytes 196612
  12.9 0.8 copy-start.7
  25.3 47.3 %copy-start.12 = (bf16[128,2048]{1,0:T(8,128)(2,1)}, bf16[128,2048]{1,0:T(8,128)(2,1)S(1)}, u32[]{:S(2)}) copy-start(bf16[128,2048]{1,0:T(8,128)(2,1)S(1)} %convert_element_type.17) | copy-start | bytes 1572868
  25.3 26.8 %copy-start.14 = (bf16[128]{0:T(256)(128)(2,1)S(1)}, bf16[128]{0:T(256)(128)(2,1)}, u32[]{:S(2)}) copy-start(bf16[128]{0:T(256)(128)(2,1)} %param.12) | copy-start | bytes 772
  25.3 26.8 %copy-start.13 = (bf16[128,128]{1,0:T(8,128)(2,1)S(1)}, bf16[128,128]{1,0:T(8,128)(2,1)}, u32[]{:S(2)}) copy-start(bf16[128,128]{1,0:T(8,128)(2,1)} %param.8) | copy-start | bytes 98308
  25.3 9.3 %collective-permute-start.2 = (bf16[8,128,128]{2,1,0:T(8,128)(2,1)S(1)}, bf16[8,128,128]{2,1,0:T(8,128)(2,1)S(1)}, u32[]{:S(2)}, u32[]{:S(2)}) collective-permute-start(bf16[8,128,128]{2,1,0:T(8,128)(2,1)S(1)} %all-to-all-done.refs_0_), channel_id=1, source_target_pairs={{0,2},{1,3},{2,0},{3,1},{4,6},{5,7},{6,4},{7,5},{8,10},{9,11},{10,... | collective-permute-start | bytes 786440 | tf_op jit(solution)/shard_map/ppermute | solution.py:35
  28.1 13.9 %collective-permute-start.7 = (bf16[128,2048]{1,0:T(8,128)(2,1)S(1)}, bf16[128,2048]{1,0:T(8,128)(2,1)S(1)}, u32[]{:S(2)}, u32[]{:S(2)}) collective-permute-start(bf16[128,2048]{1,0:T(8,128)(2,1)S(1)} %convert_element_type.17), channel_id=1, source_target_pairs={{0,0},{16,64},{32,128},{48,192},{64,16},{80,80},{96,144},{112,208}... | collective-permute-start | bytes 1572872 | tf_op jit(solution)/shard_map/ppermute | solution.py:30
  31.7 8.7 %collective-permute-start.1 = (bf16[8,128,128]{2,1,0:T(8,128)(2,1)S(1)}, bf16[8,128,128]{2,1,0:T(8,128)(2,1)S(1)}, u32[]{:S(2)}, u32[]{:S(2)}) collective-permute-start(bf16[8,128,128]{2,1,0:T(8,128)(2,1)S(1)} %all-to-all-done.refs_0_), channel_id=1, source_target_pairs={{0,3},{1,0},{2,1},{3,2},{4,7},{5,4},{6,5},{7,6},{8,11},{9,8},{10,9... | collective-permute-start | bytes 786440 | tf_op jit(solution)/shard_map/ppermute | solution.py:35
  32.6 8.8 %collective-permute-start = (bf16[8,128,128]{2,1,0:T(8,128)(2,1)S(1)}, bf16[8,128,128]{2,1,0:T(8,128)(2,1)S(1)}, u32[]{:S(2)}, u32[]{:S(2)}) collective-permute-start(bf16[8,128,128]{2,1,0:T(8,128)(2,1)S(1)} %all-to-all-done.refs_0_), channel_id=1, source_target_pairs={{0,1},{1,2},{2,3},{3,0},{4,5},{5,6},{6,7},{7,4},{8,9},{9,10},{10,1... | collective-permute-start | bytes 786440 | tf_op jit(solution)/shard_map/ppermute | solution.py:35
  33.2 8.9 %collective-permute-start.3 = (bf16[8,128,128]{2,1,0:T(8,128)(2,1)S(1)}, bf16[8,128,128]{2,1,0:T(8,128)(2,1)S(1)}, u32[]{:S(2)}, u32[]{:S(2)}) collective-permute-start(bf16[8,128,128]{2,1,0:T(8,128)(2,1)S(1)} %all-to-all-done.refs_0_), channel_id=1, source_target_pairs={{0,64},{64,0},{1,65},{65,1},{2,66},{66,2},{3,67},{67,3},{4,68},{68... | collective-permute-start | bytes 786440 | tf_op jit(solution)/shard_map/ppermute | solution.py:205
  34.6 7.5 %collective-permute-start.6 = (bf16[8,128,128]{2,1,0:T(8,128)(2,1)S(1)}, bf16[8,128,128]{2,1,0:T(8,128)(2,1)S(1)}, u32[]{:S(2)}, u32[]{:S(2)}) collective-permute-start(bf16[8,128,128]{2,1,0:T(8,128)(2,1)S(1)} %collective-permute-done.2.refs_3_), channel_id=1, source_target_pairs={{0,64},{64,0},{1,65},{65,1},{2,66},{66,2},{3,67},{67,3},{4,68},{68... | collective-permute-start | bytes 786440 | tf_op jit(solution)/shard_map/ppermute | solution.py:205
  40.4 2.2 %collective-permute-start.5 = (bf16[8,128,128]{2,1,0:T(8,128)(2,1)S(1)}, bf16[8,128,128]{2,1,0:T(8,128)(2,1)S(1)}, u32[]{:S(2)}, u32[]{:S(2)}) collective-permute-start(bf16[8,128,128]{2,1,0:T(8,128)(2,1)S(1)} %collective-permute-done.1.refs_2_), channel_id=1, source_target_pairs={{0,64},{64,0},{1,65},{65,1},{2,66},{66,2},{3,67},{67,3},{4,68},{68... | collective-permute-start | bytes 786440 | tf_op jit(solution)/shard_map/ppermute | solution.py:205
  41.4 1.5 collective-permute-start.4
  44.8 14.0 %all-to-all-start.1 = ((bf16[4,128,128]{2,1,0:T(8,128)(2,1)}), bf16[4,128,128]{2,1,0:T(8,128)(2,1)S(1)}, u32[]{:S(2)}, u32[]{:S(2)}) async-start(bf16[4,128,128]{2,1,0:T(8,128)(2,1)} %project.1), calls=%async_computation.1 | async-start | bytes 262144 | tf_op jit(solution)/shard_map/all_to_all | solution.py:235
  52.1 6.7 %collective-permute-start.8 = (bf16[144,128]{1,0:T(8,128)(2,1)S(1)}, bf16[144,128]{1,0:T(8,128)(2,1)S(1)}, u32[]{:S(2)}, u32[]{:S(2)}) collective-permute-start(bf16[144,128]{1,0:T(8,128)(2,1)S(1)} %pad_maximum_fusion.2), channel_id=1, source_target_pairs={{0,0},{16,64},{32,128},{48,192},{64,16},{80,80},{96,144},{112,208}... | collective-permute-start | bytes 110600 | tf_op jit(solution)/shard_map/ppermute | solution.py:30
  59.0 26.5 %copy-start.9 = (bf16[128,128]{1,0:T(8,128)(2,1)}, bf16[128,128]{1,0:T(8,128)(2,1)S(1)}, u32[]{:S(2)}) copy-start(bf16[128,128]{1,0:T(8,128)(2,1)S(1)} %get-tuple-element.5) | copy-start | bytes 98308
  73.3 11.0 %all-to-all-start.3 = ((bf16[4,4,64,128]{3,2,1,0:T(8,128)(2,1)}), bf16[4,4,64,128]{3,2,1,0:T(8,128)(2,1)S(1)}, u32[]{:S(2)}, u32[]{:S(2)}) async-start(bf16[4,4,64,128]{3,2,1,0:T(8,128)(2,1)} %broadcast_in_dim.22), calls=%async_computation.3 | async-start | bytes 524288 | tf_op jit(solution)/shard_map/all_to_all | solution.py:25
  78.0 3.3 %collective-permute-start.14 = (bf16[4,72,128]{2,1,0:T(8,128)(2,1)S(1)}, bf16[4,72,128]{2,1,0:T(8,128)(2,1)S(1)}, u32[]{:S(2)}, u32[]{:S(2)}) collective-permute-start(bf16[4,72,128]{2,1,0:T(8,128)(2,1)S(1)} %get-tuple-element.11), channel_id=1, source_target_pairs={{0,3},{1,0},{2,1},{3,2},{4,7},{5,4},{6,5},{7,6},{8,11},{9,8},{10,9... | collective-permute-start | bytes 221192 | tf_op jit(solution)/shard_map/ppermute | solution.py:35
  79.0 4.4 %collective-permute-start.13 = (bf16[4,72,128]{2,1,0:T(8,128)(2,1)S(1)}, bf16[4,72,128]{2,1,0:T(8,128)(2,1)S(1)}, u32[]{:S(2)}, u32[]{:S(2)}) collective-permute-start(bf16[4,72,128]{2,1,0:T(8,128)(2,1)S(1)} %get-tuple-element.11), channel_id=1, source_target_pairs={{0,1},{1,2},{2,3},{3,0},{4,5},{5,6},{6,7},{7,4},{8,9},{9,10},{10,1... | collective-permute-start | bytes 221192 | tf_op jit(solution)/shard_map/ppermute | solution.py:35
  79.6 4.7 %collective-permute-start.15 = (bf16[4,72,128]{2,1,0:T(8,128)(2,1)S(1)}, bf16[4,72,128]{2,1,0:T(8,128)(2,1)S(1)}, u32[]{:S(2)}, u32[]{:S(2)}) collective-permute-start(bf16[4,72,128]{2,1,0:T(8,128)(2,1)S(1)} %get-tuple-element.11), channel_id=1, source_target_pairs={{0,2},{1,3},{2,0},{3,1},{4,6},{5,7},{6,4},{7,5},{8,10},{9,11},{10,... | collective-permute-start | bytes 221192 | tf_op jit(solution)/shard_map/ppermute | solution.py:35
  84.3 16.1 %copy-start = (bf16[2048,2,224]{0,2,1:T(8,128)(2,1)S(1)}, bf16[2048,2,224]{0,2,1:T(8,128)(2,1)}, u32[]{:S(2)}) copy-start(bf16[2048,2,224]{0,2,1:T(8,128)(2,1)} %param.13) | copy-start | bytes 5505028
  85.5 14.9 %all-to-all-start.4 = ((bf16[4,4,4,72,128]{4,3,2,1,0:T(8,128)(2,1)}), bf16[4,4,4,72,128]{4,3,2,1,0:T(8,128)(2,1)S(1)}, u32[]{:S(2)}, u32[]{:S(2)}) async-start(bf16[4,4,4,72,128]{4,3,2,1,0:T(8,128)(2,1)} %broadcast_in_dim.23), calls=%async_computation.4 | async-start | bytes 2359296 | tf_op jit(solution)/shard_map/all_to_all | solution.py:25
  89.8 6.8 %collective-permute-start.12 = (bf16[4,4,64,128]{3,2,1,0:T(8,128)(2,1)S(1)}, bf16[4,4,64,128]{3,2,1,0:T(8,128)(2,1)S(1)}, u32[]{:S(2)}, u32[]{:S(2)}) collective-permute-start(bf16[4,4,64,128]{3,2,1,0:T(8,128)(2,1)S(1)} %all-to-all-done.3.a0), channel_id=1, source_target_pairs={{0,2},{1,3},{2,0},{3,1},{4,6},{5,7},{6,4},{7,5},{8,10},{9,11},{10,... | collective-permute-start | bytes 786440 | tf_op jit(solution)/shard_map/ppermute | solution.py:35
  90.8 8.2 %collective-permute-start.11 = (bf16[4,4,64,128]{3,2,1,0:T(8,128)(2,1)S(1)}, bf16[4,4,64,128]{3,2,1,0:T(8,128)(2,1)S(1)}, u32[]{:S(2)}, u32[]{:S(2)}) collective-permute-start(bf16[4,4,64,128]{3,2,1,0:T(8,128)(2,1)S(1)} %all-to-all-done.3.a0), channel_id=1, source_target_pairs={{0,3},{1,0},{2,1},{3,2},{4,7},{5,4},{6,5},{7,6},{8,11},{9,8},{10,9... | collective-permute-start | bytes 786440 | tf_op jit(solution)/shard_map/ppermute | solution.py:35
  92.5 7.2 %collective-permute-start.10 = (bf16[4,4,64,128]{3,2,1,0:T(8,128)(2,1)S(1)}, bf16[4,4,64,128]{3,2,1,0:T(8,128)(2,1)S(1)}, u32[]{:S(2)}, u32[]{:S(2)}) collective-permute-start(bf16[4,4,64,128]{3,2,1,0:T(8,128)(2,1)S(1)} %all-to-all-done.3.a0), channel_id=1, source_target_pairs={{0,1},{1,2},{2,3},{3,0},{4,5},{5,6},{6,7},{7,4},{8,9},{9,10},{10,1... | collective-permute-start | bytes 786440 | tf_op jit(solution)/shard_map/ppermute | solution.py:35
  99.0 0.7 copy-start.3
  99.7 0.7 copy-start.5
  100.4 1.0 copy-start.4
  101.4 0.9 copy-start.6
  122.7 6.2 %collective-permute-start.16 = (bf16[224,128]{1,0:T(8,128)(2,1)S(1)}, bf16[224,128]{1,0:T(8,128)(2,1)S(1)}, u32[]{:S(2)}, u32[]{:S(2)}) collective-permute-start(bf16[224,128]{1,0:T(8,128)(2,1)S(1)} %fusion.1), channel_id=1, source_target_pairs={{0,0},{16,64},{32,128},{48,192},{64,16},{80,80},{96,144},{112,208}... | collective-permute-start | bytes 172040 | tf_op jit(solution)/shard_map/ppermute | solution.py:30
  140.3 15.8 %all-to-all-start.7 = ((bf16[4,4,112,128]{3,2,1,0:T(8,128)(2,1)}), bf16[4,4,112,128]{3,2,1,0:T(8,128)(2,1)S(1)}, u32[]{:S(2)}, u32[]{:S(2)}) async-start(bf16[4,4,112,128]{3,2,1,0:T(8,128)(2,1)} %broadcast_in_dim.25), calls=%async_computation.7 | async-start | bytes 917504 | tf_op jit(solution)/shard_map/all_to_all | solution.py:25
  147.3 4.2 %collective-permute-start.21 = (bf16[4,112,128]{2,1,0:T(8,128)(2,1)S(1)}, bf16[4,112,128]{2,1,0:T(8,128)(2,1)S(1)}, u32[]{:S(2)}, u32[]{:S(2)}) collective-permute-start(bf16[4,112,128]{2,1,0:T(8,128)(2,1)S(1)} %get-tuple-element.8), channel_id=1, source_target_pairs={{0,3},{1,0},{2,1},{3,2},{4,7},{5,4},{6,5},{7,6},{8,11},{9,8},{10,9... | collective-permute-start | bytes 344072 | tf_op jit(solution)/shard_map/ppermute | solution.py:35
  149.7 6.4 %collective-permute-start.20 = (bf16[4,112,128]{2,1,0:T(8,128)(2,1)S(1)}, bf16[4,112,128]{2,1,0:T(8,128)(2,1)S(1)}, u32[]{:S(2)}, u32[]{:S(2)}) collective-permute-start(bf16[4,112,128]{2,1,0:T(8,128)(2,1)S(1)} %get-tuple-element.8), channel_id=1, source_target_pairs={{0,1},{1,2},{2,3},{3,0},{4,5},{5,6},{6,7},{7,4},{8,9},{9,10},{10,1... | collective-permute-start | bytes 344072 | tf_op jit(solution)/shard_map/ppermute | solution.py:35
  149.7 6.4 %collective-permute-start.22 = (bf16[4,112,128]{2,1,0:T(8,128)(2,1)S(1)}, bf16[4,112,128]{2,1,0:T(8,128)(2,1)S(1)}, u32[]{:S(2)}, u32[]{:S(2)}) collective-permute-start(bf16[4,112,128]{2,1,0:T(8,128)(2,1)S(1)} %get-tuple-element.8), channel_id=1, source_target_pairs={{0,2},{1,3},{2,0},{3,1},{4,6},{5,7},{6,4},{7,5},{8,10},{9,11},{10,... | collective-permute-start | bytes 344072 | tf_op jit(solution)/shard_map/ppermute | solution.py:35
  157.7 6.9 %copy-start.10 = (bf16[128,128]{1,0:T(8,128)(2,1)S(1)}, bf16[128,128]{1,0:T(8,128)(2,1)}, u32[]{:S(2)}) copy-start(bf16[128,128]{1,0:T(8,128)(2,1)} %copy-done.9) | copy-start | bytes 98308
  157.7 32.7 %all-to-all-start.8 = ((bf16[4,4,4,112,128]{4,3,2,1,0:T(8,128)(2,1)}), bf16[4,4,4,112,128]{4,3,2,1,0:T(8,128)(2,1)S(1)}, u32[]{:S(2)}, u32[]{:S(2)}) async-start(bf16[4,4,4,112,128]{4,3,2,1,0:T(8,128)(2,1)} %broadcast_in_dim.26), calls=%async_computation.8 | async-start | bytes 3670016 | tf_op jit(solution)/shard_map/all_to_all | solution.py:25
  161.8 27.8 %collective-permute-start.19 = (bf16[4,4,112,128]{3,2,1,0:T(8,128)(2,1)S(1)}, bf16[4,4,112,128]{3,2,1,0:T(8,128)(2,1)S(1)}, u32[]{:S(2)}, u32[]{:S(2)}) collective-permute-start(bf16[4,4,112,128]{3,2,1,0:T(8,128)(2,1)S(1)} %all-to-all-done.7.a0), channel_id=1, source_target_pairs={{0,2},{1,3},{2,0},{3,1},{4,6},{5,7},{6,4},{7,5},{8,10},{9,11},{10,... | collective-permute-start | bytes 1376264 | tf_op jit(solution)/shard_map/ppermute | solution.py:35
  162.1 27.5 %collective-permute-start.18 = (bf16[4,4,112,128]{3,2,1,0:T(8,128)(2,1)S(1)}, bf16[4,4,112,128]{3,2,1,0:T(8,128)(2,1)S(1)}, u32[]{:S(2)}, u32[]{:S(2)}) collective-permute-start(bf16[4,4,112,128]{3,2,1,0:T(8,128)(2,1)S(1)} %all-to-all-done.7.a0), channel_id=1, source_target_pairs={{0,3},{1,0},{2,1},{3,2},{4,7},{5,4},{6,5},{7,6},{8,11},{9,8},{10,9... | collective-permute-start | bytes 1376264 | tf_op jit(solution)/shard_map/ppermute | solution.py:35
  164.4 25.2 %collective-permute-start.17 = (bf16[4,4,112,128]{3,2,1,0:T(8,128)(2,1)S(1)}, bf16[4,4,112,128]{3,2,1,0:T(8,128)(2,1)S(1)}, u32[]{:S(2)}, u32[]{:S(2)}) collective-permute-start(bf16[4,4,112,128]{3,2,1,0:T(8,128)(2,1)S(1)} %all-to-all-done.7.a0), channel_id=1, source_target_pairs={{0,1},{1,2},{2,3},{3,0},{4,5},{5,6},{6,7},{7,4},{8,9},{9,10},{10,1... | collective-permute-start | bytes 1376264 | tf_op jit(solution)/shard_map/ppermute | solution.py:35
  164.7 20.4 %collective-permute-start.9 = (bf16[128,128]{1,0:T(8,128)(2,1)S(1)}, bf16[128,128]{1,0:T(8,128)(2,1)}, u32[]{:S(2)}, u32[]{:S(2)}) collective-permute-start(bf16[128,128]{1,0:T(8,128)(2,1)S(1)} %copy-done.10), channel_id=1, source_target_pairs={{0,0},{16,64},{32,128},{48,192},{64,16},{80,80},{96,144},{112,208}... | collective-permute-start | bytes 98312 | tf_op jit(solution)/shard_map/ppermute | solution.py:30
  189.6 0.8 copy-start.1
  190.4 1.0 copy-start.2

commit v2 on v1

--- a/solution.py
+++ b/solution.py
@@ -94,16 +94,55 @@
     errors_ref[...] = jnp.concatenate(done, axis=0).T
 
 
-def solved_errors(first_weight, mask, factor):
+def corner(shape):
+    return pl.BlockSpec(shape, lambda i: (0,) * len(shape))
+
+
+def solved_errors(weight, mask, factor):
+    block = corner(mask.shape)
     return pl.pallas_call(
         solve_kernel,
-        out_shape=jax.ShapeDtypeStruct(first_weight.shape, jnp.float32),
-        in_specs=[VMEM] * 3,
-        out_specs=VMEM,
+        grid=(1,),
+        out_shape=jax.ShapeDtypeStruct(mask.shape, jnp.float32),
+        in_specs=[block] * 3,
+        out_specs=block,
         name="solve",
         compiler_params=params(8),
         cost_estimate=pl.CostEstimate(flops=20_000_000, bytes_accessed=300_000, transcendentals=0),
-    )(first_weight, mask, factor)
+    )(weight, mask, factor)
+
+
+def update_kernel(first_ref, errors_ref, factor_ref, weight_ref, mask_ref, out_ref):
+    updated = weight_ref[...].astype(jnp.float32) - lax.dot_general(
+        errors_ref[0],
+        factor_ref[...],
+        (((1,), (0,)), ((), ())),
+        precision=lax.Precision.HIGHEST,
+        preferred_element_type=jnp.float32,
+    )
+    width = mask_ref.shape[1]
+    kept = jnp.where(first_ref[0] == 1, mask_ref[...].astype(jnp.float32), 1.0)
+    out_ref[:, :width] = (updated[:, :width] * kept).astype(jnp.bfloat16)
+    out_ref[:, width:] = updated[:, width:].astype(jnp.bfloat16)
+
+
+def updated_weight(is_first, errors, factor, weight, mask):
+    return pl.pallas_call(
+        update_kernel,
+        grid=(1,),
+        out_shape=jax.ShapeDtypeStruct(weight.shape, jnp.bfloat16),
+        in_specs=[
+            SMEM,
+            corner((1, *errors.shape[1:])),
+            corner(factor.shape),
+            corner(weight.shape),
+            corner(mask.shape),
+        ],
+        out_specs=corner(weight.shape),
+        name="update",
+        compiler_params=params(12),
+        cost_estimate=pl.CostEstimate(flops=400_000_000, bytes_accessed=2_200_000, transcendentals=0),
+    )(is_first, errors, factor, weight, mask)
 
 
 def columns_at(ref, block):
@@ -151,10 +190,18 @@
     block_ref[...] = jnp.concatenate([wide * gain, pair], axis=0).astype(jnp.bfloat16)
 
 
-def gate_up_kernel(from_ref, a0, a1, a2, a3, lower_ref, weight_ref, out_ref):
+def copy_kernel(in_ref, out_ref):
+    out_ref[...] = in_ref[...]
+
+
+def order_kernel(from_ref, weight_ref, out_ref):
+    out_ref[...] = ordered_columns(weight_ref, from_ref)
+
+
+def gate_up_kernel(a0, a1, a2, a3, lower_ref, weight_ref, out_ref):
     upper = (a0, a1, a2, a3)
     half = a0.shape[2]
-    weight = ordered_columns(weight_ref, from_ref)
+    weight = weight_ref[...]
     units = weight.shape[0]
     places = [(r, z) for r in range(4) for z in range(4)]
     for y in range(4):
@@ -193,10 +240,8 @@
 
 
 def body(attn_out, residual, output_weight, prune_mask, inverse_factor, norm_gain, gate_up_weight):
-    width_block = prune_mask.shape[1]
     units = gate_up_weight.shape[2]
-    kept_mask = prune_mask.astype(jnp.float32)
-    is_first = (lax.axis_index("z_low") == 0) & (lax.axis_index("core") == 0)
+    is_first = (lax.axis_index(DP) == 0).astype(jnp.int32)[None]
     order = senders()
     core = lax.axis_index("core").astype(jnp.int32)[None]
 
@@ -206,21 +251,9 @@
     gain_rows = jnp.broadcast_to(norm_gain[None], (16, norm_gain.shape[0]))
     residual_turned = turned(jnp.concatenate([residual, gain_rows], axis=0))
 
-    solved = solved_errors(
-        output_weight[:, :width_block], prune_mask, inverse_factor[:, :width_block]
-    )
-    errors = lax.all_gather(solved, DP)[0]
-    weight_cols = output_weight.astype(jnp.float32)
-    updated = weight_cols - jnp.dot(
-        errors,
-        inverse_factor,
-        precision=lax.Precision.HIGHEST,
-        preferred_element_type=jnp.float32,
-    )
-    leading = jnp.where(is_first, updated[:, :width_block] * kept_mask, updated[:, :width_block])
-    pruned_weight = lax.dynamic_update_slice_in_dim(updated, leading, 0, 1).astype(
-        jnp.bfloat16
-    )
+    solved = solved_errors(output_weight, prune_mask, inverse_factor)
+    errors = lax.all_gather(solved, DP)
+    pruned_weight = updated_weight(is_first, errors, inverse_factor, output_weight, prune_mask)
     weight_turned = turned(pruned_weight)
 
     parts = pl.pallas_call(
@@ -246,18 +279,36 @@
         cost_estimate=pl.CostEstimate(flops=300_000, bytes_accessed=250_000, transcendentals=0),
     )(parts, residual_turned)
     stream = turned(stream_turned)
+    stream = pl.pallas_call(
+        copy_kernel,
+        out_shape=jax.ShapeDtypeStruct(stream.shape, stream.dtype),
+        in_specs=[VMEM],
+        out_specs=VMEM,
+        compiler_params=params(1),
+    )(stream)
 
     flat_weight = gate_up_weight.transpose(1, 2, 0).reshape(2 * units, -1)
+    flat_weight = pl.pallas_call(
+        order_kernel,
+        out_shape=jax.ShapeDtypeStruct(flat_weight.shape, jnp.bfloat16),
+        in_specs=[SMEM, VMEM],
+        out_specs=VMEM,
+        name="order",
+        compiler_params=params(8),
+        cost_estimate=pl.CostEstimate(flops=0, bytes_accessed=3_700_000, transcendentals=0),
+    )(order, flat_weight)
     upper, lower = over_y_and_x(over_z(block), 64)
     parts = pl.pallas_call(
         gate_up_kernel,
         out_shape=jax.ShapeDtypeStruct((4, 2 * units + 16, 128), jnp.bfloat16),
-        in_specs=[SMEM] + [VMEM] * 6,
+        in_specs=[VMEM] * 6,
         out_specs=VMEM,
         name="gate_up",
         compiler_params=params(14),
-        cost_estimate=pl.CostEstimate(flops=940_000_000, bytes_accessed=4_300_000, transcendentals=0),
-    )(order, *upper, lower, flat_weight)
+        cost_estimate=pl.CostEstimate(
+            flops=940_000_000, bytes_accessed=4_300_000, transcendentals=0
+        ),
+    )(*upper, lower, flat_weight)
     parts = lax.all_to_all(parts, DP, 0, 0, tiled=True)
     sums = jnp.sum(parts.astype(jnp.float32), axis=0)
     square = sums[2 * units : 2 * units + 1] + sums[2 * units + 8 : 2 * units + 9]

time: 198 us -> 197 us (level)
  Pallas kernels: 11.3 us -> 14.2 us
  waiting for transfers between devices: 39 us -> 36.5 us
  matrix products: 2.22 us -> 0 us
    pallas_call x1 -> x4, Pallas kernels: 2.18 us -> 5.61 us  [the longest x1 2.18 us: solved_errors(): pl.pallas_call(solve_kernel, grid=(1,), out_shape=jax.ShapeDtypeStruct(ma...]
    ppermute x15, waiting for transfers between devices: 21.8 us -> 19.2 us  [round_x(): lax.ppermute(x, 'x', [(k, (k + step) % 4) for k in range(4)])]
    unnamed x31 -> x34, local copies, waits for them, and re-layouts: 7.36 us -> 9.72 us
    dot_general x1 -> x0, matrix products: 2.22 us -> none  [body(): jnp.dot(errors, inverse_factor, precision=lax.Precision.HIGHEST, preferre...]
  transfers between devices with their start and end apart: 29 -> 29, of which waited for: 15 -> 15; matrix products, arithmetic and copies ran while one was open for 2% -> 0% of each run, Pallas kernels for 1% -> 3%
where the time goes in v2:
time: 197 us; the launch traced here: 196 us
  starting transfers between devices  75.3 us (38%)
  blocking collectives  53.2 us (27%)
  waiting for transfers between devices  36.5 us (19%)
  local copies, waits for them, and re-layouts  15.8 us (8%)
  Pallas kernels  14.2 us (7%)
    all_to_all x5, starting transfers between devices, copy_for_each(): lax.all_to_all(jnp.broadcast_to(x[None], (size, *x.shape)), axis, 0, 0, t...  29 us
    all_to_all x2, blocking collectives, copy_for_each(): lax.all_to_all(jnp.broadcast_to(x[None], (size, *x.shape)), axis, 0, 0, t...  24 us
    ppermute x4, starting transfers between devices, turned(): return lax.ppermute(x, (*DP, 'y'), pairs)  21.1 us
    ppermute x15, waiting for transfers between devices, round_x(): lax.ppermute(x, 'x', [(k, (k + step) % 4) for k in range(4)])  19.2 us
    all_to_all x1, blocking collectives, body(): parts = lax.all_to_all(parts, DP, 0, 0, tiled=True)  17.6 us
    ppermute x4, waiting for transfers between devices, turned(): return lax.ppermute(x, (*DP, 'y'), pairs)  16.6 us
    ppermute x15, starting transfers between devices, round_x(): lax.ppermute(x, 'x', [(k, (k + step) % 4) for k in range(4)])  15.6 us
    unnamed x34, local copies, waits for them, and re-layouts  9.72 us
  transfers between devices with their start and end apart: 29, of which 15 were waited for; matrix products, arithmetic and copies ran while one was open for 0% of the time, Pallas kernels for 3%

profile of v2, /device:TPU:1, one launch (start us, length us, event | category | flops | bytes accessed | tf_op | source)
XLA Modules:
  0.0 196.1 jit_solution(4855298171787679584)
XLA Ops:
  0.7 1.6 broadcast_in_dim.25
  2.2 9.0 %all-to-all-start = ((bf16[8,128,128]{2,1,0:T(8,128)(2,1)}), bf16[8,128,128]{2,1,0:T(8,128)(2,1)S(1)}, u32[]{:S(2)}, u32[]{:S(2)}) async-start(bf16[8,128,128]{2,1,0:T(8,128)(2,1)} %broadcast_in_dim.25), calls=%async_computation | async-start | bytes 524288 | tf_op jit(solution)/shard_map/all_to_all | solution.py:25
  11.2 1.2 copy-done
  12.4 1.0 copy-done.2
  14.3 2.2 %solve.1 = f32[128,128]{1,0:T(8,128)S(1)} custom-call(bf16[128,2048]{1,0:T(8,128)(2,1)S(1)} %copy-done.2, s32[128,128]{1,0:T(8,128)S(1)} %copy-done.11, f32[128,2048]{1,0:T(8,128)S(1)} %copy-done), custom_call_target="tpu_custom_call" | custom-call | flops 20000000 | bytes 300000 | tf_op jit(solution)/shard_map/solve/pallas_call | solution.py:103
  16.5 7.1 %all-gather = f32[512,128]{1,0:T(8,128)S(1)} all-gather(f32[128,128]{1,0:T(8,128)S(1)} %solve.1), channel_id=2, replica_groups=mesh['z_low'=2,'core'=2,'y'=4,'z_high'=4,'x'=4] {'z_low','core'}, dimensions={0}, use_global_device_ids=true | all-gather | bytes 327680 | tf_op jit(solution)/shard_map/all_gather | solution.py:255
  23.6 1.8 update.1
  25.4 2.7 %collective-permute-start.2 = (bf16[8,128,128]{2,1,0:T(8,128)(2,1)S(1)}, bf16[8,128,128]{2,1,0:T(8,128)(2,1)S(1)}, u32[]{:S(2)}, u32[]{:S(2)}) collective-permute-start(bf16[8,128,128]{2,1,0:T(8,128)(2,1)S(1)} %all-to-all-done.refs_0_), channel_id=1, source_target_pairs={{0,2},{1,3},{2,0},{3,1},{4,6},{5,7},{6,4},{7,5},{8,10},{9,11},{10,... | collective-permute-start | bytes 786440 | tf_op jit(solution)/shard_map/ppermute | solution.py:35
  28.1 3.5 %collective-permute-start.7 = (bf16[128,2048]{1,0:T(8,128)(2,1)}, bf16[128,2048]{1,0:T(8,128)(2,1)S(1)}, u32[]{:S(2)}, u32[]{:S(2)}) collective-permute-start(bf16[128,2048]{1,0:T(8,128)(2,1)} %update.1), channel_id=1, source_target_pairs={{0,0},{16,64},{32,128},{48,192},{64,16},{80,80},{96,144},{112,208}... | collective-permute-start | bytes 1572872 | tf_op jit(solution)/shard_map/ppermute | solution.py:30
  33.2 1.4 collective-permute-done.2.refs_3_
  34.6 1.1 collective-permute-start.6
  35.7 4.6 %collective-permute-done.1.refs_2_ = bf16[8,128,128]{2,1,0:T(8,128)(2,1)S(1)} collective-permute-done((bf16[8,128,128]{2,1,0:T(8,128)(2,1)S(1)}, bf16[8,128,128]{2,1,0:T(8,128)(2,1)S(1)}, u32[]{:S(2)}, u32[]{:S(2)}) %collective-permute-start.1) | collective-permute-done | bytes 262176 | tf_op jit(solution)/shard_map/ppermute | solution.py:35
  40.3 1.0 collective-permute-start.5
  42.9 1.9 project.1
  44.8 7.5 %all-to-all-start.1 = ((bf16[4,128,128]{2,1,0:T(8,128)(2,1)}), bf16[4,128,128]{2,1,0:T(8,128)(2,1)S(1)}, u32[]{:S(2)}, u32[]{:S(2)}) async-start(bf16[4,128,128]{2,1,0:T(8,128)(2,1)} %project.1), calls=%async_computation.1 | async-start | bytes 262144 | tf_op jit(solution)/shard_map/all_to_all | solution.py:268
  52.3 4.8 %collective-permute-start.8 = (bf16[144,128]{1,0:T(8,128)(2,1)S(1)}, bf16[144,128]{1,0:T(8,128)(2,1)S(1)}, u32[]{:S(2)}, u32[]{:S(2)}) collective-permute-start(bf16[144,128]{1,0:T(8,128)(2,1)S(1)} %pad_maximum_fusion.2), channel_id=1, source_target_pairs={{0,0},{16,64},{32,128},{48,192},{64,16},{80,80},{96,144},{112,208}... | collective-permute-start | bytes 110600 | tf_op jit(solution)/shard_map/ppermute | solution.py:30
  57.1 1.9 collective-permute-done.8.residual_ref
  59.3 13.5 %all_to_all.45 = bf16[4,136,128]{2,1,0:T(8,128)(2,1)S(1)} all-to-all(bf16[4,136,128]{2,1,0:T(8,128)(2,1)S(1)} %broadcast_in_dim.27), channel_id=1, replica_groups=mesh['z_low'=2,'core'=2,'y'=4,'z_high'=4,'x'=4] {'z_high'}, dimensions={0} | all-to-all | bytes 278528 | tf_op jit(solution)/shard_map/all_to_all | solution.py:25
  73.5 4.7 %all-to-all-start.3 = ((bf16[4,4,64,128]{3,2,1,0:T(8,128)(2,1)}), bf16[4,4,64,128]{3,2,1,0:T(8,128)(2,1)S(1)}, u32[]{:S(2)}, u32[]{:S(2)}) async-start(bf16[4,4,64,128]{3,2,1,0:T(8,128)(2,1)} %broadcast_in_dim.28), calls=%async_computation.3 | async-start | bytes 524288 | tf_op jit(solution)/shard_map/all_to_all | solution.py:25
  80.4 1.1 collective-permute-done.14
  81.5 2.1 %collective-permute-done.13 = bf16[4,72,128]{2,1,0:T(8,128)(2,1)S(1)} collective-permute-done((bf16[4,72,128]{2,1,0:T(8,128)(2,1)S(1)}, bf16[4,72,128]{2,1,0:T(8,128)(2,1)S(1)}, u32[]{:S(2)}, u32[]{:S(2)}) %collective-permute-start.13) | collective-permute-done | bytes 73760 | tf_op jit(solution)/shard_map/ppermute | solution.py:35
  84.5 1.2 broadcast_in_dim.29
  85.7 4.2 %all-to-all-start.4 = ((bf16[4,4,4,72,128]{4,3,2,1,0:T(8,128)(2,1)}), bf16[4,4,4,72,128]{4,3,2,1,0:T(8,128)(2,1)S(1)}, u32[]{:S(2)}, u32[]{:S(2)}) async-start(bf16[4,4,4,72,128]{4,3,2,1,0:T(8,128)(2,1)} %broadcast_in_dim.29), calls=%async_computation.4 | async-start | bytes 2359296 | tf_op jit(solution)/shard_map/all_to_all | solution.py:25
  89.9 1.1 collective-permute-start.12
  91.0 1.6 collective-permute-start.11
  92.7 1.5 copy-done.4
  94.2 1.0 order.1.weight_ref
  95.2 1.5 collective-permute-done.12.a3
  96.7 2.5 %collective-permute-done.11.a2 = bf16[4,4,64,128]{3,2,1,0:T(8,128)(2,1)S(1)} collective-permute-done((bf16[4,4,64,128]{3,2,1,0:T(8,128)(2,1)S(1)}, bf16[4,4,64,128]{3,2,1,0:T(8,128)(2,1)S(1)}, u32[]{:S(2)}, u32[]{:S(2)}) %collective-permute-start.11) | collective-permute-done | bytes 262176 | tf_op jit(solution)/shard_map/ppermute | solution.py:35
  100.6 0.9 copy-done.8
  101.6 0.9 copy-done.10
  102.5 2.1 %gate_up.1 = bf16[4,464,128]{2,1,0:T(8,128)(2,1)S(1)} custom-call(bf16[4,4,64,128]{3,2,1,0:T(8,128)(2,1)S(1)} %all-to-all-done.3.a0, bf16[4,4,64,128]{3,2,1,0:T(8,128)(2,1)S(1)} %copy-done.10, bf16[4,4,64,128]{3,2,1,0:T(8,128)(2,1)S(1)} %copy-done.8, bf16[4,4,64,128]{3,2,1,0:T(8,128)(2,1)S(1)} %collective-permute-done.12.a3, ...), custom_call_target="tpu_custom_call" | custom-call | flops 940000000 | bytes 4300000 | tf_op jit(solution)/shard_map/gate_up/pallas_call | solution.py:301
  104.6 17.6 %all_to_all.46 = bf16[4,464,128]{2,1,0:T(8,128)(2,1)S(1)} all-to-all(bf16[4,464,128]{2,1,0:T(8,128)(2,1)S(1)} %gate_up.1), channel_id=1, replica_groups=mesh['z_low'=2,'core'=2,'y'=4,'z_high'=4,'x'=4] {'z_low','core'}, dimensions={0} | all-to-all | bytes 950272 | tf_op jit(solution)/shard_map/all_to_all | solution.py:312
  122.3 4.4 %collective-permute-start.16 = (bf16[224,128]{1,0:T(8,128)(2,1)S(1)}, bf16[224,128]{1,0:T(8,128)(2,1)S(1)}, u32[]{:S(2)}, u32[]{:S(2)}) collective-permute-start(bf16[224,128]{1,0:T(8,128)(2,1)S(1)} %fusion.1), channel_id=1, source_target_pairs={{0,0},{16,64},{32,128},{48,192},{64,16},{80,80},{96,144},{112,208}... | collective-permute-start | bytes 172040 | tf_op jit(solution)/shard_map/ppermute | solution.py:30
  126.7 1.8 collective-permute-done.16
  128.6 10.5 %all_to_all.47 = bf16[4,224,128]{2,1,0:T(8,128)(2,1)S(1)} all-to-all(bf16[4,224,128]{2,1,0:T(8,128)(2,1)S(1)} %broadcast_in_dim.30), channel_id=1, replica_groups=mesh['z_low'=2,'core'=2,'y'=4,'z_high'=4,'x'=4] {'z_high'}, dimensions={0} | all-to-all | bytes 458752 | tf_op jit(solution)/shard_map/all_to_all | solution.py:25
  139.9 7.1 %all-to-all-start.7 = ((bf16[4,4,112,128]{3,2,1,0:T(8,128)(2,1)}), bf16[4,4,112,128]{3,2,1,0:T(8,128)(2,1)S(1)}, u32[]{:S(2)}, u32[]{:S(2)}) async-start(bf16[4,4,112,128]{3,2,1,0:T(8,128)(2,1)} %broadcast_in_dim.31), calls=%async_computation.7 | async-start | bytes 917504 | tf_op jit(solution)/shard_map/all_to_all | solution.py:25
  147.0 2.3 %collective-permute-start.21 = (bf16[4,112,128]{2,1,0:T(8,128)(2,1)S(1)}, bf16[4,112,128]{2,1,0:T(8,128)(2,1)S(1)}, u32[]{:S(2)}, u32[]{:S(2)}) collective-permute-start(bf16[4,112,128]{2,1,0:T(8,128)(2,1)S(1)} %get-tuple-element.8), channel_id=1, source_target_pairs={{0,3},{1,0},{2,1},{3,2},{4,7},{5,4},{6,5},{7,6},{8,11},{9,8},{10,9... | collective-permute-start | bytes 344072 | tf_op jit(solution)/shard_map/ppermute | solution.py:35
  149.3 1.2 collective-permute-start.22
  151.1 4.6 %collective-permute-done.20 = bf16[4,112,128]{2,1,0:T(8,128)(2,1)S(1)} collective-permute-done((bf16[4,112,128]{2,1,0:T(8,128)(2,1)S(1)}, bf16[4,112,128]{2,1,0:T(8,128)(2,1)S(1)}, u32[]{:S(2)}, u32[]{:S(2)}) %collective-permute-start.20) | collective-permute-done | bytes 114720 | tf_op jit(solution)/shard_map/ppermute | solution.py:35
  155.8 1.6 broadcast_in_dim.32
  157.4 4.1 %all-to-all-start.8 = ((bf16[4,4,4,112,128]{4,3,2,1,0:T(8,128)(2,1)}), bf16[4,4,4,112,128]{4,3,2,1,0:T(8,128)(2,1)S(1)}, u32[]{:S(2)}, u32[]{:S(2)}) async-start(bf16[4,4,4,112,128]{4,3,2,1,0:T(8,128)(2,1)} %broadcast_in_dim.32), calls=%async_computation.8 | async-start | bytes 3670016 | tf_op jit(solution)/shard_map/all_to_all | solution.py:25
  161.8 2.3 %collective-permute-start.18 = (bf16[4,4,112,128]{3,2,1,0:T(8,128)(2,1)S(1)}, bf16[4,4,112,128]{3,2,1,0:T(8,128)(2,1)S(1)}, u32[]{:S(2)}, u32[]{:S(2)}) collective-permute-start(bf16[4,4,112,128]{3,2,1,0:T(8,128)(2,1)S(1)} %all-to-all-done.7.a0), channel_id=1, source_target_pairs={{0,3},{1,0},{2,1},{3,2},{4,7},{5,4},{6,5},{7,6},{8,11},{9,8},{10,9... | collective-permute-start | bytes 1376264 | tf_op jit(solution)/shard_map/ppermute | solution.py:35
  164.3 8.4 %collective-permute-start.9 = (bf16[128,128]{1,0:T(8,128)(2,1)S(1)}, bf16[128,128]{1,0:T(8,128)(2,1)S(1)}, u32[]{:S(2)}, u32[]{:S(2)}) collective-permute-start(bf16[128,128]{1,0:T(8,128)(2,1)S(1)} %copy-done.14), channel_id=1, source_target_pairs={{0,0},{16,64},{32,128},{48,192},{64,16},{80,80},{96,144},{112,208}... | collective-permute-start | bytes 98312 | tf_op jit(solution)/shard_map/ppermute | solution.py:30
  172.7 12.0 %collective-permute-done.9.in_ref = bf16[128,128]{1,0:T(8,128)(2,1)S(1)} collective-permute-done((bf16[128,128]{1,0:T(8,128)(2,1)S(1)}, bf16[128,128]{1,0:T(8,128)(2,1)S(1)}, u32[]{:S(2)}, u32[]{:S(2)}) %collective-permute-start.9) | collective-permute-done | bytes 32800 | tf_op jit(solution)/shard_map/ppermute | solution.py:30
  185.3 4.5 %all-gather.1 = bf16[896,128]{1,0:T(8,128)(2,1)S(1)} all-gather(bf16[224,128]{1,0:T(8,128)(2,1)S(1)} %fusion.1), channel_id=3, replica_groups=mesh['z_low'=2,'core'=2,'y'=4,'z_high'=4,'x'=4] {'z_low','core'}, dimensions={0}, use_global_device_ids=true | all-gather | bytes 286720 | tf_op jit(solution)/shard_map/all_gather | solution.py:322
  190.7 1.0 copy-done.6
  191.7 4.4 %hessian.1 = f32[224,3584]{1,0:T(8,128)} custom-call(s32[4]{0:T(128)S(1)} %pad_add_fusion.from_ref, bf16[4,224,128]{2,1,0:T(8,128)(2,1)S(1)} %bitcast.25, bf16[4,4,112,128]{3,2,1,0:T(8,128)(2,1)S(1)} %all-to-all-done.7.a0, bf16[4,4,112,128]{3,2,1,0:T(8,128)(2,1)S(1)} %copy-done.6, bf16[4,4,112,128]{3,2,1,0:T(8,128)(2,1)S(1)} %collective-permute-done.18.a2, ...), custom_call_target="tpu_custom_call" | custom-call | flops 822000000 | bytes 7100000 | tf_op jit(solution)/shard_map/hessian/pallas_call | solution.py:324
  (75 shorter events, 13.2 us)
Async XLA Ops:
  0.6 22.9 %copy-start.12 = (s32[128,128]{1,0:T(8,128)S(1)}, s32[128,128]{1,0:T(8,128)}, u32[]{:S(2)}) copy-start(s32[128,128]{1,0:T(8,128)} %mask_ref.3) | copy-start | bytes 196612
  0.6 22.9 %copy-start.3 = (bf16[128,2048]{1,0:T(8,128)(2,1)S(1)}, bf16[128,2048]{1,0:T(8,128)(2,1)}, u32[]{:S(2)}) copy-start(bf16[128,2048]{1,0:T(8,128)(2,1)} %weight_ref.3) | copy-start | bytes 1572868
  2.2 23.2 %all-to-all-start = ((bf16[8,128,128]{2,1,0:T(8,128)(2,1)}), bf16[8,128,128]{2,1,0:T(8,128)(2,1)S(1)}, u32[]{:S(2)}, u32[]{:S(2)}) async-start(bf16[8,128,128]{2,1,0:T(8,128)(2,1)} %broadcast_in_dim.25), calls=%async_computation | async-start | bytes 524288 | tf_op jit(solution)/shard_map/all_to_all | solution.py:25
  11.2 1.2 copy-start
  12.4 1.0 copy-start.2
  13.5 0.8 copy-start.11
  14.3 9.3 %copy-start.1 = (f32[128,2048]{1,0:T(8,128)S(1)}, f32[128,2048]{1,0:T(8,128)}, u32[]{:S(2)}) copy-start(f32[128,2048]{1,0:T(8,128)} %factor_ref.3) | copy-start | bytes 3145732
  25.4 26.9 %copy-start.16 = (bf16[128]{0:T(256)(128)(2,1)S(1)}, bf16[128]{0:T(256)(128)(2,1)}, u32[]{:S(2)}) copy-start(bf16[128]{0:T(256)(128)(2,1)} %param.12) | copy-start | bytes 772
  25.4 26.9 %copy-start.15 = (bf16[128,128]{1,0:T(8,128)(2,1)S(1)}, bf16[128,128]{1,0:T(8,128)(2,1)}, u32[]{:S(2)}) copy-start(bf16[128,128]{1,0:T(8,128)(2,1)} %param.8) | copy-start | bytes 98308
  25.4 9.2 %collective-permute-start.2 = (bf16[8,128,128]{2,1,0:T(8,128)(2,1)S(1)}, bf16[8,128,128]{2,1,0:T(8,128)(2,1)S(1)}, u32[]{:S(2)}, u32[]{:S(2)}) collective-permute-start(bf16[8,128,128]{2,1,0:T(8,128)(2,1)S(1)} %all-to-all-done.refs_0_), channel_id=1, source_target_pairs={{0,2},{1,3},{2,0},{3,1},{4,6},{5,7},{6,4},{7,5},{8,10},{9,11},{10,... | collective-permute-start | bytes 786440 | tf_op jit(solution)/shard_map/ppermute | solution.py:35
  28.1 14.1 %collective-permute-start.7 = (bf16[128,2048]{1,0:T(8,128)(2,1)}, bf16[128,2048]{1,0:T(8,128)(2,1)S(1)}, u32[]{:S(2)}, u32[]{:S(2)}) collective-permute-start(bf16[128,2048]{1,0:T(8,128)(2,1)} %update.1), channel_id=1, source_target_pairs={{0,0},{16,64},{32,128},{48,192},{64,16},{80,80},{96,144},{112,208}... | collective-permute-start | bytes 1572872 | tf_op jit(solution)/shard_map/ppermute | solution.py:30
  31.7 8.7 %collective-permute-start.1 = (bf16[8,128,128]{2,1,0:T(8,128)(2,1)S(1)}, bf16[8,128,128]{2,1,0:T(8,128)(2,1)S(1)}, u32[]{:S(2)}, u32[]{:S(2)}) collective-permute-start(bf16[8,128,128]{2,1,0:T(8,128)(2,1)S(1)} %all-to-all-done.refs_0_), channel_id=1, source_target_pairs={{0,3},{1,0},{2,1},{3,2},{4,7},{5,4},{6,5},{7,6},{8,11},{9,8},{10,9... | collective-permute-start | bytes 786440 | tf_op jit(solution)/shard_map/ppermute | solution.py:35
  32.6 8.7 %collective-permute-start = (bf16[8,128,128]{2,1,0:T(8,128)(2,1)S(1)}, bf16[8,128,128]{2,1,0:T(8,128)(2,1)S(1)}, u32[]{:S(2)}, u32[]{:S(2)}) collective-permute-start(bf16[8,128,128]{2,1,0:T(8,128)(2,1)S(1)} %all-to-all-done.refs_0_), channel_id=1, source_target_pairs={{0,1},{1,2},{2,3},{3,0},{4,5},{5,6},{6,7},{7,4},{8,9},{9,10},{10,1... | collective-permute-start | bytes 786440 | tf_op jit(solution)/shard_map/ppermute | solution.py:35
  33.2 9.1 %collective-permute-start.3 = (bf16[8,128,128]{2,1,0:T(8,128)(2,1)S(1)}, bf16[8,128,128]{2,1,0:T(8,128)(2,1)S(1)}, u32[]{:S(2)}, u32[]{:S(2)}) collective-permute-start(bf16[8,128,128]{2,1,0:T(8,128)(2,1)S(1)} %all-to-all-done.refs_0_), channel_id=1, source_target_pairs={{0,64},{64,0},{1,65},{65,1},{2,66},{66,2},{3,67},{67,3},{4,68},{68... | collective-permute-start | bytes 786440 | tf_op jit(solution)/shard_map/ppermute | solution.py:250
  34.6 7.7 %collective-permute-start.6 = (bf16[8,128,128]{2,1,0:T(8,128)(2,1)S(1)}, bf16[8,128,128]{2,1,0:T(8,128)(2,1)S(1)}, u32[]{:S(2)}, u32[]{:S(2)}) collective-permute-start(bf16[8,128,128]{2,1,0:T(8,128)(2,1)S(1)} %collective-permute-done.2.refs_3_), channel_id=1, source_target_pairs={{0,64},{64,0},{1,65},{65,1},{2,66},{66,2},{3,67},{67,3},{4,68},{68... | collective-permute-start | bytes 786440 | tf_op jit(solution)/shard_map/ppermute | solution.py:250
  40.3 2.2 %collective-permute-start.5 = (bf16[8,128,128]{2,1,0:T(8,128)(2,1)S(1)}, bf16[8,128,128]{2,1,0:T(8,128)(2,1)S(1)}, u32[]{:S(2)}, u32[]{:S(2)}) collective-permute-start(bf16[8,128,128]{2,1,0:T(8,128)(2,1)S(1)} %collective-permute-done.1.refs_2_), channel_id=1, source_target_pairs={{0,64},{64,0},{1,65},{65,1},{2,66},{66,2},{3,67},{67,3},{4,68},{68... | collective-permute-start | bytes 786440 | tf_op jit(solution)/shard_map/ppermute | solution.py:250
  41.3 1.5 collective-permute-start.4
  44.8 14.2 %all-to-all-start.1 = ((bf16[4,128,128]{2,1,0:T(8,128)(2,1)}), bf16[4,128,128]{2,1,0:T(8,128)(2,1)S(1)}, u32[]{:S(2)}, u32[]{:S(2)}) async-start(bf16[4,128,128]{2,1,0:T(8,128)(2,1)} %project.1), calls=%async_computation.1 | async-start | bytes 262144 | tf_op jit(solution)/shard_map/all_to_all | solution.py:268
  52.3 6.7 %collective-permute-start.8 = (bf16[144,128]{1,0:T(8,128)(2,1)S(1)}, bf16[144,128]{1,0:T(8,128)(2,1)S(1)}, u32[]{:S(2)}, u32[]{:S(2)}) collective-permute-start(bf16[144,128]{1,0:T(8,128)(2,1)S(1)} %pad_maximum_fusion.2), channel_id=1, source_target_pairs={{0,0},{16,64},{32,128},{48,192},{64,16},{80,80},{96,144},{112,208}... | collective-permute-start | bytes 110600 | tf_op jit(solution)/shard_map/ppermute | solution.py:30
  59.2 26.5 %copy-start.13 = (bf16[128,128]{1,0:T(8,128)(2,1)}, bf16[128,128]{1,0:T(8,128)(2,1)S(1)}, u32[]{:S(2)}) copy-start(bf16[128,128]{1,0:T(8,128)(2,1)S(1)} %get-tuple-element.5) | copy-start | bytes 98308
  73.5 11.0 %all-to-all-start.3 = ((bf16[4,4,64,128]{3,2,1,0:T(8,128)(2,1)}), bf16[4,4,64,128]{3,2,1,0:T(8,128)(2,1)S(1)}, u32[]{:S(2)}, u32[]{:S(2)}) async-start(bf16[4,4,64,128]{3,2,1,0:T(8,128)(2,1)} %broadcast_in_dim.28), calls=%async_computation.3 | async-start | bytes 524288 | tf_op jit(solution)/shard_map/all_to_all | solution.py:25
  78.2 3.3 %collective-permute-start.14 = (bf16[4,72,128]{2,1,0:T(8,128)(2,1)S(1)}, bf16[4,72,128]{2,1,0:T(8,128)(2,1)S(1)}, u32[]{:S(2)}, u32[]{:S(2)}) collective-permute-start(bf16[4,72,128]{2,1,0:T(8,128)(2,1)S(1)} %get-tuple-element.11), channel_id=1, source_target_pairs={{0,3},{1,0},{2,1},{3,2},{4,7},{5,4},{6,5},{7,6},{8,11},{9,8},{10,9... | collective-permute-start | bytes 221192 | tf_op jit(solution)/shard_map/ppermute | solution.py:35
  79.2 4.4 %collective-permute-start.13 = (bf16[4,72,128]{2,1,0:T(8,128)(2,1)S(1)}, bf16[4,72,128]{2,1,0:T(8,128)(2,1)S(1)}, u32[]{:S(2)}, u32[]{:S(2)}) collective-permute-start(bf16[4,72,128]{2,1,0:T(8,128)(2,1)S(1)} %get-tuple-element.11), channel_id=1, source_target_pairs={{0,1},{1,2},{2,3},{3,0},{4,5},{5,6},{6,7},{7,4},{8,9},{9,10},{10,1... | collective-permute-start | bytes 221192 | tf_op jit(solution)/shard_map/ppermute | solution.py:35
  79.8 4.7 %collective-permute-start.15 = (bf16[4,72,128]{2,1,0:T(8,128)(2,1)S(1)}, bf16[4,72,128]{2,1,0:T(8,128)(2,1)S(1)}, u32[]{:S(2)}, u32[]{:S(2)}) collective-permute-start(bf16[4,72,128]{2,1,0:T(8,128)(2,1)S(1)} %get-tuple-element.11), channel_id=1, source_target_pairs={{0,2},{1,3},{2,0},{3,1},{4,6},{5,7},{6,4},{7,5},{8,10},{9,11},{10,... | collective-permute-start | bytes 221192 | tf_op jit(solution)/shard_map/ppermute | solution.py:35
  85.7 14.9 %all-to-all-start.4 = ((bf16[4,4,4,72,128]{4,3,2,1,0:T(8,128)(2,1)}), bf16[4,4,4,72,128]{4,3,2,1,0:T(8,128)(2,1)S(1)}, u32[]{:S(2)}, u32[]{:S(2)}) async-start(bf16[4,4,4,72,128]{4,3,2,1,0:T(8,128)(2,1)} %broadcast_in_dim.29), calls=%async_computation.4 | async-start | bytes 2359296 | tf_op jit(solution)/shard_map/all_to_all | solution.py:25
  89.9 6.8 %collective-permute-start.12 = (bf16[4,4,64,128]{3,2,1,0:T(8,128)(2,1)S(1)}, bf16[4,4,64,128]{3,2,1,0:T(8,128)(2,1)S(1)}, u32[]{:S(2)}, u32[]{:S(2)}) collective-permute-start(bf16[4,4,64,128]{3,2,1,0:T(8,128)(2,1)S(1)} %all-to-all-done.3.a0), channel_id=1, source_target_pairs={{0,2},{1,3},{2,0},{3,1},{4,6},{5,7},{6,4},{7,5},{8,10},{9,11},{10,... | collective-permute-start | bytes 786440 | tf_op jit(solution)/shard_map/ppermute | solution.py:35
  91.0 8.2 %collective-permute-start.11 = (bf16[4,4,64,128]{3,2,1,0:T(8,128)(2,1)S(1)}, bf16[4,4,64,128]{3,2,1,0:T(8,128)(2,1)S(1)}, u32[]{:S(2)}, u32[]{:S(2)}) collective-permute-start(bf16[4,4,64,128]{3,2,1,0:T(8,128)(2,1)S(1)} %all-to-all-done.3.a0), channel_id=1, source_target_pairs={{0,3},{1,0},{2,1},{3,2},{4,7},{5,4},{6,5},{7,6},{8,11},{9,8},{10,9... | collective-permute-start | bytes 786440 | tf_op jit(solution)/shard_map/ppermute | solution.py:35
  92.7 7.2 %collective-permute-start.10 = (bf16[4,4,64,128]{3,2,1,0:T(8,128)(2,1)S(1)}, bf16[4,4,64,128]{3,2,1,0:T(8,128)(2,1)S(1)}, u32[]{:S(2)}, u32[]{:S(2)}) collective-permute-start(bf16[4,4,64,128]{3,2,1,0:T(8,128)(2,1)S(1)} %all-to-all-done.3.a0), channel_id=1, source_target_pairs={{0,1},{1,2},{2,3},{3,0},{4,5},{5,6},{6,7},{7,4},{8,9},{9,10},{10,1... | collective-permute-start | bytes 786440 | tf_op jit(solution)/shard_map/ppermute | solution.py:35
  92.7 1.5 copy-start.4
  99.2 0.7 copy-start.7
  99.9 0.7 copy-start.9
  100.6 1.0 copy-start.8
  101.6 0.9 copy-start.10
  122.3 6.2 %collective-permute-start.16 = (bf16[224,128]{1,0:T(8,128)(2,1)S(1)}, bf16[224,128]{1,0:T(8,128)(2,1)S(1)}, u32[]{:S(2)}, u32[]{:S(2)}) collective-permute-start(bf16[224,128]{1,0:T(8,128)(2,1)S(1)} %fusion.1), channel_id=1, source_target_pairs={{0,0},{16,64},{32,128},{48,192},{64,16},{80,80},{96,144},{112,208}... | collective-permute-start | bytes 172040 | tf_op jit(solution)/shard_map/ppermute | solution.py:30
  139.9 15.8 %all-to-all-start.7 = ((bf16[4,4,112,128]{3,2,1,0:T(8,128)(2,1)}), bf16[4,4,112,128]{3,2,1,0:T(8,128)(2,1)S(1)}, u32[]{:S(2)}, u32[]{:S(2)}) async-start(bf16[4,4,112,128]{3,2,1,0:T(8,128)(2,1)} %broadcast_in_dim.31), calls=%async_computation.7 | async-start | bytes 917504 | tf_op jit(solution)/shard_map/all_to_all | solution.py:25
  147.0 4.1 %collective-permute-start.21 = (bf16[4,112,128]{2,1,0:T(8,128)(2,1)S(1)}, bf16[4,112,128]{2,1,0:T(8,128)(2,1)S(1)}, u32[]{:S(2)}, u32[]{:S(2)}) collective-permute-start(bf16[4,112,128]{2,1,0:T(8,128)(2,1)S(1)} %get-tuple-element.8), channel_id=1, source_target_pairs={{0,3},{1,0},{2,1},{3,2},{4,7},{5,4},{6,5},{7,6},{8,11},{9,8},{10,9... | collective-permute-start | bytes 344072 | tf_op jit(solution)/shard_map/ppermute | solution.py:35
  149.3 6.4 %collective-permute-start.20 = (bf16[4,112,128]{2,1,0:T(8,128)(2,1)S(1)}, bf16[4,112,128]{2,1,0:T(8,128)(2,1)S(1)}, u32[]{:S(2)}, u32[]{:S(2)}) collective-permute-start(bf16[4,112,128]{2,1,0:T(8,128)(2,1)S(1)} %get-tuple-element.8), channel_id=1, source_target_pairs={{0,1},{1,2},{2,3},{3,0},{4,5},{5,6},{6,7},{7,4},{8,9},{9,10},{10,1... | collective-permute-start | bytes 344072 | tf_op jit(solution)/shard_map/ppermute | solution.py:35
  149.3 6.4 %collective-permute-start.22 = (bf16[4,112,128]{2,1,0:T(8,128)(2,1)S(1)}, bf16[4,112,128]{2,1,0:T(8,128)(2,1)S(1)}, u32[]{:S(2)}, u32[]{:S(2)}) collective-permute-start(bf16[4,112,128]{2,1,0:T(8,128)(2,1)S(1)} %get-tuple-element.8), channel_id=1, source_target_pairs={{0,2},{1,3},{2,0},{3,1},{4,6},{5,7},{6,4},{7,5},{8,10},{9,11},{10,... | collective-permute-start | bytes 344072 | tf_op jit(solution)/shard_map/ppermute | solution.py:35
  157.4 6.9 %copy-start.14 = (bf16[128,128]{1,0:T(8,128)(2,1)S(1)}, bf16[128,128]{1,0:T(8,128)(2,1)}, u32[]{:S(2)}) copy-start(bf16[128,128]{1,0:T(8,128)(2,1)} %copy-done.13) | copy-start | bytes 98308
  157.4 33.3 %all-to-all-start.8 = ((bf16[4,4,4,112,128]{4,3,2,1,0:T(8,128)(2,1)}), bf16[4,4,4,112,128]{4,3,2,1,0:T(8,128)(2,1)S(1)}, u32[]{:S(2)}, u32[]{:S(2)}) async-start(bf16[4,4,4,112,128]{4,3,2,1,0:T(8,128)(2,1)} %broadcast_in_dim.32), calls=%async_computation.8 | async-start | bytes 3670016 | tf_op jit(solution)/shard_map/all_to_all | solution.py:25
  161.4 28.4 %collective-permute-start.19 = (bf16[4,4,112,128]{3,2,1,0:T(8,128)(2,1)S(1)}, bf16[4,4,112,128]{3,2,1,0:T(8,128)(2,1)S(1)}, u32[]{:S(2)}, u32[]{:S(2)}) collective-permute-start(bf16[4,4,112,128]{3,2,1,0:T(8,128)(2,1)S(1)} %all-to-all-done.7.a0), channel_id=1, source_target_pairs={{0,2},{1,3},{2,0},{3,1},{4,6},{5,7},{6,4},{7,5},{8,10},{9,11},{10,... | collective-permute-start | bytes 1376264 | tf_op jit(solution)/shard_map/ppermute | solution.py:35
  161.8 28.1 %collective-permute-start.18 = (bf16[4,4,112,128]{3,2,1,0:T(8,128)(2,1)S(1)}, bf16[4,4,112,128]{3,2,1,0:T(8,128)(2,1)S(1)}, u32[]{:S(2)}, u32[]{:S(2)}) collective-permute-start(bf16[4,4,112,128]{3,2,1,0:T(8,128)(2,1)S(1)} %all-to-all-done.7.a0), channel_id=1, source_target_pairs={{0,3},{1,0},{2,1},{3,2},{4,7},{5,4},{6,5},{7,6},{8,11},{9,8},{10,9... | collective-permute-start | bytes 1376264 | tf_op jit(solution)/shard_map/ppermute | solution.py:35
  164.0 25.8 %collective-permute-start.17 = (bf16[4,4,112,128]{3,2,1,0:T(8,128)(2,1)S(1)}, bf16[4,4,112,128]{3,2,1,0:T(8,128)(2,1)S(1)}, u32[]{:S(2)}, u32[]{:S(2)}) collective-permute-start(bf16[4,4,112,128]{3,2,1,0:T(8,128)(2,1)S(1)} %all-to-all-done.7.a0), channel_id=1, source_target_pairs={{0,1},{1,2},{2,3},{3,0},{4,5},{5,6},{6,7},{7,4},{8,9},{9,10},{10,1... | collective-permute-start | bytes 1376264 | tf_op jit(solution)/shard_map/ppermute | solution.py:35
  164.3 20.4 %collective-permute-start.9 = (bf16[128,128]{1,0:T(8,128)(2,1)S(1)}, bf16[128,128]{1,0:T(8,128)(2,1)S(1)}, u32[]{:S(2)}, u32[]{:S(2)}) collective-permute-start(bf16[128,128]{1,0:T(8,128)(2,1)S(1)} %copy-done.14), channel_id=1, source_target_pairs={{0,0},{16,64},{32,128},{48,192},{64,16},{80,80},{96,144},{112,208}... | collective-permute-start | bytes 98312 | tf_op jit(solution)/shard_map/ppermute | solution.py:30
  189.9 0.8 copy-start.5
  190.6 1.0 copy-start.6

commit v3 on v2

--- a/solution.py
+++ b/solution.py
@@ -53,8 +53,18 @@
     return jnp.stack([here] + [(here + 4 - step) % 4 for step in STEPS]).astype(jnp.int32)
 
 
-def solve_kernel(weight_ref, mask_ref, factor_ref, errors_ref):
+def solve_kernel(weight_hbm, mask_hbm, factor_hbm, errors_ref, weight_ref, mask_ref, factor_ref, sems):
     size = factor_ref.shape[0]
+    copies = [
+        pltpu.make_async_copy(source.at[:, pl.ds(0, size)], target, sems.at[k])
+        for k, (source, target) in enumerate(
+            ((weight_hbm, weight_ref), (mask_hbm, mask_ref), (factor_hbm, factor_ref))
+        )
+    ]
+    for copy in copies:
+        copy.start()
+    for copy in copies:
+        copy.wait()
     step = 8
     count = size // step
     factor = factor_ref[...]
@@ -99,15 +109,19 @@
 
 
 def solved_errors(weight, mask, factor):
-    block = corner(mask.shape)
     return pl.pallas_call(
         solve_kernel,
-        grid=(1,),
         out_shape=jax.ShapeDtypeStruct(mask.shape, jnp.float32),
-        in_specs=[block] * 3,
-        out_specs=block,
+        in_specs=[pl.BlockSpec(memory_space=pltpu.HBM)] * 3,
+        out_specs=VMEM,
+        scratch_shapes=[
+            pltpu.VMEM(mask.shape, weight.dtype),
+            pltpu.VMEM(mask.shape, mask.dtype),
+            pltpu.VMEM(mask.shape, factor.dtype),
+            pltpu.SemaphoreType.DMA((3,)),
+        ],
         name="solve",
-        compiler_params=params(8),
+        compiler_params=params(60),
         cost_estimate=pl.CostEstimate(flops=20_000_000, bytes_accessed=300_000, transcendentals=0),
     )(weight, mask, factor)
 
@@ -191,7 +205,8 @@
 
 
 def copy_kernel(in_ref, out_ref):
-    out_ref[...] = in_ref[...]
+    rows = out_ref.shape[0]
+    out_ref[...] = in_ref[in_ref.shape[0] - rows :]
 
 
 def order_kernel(from_ref, weight_ref, out_ref):
@@ -223,6 +238,21 @@
         out_ref[y, units:, :] = jnp.concatenate([big, rest], axis=0)
 
 
+def hidden_kernel(parts_ref, stream_ref, hidden_ref, both_ref):
+    units = hidden_ref.shape[0]
+    sums = parts_ref[0].astype(jnp.float32)
+    for k in range(1, 4):
+        sums = sums + parts_ref[k].astype(jnp.float32)
+    square = sums[2 * units : 2 * units + 8] + sums[2 * units + 8 :]
+    inverse = lax.rsqrt(square / 8192 + 1e-05)[:1]
+    gate = sums[:units] * inverse
+    up = sums[units : 2 * units] * inverse
+    hidden = (gate / (1.0 + jnp.exp(-gate)) * up).astype(jnp.bfloat16)
+    hidden_ref[...] = hidden
+    both_ref[:units] = hidden
+    both_ref[units:] = stream_ref[...]
+
+
 def hessian_kernel(from_ref, rows_ref, a0, a1, a2, a3, lower_ref, out_ref, right_ref):
     upper = (a0, a1, a2, a3)
     units = rows_ref.shape[1]
@@ -278,15 +308,6 @@
         compiler_params=params(4),
         cost_estimate=pl.CostEstimate(flops=300_000, bytes_accessed=250_000, transcendentals=0),
     )(parts, residual_turned)
-    stream = turned(stream_turned)
-    stream = pl.pallas_call(
-        copy_kernel,
-        out_shape=jax.ShapeDtypeStruct(stream.shape, stream.dtype),
-        in_specs=[VMEM],
-        out_specs=VMEM,
-        compiler_params=params(1),
-    )(stream)
-
     flat_weight = gate_up_weight.transpose(1, 2, 0).reshape(2 * units, -1)
     flat_weight = pl.pallas_call(
         order_kernel,
@@ -310,14 +331,30 @@
         ),
     )(*upper, lower, flat_weight)
     parts = lax.all_to_all(parts, DP, 0, 0, tiled=True)
-    sums = jnp.sum(parts.astype(jnp.float32), axis=0)
-    square = sums[2 * units : 2 * units + 1] + sums[2 * units + 8 : 2 * units + 9]
-    inverse = lax.rsqrt(square / 8192 + 1e-05)
-    gate_part = sums[:units] * inverse
-    up_part = sums[units : 2 * units] * inverse
-    hidden = (jax.nn.silu(gate_part) * up_part).astype(jnp.bfloat16)
-
-    hidden_turned = turned(hidden)
+    hidden, both = pl.pallas_call(
+        hidden_kernel,
+        out_shape=(
+            jax.ShapeDtypeStruct((units, 128), jnp.bfloat16),
+            jax.ShapeDtypeStruct((units + 128, 128), jnp.bfloat16),
+        ),
+        in_specs=[VMEM] * 2,
+        out_specs=[VMEM] * 2,
+        name="hidden",
+        compiler_params=params(6),
+        cost_estimate=pl.CostEstimate(
+            flops=1_000_000, bytes_accessed=700_000, transcendentals=60_000
+        ),
+    )(parts, stream_turned)
+
+    both = turned(both)
+    stream = pl.pallas_call(
+        copy_kernel,
+        out_shape=jax.ShapeDtypeStruct((128, 128), jnp.bfloat16),
+        in_specs=[VMEM],
+        out_specs=VMEM,
+        compiler_params=params(1),
+    )(both)
+    hidden_turned = both[:units]
     upper, lower = over_y_and_x(over_z(hidden_turned), units // 2)
     hidden_rows = lax.all_gather(hidden, DP)
     piece = pl.BlockSpec((4, 1, units // 2, 128), lambda z: (0, z, 0, 0))

time: 197 us -> 192 us (0.975)
  starting transfers between devices: 75.3 us -> 67.2 us
  blocking collectives: 53.2 us -> 59.5 us
  waiting for transfers between devices: 36.5 us -> 33.4 us
    ppermute x4 -> x3, waiting for transfers between devices: 16.6 us -> 4.98 us  [turned(): return lax.ppermute(x, (*DP, 'y'), pairs)]
    ppermute x15, waiting for transfers between devices: 19.2 us -> 27.8 us  [round_x(): lax.ppermute(x, 'x', [(k, (k + step) % 4) for k in range(4)])]
    ppermute x4 -> x3, starting transfers between devices: 21.1 us -> 12.7 us  [turned(): return lax.ppermute(x, (*DP, 'y'), pairs)]
    all_gather x1, blocking collectives: 4.52 us -> 10.6 us  [body(): hidden_rows = lax.all_gather(hidden, DP)]
    unnamed x34 -> x30, local copies, waits for them, and re-layouts: 9.72 us -> 7.89 us
    pallas_call x2 -> x3, Pallas kernels: 2.8 us -> 4.44 us  [the longest x1 3.73 us: solved_errors(): pl.pallas_call(solve_kernel, out_shape=jax.ShapeDtypeStruct(mask.shape, j...]
  transfers between devices with their start and end apart: 29 -> 28, of which waited for: 15 -> 16; matrix products, arithmetic and copies ran while one was open for 0% -> 0% of each run, Pallas kernels for 3% -> 4%
where the time goes in v3:
time: 192 us; the launch traced here: 191 us
  starting transfers between devices  67.2 us (35%)
  blocking collectives  59.5 us (31%)
  waiting for transfers between devices  33.4 us (17%)
  Pallas kernels  15.8 us (8%)
  local copies, waits for them, and re-layouts  14 us (7%)
    all_to_all x5, starting transfers between devices, copy_for_each(): lax.all_to_all(jnp.broadcast_to(x[None], (size, *x.shape)), axis, 0, 0, t...  29.3 us
    ppermute x15, waiting for transfers between devices, round_x(): lax.ppermute(x, 'x', [(k, (k + step) % 4) for k in range(4)])  27.8 us
    all_to_all x2, blocking collectives, copy_for_each(): lax.all_to_all(jnp.broadcast_to(x[None], (size, *x.shape)), axis, 0, 0, t...  24 us
    all_to_all x1, blocking collectives, body(): parts = lax.all_to_all(parts, DP, 0, 0, tiled=True)  17.6 us
    ppermute x15, starting transfers between devices, round_x(): lax.ppermute(x, 'x', [(k, (k + step) % 4) for k in range(4)])  15.6 us
    ppermute x3, starting transfers between devices, turned(): return lax.ppermute(x, (*DP, 'y'), pairs)  12.7 us
    all_gather x1, blocking collectives, body(): hidden_rows = lax.all_gather(hidden, DP)  10.6 us
    unnamed x30, local copies, waits for them, and re-layouts  7.89 us
  transfers between devices with their start and end apart: 28, of which 16 were waited for; matrix products, arithmetic and copies ran while one was open for 0% of the time, Pallas kernels for 4%

profile of v3, /device:TPU:1, one launch (start us, length us, event | category | flops | bytes accessed | tf_op | source)
XLA Modules:
  0.0 190.9 jit_solution(8744844117201393616)
XLA Ops:
  0.7 1.6 broadcast_in_dim.25
  2.3 9.0 %all-to-all-start = ((bf16[8,128,128]{2,1,0:T(8,128)(2,1)}), bf16[8,128,128]{2,1,0:T(8,128)(2,1)S(1)}, u32[]{:S(2)}, u32[]{:S(2)}) async-start(bf16[8,128,128]{2,1,0:T(8,128)(2,1)} %broadcast_in_dim.25), calls=%async_computation | async-start | bytes 524288 | tf_op jit(solution)/shard_map/all_to_all | solution.py:25
  11.3 3.7 %solve.1 = f32[128,128]{1,0:T(8,128)} custom-call(bf16[128,2048]{1,0:T(8,128)(2,1)} %weight_ref.1, s32[128,128]{1,0:T(8,128)} %mask_ref.1, f32[128,2048]{1,0:T(8,128)} %factor_ref.1), custom_call_target="tpu_custom_call" | custom-call | flops 20000000 | bytes 300000 | tf_op jit(solution)/shard_map/solve/pallas_call | solution.py:112
  15.0 7.3 %all-gather = f32[512,128]{1,0:T(8,128)S(1)} all-gather(f32[128,128]{1,0:T(8,128)} %solve.1), channel_id=2, replica_groups=mesh['z_low'=2,'core'=2,'y'=4,'z_high'=4,'x'=4] {'z_low','core'}, dimensions={0}, use_global_device_ids=true | all-gather | bytes 327680 | tf_op jit(solution)/shard_map/all_gather | solution.py:285
  22.3 1.8 update.1
  24.1 2.7 %collective-permute-start.2 = (bf16[8,128,128]{2,1,0:T(8,128)(2,1)S(1)}, bf16[8,128,128]{2,1,0:T(8,128)(2,1)S(1)}, u32[]{:S(2)}, u32[]{:S(2)}) collective-permute-start(bf16[8,128,128]{2,1,0:T(8,128)(2,1)S(1)} %all-to-all-done.refs_0_), channel_id=1, source_target_pairs={{0,2},{1,3},{2,0},{3,1},{4,6},{5,7},{6,4},{7,5},{8,10},{9,11},{10,... | collective-permute-start | bytes 786440 | tf_op jit(solution)/shard_map/ppermute | solution.py:35
  26.9 3.5 %collective-permute-start.7 = (bf16[128,2048]{1,0:T(8,128)(2,1)}, bf16[128,2048]{1,0:T(8,128)(2,1)S(1)}, u32[]{:S(2)}, u32[]{:S(2)}) collective-permute-start(bf16[128,2048]{1,0:T(8,128)(2,1)} %update.1), channel_id=1, source_target_pairs={{0,0},{16,64},{32,128},{48,192},{64,16},{80,80},{96,144},{112,208}... | collective-permute-start | bytes 1572872 | tf_op jit(solution)/shard_map/ppermute | solution.py:30
  30.4 0.9 collective-permute-start.1
  31.9 1.4 collective-permute-done.2.refs_3_
  33.3 1.1 collective-permute-start.6
  34.4 4.6 %collective-permute-done.1.refs_2_ = bf16[8,128,128]{2,1,0:T(8,128)(2,1)S(1)} collective-permute-done((bf16[8,128,128]{2,1,0:T(8,128)(2,1)S(1)}, bf16[8,128,128]{2,1,0:T(8,128)(2,1)S(1)}, u32[]{:S(2)}, u32[]{:S(2)}) %collective-permute-start.1) | collective-permute-done | bytes 262176 | tf_op jit(solution)/shard_map/ppermute | solution.py:35
  39.0 1.0 collective-permute-start.5
  41.6 1.9 %project.1 = bf16[4,128,128]{2,1,0:T(8,128)(2,1)} custom-call(s32[4]{0:T(128)S(1)} %pad_add_fusion.from_ref, s32[1]{0:T(128)} %bitcast.6.core_ref, bf16[8,128,128]{2,1,0:T(8,128)(2,1)S(1)} %all-to-all-done.refs_0_, bf16[8,128,128]{2,1,0:T(8,128)(2,1)S(1)} %collective-permute-done.refs_1_, bf16[8,128,128]{2,1,0:T(8,128)(2,1)S(1)} %collective-permute-done.1.refs_2_, ...), custom_call_target="tpu_custom_call" | custom-call | flops 268000000 | bytes 2700000 | tf_op jit(solution)/shard_map/project/pallas_call | solution.py:289
  43.5 7.5 %all-to-all-start.1 = ((bf16[4,128,128]{2,1,0:T(8,128)(2,1)}), bf16[4,128,128]{2,1,0:T(8,128)(2,1)S(1)}, u32[]{:S(2)}, u32[]{:S(2)}) async-start(bf16[4,128,128]{2,1,0:T(8,128)(2,1)} %project.1), calls=%async_computation.1 | async-start | bytes 262144 | tf_op jit(solution)/shard_map/all_to_all | solution.py:298
  51.0 4.8 %collective-permute-start.8 = (bf16[144,128]{1,0:T(8,128)(2,1)S(1)}, bf16[144,128]{1,0:T(8,128)(2,1)S(1)}, u32[]{:S(2)}, u32[]{:S(2)}) collective-permute-start(bf16[144,128]{1,0:T(8,128)(2,1)S(1)} %pad_maximum_fusion.2), channel_id=1, source_target_pairs={{0,0},{16,64},{32,128},{48,192},{64,16},{80,80},{96,144},{112,208}... | collective-permute-start | bytes 110600 | tf_op jit(solution)/shard_map/ppermute | solution.py:30
  55.8 1.9 %collective-permute-done.8.residual_ref = bf16[144,128]{1,0:T(8,128)(2,1)S(1)} collective-permute-done((bf16[144,128]{1,0:T(8,128)(2,1)S(1)}, bf16[144,128]{1,0:T(8,128)(2,1)S(1)}, u32[]{:S(2)}, u32[]{:S(2)}) %collective-permute-start.8) | collective-permute-done | bytes 36896 | tf_op jit(solution)/shard_map/ppermute | solution.py:30
  58.6 13.5 %all_to_all.45 = bf16[4,136,128]{2,1,0:T(8,128)(2,1)S(1)} all-to-all(bf16[4,136,128]{2,1,0:T(8,128)(2,1)S(1)} %broadcast_in_dim.27), channel_id=1, replica_groups=mesh['z_low'=2,'core'=2,'y'=4,'z_high'=4,'x'=4] {'z_high'}, dimensions={0} | all-to-all | bytes 278528 | tf_op jit(solution)/shard_map/all_to_all | solution.py:25
  72.9 4.7 %all-to-all-start.3 = ((bf16[4,4,64,128]{3,2,1,0:T(8,128)(2,1)}), bf16[4,4,64,128]{3,2,1,0:T(8,128)(2,1)S(1)}, u32[]{:S(2)}, u32[]{:S(2)}) async-start(bf16[4,4,64,128]{3,2,1,0:T(8,128)(2,1)} %broadcast_in_dim.28), calls=%async_computation.3 | async-start | bytes 524288 | tf_op jit(solution)/shard_map/all_to_all | solution.py:25
  77.6 0.9 collective-permute-start.13
  79.8 1.1 collective-permute-done.13
  80.8 2.1 %collective-permute-done.12 = bf16[4,72,128]{2,1,0:T(8,128)(2,1)S(1)} collective-permute-done((bf16[4,72,128]{2,1,0:T(8,128)(2,1)S(1)}, bf16[4,72,128]{2,1,0:T(8,128)(2,1)S(1)}, u32[]{:S(2)}, u32[]{:S(2)}) %collective-permute-start.12) | collective-permute-done | bytes 73760 | tf_op jit(solution)/shard_map/ppermute | solution.py:35
  82.9 0.9 collective-permute-done.14
  83.9 1.2 broadcast_in_dim.29
  85.0 4.2 %all-to-all-start.4 = ((bf16[4,4,4,72,128]{4,3,2,1,0:T(8,128)(2,1)}), bf16[4,4,4,72,128]{4,3,2,1,0:T(8,128)(2,1)S(1)}, u32[]{:S(2)}, u32[]{:S(2)}) async-start(bf16[4,4,4,72,128]{4,3,2,1,0:T(8,128)(2,1)} %broadcast_in_dim.29), calls=%async_computation.4 | async-start | bytes 2359296 | tf_op jit(solution)/shard_map/all_to_all | solution.py:25
  89.3 1.1 collective-permute-start.11
  90.4 1.7 collective-permute-start.10
  92.0 1.5 copy-done.2
  93.5 1.0 order.1.weight_ref
  94.6 1.5 collective-permute-done.11.a3
  96.0 2.5 %collective-permute-done.10.a2 = bf16[4,4,64,128]{3,2,1,0:T(8,128)(2,1)S(1)} collective-permute-done((bf16[4,4,64,128]{3,2,1,0:T(8,128)(2,1)S(1)}, bf16[4,4,64,128]{3,2,1,0:T(8,128)(2,1)S(1)}, u32[]{:S(2)}, u32[]{:S(2)}) %collective-permute-start.10) | collective-permute-done | bytes 262176 | tf_op jit(solution)/shard_map/ppermute | solution.py:35
  99.9 0.9 copy-done.6
  100.9 0.9 copy-done.8
  101.9 2.1 %gate_up.1 = bf16[4,464,128]{2,1,0:T(8,128)(2,1)S(1)} custom-call(bf16[4,4,64,128]{3,2,1,0:T(8,128)(2,1)S(1)} %all-to-all-done.3.a0, bf16[4,4,64,128]{3,2,1,0:T(8,128)(2,1)S(1)} %copy-done.8, bf16[4,4,64,128]{3,2,1,0:T(8,128)(2,1)S(1)} %copy-done.6, bf16[4,4,64,128]{3,2,1,0:T(8,128)(2,1)S(1)} %collective-permute-done.11.a3, ...), custom_call_target="tpu_custom_call" | custom-call | flops 940000000 | bytes 4300000 | tf_op jit(solution)/shard_map/gate_up/pallas_call | solution.py:322
  103.9 17.6 %all_to_all.46.parts_ref = bf16[4,464,128]{2,1,0:T(8,128)(2,1)S(1)} all-to-all(bf16[4,464,128]{2,1,0:T(8,128)(2,1)S(1)} %gate_up.1), channel_id=1, replica_groups=mesh['z_low'=2,'core'=2,'y'=4,'z_high'=4,'x'=4] {'z_low','core'}, dimensions={0} | all-to-all | bytes 950272 | tf_op jit(solution)/shard_map/all_to_all | solution.py:333
  122.2 4.4 %collective-permute-start.15 = (bf16[352,128]{1,0:T(8,128)(2,1)S(1)}, bf16[352,128]{1,0:T(8,128)(2,1)S(1)}, u32[]{:S(2)}, u32[]{:S(2)}) collective-permute-start(bf16[352,128]{1,0:T(8,128)(2,1)S(1)} %get-tuple-element.9), channel_id=1, source_target_pairs={{0,0},{16,64},{32,128},{48,192},{64,16},{80,80},{96,144},{112,208}... | collective-permute-start | bytes 270344 | tf_op jit(solution)/shard_map/ppermute | solution.py:30
  126.6 2.2 %collective-permute-done.15.in_ref = bf16[352,128]{1,0:T(8,128)(2,1)S(1)} collective-permute-done((bf16[352,128]{1,0:T(8,128)(2,1)S(1)}, bf16[352,128]{1,0:T(8,128)(2,1)S(1)}, u32[]{:S(2)}, u32[]{:S(2)}) %collective-permute-start.15) | collective-permute-done | bytes 90144 | tf_op jit(solution)/shard_map/ppermute | solution.py:30
  128.9 10.5 %all_to_all.47 = bf16[4,224,128]{2,1,0:T(8,128)(2,1)S(1)} all-to-all(bf16[4,224,128]{2,1,0:T(8,128)(2,1)S(1)} %broadcast_in_dim.30), channel_id=1, replica_groups=mesh['z_low'=2,'core'=2,'y'=4,'z_high'=4,'x'=4] {'z_high'}, dimensions={0} | all-to-all | bytes 458752 | tf_op jit(solution)/shard_map/all_to_all | solution.py:25
  140.2 7.4 %all-to-all-start.7 = ((bf16[4,4,112,128]{3,2,1,0:T(8,128)(2,1)}), bf16[4,4,112,128]{3,2,1,0:T(8,128)(2,1)S(1)}, u32[]{:S(2)}, u32[]{:S(2)}) async-start(bf16[4,4,112,128]{3,2,1,0:T(8,128)(2,1)} %broadcast_in_dim.31), calls=%async_computation.7 | async-start | bytes 917504 | tf_op jit(solution)/shard_map/all_to_all | solution.py:25
  147.6 2.3 %collective-permute-start.20 = (bf16[4,112,128]{2,1,0:T(8,128)(2,1)S(1)}, bf16[4,112,128]{2,1,0:T(8,128)(2,1)S(1)}, u32[]{:S(2)}, u32[]{:S(2)}) collective-permute-start(bf16[4,112,128]{2,1,0:T(8,128)(2,1)S(1)} %get-tuple-element.12), channel_id=1, source_target_pairs={{0,3},{1,0},{2,1},{3,2},{4,7},{5,4},{6,5},{7,6},{8,11},{9,8},{10,9... | collective-permute-start | bytes 344072 | tf_op jit(solution)/shard_map/ppermute | solution.py:35
  150.0 1.2 collective-permute-start.21
  151.8 4.6 %collective-permute-done.19 = bf16[4,112,128]{2,1,0:T(8,128)(2,1)S(1)} collective-permute-done((bf16[4,112,128]{2,1,0:T(8,128)(2,1)S(1)}, bf16[4,112,128]{2,1,0:T(8,128)(2,1)S(1)}, u32[]{:S(2)}, u32[]{:S(2)}) %collective-permute-start.19) | collective-permute-done | bytes 114720 | tf_op jit(solution)/shard_map/ppermute | solution.py:35
  156.4 1.6 broadcast_in_dim.32
  158.0 3.9 %all-to-all-start.8 = ((bf16[4,4,4,112,128]{4,3,2,1,0:T(8,128)(2,1)}), bf16[4,4,4,112,128]{4,3,2,1,0:T(8,128)(2,1)S(1)}, u32[]{:S(2)}, u32[]{:S(2)}) async-start(bf16[4,4,4,112,128]{4,3,2,1,0:T(8,128)(2,1)} %broadcast_in_dim.32), calls=%async_computation.8 | async-start | bytes 3670016 | tf_op jit(solution)/shard_map/all_to_all | solution.py:25
  162.3 2.3 %collective-permute-start.17 = (bf16[4,4,112,128]{3,2,1,0:T(8,128)(2,1)S(1)}, bf16[4,4,112,128]{3,2,1,0:T(8,128)(2,1)S(1)}, u32[]{:S(2)}, u32[]{:S(2)}) collective-permute-start(bf16[4,4,112,128]{3,2,1,0:T(8,128)(2,1)S(1)} %all-to-all-done.7.a0), channel_id=1, source_target_pairs={{0,3},{1,0},{2,1},{3,2},{4,7},{5,4},{6,5},{7,6},{8,11},{9,8},{10,9... | collective-permute-start | bytes 1376264 | tf_op jit(solution)/shard_map/ppermute | solution.py:35
  164.8 10.6 %all-gather.1 = bf16[896,128]{1,0:T(8,128)(2,1)S(1)} all-gather(bf16[224,128]{1,0:T(8,128)(2,1)} %copy-done.10), channel_id=3, replica_groups=mesh['z_low'=2,'core'=2,'y'=4,'z_high'=4,'x'=4] {'z_low','core'}, dimensions={0}, use_global_device_ids=true | all-gather | bytes 286720 | tf_op jit(solution)/shard_map/all_gather | solution.py:359
  176.0 8.5 %collective-permute-done.17.a2 = bf16[4,4,112,128]{3,2,1,0:T(8,128)(2,1)S(1)} collective-permute-done((bf16[4,4,112,128]{3,2,1,0:T(8,128)(2,1)S(1)}, bf16[4,4,112,128]{3,2,1,0:T(8,128)(2,1)S(1)}, u32[]{:S(2)}, u32[]{:S(2)}) %collective-permute-start.17) | collective-permute-done | bytes 458784 | tf_op jit(solution)/shard_map/ppermute | solution.py:35
  185.5 1.0 copy-done.4
  186.5 4.4 %hessian.1 = f32[224,3584]{1,0:T(8,128)} custom-call(s32[4]{0:T(128)S(1)} %pad_add_fusion.from_ref, bf16[4,224,128]{2,1,0:T(8,128)(2,1)S(1)} %bitcast.23, bf16[4,4,112,128]{3,2,1,0:T(8,128)(2,1)S(1)} %all-to-all-done.7.a0, bf16[4,4,112,128]{3,2,1,0:T(8,128)(2,1)S(1)} %copy-done.4, bf16[4,4,112,128]{3,2,1,0:T(8,128)(2,1)S(1)} %collective-permute-done.17.a2, ...), custom_call_target="tpu_custom_call" | custom-call | flops 822000000 | bytes 7100000 | tf_op jit(solution)/shard_map/hessian/pallas_call | solution.py:361
  (68 shorter events, 11.0 us)
Async XLA Ops:
  0.6 21.7 %copy-start = (f32[128,2048]{1,0:T(8,128)S(1)}, f32[128,2048]{1,0:T(8,128)}, u32[]{:S(2)}) copy-start(f32[128,2048]{1,0:T(8,128)} %factor_ref.1) | copy-start | bytes 3145732
  0.6 21.7 %copy-start.9 = (s32[128,128]{1,0:T(8,128)S(1)}, s32[128,128]{1,0:T(8,128)}, u32[]{:S(2)}) copy-start(s32[128,128]{1,0:T(8,128)} %mask_ref.1) | copy-start | bytes 196612
  0.7 21.6 %copy-start.1 = (bf16[128,2048]{1,0:T(8,128)(2,1)S(1)}, bf16[128,2048]{1,0:T(8,128)(2,1)}, u32[]{:S(2)}) copy-start(bf16[128,2048]{1,0:T(8,128)(2,1)} %weight_ref.1) | copy-start | bytes 1572868
  2.3 21.8 %all-to-all-start = ((bf16[8,128,128]{2,1,0:T(8,128)(2,1)}), bf16[8,128,128]{2,1,0:T(8,128)(2,1)S(1)}, u32[]{:S(2)}, u32[]{:S(2)}) async-start(bf16[8,128,128]{2,1,0:T(8,128)(2,1)} %broadcast_in_dim.25), calls=%async_computation | async-start | bytes 524288 | tf_op jit(solution)/shard_map/all_to_all | solution.py:25
  24.1 26.9 %copy-start.14 = (bf16[128]{0:T(256)(128)(2,1)S(1)}, bf16[128]{0:T(256)(128)(2,1)}, u32[]{:S(2)}) copy-start(bf16[128]{0:T(256)(128)(2,1)} %param.12) | copy-start | bytes 772
  24.1 26.9 %copy-start.13 = (bf16[128,128]{1,0:T(8,128)(2,1)S(1)}, bf16[128,128]{1,0:T(8,128)(2,1)}, u32[]{:S(2)}) copy-start(bf16[128,128]{1,0:T(8,128)(2,1)} %param.8) | copy-start | bytes 98308
  24.1 9.2 %collective-permute-start.2 = (bf16[8,128,128]{2,1,0:T(8,128)(2,1)S(1)}, bf16[8,128,128]{2,1,0:T(8,128)(2,1)S(1)}, u32[]{:S(2)}, u32[]{:S(2)}) collective-permute-start(bf16[8,128,128]{2,1,0:T(8,128)(2,1)S(1)} %all-to-all-done.refs_0_), channel_id=1, source_target_pairs={{0,2},{1,3},{2,0},{3,1},{4,6},{5,7},{6,4},{7,5},{8,10},{9,11},{10,... | collective-permute-start | bytes 786440 | tf_op jit(solution)/shard_map/ppermute | solution.py:35
  26.9 14.1 %collective-permute-start.7 = (bf16[128,2048]{1,0:T(8,128)(2,1)}, bf16[128,2048]{1,0:T(8,128)(2,1)S(1)}, u32[]{:S(2)}, u32[]{:S(2)}) collective-permute-start(bf16[128,2048]{1,0:T(8,128)(2,1)} %update.1), channel_id=1, source_target_pairs={{0,0},{16,64},{32,128},{48,192},{64,16},{80,80},{96,144},{112,208}... | collective-permute-start | bytes 1572872 | tf_op jit(solution)/shard_map/ppermute | solution.py:30
  30.4 8.6 %collective-permute-start.1 = (bf16[8,128,128]{2,1,0:T(8,128)(2,1)S(1)}, bf16[8,128,128]{2,1,0:T(8,128)(2,1)S(1)}, u32[]{:S(2)}, u32[]{:S(2)}) collective-permute-start(bf16[8,128,128]{2,1,0:T(8,128)(2,1)S(1)} %all-to-all-done.refs_0_), channel_id=1, source_target_pairs={{0,3},{1,0},{2,1},{3,2},{4,7},{5,4},{6,5},{7,6},{8,11},{9,8},{10,9... | collective-permute-start | bytes 786440 | tf_op jit(solution)/shard_map/ppermute | solution.py:35
  31.3 8.7 %collective-permute-start = (bf16[8,128,128]{2,1,0:T(8,128)(2,1)S(1)}, bf16[8,128,128]{2,1,0:T(8,128)(2,1)S(1)}, u32[]{:S(2)}, u32[]{:S(2)}) collective-permute-start(bf16[8,128,128]{2,1,0:T(8,128)(2,1)S(1)} %all-to-all-done.refs_0_), channel_id=1, source_target_pairs={{0,1},{1,2},{2,3},{3,0},{4,5},{5,6},{6,7},{7,4},{8,9},{9,10},{10,1... | collective-permute-start | bytes 786440 | tf_op jit(solution)/shard_map/ppermute | solution.py:35
  31.9 9.1 %collective-permute-start.3 = (bf16[8,128,128]{2,1,0:T(8,128)(2,1)S(1)}, bf16[8,128,128]{2,1,0:T(8,128)(2,1)S(1)}, u32[]{:S(2)}, u32[]{:S(2)}) collective-permute-start(bf16[8,128,128]{2,1,0:T(8,128)(2,1)S(1)} %all-to-all-done.refs_0_), channel_id=1, source_target_pairs={{0,64},{64,0},{1,65},{65,1},{2,66},{66,2},{3,67},{67,3},{4,68},{68... | collective-permute-start | bytes 786440 | tf_op jit(solution)/shard_map/ppermute | solution.py:280
  33.3 7.7 %collective-permute-start.6 = (bf16[8,128,128]{2,1,0:T(8,128)(2,1)S(1)}, bf16[8,128,128]{2,1,0:T(8,128)(2,1)S(1)}, u32[]{:S(2)}, u32[]{:S(2)}) collective-permute-start(bf16[8,128,128]{2,1,0:T(8,128)(2,1)S(1)} %collective-permute-done.2.refs_3_), channel_id=1, source_target_pairs={{0,64},{64,0},{1,65},{65,1},{2,66},{66,2},{3,67},{67,3},{4,68},{68... | collective-permute-start | bytes 786440 | tf_op jit(solution)/shard_map/ppermute | solution.py:280
  39.0 2.2 %collective-permute-start.5 = (bf16[8,128,128]{2,1,0:T(8,128)(2,1)S(1)}, bf16[8,128,128]{2,1,0:T(8,128)(2,1)S(1)}, u32[]{:S(2)}, u32[]{:S(2)}) collective-permute-start(bf16[8,128,128]{2,1,0:T(8,128)(2,1)S(1)} %collective-permute-done.1.refs_2_), channel_id=1, source_target_pairs={{0,64},{64,0},{1,65},{65,1},{2,66},{66,2},{3,67},{67,3},{4,68},{68... | collective-permute-start | bytes 786440 | tf_op jit(solution)/shard_map/ppermute | solution.py:280
  40.1 1.5 collective-permute-start.4
  43.5 14.2 %all-to-all-start.1 = ((bf16[4,128,128]{2,1,0:T(8,128)(2,1)}), bf16[4,128,128]{2,1,0:T(8,128)(2,1)S(1)}, u32[]{:S(2)}, u32[]{:S(2)}) async-start(bf16[4,128,128]{2,1,0:T(8,128)(2,1)} %project.1), calls=%async_computation.1 | async-start | bytes 262144 | tf_op jit(solution)/shard_map/all_to_all | solution.py:298
  51.0 6.7 %collective-permute-start.8 = (bf16[144,128]{1,0:T(8,128)(2,1)S(1)}, bf16[144,128]{1,0:T(8,128)(2,1)S(1)}, u32[]{:S(2)}, u32[]{:S(2)}) collective-permute-start(bf16[144,128]{1,0:T(8,128)(2,1)S(1)} %pad_maximum_fusion.2), channel_id=1, source_target_pairs={{0,0},{16,64},{32,128},{48,192},{64,16},{80,80},{96,144},{112,208}... | collective-permute-start | bytes 110600 | tf_op jit(solution)/shard_map/ppermute | solution.py:30
  57.9 0.6 copy-start.11
  72.9 11.0 %all-to-all-start.3 = ((bf16[4,4,64,128]{3,2,1,0:T(8,128)(2,1)}), bf16[4,4,64,128]{3,2,1,0:T(8,128)(2,1)S(1)}, u32[]{:S(2)}, u32[]{:S(2)}) async-start(bf16[4,4,64,128]{3,2,1,0:T(8,128)(2,1)} %broadcast_in_dim.28), calls=%async_computation.3 | async-start | bytes 524288 | tf_op jit(solution)/shard_map/all_to_all | solution.py:25
  77.6 3.3 %collective-permute-start.13 = (bf16[4,72,128]{2,1,0:T(8,128)(2,1)S(1)}, bf16[4,72,128]{2,1,0:T(8,128)(2,1)S(1)}, u32[]{:S(2)}, u32[]{:S(2)}) collective-permute-start(bf16[4,72,128]{2,1,0:T(8,128)(2,1)S(1)} %get-tuple-element.15), channel_id=1, source_target_pairs={{0,3},{1,0},{2,1},{3,2},{4,7},{5,4},{6,5},{7,6},{8,11},{9,8},{10,9... | collective-permute-start | bytes 221192 | tf_op jit(solution)/shard_map/ppermute | solution.py:35
  78.5 4.4 %collective-permute-start.12 = (bf16[4,72,128]{2,1,0:T(8,128)(2,1)S(1)}, bf16[4,72,128]{2,1,0:T(8,128)(2,1)S(1)}, u32[]{:S(2)}, u32[]{:S(2)}) collective-permute-start(bf16[4,72,128]{2,1,0:T(8,128)(2,1)S(1)} %get-tuple-element.15), channel_id=1, source_target_pairs={{0,1},{1,2},{2,3},{3,0},{4,5},{5,6},{6,7},{7,4},{8,9},{9,10},{10,1... | collective-permute-start | bytes 221192 | tf_op jit(solution)/shard_map/ppermute | solution.py:35
  79.1 4.7 %collective-permute-start.14 = (bf16[4,72,128]{2,1,0:T(8,128)(2,1)S(1)}, bf16[4,72,128]{2,1,0:T(8,128)(2,1)S(1)}, u32[]{:S(2)}, u32[]{:S(2)}) collective-permute-start(bf16[4,72,128]{2,1,0:T(8,128)(2,1)S(1)} %get-tuple-element.15), channel_id=1, source_target_pairs={{0,2},{1,3},{2,0},{3,1},{4,6},{5,7},{6,4},{7,5},{8,10},{9,11},{10,... | collective-permute-start | bytes 221192 | tf_op jit(solution)/shard_map/ppermute | solution.py:35
  85.0 14.9 %all-to-all-start.4 = ((bf16[4,4,4,72,128]{4,3,2,1,0:T(8,128)(2,1)}), bf16[4,4,4,72,128]{4,3,2,1,0:T(8,128)(2,1)S(1)}, u32[]{:S(2)}, u32[]{:S(2)}) async-start(bf16[4,4,4,72,128]{4,3,2,1,0:T(8,128)(2,1)} %broadcast_in_dim.29), calls=%async_computation.4 | async-start | bytes 2359296 | tf_op jit(solution)/shard_map/all_to_all | solution.py:25
  89.3 6.8 %collective-permute-start.11 = (bf16[4,4,64,128]{3,2,1,0:T(8,128)(2,1)S(1)}, bf16[4,4,64,128]{3,2,1,0:T(8,128)(2,1)S(1)}, u32[]{:S(2)}, u32[]{:S(2)}) collective-permute-start(bf16[4,4,64,128]{3,2,1,0:T(8,128)(2,1)S(1)} %all-to-all-done.3.a0), channel_id=1, source_target_pairs={{0,2},{1,3},{2,0},{3,1},{4,6},{5,7},{6,4},{7,5},{8,10},{9,11},{10,... | collective-permute-start | bytes 786440 | tf_op jit(solution)/shard_map/ppermute | solution.py:35
  90.4 8.2 %collective-permute-start.10 = (bf16[4,4,64,128]{3,2,1,0:T(8,128)(2,1)S(1)}, bf16[4,4,64,128]{3,2,1,0:T(8,128)(2,1)S(1)}, u32[]{:S(2)}, u32[]{:S(2)}) collective-permute-start(bf16[4,4,64,128]{3,2,1,0:T(8,128)(2,1)S(1)} %all-to-all-done.3.a0), channel_id=1, source_target_pairs={{0,3},{1,0},{2,1},{3,2},{4,7},{5,4},{6,5},{7,6},{8,11},{9,8},{10,9... | collective-permute-start | bytes 786440 | tf_op jit(solution)/shard_map/ppermute | solution.py:35
  92.0 7.2 %collective-permute-start.9 = (bf16[4,4,64,128]{3,2,1,0:T(8,128)(2,1)S(1)}, bf16[4,4,64,128]{3,2,1,0:T(8,128)(2,1)S(1)}, u32[]{:S(2)}, u32[]{:S(2)}) collective-permute-start(bf16[4,4,64,128]{3,2,1,0:T(8,128)(2,1)S(1)} %all-to-all-done.3.a0), channel_id=1, source_target_pairs={{0,1},{1,2},{2,3},{3,0},{4,5},{5,6},{6,7},{7,4},{8,9},{9,10},{10,1... | collective-permute-start | bytes 786440 | tf_op jit(solution)/shard_map/ppermute | solution.py:35
  92.0 1.5 copy-start.2
  98.5 0.7 copy-start.5
  99.2 0.7 copy-start.7
  99.9 1.0 copy-start.6
  100.9 0.9 copy-start.8
  101.8 19.7 %copy-start.12 = (bf16[128,128]{1,0:T(8,128)(2,1)S(1)}, bf16[128,128]{1,0:T(8,128)(2,1)}, u32[]{:S(2)}) copy-start(bf16[128,128]{1,0:T(8,128)(2,1)} %copy-done.11) | copy-start | bytes 98308
  121.6 0.6 copy-start.10
  122.2 6.6 %collective-permute-start.15 = (bf16[352,128]{1,0:T(8,128)(2,1)S(1)}, bf16[352,128]{1,0:T(8,128)(2,1)S(1)}, u32[]{:S(2)}, u32[]{:S(2)}) collective-permute-start(bf16[352,128]{1,0:T(8,128)(2,1)S(1)} %get-tuple-element.9), channel_id=1, source_target_pairs={{0,0},{16,64},{32,128},{48,192},{64,16},{80,80},{96,144},{112,208}... | collective-permute-start | bytes 270344 | tf_op jit(solution)/shard_map/ppermute | solution.py:30
  140.2 16.2 %all-to-all-start.7 = ((bf16[4,4,112,128]{3,2,1,0:T(8,128)(2,1)}), bf16[4,4,112,128]{3,2,1,0:T(8,128)(2,1)S(1)}, u32[]{:S(2)}, u32[]{:S(2)}) async-start(bf16[4,4,112,128]{3,2,1,0:T(8,128)(2,1)} %broadcast_in_dim.31), calls=%async_computation.7 | async-start | bytes 917504 | tf_op jit(solution)/shard_map/all_to_all | solution.py:25
  147.6 4.1 %collective-permute-start.20 = (bf16[4,112,128]{2,1,0:T(8,128)(2,1)S(1)}, bf16[4,112,128]{2,1,0:T(8,128)(2,1)S(1)}, u32[]{:S(2)}, u32[]{:S(2)}) collective-permute-start(bf16[4,112,128]{2,1,0:T(8,128)(2,1)S(1)} %get-tuple-element.12), channel_id=1, source_target_pairs={{0,3},{1,0},{2,1},{3,2},{4,7},{5,4},{6,5},{7,6},{8,11},{9,8},{10,9... | collective-permute-start | bytes 344072 | tf_op jit(solution)/shard_map/ppermute | solution.py:35
  150.0 6.4 %collective-permute-start.19 = (bf16[4,112,128]{2,1,0:T(8,128)(2,1)S(1)}, bf16[4,112,128]{2,1,0:T(8,128)(2,1)S(1)}, u32[]{:S(2)}, u32[]{:S(2)}) collective-permute-start(bf16[4,112,128]{2,1,0:T(8,128)(2,1)S(1)} %get-tuple-element.12), channel_id=1, source_target_pairs={{0,1},{1,2},{2,3},{3,0},{4,5},{5,6},{6,7},{7,4},{8,9},{9,10},{10,1... | collective-permute-start | bytes 344072 | tf_op jit(solution)/shard_map/ppermute | solution.py:35
  150.0 6.4 %collective-permute-start.21 = (bf16[4,112,128]{2,1,0:T(8,128)(2,1)S(1)}, bf16[4,112,128]{2,1,0:T(8,128)(2,1)S(1)}, u32[]{:S(2)}, u32[]{:S(2)}) collective-permute-start(bf16[4,112,128]{2,1,0:T(8,128)(2,1)S(1)} %get-tuple-element.12), channel_id=1, source_target_pairs={{0,2},{1,3},{2,0},{3,1},{4,6},{5,7},{6,4},{7,5},{8,10},{9,11},{10,... | collective-permute-start | bytes 344072 | tf_op jit(solution)/shard_map/ppermute | solution.py:35
  158.0 27.5 %all-to-all-start.8 = ((bf16[4,4,4,112,128]{4,3,2,1,0:T(8,128)(2,1)}), bf16[4,4,4,112,128]{4,3,2,1,0:T(8,128)(2,1)S(1)}, u32[]{:S(2)}, u32[]{:S(2)}) async-start(bf16[4,4,4,112,128]{4,3,2,1,0:T(8,128)(2,1)} %broadcast_in_dim.32), calls=%async_computation.8 | async-start | bytes 3670016 | tf_op jit(solution)/shard_map/all_to_all | solution.py:25
  162.0 14.1 %collective-permute-start.18 = (bf16[4,4,112,128]{3,2,1,0:T(8,128)(2,1)S(1)}, bf16[4,4,112,128]{3,2,1,0:T(8,128)(2,1)S(1)}, u32[]{:S(2)}, u32[]{:S(2)}) collective-permute-start(bf16[4,4,112,128]{3,2,1,0:T(8,128)(2,1)S(1)} %all-to-all-done.7.a0), channel_id=1, source_target_pairs={{0,2},{1,3},{2,0},{3,1},{4,6},{5,7},{6,4},{7,5},{8,10},{9,11},{10,... | collective-permute-start | bytes 1376264 | tf_op jit(solution)/shard_map/ppermute | solution.py:35
  162.3 22.3 %collective-permute-start.17 = (bf16[4,4,112,128]{3,2,1,0:T(8,128)(2,1)S(1)}, bf16[4,4,112,128]{3,2,1,0:T(8,128)(2,1)S(1)}, u32[]{:S(2)}, u32[]{:S(2)}) collective-permute-start(bf16[4,4,112,128]{3,2,1,0:T(8,128)(2,1)S(1)} %all-to-all-done.7.a0), channel_id=1, source_target_pairs={{0,3},{1,0},{2,1},{3,2},{4,7},{5,4},{6,5},{7,6},{8,11},{9,8},{10,9... | collective-permute-start | bytes 1376264 | tf_op jit(solution)/shard_map/ppermute | solution.py:35
  164.5 20.1 %collective-permute-start.16 = (bf16[4,4,112,128]{3,2,1,0:T(8,128)(2,1)S(1)}, bf16[4,4,112,128]{3,2,1,0:T(8,128)(2,1)S(1)}, u32[]{:S(2)}, u32[]{:S(2)}) collective-permute-start(bf16[4,4,112,128]{3,2,1,0:T(8,128)(2,1)S(1)} %all-to-all-done.7.a0), channel_id=1, source_target_pairs={{0,1},{1,2},{2,3},{3,0},{4,5},{5,6},{6,7},{7,4},{8,9},{9,10},{10,1... | collective-permute-start | bytes 1376264 | tf_op jit(solution)/shard_map/ppermute | solution.py:35
  184.7 0.8 copy-start.3
  185.5 1.0 copy-start.4

commit v4 on v3

--- a/solution.py
+++ b/solution.py
@@ -30,17 +30,17 @@
     return lax.ppermute(x, (*DP, "y"), pairs)
 
 
-def round_x(x):
+def round_trip(x, axis):
     return [x] + [
-        lax.ppermute(x, "x", [(k, (k + step) % 4) for k in range(4)]) for step in STEPS
+        lax.ppermute(x, axis, [(k, (k + step) % 4) for k in range(4)]) for step in STEPS
     ]
 
 
 def over_y_and_x(x, half):
-    lower = jnp.stack(round_x(x[:, half:]))
-    upper = copy_for_each(x[:, :half], "y")
-    upper = round_x(upper)
-    lower = copy_for_each(lower, "y")
+    lower = jnp.stack(round_trip(x[:, half:], "x"))
+    upper = jnp.stack(round_trip(x[:, :half], "y"))
+    upper = round_trip(upper, "x")
+    lower = round_trip(lower, "y")
     return upper, lower
 
 
@@ -48,8 +48,8 @@
     return copy_for_each(x, "z_high")
 
 
-def senders():
-    here = lax.axis_index("x")
+def senders(axis):
+    here = lax.axis_index(axis)
     return jnp.stack([here] + [(here + 4 - step) % 4 for step in STEPS]).astype(jnp.int32)
 
 
@@ -213,36 +213,47 @@
     out_ref[...] = ordered_columns(weight_ref, from_ref)
 
 
-def gate_up_kernel(a0, a1, a2, a3, lower_ref, weight_ref, out_ref):
-    upper = (a0, a1, a2, a3)
-    half = a0.shape[2]
+def gate_up_kernel(group_ref, core_ref, *refs):
+    upper, lower, weight_ref = refs[:4], refs[4:8], refs[8]
+    keep_ref, send_ref, part_ref = refs[9:]
+    half = upper[0].shape[2]
     weight = weight_ref[...]
     units = weight.shape[0]
     places = [(r, z) for r in range(4) for z in range(4)]
-    for y in range(4):
-        high = jnp.concatenate([upper[r][y, z] for r, z in places], axis=1)
-        low = jnp.concatenate([lower_ref[y, r, z, :half] for r, z in places], axis=1)
-        part = lax.dot_general(
+    for k in range(4):
+        high = jnp.concatenate([upper[r][k, z] for r, z in places], axis=1)
+        low = jnp.concatenate([lower[k][r, z, :half] for r, z in places], axis=1)
+        square = jnp.zeros((8, LANES), jnp.float32)
+        for r, z in places:
+            square = square + lower[k][r, z, half:].astype(jnp.float32)
+        group = group_ref[k]
+        part_ref[group, :units, :] = lax.dot_general(
             weight,
             jnp.concatenate([high, low], axis=0),
             NT,
             preferred_element_type=jnp.float32,
         )
-        square = jnp.zeros((8, LANES), jnp.float32)
-        for r, z in places:
-            square = square + lower_ref[y, r, z, half:].astype(jnp.float32)
         total = jnp.broadcast_to(square[0:1] + square[1:2], square.shape)
-        big = total.astype(jnp.bfloat16)
-        rest = (total - big.astype(jnp.float32)).astype(jnp.bfloat16)
-        out_ref[y, :units, :] = part.astype(jnp.bfloat16)
-        out_ref[y, units:, :] = jnp.concatenate([big, rest], axis=0)
-
-
-def hidden_kernel(parts_ref, stream_ref, hidden_ref, both_ref):
+        big = total.astype(jnp.bfloat16).astype(jnp.float32)
+        part_ref[group, units:, :] = jnp.concatenate([big, total - big], axis=0)
+    for low_z in range(2):
+        keep_ref[low_z] = part_ref[low_z * 2 + core_ref[0]]
+        send_ref[low_z] = part_ref[low_z * 2 + 1 - core_ref[0]].astype(jnp.bfloat16)
+
+
+def pair_kernel(low_ref, keep_ref, got_ref, next_keep_ref, next_send_ref):
+    for ref, place in ((next_keep_ref, low_ref[0]), (next_send_ref, 1 - low_ref[0])):
+        total = keep_ref[place] + got_ref[place].astype(jnp.float32)
+        rows = total.shape[0] - 16
+        ref[:rows] = total[:rows].astype(ref.dtype)
+        square = total[rows : rows + 8] + total[rows + 8 :]
+        big = square.astype(jnp.bfloat16).astype(jnp.float32)
+        ref[rows:] = jnp.concatenate([big, square - big], axis=0).astype(ref.dtype)
+
+
+def hidden_kernel(keep_ref, got_ref, stream_ref, hidden_ref, both_ref):
     units = hidden_ref.shape[0]
-    sums = parts_ref[0].astype(jnp.float32)
-    for k in range(1, 4):
-        sums = sums + parts_ref[k].astype(jnp.float32)
+    sums = keep_ref[...] + got_ref[...].astype(jnp.float32)
     square = sums[2 * units : 2 * units + 8] + sums[2 * units + 8 :]
     inverse = lax.rsqrt(square / 8192 + 1e-05)[:1]
     gate = sums[:units] * inverse
@@ -253,17 +264,17 @@
     both_ref[units:] = stream_ref[...]
 
 
-def hessian_kernel(from_ref, rows_ref, a0, a1, a2, a3, lower_ref, out_ref, right_ref):
-    upper = (a0, a1, a2, a3)
+def hessian_kernel(from_ref, group_ref, rows_ref, *refs):
+    upper, lower, out_ref, right_ref = refs[:4], refs[4:8], refs[8], refs[9]
     units = rows_ref.shape[1]
     half = units // 2
     for r in range(4):
         base = from_ref[r] * units
-        for y in range(4):
-            lanes = slice(y * LANES, (y + 1) * LANES)
-            right_ref[pl.ds(pl.multiple_of(base, 16), half), lanes] = upper[r][y, 0]
-            right_ref[pl.ds(pl.multiple_of(base + half, 16), half), lanes] = lower_ref[y, r, 0]
-    left = jnp.concatenate([rows_ref[t] for t in range(4)], axis=1)
+        for k in range(4):
+            lanes = slice(k * LANES, (k + 1) * LANES)
+            right_ref[pl.ds(pl.multiple_of(base, 16), half), lanes] = upper[r][k, 0]
+            right_ref[pl.ds(pl.multiple_of(base + half, 16), half), lanes] = lower[k][r, 0]
+    left = jnp.concatenate([rows_ref[group_ref[k]] for k in range(4)], axis=1)
     out_ref[...] = (2.0 / 512) * lax.dot_general(
         left, right_ref[...], NT, preferred_element_type=jnp.float32
     )
@@ -272,11 +283,13 @@
 def body(attn_out, residual, output_weight, prune_mask, inverse_factor, norm_gain, gate_up_weight):
     units = gate_up_weight.shape[2]
     is_first = (lax.axis_index(DP) == 0).astype(jnp.int32)[None]
-    order = senders()
+    order = senders("x")
+    groups = senders("y")
     core = lax.axis_index("core").astype(jnp.int32)[None]
+    low_z = lax.axis_index("z_low").astype(jnp.int32)[None]
 
     mine = copy_for_each(attn_out, ("z_high", "z_low"))
-    mine = round_x(mine)
+    mine = round_trip(mine, "x")
     other = [lax.ppermute(block, "core", [(0, 1), (1, 0)]) for block in mine]
     gain_rows = jnp.broadcast_to(norm_gain[None], (16, norm_gain.shape[0]))
     residual_turned = turned(jnp.concatenate([residual, gain_rows], axis=0))
@@ -319,32 +332,50 @@
         cost_estimate=pl.CostEstimate(flops=0, bytes_accessed=3_700_000, transcendentals=0),
     )(order, flat_weight)
     upper, lower = over_y_and_x(over_z(block), 64)
-    parts = pl.pallas_call(
+    sums = (2, 2 * units + 16, 128)
+    keep, send = pl.pallas_call(
         gate_up_kernel,
-        out_shape=jax.ShapeDtypeStruct((4, 2 * units + 16, 128), jnp.bfloat16),
-        in_specs=[VMEM] * 6,
-        out_specs=VMEM,
+        out_shape=(
+            jax.ShapeDtypeStruct(sums, jnp.float32),
+            jax.ShapeDtypeStruct(sums, jnp.bfloat16),
+        ),
+        in_specs=[SMEM] * 2 + [VMEM] * 9,
+        out_specs=[VMEM] * 2,
+        scratch_shapes=[pltpu.VMEM((4, *sums[1:]), jnp.float32)],
         name="gate_up",
         compiler_params=params(14),
         cost_estimate=pl.CostEstimate(
             flops=940_000_000, bytes_accessed=4_300_000, transcendentals=0
         ),
-    )(*upper, lower, flat_weight)
-    parts = lax.all_to_all(parts, DP, 0, 0, tiled=True)
+    )(groups, core, *upper, *lower, flat_weight)
+    got = lax.ppermute(send, "core", [(0, 1), (1, 0)])
+    keep, send = pl.pallas_call(
+        pair_kernel,
+        out_shape=(
+            jax.ShapeDtypeStruct(sums[1:], jnp.float32),
+            jax.ShapeDtypeStruct(sums[1:], jnp.bfloat16),
+        ),
+        in_specs=[SMEM] + [VMEM] * 2,
+        out_specs=[VMEM] * 2,
+        name="pair",
+        compiler_params=params(6),
+        cost_estimate=pl.CostEstimate(flops=300_000, bytes_accessed=1_000_000, transcendentals=0),
+    )(low_z, keep, got)
+    got = lax.ppermute(send, "z_low", [(0, 1), (1, 0)])
     hidden, both = pl.pallas_call(
         hidden_kernel,
         out_shape=(
             jax.ShapeDtypeStruct((units, 128), jnp.bfloat16),
             jax.ShapeDtypeStruct((units + 128, 128), jnp.bfloat16),
         ),
-        in_specs=[VMEM] * 2,
+        in_specs=[VMEM] * 3,
         out_specs=[VMEM] * 2,
         name="hidden",
         compiler_params=params(6),
         cost_estimate=pl.CostEstimate(
             flops=1_000_000, bytes_accessed=700_000, transcendentals=60_000
         ),
-    )(parts, stream_turned)
+    )(keep, got, stream_turned)
 
     both = turned(both)
     stream = pl.pallas_call(
@@ -364,16 +395,16 @@
         out_shape=jax.ShapeDtypeStruct((units, 16 * units), jnp.float32),
         in_specs=[
             SMEM,
+            SMEM,
             pl.BlockSpec((4, units, 128), lambda z: (0, 0, 0)),
-            *[piece] * 4,
-            pl.BlockSpec((4, 4, 1, units // 2, 128), lambda z: (0, 0, z, 0, 0)),
+            *[piece] * 8,
         ],
         out_specs=pl.BlockSpec((units, 4 * units), lambda z: (0, z)),
         scratch_shapes=[pltpu.VMEM((4 * units, 4 * LANES), jnp.bfloat16)],
         name="hessian",
         compiler_params=params(14),
         cost_estimate=pl.CostEstimate(flops=822_000_000, bytes_accessed=7_100_000, transcendentals=0),
-    )(order, hidden_rows, *upper, lower)
+    )(order, groups, hidden_rows, *upper, *lower)
     return (pruned_weight, stream, hessian)
 
 

time: 192 us -> 193 us (level)
  waiting for transfers between devices: 33.4 us -> 52.2 us
  blocking collectives: 59.5 us -> 45.1 us
  local copies, waits for them, and re-layouts: 14 us -> 3.94 us
  starting transfers between devices: 67.2 us -> 71.4 us
    ppermute x15 -> x29, starting transfers between devices: 15.6 us -> 40.4 us  [the longest x27 30.6 us: round_trip(): lax.ppermute(x, axis, [(k, (k + step) % 4) for k in range(4)])]
    all_to_all x5 -> x1, starting transfers between devices: 29.3 us -> 9 us  [copy_for_each(): lax.all_to_all(jnp.broadcast_to(x[None], (size, *x.shape)), axis, 0, 0, t...]
    ppermute x15 -> x29, waiting for transfers between devices: 27.8 us -> 45.7 us  [the longest x27 40.2 us: round_trip(): lax.ppermute(x, axis, [(k, (k + step) % 4) for k in range(4)])]
    all_to_all x1 -> x0, blocking collectives: 17.6 us -> none  [body(): parts = lax.all_to_all(parts, DP, 0, 0, tiled=True)]
    unnamed x30 -> x16, local copies, waits for them, and re-layouts: 7.89 us -> 2.17 us
    broadcast_in_dim x7 -> x3, local copies, waits for them, and re-layouts: 6.01 us -> 1.66 us  [copy_for_each(): jnp.broadcast_to(x[None], (size, *x.shape))]
    all_gather x1, blocking collectives: 10.6 us -> 13.2 us  [body(): hidden_rows = lax.all_gather(hidden, DP)]
  transfers between devices with their start and end apart: 28 -> 38, of which waited for: 16 -> 22; matrix products, arithmetic and copies ran while one was open for 0% -> 0% of each run, Pallas kernels for 4% -> 4%
where the time goes in v4:
time: 193 us; the launch traced here: 191 us
  starting transfers between devices  71.4 us (37%)
  waiting for transfers between devices  52.2 us (27%)
  blocking collectives  45.1 us (23%)
  Pallas kernels  17 us (9%)
  local copies, waits for them, and re-layouts  3.94 us (2%)
    ppermute x27, waiting for transfers between devices, round_trip(): lax.ppermute(x, axis, [(k, (k + step) % 4) for k in range(4)])  40.2 us
    ppermute x27, starting transfers between devices, round_trip(): lax.ppermute(x, axis, [(k, (k + step) % 4) for k in range(4)])  30.6 us
    all_to_all x2, blocking collectives, copy_for_each(): lax.all_to_all(jnp.broadcast_to(x[None], (size, *x.shape)), axis, 0, 0, t...  24.6 us
    all_gather x1, blocking collectives, body(): hidden_rows = lax.all_gather(hidden, DP)  13.2 us
    ppermute x3, starting transfers between devices, turned(): return lax.ppermute(x, (*DP, 'y'), pairs)  12.4 us
    ppermute x1, starting transfers between devices, body(): got = lax.ppermute(send, 'core', [(0, 1), (1, 0)])  9.73 us
    all_to_all x1, starting transfers between devices, copy_for_each(): lax.all_to_all(jnp.broadcast_to(x[None], (size, *x.shape)), axis, 0, 0, t...  9 us
    all_to_all x1, starting transfers between devices, body(): parts = lax.all_to_all(parts, 'y', 0, 0, tiled=True)  7.46 us
  transfers between devices with their start and end apart: 38, of which 22 were waited for; matrix products, arithmetic and copies ran while one was open for 0% of the time, Pallas kernels for 4%

profile of v4, /device:TPU:1, one launch (start us, length us, event | category | flops | bytes accessed | tf_op | source)
XLA Modules:
  0.0 190.9 jit_solution(12135234953926949426)
XLA Ops:
  0.7 1.6 broadcast_in_dim.39
  2.3 9.0 %all-to-all-start = ((bf16[8,128,128]{2,1,0:T(8,128)(2,1)}), bf16[8,128,128]{2,1,0:T(8,128)(2,1)S(1)}, u32[]{:S(2)}, u32[]{:S(2)}) async-start(bf16[8,128,128]{2,1,0:T(8,128)(2,1)} %broadcast_in_dim.39), calls=%async_computation | async-start | bytes 524288 | tf_op jit(solution)/shard_map/all_to_all | solution.py:25
  11.3 3.7 %solve.1 = f32[128,128]{1,0:T(8,128)} custom-call(bf16[128,2048]{1,0:T(8,128)(2,1)} %weight_ref.1, s32[128,128]{1,0:T(8,128)} %mask_ref.1, f32[128,2048]{1,0:T(8,128)} %factor_ref.1), custom_call_target="tpu_custom_call" | custom-call | flops 20000000 | bytes 300000 | tf_op jit(solution)/shard_map/solve/pallas_call | solution.py:112
  15.0 7.3 %all-gather = f32[512,128]{1,0:T(8,128)S(1)} all-gather(f32[128,128]{1,0:T(8,128)} %solve.1), channel_id=2, replica_groups=mesh['z_low'=2,'core'=2,'y'=4,'z_high'=4,'x'=4] {'z_low','core'}, dimensions={0}, use_global_device_ids=true | all-gather | bytes 327680 | tf_op jit(solution)/shard_map/all_gather | solution.py:298
  22.3 1.8 update.1
  24.1 2.7 %collective-permute-start.2 = (bf16[8,128,128]{2,1,0:T(8,128)(2,1)S(1)}, bf16[8,128,128]{2,1,0:T(8,128)(2,1)S(1)}, u32[]{:S(2)}, u32[]{:S(2)}) collective-permute-start(bf16[8,128,128]{2,1,0:T(8,128)(2,1)S(1)} %all-to-all-done.refs_0_), channel_id=1, source_target_pairs={{0,2},{1,3},{2,0},{3,1},{4,6},{5,7},{6,4},{7,5},{8,10},{9,11},{10,... | collective-permute-start | bytes 786440 | tf_op jit(solution)/shard_map/ppermute | solution.py:35
  26.9 3.5 %collective-permute-start.7 = (bf16[128,2048]{1,0:T(8,128)(2,1)}, bf16[128,2048]{1,0:T(8,128)(2,1)S(1)}, u32[]{:S(2)}, u32[]{:S(2)}) collective-permute-start(bf16[128,2048]{1,0:T(8,128)(2,1)} %update.1), channel_id=1, source_target_pairs={{0,0},{16,64},{32,128},{48,192},{64,16},{80,80},{96,144},{112,208}... | collective-permute-start | bytes 1572872 | tf_op jit(solution)/shard_map/ppermute | solution.py:30
  30.4 0.9 collective-permute-start.1
  31.9 1.4 collective-permute-done.2.refs_3_
  33.3 1.1 collective-permute-start.6
  34.4 4.6 %collective-permute-done.1.refs_2_ = bf16[8,128,128]{2,1,0:T(8,128)(2,1)S(1)} collective-permute-done((bf16[8,128,128]{2,1,0:T(8,128)(2,1)S(1)}, bf16[8,128,128]{2,1,0:T(8,128)(2,1)S(1)}, u32[]{:S(2)}, u32[]{:S(2)}) %collective-permute-start.1) | collective-permute-done | bytes 262176 | tf_op jit(solution)/shard_map/ppermute | solution.py:35
  39.0 1.0 collective-permute-start.5
  41.6 1.9 %project.1 = bf16[4,128,128]{2,1,0:T(8,128)(2,1)} custom-call(s32[4]{0:T(128)S(1)} %pad_add_fusion.1.from_ref, s32[1]{0:T(128)} %bitcast.7.core_ref, bf16[8,128,128]{2,1,0:T(8,128)(2,1)S(1)} %all-to-all-done.refs_0_, bf16[8,128,128]{2,1,0:T(8,128)(2,1)S(1)} %collective-permute-done.refs_1_, bf16[8,128,128]{2,1,0:T(8,128)(2,1)S(1)} %collective-permute-done.1.refs_2_, ...), custom_call_target="tpu_custom_call" | custom-call | flops 268000000 | bytes 2700000 | tf_op jit(solution)/shard_map/project/pallas_call | solution.py:302
  43.5 7.5 %all-to-all-start.1 = ((bf16[4,128,128]{2,1,0:T(8,128)(2,1)}), bf16[4,128,128]{2,1,0:T(8,128)(2,1)S(1)}, u32[]{:S(2)}, u32[]{:S(2)}) async-start(bf16[4,128,128]{2,1,0:T(8,128)(2,1)} %project.1), calls=%async_computation.1 | async-start | bytes 262144 | tf_op jit(solution)/shard_map/all_to_all | solution.py:311
  51.0 4.8 %collective-permute-start.8 = (bf16[144,128]{1,0:T(8,128)(2,1)S(1)}, bf16[144,128]{1,0:T(8,128)(2,1)S(1)}, u32[]{:S(2)}, u32[]{:S(2)}) collective-permute-start(bf16[144,128]{1,0:T(8,128)(2,1)S(1)} %pad_maximum_fusion.4), channel_id=1, source_target_pairs={{0,0},{16,64},{32,128},{48,192},{64,16},{80,80},{96,144},{112,208}... | collective-permute-start | bytes 110600 | tf_op jit(solution)/shard_map/ppermute | solution.py:30
  55.8 1.9 %collective-permute-done.8.residual_ref = bf16[144,128]{1,0:T(8,128)(2,1)S(1)} collective-permute-done((bf16[144,128]{1,0:T(8,128)(2,1)S(1)}, bf16[144,128]{1,0:T(8,128)(2,1)S(1)}, u32[]{:S(2)}, u32[]{:S(2)}) %collective-permute-start.8) | collective-permute-done | bytes 36896 | tf_op jit(solution)/shard_map/ppermute | solution.py:30
  58.6 13.5 %all_to_all.20 = bf16[4,136,128]{2,1,0:T(8,128)(2,1)S(1)} all-to-all(bf16[4,136,128]{2,1,0:T(8,128)(2,1)S(1)} %broadcast_in_dim.41), channel_id=1, replica_groups=mesh['z_low'=2,'core'=2,'y'=4,'z_high'=4,'x'=4] {'z_high'}, dimensions={0} | all-to-all | bytes 278528 | tf_op jit(solution)/shard_map/all_to_all | solution.py:25
  72.1 3.5 %collective-permute-start.10 = (bf16[4,64,128]{2,1,0:T(8,128)(2,1)S(1)}, bf16[4,64,128]{2,1,0:T(8,128)(2,1)S(1)}, u32[]{:S(2)}, u32[]{:S(2)}) collective-permute-start(bf16[4,64,128]{2,1,0:T(8,128)(2,1)S(1)} %get-tuple-element.26), channel_id=1, source_target_pairs={{0,48},{16,0},{32,16},{48,32},{1,49},{17,1},{33,17},{49,33},{2,50}... | collective-permute-start | bytes 196616 | tf_op jit(solution)/shard_map/ppermute | solution.py:35
  75.6 1.3 collective-permute-start.11
  76.9 3.7 %collective-permute-done.9 = bf16[4,64,128]{2,1,0:T(8,128)(2,1)S(1)} collective-permute-done((bf16[4,64,128]{2,1,0:T(8,128)(2,1)S(1)}, bf16[4,64,128]{2,1,0:T(8,128)(2,1)S(1)}, u32[]{:S(2)}, u32[]{:S(2)}) %collective-permute-start.9) | collective-permute-done | bytes 65568 | tf_op jit(solution)/shard_map/ppermute | solution.py:35
  81.0 2.8 %collective-permute-start.16 = (bf16[4,72,128]{2,1,0:T(8,128)(2,1)S(1)}, bf16[4,72,128]{2,1,0:T(8,128)(2,1)S(1)}, u32[]{:S(2)}, u32[]{:S(2)}) collective-permute-start(bf16[4,72,128]{2,1,0:T(8,128)(2,1)S(1)} %get-tuple-element.24), channel_id=1, source_target_pairs={{0,3},{1,0},{2,1},{3,2},{4,7},{5,4},{6,5},{7,6},{8,11},{9,8},{10,9... | collective-permute-start | bytes 221192 | tf_op jit(solution)/shard_map/ppermute | solution.py:35
  83.8 1.7 collective-permute-start.17
  85.5 1.3 collective-permute-done.16
  86.8 1.5 collective-permute-done.15
  89.1 0.9 collective-permute-start.20
  90.1 1.5 collective-permute-start.19
  92.1 2.6 %collective-permute-start.13 = (bf16[4,4,64,128]{3,2,1,0:T(8,128)(2,1)S(1)}, bf16[4,4,64,128]{3,2,1,0:T(8,128)(2,1)}, u32[]{:S(2)}, u32[]{:S(2)}) collective-permute-start(bf16[4,4,64,128]{3,2,1,0:T(8,128)(2,1)S(1)} %pad_maximum_fusion.3.refs_0_), channel_id=1, source_target_pairs={{0,3},{1,0},{2,1},{3,2},{4,7},{5,4},{6,5},{7,6},{8,11},{9,8},{10,9... | collective-permute-start | bytes 786440 | tf_op jit(solution)/shard_map/ppermute | solution.py:35
  94.7 1.5 copy-done.2
  96.2 1.0 order.1.refs_8_
  98.0 3.4 %collective-permute-done.12.refs_1_ = bf16[4,4,64,128]{3,2,1,0:T(8,128)(2,1)} collective-permute-done((bf16[4,4,64,128]{3,2,1,0:T(8,128)(2,1)S(1)}, bf16[4,4,64,128]{3,2,1,0:T(8,128)(2,1)}, u32[]{:S(2)}, u32[]{:S(2)}) %collective-permute-start.12) | collective-permute-done | bytes 262176 | tf_op jit(solution)/shard_map/ppermute | solution.py:35
  101.4 3.2 %gate_up.1 = (f32[2,464,128]{2,1,0:T(8,128)S(1)}, bf16[2,464,128]{2,1,0:T(8,128)(2,1)S(1)}) custom-call(s32[4]{0:T(128)S(1)} %pad_add_fusion.group_ref, s32[1]{0:T(128)} %bitcast.7.core_ref, bf16[4,4,64,128]{3,2,1,0:T(8,128)(2,1)S(1)} %pad_maximum_fusion.3.refs_0_, bf16[4,4,64,128]{3,2,1,0:T(8,128)(2,1)} %collective-permute-done.12.refs_1_, ...), custom_call_target="tpu_custom_call" | custom-call | flops 940000000 | bytes 4300000 | tf_op jit(solution)/shard_map/gate_up/pallas_call | solution.py:336
  104.6 9.7 %collective-permute-start.21 = (bf16[2,464,128]{2,1,0:T(8,128)(2,1)S(1)}, bf16[2,464,128]{2,1,0:T(8,128)(2,1)S(1)}, u32[]{:S(2)}, u32[]{:S(2)}) collective-permute-start(bf16[2,464,128]{2,1,0:T(8,128)(2,1)S(1)} %get-tuple-element.13), channel_id=1, source_target_pairs={{0,64},{64,0},{1,65},{65,1},{2,66},{66,2},{3,67},{67,3},{4,68},{68... | collective-permute-start | bytes 712712 | tf_op jit(solution)/shard_map/ppermute | solution.py:351
  114.3 1.1 collective-permute-done.21.got_ref
  115.6 4.4 %collective-permute-done.22.got_ref = bf16[464,128]{1,0:T(8,128)(2,1)S(1)} collective-permute-done((bf16[464,128]{1,0:T(8,128)(2,1)S(1)}, bf16[464,128]{1,0:T(8,128)(2,1)S(1)}, u32[]{:S(2)}, u32[]{:S(2)}) %collective-permute-start.22) | collective-permute-done | bytes 118816 | tf_op jit(solution)/shard_map/ppermute | solution.py:364
  120.1 4.0 %collective-permute-start.23 = (bf16[352,128]{1,0:T(8,128)(2,1)S(1)}, bf16[352,128]{1,0:T(8,128)(2,1)S(1)}, u32[]{:S(2)}, u32[]{:S(2)}) collective-permute-start(bf16[352,128]{1,0:T(8,128)(2,1)S(1)} %get-tuple-element.17), channel_id=1, source_target_pairs={{0,0},{16,64},{32,128},{48,192},{64,16},{80,80},{96,144},{112,208}... | collective-permute-start | bytes 270344 | tf_op jit(solution)/shard_map/ppermute | solution.py:30
  124.1 3.2 %collective-permute-done.23.in_ref = bf16[352,128]{1,0:T(8,128)(2,1)S(1)} collective-permute-done((bf16[352,128]{1,0:T(8,128)(2,1)S(1)}, bf16[352,128]{1,0:T(8,128)(2,1)S(1)}, u32[]{:S(2)}, u32[]{:S(2)}) %collective-permute-start.23) | collective-permute-done | bytes 90144 | tf_op jit(solution)/shard_map/ppermute | solution.py:30
  127.3 11.1 %all_to_all.21 = bf16[4,224,128]{2,1,0:T(8,128)(2,1)S(1)} all-to-all(bf16[4,224,128]{2,1,0:T(8,128)(2,1)S(1)} %broadcast_in_dim.42), channel_id=1, replica_groups=mesh['z_low'=2,'core'=2,'y'=4,'z_high'=4,'x'=4] {'z_high'}, dimensions={0} | all-to-all | bytes 458752 | tf_op jit(solution)/shard_map/all_to_all | solution.py:25
  138.5 2.0 %collective-permute-start.25 = (bf16[4,112,128]{2,1,0:T(8,128)(2,1)S(1)}, bf16[4,112,128]{2,1,0:T(8,128)(2,1)S(1)}, u32[]{:S(2)}, u32[]{:S(2)}) collective-permute-start(bf16[4,112,128]{2,1,0:T(8,128)(2,1)S(1)} %get-tuple-element.22), channel_id=1, source_target_pairs={{0,48},{16,0},{32,16},{48,32},{1,49},{17,1},{33,17},{49,33},{2,50}... | collective-permute-start | bytes 344072 | tf_op jit(solution)/shard_map/ppermute | solution.py:35
  140.5 1.3 collective-permute-start.26
  142.3 4.3 %collective-permute-done.24 = bf16[4,112,128]{2,1,0:T(8,128)(2,1)S(1)} collective-permute-done((bf16[4,112,128]{2,1,0:T(8,128)(2,1)S(1)}, bf16[4,112,128]{2,1,0:T(8,128)(2,1)S(1)}, u32[]{:S(2)}, u32[]{:S(2)}) %collective-permute-start.24) | collective-permute-done | bytes 114720 | tf_op jit(solution)/shard_map/ppermute | solution.py:35
  146.8 0.9 collective-permute-start.31
  148.3 2.9 %collective-permute-start.32 = (bf16[4,112,128]{2,1,0:T(8,128)(2,1)S(1)}, bf16[4,112,128]{2,1,0:T(8,128)(2,1)S(1)}, u32[]{:S(2)}, u32[]{:S(2)}) collective-permute-start(bf16[4,112,128]{2,1,0:T(8,128)(2,1)S(1)} %get-tuple-element.21), channel_id=1, source_target_pairs={{0,2},{1,3},{2,0},{3,1},{4,6},{5,7},{6,4},{7,5},{8,10},{9,11},{10,... | collective-permute-start | bytes 344072 | tf_op jit(solution)/shard_map/ppermute | solution.py:35
  151.8 8.1 %collective-permute-done.31 = bf16[4,112,128]{2,1,0:T(8,128)(2,1)S(1)} collective-permute-done((bf16[4,112,128]{2,1,0:T(8,128)(2,1)S(1)}, bf16[4,112,128]{2,1,0:T(8,128)(2,1)S(1)}, u32[]{:S(2)}, u32[]{:S(2)}) %collective-permute-start.31) | collective-permute-done | bytes 114720 | tf_op jit(solution)/shard_map/ppermute | solution.py:35
  160.5 3.4 %collective-permute-done.30 = bf16[4,112,128]{2,1,0:T(8,128)(2,1)S(1)} collective-permute-done((bf16[4,112,128]{2,1,0:T(8,128)(2,1)S(1)}, bf16[4,112,128]{2,1,0:T(8,128)(2,1)S(1)}, u32[]{:S(2)}, u32[]{:S(2)}) %collective-permute-start.30) | collective-permute-done | bytes 114720 | tf_op jit(solution)/shard_map/ppermute | solution.py:35
  164.0 1.7 collective-permute-start.34
  166.2 13.2 %all-gather.1 = bf16[896,128]{1,0:T(8,128)(2,1)S(1)} all-gather(bf16[224,128]{1,0:T(8,128)(2,1)S(1)} %get-tuple-element.18), channel_id=3, replica_groups=mesh['z_low'=2,'core'=2,'y'=4,'z_high'=4,'x'=4] {'z_low','core'}, dimensions={0}, use_global_device_ids=true | all-gather | bytes 286720 | tf_op jit(solution)/shard_map/all_gather | solution.py:390
  180.0 5.6 %collective-permute-done.34.refs_6_ = bf16[4,4,112,128]{3,2,1,0:T(8,128)(2,1)S(1)} collective-permute-done((bf16[4,4,112,128]{3,2,1,0:T(8,128)(2,1)S(1)}, bf16[4,4,112,128]{3,2,1,0:T(8,128)(2,1)S(1)}, u32[]{:S(2)}, u32[]{:S(2)}) %collective-permute-start.34) | collective-permute-done | bytes 458784 | tf_op jit(solution)/shard_map/ppermute | solution.py:35
  186.4 4.4 %hessian.1 = f32[224,3584]{1,0:T(8,128)} custom-call(s32[4]{0:T(128)S(1)} %pad_add_fusion.1.from_ref, s32[4]{0:T(128)S(1)} %pad_add_fusion.group_ref, bf16[4,224,128]{2,1,0:T(8,128)(2,1)S(1)} %bitcast.38, bf16[4,4,112,128]{3,2,1,0:T(8,128)(2,1)S(1)} %pad_maximum_fusion.refs_0_, bf16[4,4,112,128]{3,2,1,0:T(8,128)(2,1)S(1)} %collective-permute-done.27.refs_1_, ...), custom_call_target="tpu_custom_call" | custom-call | flops 822000000 | bytes 7100000 | tf_op jit(solution)/shard_map/hessian/pallas_call | solution.py:392
  (73 shorter events, 10.5 us)
Async XLA Ops:
  0.6 21.7 %copy-start = (f32[128,2048]{1,0:T(8,128)S(1)}, f32[128,2048]{1,0:T(8,128)}, u32[]{:S(2)}) copy-start(f32[128,2048]{1,0:T(8,128)} %factor_ref.1) | copy-start | bytes 3145732
  0.6 21.7 %copy-start.3 = (s32[128,128]{1,0:T(8,128)S(1)}, s32[128,128]{1,0:T(8,128)}, u32[]{:S(2)}) copy-start(s32[128,128]{1,0:T(8,128)} %mask_ref.1) | copy-start | bytes 196612
  0.7 21.6 %copy-start.1 = (bf16[128,2048]{1,0:T(8,128)(2,1)S(1)}, bf16[128,2048]{1,0:T(8,128)(2,1)}, u32[]{:S(2)}) copy-start(bf16[128,2048]{1,0:T(8,128)(2,1)} %weight_ref.1) | copy-start | bytes 1572868
  2.3 21.8 %all-to-all-start = ((bf16[8,128,128]{2,1,0:T(8,128)(2,1)}), bf16[8,128,128]{2,1,0:T(8,128)(2,1)S(1)}, u32[]{:S(2)}, u32[]{:S(2)}) async-start(bf16[8,128,128]{2,1,0:T(8,128)(2,1)} %broadcast_in_dim.39), calls=%async_computation | async-start | bytes 524288 | tf_op jit(solution)/shard_map/all_to_all | solution.py:25
  24.1 26.9 %copy-start.7 = (bf16[128]{0:T(256)(128)(2,1)S(1)}, bf16[128]{0:T(256)(128)(2,1)}, u32[]{:S(2)}) copy-start(bf16[128]{0:T(256)(128)(2,1)} %param.12) | copy-start | bytes 772
  24.1 26.9 %copy-start.6 = (bf16[128,128]{1,0:T(8,128)(2,1)S(1)}, bf16[128,128]{1,0:T(8,128)(2,1)}, u32[]{:S(2)}) copy-start(bf16[128,128]{1,0:T(8,128)(2,1)} %param.8) | copy-start | bytes 98308
  24.1 9.2 %collective-permute-start.2 = (bf16[8,128,128]{2,1,0:T(8,128)(2,1)S(1)}, bf16[8,128,128]{2,1,0:T(8,128)(2,1)S(1)}, u32[]{:S(2)}, u32[]{:S(2)}) collective-permute-start(bf16[8,128,128]{2,1,0:T(8,128)(2,1)S(1)} %all-to-all-done.refs_0_), channel_id=1, source_target_pairs={{0,2},{1,3},{2,0},{3,1},{4,6},{5,7},{6,4},{7,5},{8,10},{9,11},{10,... | collective-permute-start | bytes 786440 | tf_op jit(solution)/shard_map/ppermute | solution.py:35
  26.9 14.1 %collective-permute-start.7 = (bf16[128,2048]{1,0:T(8,128)(2,1)}, bf16[128,2048]{1,0:T(8,128)(2,1)S(1)}, u32[]{:S(2)}, u32[]{:S(2)}) collective-permute-start(bf16[128,2048]{1,0:T(8,128)(2,1)} %update.1), channel_id=1, source_target_pairs={{0,0},{16,64},{32,128},{48,192},{64,16},{80,80},{96,144},{112,208}... | collective-permute-start | bytes 1572872 | tf_op jit(solution)/shard_map/ppermute | solution.py:30
  30.4 8.6 %collective-permute-start.1 = (bf16[8,128,128]{2,1,0:T(8,128)(2,1)S(1)}, bf16[8,128,128]{2,1,0:T(8,128)(2,1)S(1)}, u32[]{:S(2)}, u32[]{:S(2)}) collective-permute-start(bf16[8,128,128]{2,1,0:T(8,128)(2,1)S(1)} %all-to-all-done.refs_0_), channel_id=1, source_target_pairs={{0,3},{1,0},{2,1},{3,2},{4,7},{5,4},{6,5},{7,6},{8,11},{9,8},{10,9... | collective-permute-start | bytes 786440 | tf_op jit(solution)/shard_map/ppermute | solution.py:35
  31.3 8.7 %collective-permute-start = (bf16[8,128,128]{2,1,0:T(8,128)(2,1)S(1)}, bf16[8,128,128]{2,1,0:T(8,128)(2,1)S(1)}, u32[]{:S(2)}, u32[]{:S(2)}) collective-permute-start(bf16[8,128,128]{2,1,0:T(8,128)(2,1)S(1)} %all-to-all-done.refs_0_), channel_id=1, source_target_pairs={{0,1},{1,2},{2,3},{3,0},{4,5},{5,6},{6,7},{7,4},{8,9},{9,10},{10,1... | collective-permute-start | bytes 786440 | tf_op jit(solution)/shard_map/ppermute | solution.py:35
  31.9 9.1 %collective-permute-start.3 = (bf16[8,128,128]{2,1,0:T(8,128)(2,1)S(1)}, bf16[8,128,128]{2,1,0:T(8,128)(2,1)S(1)}, u32[]{:S(2)}, u32[]{:S(2)}) collective-permute-start(bf16[8,128,128]{2,1,0:T(8,128)(2,1)S(1)} %all-to-all-done.refs_0_), channel_id=1, source_target_pairs={{0,64},{64,0},{1,65},{65,1},{2,66},{66,2},{3,67},{67,3},{4,68},{68... | collective-permute-start | bytes 786440 | tf_op jit(solution)/shard_map/ppermute | solution.py:293
  33.3 7.7 %collective-permute-start.6 = (bf16[8,128,128]{2,1,0:T(8,128)(2,1)S(1)}, bf16[8,128,128]{2,1,0:T(8,128)(2,1)S(1)}, u32[]{:S(2)}, u32[]{:S(2)}) collective-permute-start(bf16[8,128,128]{2,1,0:T(8,128)(2,1)S(1)} %collective-permute-done.2.refs_3_), channel_id=1, source_target_pairs={{0,64},{64,0},{1,65},{65,1},{2,66},{66,2},{3,67},{67,3},{4,68},{68... | collective-permute-start | bytes 786440 | tf_op jit(solution)/shard_map/ppermute | solution.py:293
  39.0 2.2 %collective-permute-start.5 = (bf16[8,128,128]{2,1,0:T(8,128)(2,1)S(1)}, bf16[8,128,128]{2,1,0:T(8,128)(2,1)S(1)}, u32[]{:S(2)}, u32[]{:S(2)}) collective-permute-start(bf16[8,128,128]{2,1,0:T(8,128)(2,1)S(1)} %collective-permute-done.1.refs_2_), channel_id=1, source_target_pairs={{0,64},{64,0},{1,65},{65,1},{2,66},{66,2},{3,67},{67,3},{4,68},{68... | collective-permute-start | bytes 786440 | tf_op jit(solution)/shard_map/ppermute | solution.py:293
  40.1 1.5 collective-permute-start.4
  43.5 14.2 %all-to-all-start.1 = ((bf16[4,128,128]{2,1,0:T(8,128)(2,1)}), bf16[4,128,128]{2,1,0:T(8,128)(2,1)S(1)}, u32[]{:S(2)}, u32[]{:S(2)}) async-start(bf16[4,128,128]{2,1,0:T(8,128)(2,1)} %project.1), calls=%async_computation.1 | async-start | bytes 262144 | tf_op jit(solution)/shard_map/all_to_all | solution.py:311
  51.0 6.7 %collective-permute-start.8 = (bf16[144,128]{1,0:T(8,128)(2,1)S(1)}, bf16[144,128]{1,0:T(8,128)(2,1)S(1)}, u32[]{:S(2)}, u32[]{:S(2)}) collective-permute-start(bf16[144,128]{1,0:T(8,128)(2,1)S(1)} %pad_maximum_fusion.4), channel_id=1, source_target_pairs={{0,0},{16,64},{32,128},{48,192},{64,16},{80,80},{96,144},{112,208}... | collective-permute-start | bytes 110600 | tf_op jit(solution)/shard_map/ppermute | solution.py:30
  57.9 0.6 copy-start.4
  72.1 4.8 %collective-permute-start.10 = (bf16[4,64,128]{2,1,0:T(8,128)(2,1)S(1)}, bf16[4,64,128]{2,1,0:T(8,128)(2,1)S(1)}, u32[]{:S(2)}, u32[]{:S(2)}) collective-permute-start(bf16[4,64,128]{2,1,0:T(8,128)(2,1)S(1)} %get-tuple-element.26), channel_id=1, source_target_pairs={{0,48},{16,0},{32,16},{48,32},{1,49},{17,1},{33,17},{49,33},{2,50}... | collective-permute-start | bytes 196616 | tf_op jit(solution)/shard_map/ppermute | solution.py:35
  75.6 5.0 %collective-permute-start.9 = (bf16[4,64,128]{2,1,0:T(8,128)(2,1)S(1)}, bf16[4,64,128]{2,1,0:T(8,128)(2,1)S(1)}, u32[]{:S(2)}, u32[]{:S(2)}) collective-permute-start(bf16[4,64,128]{2,1,0:T(8,128)(2,1)S(1)} %get-tuple-element.26), channel_id=1, source_target_pairs={{0,16},{16,32},{32,48},{48,0},{1,17},{17,33},{33,49},{49,1},{2,18}... | collective-permute-start | bytes 196616 | tf_op jit(solution)/shard_map/ppermute | solution.py:35
  75.6 5.0 %collective-permute-start.11 = (bf16[4,64,128]{2,1,0:T(8,128)(2,1)S(1)}, bf16[4,64,128]{2,1,0:T(8,128)(2,1)S(1)}, u32[]{:S(2)}, u32[]{:S(2)}) collective-permute-start(bf16[4,64,128]{2,1,0:T(8,128)(2,1)S(1)} %get-tuple-element.26), channel_id=1, source_target_pairs={{0,32},{16,48},{32,0},{48,16},{1,33},{17,49},{33,1},{49,17},{2,34}... | collective-permute-start | bytes 196616 | tf_op jit(solution)/shard_map/ppermute | solution.py:35
  80.7 14.0 %collective-permute-start.14 = (bf16[4,4,64,128]{3,2,1,0:T(8,128)(2,1)S(1)}, bf16[4,4,64,128]{3,2,1,0:T(8,128)(2,1)S(1)}, u32[]{:S(2)}, u32[]{:S(2)}) collective-permute-start(bf16[4,4,64,128]{3,2,1,0:T(8,128)(2,1)S(1)} %pad_maximum_fusion.3.refs_0_), channel_id=1, source_target_pairs={{0,2},{1,3},{2,0},{3,1},{4,6},{5,7},{6,4},{7,5},{8,10},{9,11},{10,... | collective-permute-start | bytes 786440 | tf_op jit(solution)/shard_map/ppermute | solution.py:35
  81.0 5.7 %collective-permute-start.16 = (bf16[4,72,128]{2,1,0:T(8,128)(2,1)S(1)}, bf16[4,72,128]{2,1,0:T(8,128)(2,1)S(1)}, u32[]{:S(2)}, u32[]{:S(2)}) collective-permute-start(bf16[4,72,128]{2,1,0:T(8,128)(2,1)S(1)} %get-tuple-element.24), channel_id=1, source_target_pairs={{0,3},{1,0},{2,1},{3,2},{4,7},{5,4},{6,5},{7,6},{8,11},{9,8},{10,9... | collective-permute-start | bytes 221192 | tf_op jit(solution)/shard_map/ppermute | solution.py:35
  83.8 4.5 %collective-permute-start.15 = (bf16[4,72,128]{2,1,0:T(8,128)(2,1)S(1)}, bf16[4,72,128]{2,1,0:T(8,128)(2,1)S(1)}, u32[]{:S(2)}, u32[]{:S(2)}) collective-permute-start(bf16[4,72,128]{2,1,0:T(8,128)(2,1)S(1)} %get-tuple-element.24), channel_id=1, source_target_pairs={{0,1},{1,2},{2,3},{3,0},{4,5},{5,6},{6,7},{7,4},{8,9},{9,10},{10,1... | collective-permute-start | bytes 221192 | tf_op jit(solution)/shard_map/ppermute | solution.py:35
  83.8 5.3 %collective-permute-start.17 = (bf16[4,72,128]{2,1,0:T(8,128)(2,1)S(1)}, bf16[4,72,128]{2,1,0:T(8,128)(2,1)S(1)}, u32[]{:S(2)}, u32[]{:S(2)}) collective-permute-start(bf16[4,72,128]{2,1,0:T(8,128)(2,1)S(1)} %get-tuple-element.24), channel_id=1, source_target_pairs={{0,2},{1,3},{2,0},{3,1},{4,6},{5,7},{6,4},{7,5},{8,10},{9,11},{10,... | collective-permute-start | bytes 221192 | tf_op jit(solution)/shard_map/ppermute | solution.py:35
  89.1 12.3 %collective-permute-start.20 = (bf16[4,4,72,128]{3,2,1,0:T(8,128)(2,1)S(1)}, bf16[4,4,72,128]{3,2,1,0:T(8,128)(2,1)S(1)}, u32[]{:S(2)}, u32[]{:S(2)}) collective-permute-start(bf16[4,4,72,128]{3,2,1,0:T(8,128)(2,1)S(1)} %pad_maximum_fusion.2.refs_4_), channel_id=1, source_target_pairs={{0,32},{16,48},{32,0},{48,16},{1,33},{17,49},{33,1},{49,17},{2,34}... | collective-permute-start | bytes 884744 | tf_op jit(solution)/shard_map/ppermute | solution.py:35
  90.1 11.3 %collective-permute-start.19 = (bf16[4,4,72,128]{3,2,1,0:T(8,128)(2,1)S(1)}, bf16[4,4,72,128]{3,2,1,0:T(8,128)(2,1)S(1)}, u32[]{:S(2)}, u32[]{:S(2)}) collective-permute-start(bf16[4,4,72,128]{3,2,1,0:T(8,128)(2,1)S(1)} %pad_maximum_fusion.2.refs_4_), channel_id=1, source_target_pairs={{0,48},{16,0},{32,16},{48,32},{1,49},{17,1},{33,17},{49,33},{2,50}... | collective-permute-start | bytes 884744 | tf_op jit(solution)/shard_map/ppermute | solution.py:35
  91.6 9.8 %collective-permute-start.18 = (bf16[4,4,72,128]{3,2,1,0:T(8,128)(2,1)S(1)}, bf16[4,4,72,128]{3,2,1,0:T(8,128)(2,1)S(1)}, u32[]{:S(2)}, u32[]{:S(2)}) collective-permute-start(bf16[4,4,72,128]{3,2,1,0:T(8,128)(2,1)S(1)} %pad_maximum_fusion.2.refs_4_), channel_id=1, source_target_pairs={{0,16},{16,32},{32,48},{48,0},{1,17},{17,33},{33,49},{49,1},{2,18}... | collective-permute-start | bytes 884744 | tf_op jit(solution)/shard_map/ppermute | solution.py:35
  92.1 5.9 %collective-permute-start.13 = (bf16[4,4,64,128]{3,2,1,0:T(8,128)(2,1)S(1)}, bf16[4,4,64,128]{3,2,1,0:T(8,128)(2,1)}, u32[]{:S(2)}, u32[]{:S(2)}) collective-permute-start(bf16[4,4,64,128]{3,2,1,0:T(8,128)(2,1)S(1)} %pad_maximum_fusion.3.refs_0_), channel_id=1, source_target_pairs={{0,3},{1,0},{2,1},{3,2},{4,7},{5,4},{6,5},{7,6},{8,11},{9,8},{10,9... | collective-permute-start | bytes 786440 | tf_op jit(solution)/shard_map/ppermute | solution.py:35
  94.6 6.7 %collective-permute-start.12 = (bf16[4,4,64,128]{3,2,1,0:T(8,128)(2,1)S(1)}, bf16[4,4,64,128]{3,2,1,0:T(8,128)(2,1)}, u32[]{:S(2)}, u32[]{:S(2)}) collective-permute-start(bf16[4,4,64,128]{3,2,1,0:T(8,128)(2,1)S(1)} %pad_maximum_fusion.3.refs_0_), channel_id=1, source_target_pairs={{0,1},{1,2},{2,3},{3,0},{4,5},{5,6},{6,7},{7,4},{8,9},{9,10},{10,1... | collective-permute-start | bytes 786440 | tf_op jit(solution)/shard_map/ppermute | solution.py:35
  94.7 1.5 copy-start.2
  97.3 22.7 %copy-start.5 = (bf16[128,128]{1,0:T(8,128)(2,1)S(1)}, bf16[128,128]{1,0:T(8,128)(2,1)}, u32[]{:S(2)}) copy-start(bf16[128,128]{1,0:T(8,128)(2,1)} %copy-done.4) | copy-start | bytes 98308
  104.6 10.9 %collective-permute-start.21 = (bf16[2,464,128]{2,1,0:T(8,128)(2,1)S(1)}, bf16[2,464,128]{2,1,0:T(8,128)(2,1)S(1)}, u32[]{:S(2)}, u32[]{:S(2)}) collective-permute-start(bf16[2,464,128]{2,1,0:T(8,128)(2,1)S(1)} %get-tuple-element.13), channel_id=1, source_target_pairs={{0,64},{64,0},{1,65},{65,1},{2,66},{66,2},{3,67},{67,3},{4,68},{68... | collective-permute-start | bytes 712712 | tf_op jit(solution)/shard_map/ppermute | solution.py:351
  115.5 4.5 %collective-permute-start.22 = (bf16[464,128]{1,0:T(8,128)(2,1)S(1)}, bf16[464,128]{1,0:T(8,128)(2,1)S(1)}, u32[]{:S(2)}, u32[]{:S(2)}) collective-permute-start(bf16[464,128]{1,0:T(8,128)(2,1)S(1)} %get-tuple-element.15), channel_id=1, source_target_pairs={{0,128},{128,0},{1,129},{129,1},{2,130},{130,2},{3,131},{131,3},{4... | collective-permute-start | bytes 356360 | tf_op jit(solution)/shard_map/ppermute | solution.py:364
  120.1 7.2 %collective-permute-start.23 = (bf16[352,128]{1,0:T(8,128)(2,1)S(1)}, bf16[352,128]{1,0:T(8,128)(2,1)S(1)}, u32[]{:S(2)}, u32[]{:S(2)}) collective-permute-start(bf16[352,128]{1,0:T(8,128)(2,1)S(1)} %get-tuple-element.17), channel_id=1, source_target_pairs={{0,0},{16,64},{32,128},{48,192},{64,16},{80,80},{96,144},{112,208}... | collective-permute-start | bytes 270344 | tf_op jit(solution)/shard_map/ppermute | solution.py:30
  138.5 3.8 %collective-permute-start.25 = (bf16[4,112,128]{2,1,0:T(8,128)(2,1)S(1)}, bf16[4,112,128]{2,1,0:T(8,128)(2,1)S(1)}, u32[]{:S(2)}, u32[]{:S(2)}) collective-permute-start(bf16[4,112,128]{2,1,0:T(8,128)(2,1)S(1)} %get-tuple-element.22), channel_id=1, source_target_pairs={{0,48},{16,0},{32,16},{48,32},{1,49},{17,1},{33,17},{49,33},{2,50}... | collective-permute-start | bytes 344072 | tf_op jit(solution)/shard_map/ppermute | solution.py:35
  140.5 6.1 %collective-permute-start.24 = (bf16[4,112,128]{2,1,0:T(8,128)(2,1)S(1)}, bf16[4,112,128]{2,1,0:T(8,128)(2,1)S(1)}, u32[]{:S(2)}, u32[]{:S(2)}) collective-permute-start(bf16[4,112,128]{2,1,0:T(8,128)(2,1)S(1)} %get-tuple-element.22), channel_id=1, source_target_pairs={{0,16},{16,32},{32,48},{48,0},{1,17},{17,33},{33,49},{49,1},{2,18}... | collective-permute-start | bytes 344072 | tf_op jit(solution)/shard_map/ppermute | solution.py:35
  140.5 6.1 %collective-permute-start.26 = (bf16[4,112,128]{2,1,0:T(8,128)(2,1)S(1)}, bf16[4,112,128]{2,1,0:T(8,128)(2,1)S(1)}, u32[]{:S(2)}, u32[]{:S(2)}) collective-permute-start(bf16[4,112,128]{2,1,0:T(8,128)(2,1)S(1)} %get-tuple-element.22), channel_id=1, source_target_pairs={{0,32},{16,48},{32,0},{48,16},{1,33},{17,49},{33,1},{49,17},{2,34}... | collective-permute-start | bytes 344072 | tf_op jit(solution)/shard_map/ppermute | solution.py:35
  146.7 19.0 %collective-permute-start.29 = (bf16[4,4,112,128]{3,2,1,0:T(8,128)(2,1)S(1)}, bf16[4,4,112,128]{3,2,1,0:T(8,128)(2,1)S(1)}, u32[]{:S(2)}, u32[]{:S(2)}) collective-permute-start(bf16[4,4,112,128]{3,2,1,0:T(8,128)(2,1)S(1)} %pad_maximum_fusion.refs_0_), channel_id=1, source_target_pairs={{0,2},{1,3},{2,0},{3,1},{4,6},{5,7},{6,4},{7,5},{8,10},{9,11},{10,... | collective-permute-start | bytes 1376264 | tf_op jit(solution)/shard_map/ppermute | solution.py:35
  146.8 13.2 %collective-permute-start.31 = (bf16[4,112,128]{2,1,0:T(8,128)(2,1)S(1)}, bf16[4,112,128]{2,1,0:T(8,128)(2,1)S(1)}, u32[]{:S(2)}, u32[]{:S(2)}) collective-permute-start(bf16[4,112,128]{2,1,0:T(8,128)(2,1)S(1)} %get-tuple-element.21), channel_id=1, source_target_pairs={{0,3},{1,0},{2,1},{3,2},{4,7},{5,4},{6,5},{7,6},{8,11},{9,8},{10,9... | collective-permute-start | bytes 344072 | tf_op jit(solution)/shard_map/ppermute | solution.py:35
  147.7 16.2 %collective-permute-start.30 = (bf16[4,112,128]{2,1,0:T(8,128)(2,1)S(1)}, bf16[4,112,128]{2,1,0:T(8,128)(2,1)S(1)}, u32[]{:S(2)}, u32[]{:S(2)}) collective-permute-start(bf16[4,112,128]{2,1,0:T(8,128)(2,1)S(1)} %get-tuple-element.21), channel_id=1, source_target_pairs={{0,1},{1,2},{2,3},{3,0},{4,5},{5,6},{6,7},{7,4},{8,9},{9,10},{10,1... | collective-permute-start | bytes 344072 | tf_op jit(solution)/shard_map/ppermute | solution.py:35
  148.3 15.6 %collective-permute-start.32 = (bf16[4,112,128]{2,1,0:T(8,128)(2,1)S(1)}, bf16[4,112,128]{2,1,0:T(8,128)(2,1)S(1)}, u32[]{:S(2)}, u32[]{:S(2)}) collective-permute-start(bf16[4,112,128]{2,1,0:T(8,128)(2,1)S(1)} %get-tuple-element.21), channel_id=1, source_target_pairs={{0,2},{1,3},{2,0},{3,1},{4,6},{5,7},{6,4},{7,5},{8,10},{9,11},{10,... | collective-permute-start | bytes 344072 | tf_op jit(solution)/shard_map/ppermute | solution.py:35
  151.2 28.8 %collective-permute-start.28 = (bf16[4,4,112,128]{3,2,1,0:T(8,128)(2,1)S(1)}, bf16[4,4,112,128]{3,2,1,0:T(8,128)(2,1)S(1)}, u32[]{:S(2)}, u32[]{:S(2)}) collective-permute-start(bf16[4,4,112,128]{3,2,1,0:T(8,128)(2,1)S(1)} %pad_maximum_fusion.refs_0_), channel_id=1, source_target_pairs={{0,3},{1,0},{2,1},{3,2},{4,7},{5,4},{6,5},{7,6},{8,11},{9,8},{10,9... | collective-permute-start | bytes 1376264 | tf_op jit(solution)/shard_map/ppermute | solution.py:35
  159.9 20.1 %collective-permute-start.27 = (bf16[4,4,112,128]{3,2,1,0:T(8,128)(2,1)S(1)}, bf16[4,4,112,128]{3,2,1,0:T(8,128)(2,1)S(1)}, u32[]{:S(2)}, u32[]{:S(2)}) collective-permute-start(bf16[4,4,112,128]{3,2,1,0:T(8,128)(2,1)S(1)} %pad_maximum_fusion.refs_0_), channel_id=1, source_target_pairs={{0,1},{1,2},{2,3},{3,0},{4,5},{5,6},{6,7},{7,4},{8,9},{9,10},{10,1... | collective-permute-start | bytes 1376264 | tf_op jit(solution)/shard_map/ppermute | solution.py:35
  163.9 16.1 %collective-permute-start.35 = (bf16[4,4,112,128]{3,2,1,0:T(8,128)(2,1)S(1)}, bf16[4,4,112,128]{3,2,1,0:T(8,128)(2,1)S(1)}, u32[]{:S(2)}, u32[]{:S(2)}) collective-permute-start(bf16[4,4,112,128]{3,2,1,0:T(8,128)(2,1)S(1)} %pad_maximum_fusion.1.refs_4_), channel_id=1, source_target_pairs={{0,32},{16,48},{32,0},{48,16},{1,33},{17,49},{33,1},{49,17},{2,34}... | collective-permute-start | bytes 1376264 | tf_op jit(solution)/shard_map/ppermute | solution.py:35
  164.0 21.5 %collective-permute-start.34 = (bf16[4,4,112,128]{3,2,1,0:T(8,128)(2,1)S(1)}, bf16[4,4,112,128]{3,2,1,0:T(8,128)(2,1)S(1)}, u32[]{:S(2)}, u32[]{:S(2)}) collective-permute-start(bf16[4,4,112,128]{3,2,1,0:T(8,128)(2,1)S(1)} %pad_maximum_fusion.1.refs_4_), channel_id=1, source_target_pairs={{0,48},{16,0},{32,16},{48,32},{1,49},{17,1},{33,17},{49,33},{2,50}... | collective-permute-start | bytes 1376264 | tf_op jit(solution)/shard_map/ppermute | solution.py:35
  165.7 20.7 %collective-permute-start.33 = (bf16[4,4,112,128]{3,2,1,0:T(8,128)(2,1)S(1)}, bf16[4,4,112,128]{3,2,1,0:T(8,128)(2,1)S(1)}, u32[]{:S(2)}, u32[]{:S(2)}) collective-permute-start(bf16[4,4,112,128]{3,2,1,0:T(8,128)(2,1)S(1)} %pad_maximum_fusion.1.refs_4_), channel_id=1, source_target_pairs={{0,16},{16,32},{32,48},{48,0},{1,17},{17,33},{33,49},{49,1},{2,18}... | collective-permute-start | bytes 1376264 | tf_op jit(solution)/shard_map/ppermute | solution.py:35

commit v5 on v4

--- a/solution.py
+++ b/solution.py
@@ -31,9 +31,10 @@
 
 
 def round_trip(x, axis):
-    return [x] + [
-        lax.ppermute(x, axis, [(k, (k + step) % 4) for k in range(4)]) for step in STEPS
-    ]
+    blocks = [x]
+    for step in STEPS:
+        blocks.append(lax.ppermute(x, axis, [(k, (k + step) % 4) for k in range(4)]))
+    return blocks
 
 
 def over_y_and_x(x, half):
@@ -126,28 +127,32 @@
     )(weight, mask, factor)
 
 
-def update_kernel(first_ref, errors_ref, factor_ref, weight_ref, mask_ref, out_ref):
+def update_kernel(
+    place_ref, solved_ref, e1, e2, e3, factor_ref, weight_ref, mask_ref, out_ref
+):
+    is_first = place_ref[0] == 0
+    errors = jnp.where(is_first, solved_ref[...], e1[...] + e2[...] + e3[...])
     updated = weight_ref[...].astype(jnp.float32) - lax.dot_general(
-        errors_ref[0],
+        errors,
         factor_ref[...],
         (((1,), (0,)), ((), ())),
         precision=lax.Precision.HIGHEST,
         preferred_element_type=jnp.float32,
     )
     width = mask_ref.shape[1]
-    kept = jnp.where(first_ref[0] == 1, mask_ref[...].astype(jnp.float32), 1.0)
+    kept = jnp.where(is_first, mask_ref[...].astype(jnp.float32), 1.0)
     out_ref[:, :width] = (updated[:, :width] * kept).astype(jnp.bfloat16)
     out_ref[:, width:] = updated[:, width:].astype(jnp.bfloat16)
 
 
-def updated_weight(is_first, errors, factor, weight, mask):
+def updated_weight(place, errors, factor, weight, mask):
     return pl.pallas_call(
         update_kernel,
         grid=(1,),
         out_shape=jax.ShapeDtypeStruct(weight.shape, jnp.bfloat16),
         in_specs=[
             SMEM,
-            corner((1, *errors.shape[1:])),
+            *[corner(mask.shape)] * 4,
             corner(factor.shape),
             corner(weight.shape),
             corner(mask.shape),
@@ -156,7 +161,7 @@
         name="update",
         compiler_params=params(12),
         cost_estimate=pl.CostEstimate(flops=400_000_000, bytes_accessed=2_200_000, transcendentals=0),
-    )(is_first, errors, factor, weight, mask)
+    )(place, *errors, factor, weight, mask)
 
 
 def columns_at(ref, block):
@@ -264,25 +269,41 @@
     both_ref[units:] = stream_ref[...]
 
 
-def hessian_kernel(from_ref, group_ref, rows_ref, *refs):
-    upper, lower, out_ref, right_ref = refs[:4], refs[4:8], refs[8], refs[9]
-    units = rows_ref.shape[1]
+def hessian_kernel(from_ref, group_ref, place_ref, near_ref, far_ref, *refs):
+    upper, lower, out_ref, left_ref, right_ref = refs[:4], refs[4:8], *refs[8:]
+    units = near_ref.shape[1]
     half = units // 2
-    for r in range(4):
-        base = from_ref[r] * units
-        for k in range(4):
-            lanes = slice(k * LANES, (k + 1) * LANES)
-            right_ref[pl.ds(pl.multiple_of(base, 16), half), lanes] = upper[r][k, 0]
-            right_ref[pl.ds(pl.multiple_of(base + half, 16), half), lanes] = lower[k][r, 0]
-    left = jnp.concatenate([rows_ref[group_ref[k]] for k in range(4)], axis=1)
+    z = pl.program_id(0)
+    part = pl.program_id(1)
+
+    def lanes(group):
+        return pl.ds(pl.multiple_of(group * LANES, LANES), LANES)
+
+    @pl.when((z == 0) & (part == 0))
+    def _():
+        place = place_ref[0]
+        for k in range(2):
+            left_ref[:, lanes(jnp.bitwise_xor(place, k))] = near_ref[k]
+            left_ref[:, lanes(jnp.bitwise_xor(place, 2 + k))] = far_ref[k]
+
+    @pl.when(part == 0)
+    def _():
+        for r in range(4):
+            base = from_ref[r] * units
+            for k in range(4):
+                group = lanes(group_ref[k])
+                right_ref[pl.ds(pl.multiple_of(base, 16), half), group] = upper[r][k, z]
+                right_ref[pl.ds(pl.multiple_of(base + half, 16), half), group] = lower[k][r, z]
+
+    rows = pl.ds(pl.multiple_of(part * half, 16), half)
     out_ref[...] = (2.0 / 512) * lax.dot_general(
-        left, right_ref[...], NT, preferred_element_type=jnp.float32
+        left_ref[rows, :], right_ref[...], NT, preferred_element_type=jnp.float32
     )
 
 
 def body(attn_out, residual, output_weight, prune_mask, inverse_factor, norm_gain, gate_up_weight):
     units = gate_up_weight.shape[2]
-    is_first = (lax.axis_index(DP) == 0).astype(jnp.int32)[None]
+    place = lax.axis_index(DP).astype(jnp.int32)[None]
     order = senders("x")
     groups = senders("y")
     core = lax.axis_index("core").astype(jnp.int32)[None]
@@ -295,8 +316,8 @@
     residual_turned = turned(jnp.concatenate([residual, gain_rows], axis=0))
 
     solved = solved_errors(output_weight, prune_mask, inverse_factor)
-    errors = lax.all_gather(solved, DP)
-    pruned_weight = updated_weight(is_first, errors, inverse_factor, output_weight, prune_mask)
+    errors = [solved] + [lax.ppermute(solved, DP, [(0, k)]) for k in range(1, 4)]
+    pruned_weight = updated_weight(place, errors, inverse_factor, output_weight, prune_mask)
     weight_turned = turned(pruned_weight)
 
     parts = pl.pallas_call(
@@ -387,24 +408,23 @@
     )(both)
     hidden_turned = both[:units]
     upper, lower = over_y_and_x(over_z(hidden_turned), units // 2)
-    hidden_rows = lax.all_gather(hidden, DP)
-    piece = pl.BlockSpec((4, 1, units // 2, 128), lambda z: (0, z, 0, 0))
+    other = lax.ppermute(hidden, "core", [(0, 1), (1, 0)])
+    near = jnp.stack([hidden, other])
+    far = lax.ppermute(near, "z_low", [(0, 1), (1, 0)])
     hessian = pl.pallas_call(
         hessian_kernel,
-        grid=(4,),
+        grid=(4, 2),
         out_shape=jax.ShapeDtypeStruct((units, 16 * units), jnp.float32),
-        in_specs=[
-            SMEM,
-            SMEM,
-            pl.BlockSpec((4, units, 128), lambda z: (0, 0, 0)),
-            *[piece] * 8,
+        in_specs=[SMEM] * 3 + [VMEM] * 10,
+        out_specs=pl.BlockSpec((units // 2, 4 * units), lambda z, part: (part, z)),
+        scratch_shapes=[
+            pltpu.VMEM((units, 4 * LANES), jnp.bfloat16),
+            pltpu.VMEM((4 * units, 4 * LANES), jnp.bfloat16),
         ],
-        out_specs=pl.BlockSpec((units, 4 * units), lambda z: (0, z)),
-        scratch_shapes=[pltpu.VMEM((4 * units, 4 * LANES), jnp.bfloat16)],
         name="hessian",
         compiler_params=params(14),
         cost_estimate=pl.CostEstimate(flops=822_000_000, bytes_accessed=7_100_000, transcendentals=0),
-    )(order, groups, hidden_rows, *upper, *lower)
+    )(order, groups, place, near, far, *upper, *lower)
     return (pruned_weight, stream, hessian)
 
 

time: 193 us -> 196 us (1.016)
  blocking collectives: 45.1 us -> 23.6 us
  waiting for transfers between devices: 52.2 us -> 64.6 us
  starting transfers between devices: 71.4 us -> 81.8 us
  Pallas kernels: 17 us -> 19.1 us
    all_gather x2 -> x0, blocking collectives: 20.5 us -> none  [the longest x1 13.2 us: body(): hidden_rows = lax.all_gather(hidden, DP)]
    ppermute x0 -> x5, starting transfers between devices: none -> 7.32 us  [the longest x1 4.61 us: body(): other = lax.ppermute(hidden, 'core', [(0, 1), (1, 0)])]
    ppermute x27, waiting for transfers between devices: 40.2 us -> 47.4 us  [round_trip(): lax.ppermute(x, axis, [(k, (k + step) % 4) for k in range(4)])]
    ppermute x0 -> x5, waiting for transfers between devices: none -> 5.13 us  [the longest x3 5.13 us: body(): lax.ppermute(solved, DP, [(0, k)])]
    ppermute x27, starting transfers between devices: 30.6 us -> 34.2 us  [round_trip(): lax.ppermute(x, axis, [(k, (k + step) % 4) for k in range(4)])]
    pallas_call x1, Pallas kernels: 4.44 us -> 6.56 us  [body(): pl.pallas_call(hessian_kernel, grid=(4, 2), out_shape=jax.ShapeDtypeStruc...]
  transfers between devices with their start and end apart: 38 -> 43, of which waited for: 22 -> 24; matrix products, arithmetic and copies ran while one was open for 0% -> 0% of each run, Pallas kernels for 4% -> 4%
where the time goes in v5:
time: 196 us; the launch traced here: 195 us
  starting transfers between devices  81.8 us (42%)
  waiting for transfers between devices  64.6 us (33%)
  blocking collectives  23.6 us (12%)
  Pallas kernels  19.1 us (10%)
  local copies, waits for them, and re-layouts  4.77 us (2%)
    ppermute x27, waiting for transfers between devices, round_trip(): lax.ppermute(x, axis, [(k, (k + step) % 4) for k in range(4)])  47.4 us
    ppermute x27, starting transfers between devices, round_trip(): lax.ppermute(x, axis, [(k, (k + step) % 4) for k in range(4)])  34.2 us
    all_to_all x2, blocking collectives, copy_for_each(): lax.all_to_all(jnp.broadcast_to(x[None], (size, *x.shape)), axis, 0, 0, t...  23.6 us
    ppermute x3, starting transfers between devices, turned(): return lax.ppermute(x, (*DP, 'y'), pairs)  12.3 us
    ppermute x1, starting transfers between devices, body(): got = lax.ppermute(send, 'core', [(0, 1), (1, 0)])  9.22 us
    all_to_all x1, starting transfers between devices, copy_for_each(): lax.all_to_all(jnp.broadcast_to(x[None], (size, *x.shape)), axis, 0, 0, t...  9 us
    all_to_all x1, starting transfers between devices, body(): parts = lax.all_to_all(parts, 'y', 0, 0, tiled=True)  7.46 us
    pallas_call x1, Pallas kernels, body(): pl.pallas_call(hessian_kernel, grid=(4, 2), out_shape=jax.ShapeDtypeStruc...  6.56 us
  transfers between devices with their start and end apart: 43, of which 24 were waited for; matrix products, arithmetic and copies ran while one was open for 0% of the time, Pallas kernels for 4%

profile of v5, /device:TPU:1, one launch (start us, length us, event | category | flops | bytes accessed | tf_op | source)
XLA Modules:
  0.0 195.3 jit_solution(11062945841450127485)
XLA Ops:
  0.7 1.6 broadcast_in_dim.17
  2.3 9.0 %all-to-all-start = ((bf16[8,128,128]{2,1,0:T(8,128)(2,1)}), bf16[8,128,128]{2,1,0:T(8,128)(2,1)S(1)}, u32[]{:S(2)}, u32[]{:S(2)}) async-start(bf16[8,128,128]{2,1,0:T(8,128)(2,1)} %broadcast_in_dim.17), calls=%async_computation | async-start | bytes 524288 | tf_op jit(solution)/shard_map/all_to_all | solution.py:25
  11.3 3.7 %solve.1.solved_ref = f32[128,128]{1,0:T(8,128)} custom-call(bf16[128,2048]{1,0:T(8,128)(2,1)} %weight_ref.1, s32[128,128]{1,0:T(8,128)} %mask_ref.1, f32[128,2048]{1,0:T(8,128)} %factor_ref.1), custom_call_target="tpu_custom_call" | custom-call | flops 20000000 | bytes 300000 | tf_op jit(solution)/shard_map/solve/pallas_call | solution.py:113
  16.4 1.3 collective-permute-start
  17.7 5.1 %collective-permute-done.e1 = f32[128,128]{1,0:T(8,128)S(1)} collective-permute-done((f32[128,128]{1,0:T(8,128)}, f32[128,128]{1,0:T(8,128)S(1)}, u32[]{:S(2)}, u32[]{:S(2)}) %collective-permute-start) | collective-permute-done | bytes 65568 | tf_op jit(solution)/shard_map/ppermute | solution.py:319
  23.7 1.8 update.1
  25.5 2.7 %collective-permute-start.5 = (bf16[8,128,128]{2,1,0:T(8,128)(2,1)S(1)}, bf16[8,128,128]{2,1,0:T(8,128)(2,1)S(1)}, u32[]{:S(2)}, u32[]{:S(2)}) collective-permute-start(bf16[8,128,128]{2,1,0:T(8,128)(2,1)S(1)} %all-to-all-done.refs_0_), channel_id=1, source_target_pairs={{0,2},{1,3},{2,0},{3,1},{4,6},{5,7},{6,4},{7,5},{8,10},{9,11},{10,... | collective-permute-start | bytes 786440 | tf_op jit(solution)/shard_map/ppermute | solution.py:36
  28.2 3.5 %collective-permute-start.10 = (bf16[128,2048]{1,0:T(8,128)(2,1)}, bf16[128,2048]{1,0:T(8,128)(2,1)S(1)}, u32[]{:S(2)}, u32[]{:S(2)}) collective-permute-start(bf16[128,2048]{1,0:T(8,128)(2,1)} %update.1), channel_id=1, source_target_pairs={{0,0},{16,64},{32,128},{48,192},{64,16},{80,80},{96,144},{112,208}... | collective-permute-start | bytes 1572872 | tf_op jit(solution)/shard_map/ppermute | solution.py:30
  33.3 1.4 collective-permute-done.5.refs_3_
  34.7 1.1 collective-permute-start.9
  35.8 4.6 %collective-permute-done.4.refs_2_ = bf16[8,128,128]{2,1,0:T(8,128)(2,1)S(1)} collective-permute-done((bf16[8,128,128]{2,1,0:T(8,128)(2,1)S(1)}, bf16[8,128,128]{2,1,0:T(8,128)(2,1)S(1)}, u32[]{:S(2)}, u32[]{:S(2)}) %collective-permute-start.4) | collective-permute-done | bytes 262176 | tf_op jit(solution)/shard_map/ppermute | solution.py:36
  42.9 1.9 project.1
  44.9 7.5 %all-to-all-start.1 = ((bf16[4,128,128]{2,1,0:T(8,128)(2,1)}), bf16[4,128,128]{2,1,0:T(8,128)(2,1)S(1)}, u32[]{:S(2)}, u32[]{:S(2)}) async-start(bf16[4,128,128]{2,1,0:T(8,128)(2,1)} %project.1), calls=%async_computation.1 | async-start | bytes 262144 | tf_op jit(solution)/shard_map/all_to_all | solution.py:332
  52.3 4.8 %collective-permute-start.11 = (bf16[144,128]{1,0:T(8,128)(2,1)S(1)}, bf16[144,128]{1,0:T(8,128)(2,1)S(1)}, u32[]{:S(2)}, u32[]{:S(2)}) collective-permute-start(bf16[144,128]{1,0:T(8,128)(2,1)S(1)} %pad_maximum_fusion.5), channel_id=1, source_target_pairs={{0,0},{16,64},{32,128},{48,192},{64,16},{80,80},{96,144},{112,208}... | collective-permute-start | bytes 110600 | tf_op jit(solution)/shard_map/ppermute | solution.py:30
  57.2 1.9 collective-permute-done.11.residual_ref
  60.0 12.5 %all_to_all.20 = bf16[4,136,128]{2,1,0:T(8,128)(2,1)S(1)} all-to-all(bf16[4,136,128]{2,1,0:T(8,128)(2,1)S(1)} %broadcast_in_dim.38), channel_id=1, replica_groups=mesh['z_low'=2,'core'=2,'y'=4,'z_high'=4,'x'=4] {'z_high'}, dimensions={0} | all-to-all | bytes 278528 | tf_op jit(solution)/shard_map/all_to_all | solution.py:25
  72.5 3.7 %collective-permute-start.13 = (bf16[4,64,128]{2,1,0:T(8,128)(2,1)S(1)}, bf16[4,64,128]{2,1,0:T(8,128)(2,1)S(1)}, u32[]{:S(2)}, u32[]{:S(2)}) collective-permute-start(bf16[4,64,128]{2,1,0:T(8,128)(2,1)S(1)} %get-tuple-element.26), channel_id=1, source_target_pairs={{0,48},{16,0},{32,16},{48,32},{1,49},{17,1},{33,17},{49,33},{2,50}... | collective-permute-start | bytes 196616 | tf_op jit(solution)/shard_map/ppermute | solution.py:36
  76.2 1.3 collective-permute-start.14
  77.5 3.7 %collective-permute-done.12 = bf16[4,64,128]{2,1,0:T(8,128)(2,1)S(1)} collective-permute-done((bf16[4,64,128]{2,1,0:T(8,128)(2,1)S(1)}, bf16[4,64,128]{2,1,0:T(8,128)(2,1)S(1)}, u32[]{:S(2)}, u32[]{:S(2)}) %collective-permute-start.12) | collective-permute-done | bytes 65568 | tf_op jit(solution)/shard_map/ppermute | solution.py:36
  81.6 2.7 %collective-permute-start.19 = (bf16[4,72,128]{2,1,0:T(8,128)(2,1)S(1)}, bf16[4,72,128]{2,1,0:T(8,128)(2,1)S(1)}, u32[]{:S(2)}, u32[]{:S(2)}) collective-permute-start(bf16[4,72,128]{2,1,0:T(8,128)(2,1)S(1)} %get-tuple-element.24), channel_id=1, source_target_pairs={{0,3},{1,0},{2,1},{3,2},{4,7},{5,4},{6,5},{7,6},{8,11},{9,8},{10,9... | collective-permute-start | bytes 221192 | tf_op jit(solution)/shard_map/ppermute | solution.py:36
  84.3 1.7 collective-permute-start.20
  86.1 1.3 collective-permute-done.19
  87.3 1.5 collective-permute-done.18
  90.6 1.5 collective-permute-start.22
  92.6 2.7 %collective-permute-start.16 = (bf16[4,4,64,128]{3,2,1,0:T(8,128)(2,1)S(1)}, bf16[4,4,64,128]{3,2,1,0:T(8,128)(2,1)}, u32[]{:S(2)}, u32[]{:S(2)}) collective-permute-start(bf16[4,4,64,128]{3,2,1,0:T(8,128)(2,1)S(1)} %pad_maximum_fusion.3.refs_0_), channel_id=1, source_target_pairs={{0,3},{1,0},{2,1},{3,2},{4,7},{5,4},{6,5},{7,6},{8,11},{9,8},{10,9... | collective-permute-start | bytes 786440 | tf_op jit(solution)/shard_map/ppermute | solution.py:36
  95.3 1.5 copy-done.2
  98.6 3.4 %collective-permute-done.15.refs_1_ = bf16[4,4,64,128]{3,2,1,0:T(8,128)(2,1)} collective-permute-done((bf16[4,4,64,128]{3,2,1,0:T(8,128)(2,1)S(1)}, bf16[4,4,64,128]{3,2,1,0:T(8,128)(2,1)}, u32[]{:S(2)}, u32[]{:S(2)}) %collective-permute-start.15) | collective-permute-done | bytes 262176 | tf_op jit(solution)/shard_map/ppermute | solution.py:36
  102.1 3.2 %gate_up.1 = (f32[2,464,128]{2,1,0:T(8,128)S(1)}, bf16[2,464,128]{2,1,0:T(8,128)(2,1)S(1)}) custom-call(s32[4]{0:T(128)S(1)} %pad_add_fusion.group_ref, s32[1]{0:T(128)} %bitcast.6.core_ref, bf16[4,4,64,128]{3,2,1,0:T(8,128)(2,1)S(1)} %pad_maximum_fusion.3.refs_0_, bf16[4,4,64,128]{3,2,1,0:T(8,128)(2,1)} %collective-permute-done.15.refs_1_, ...), custom_call_target="tpu_custom_call" | custom-call | flops 940000000 | bytes 4300000 | tf_op jit(solution)/shard_map/gate_up/pallas_call | solution.py:357
  105.2 9.2 %collective-permute-start.24 = (bf16[2,464,128]{2,1,0:T(8,128)(2,1)S(1)}, bf16[2,464,128]{2,1,0:T(8,128)(2,1)S(1)}, u32[]{:S(2)}, u32[]{:S(2)}) collective-permute-start(bf16[2,464,128]{2,1,0:T(8,128)(2,1)S(1)} %get-tuple-element.13), channel_id=1, source_target_pairs={{0,64},{64,0},{1,65},{65,1},{2,66},{66,2},{3,67},{67,3},{4,68},{68... | collective-permute-start | bytes 712712 | tf_op jit(solution)/shard_map/ppermute | solution.py:372
  114.5 1.1 collective-permute-done.24.got_ref
  115.8 4.4 %collective-permute-done.25.got_ref = bf16[464,128]{1,0:T(8,128)(2,1)S(1)} collective-permute-done((bf16[464,128]{1,0:T(8,128)(2,1)S(1)}, bf16[464,128]{1,0:T(8,128)(2,1)S(1)}, u32[]{:S(2)}, u32[]{:S(2)}) %collective-permute-start.25) | collective-permute-done | bytes 118816 | tf_op jit(solution)/shard_map/ppermute | solution.py:385
  120.2 4.0 %collective-permute-start.26 = (bf16[352,128]{1,0:T(8,128)(2,1)S(1)}, bf16[352,128]{1,0:T(8,128)(2,1)S(1)}, u32[]{:S(2)}, u32[]{:S(2)}) collective-permute-start(bf16[352,128]{1,0:T(8,128)(2,1)S(1)} %get-tuple-element.17), channel_id=1, source_target_pairs={{0,0},{16,64},{32,128},{48,192},{64,16},{80,80},{96,144},{112,208}... | collective-permute-start | bytes 270344 | tf_op jit(solution)/shard_map/ppermute | solution.py:30
  124.3 3.2 %collective-permute-done.26.in_ref = bf16[352,128]{1,0:T(8,128)(2,1)S(1)} collective-permute-done((bf16[352,128]{1,0:T(8,128)(2,1)S(1)}, bf16[352,128]{1,0:T(8,128)(2,1)S(1)}, u32[]{:S(2)}, u32[]{:S(2)}) %collective-permute-start.26) | collective-permute-done | bytes 90144 | tf_op jit(solution)/shard_map/ppermute | solution.py:30
  127.5 11.1 %all_to_all.21 = bf16[4,224,128]{2,1,0:T(8,128)(2,1)S(1)} all-to-all(bf16[4,224,128]{2,1,0:T(8,128)(2,1)S(1)} %broadcast_in_dim.39), channel_id=1, replica_groups=mesh['z_low'=2,'core'=2,'y'=4,'z_high'=4,'x'=4] {'z_high'}, dimensions={0} | all-to-all | bytes 458752 | tf_op jit(solution)/shard_map/all_to_all | solution.py:25
  138.6 2.0 %collective-permute-start.30 = (bf16[4,112,128]{2,1,0:T(8,128)(2,1)S(1)}, bf16[4,112,128]{2,1,0:T(8,128)(2,1)S(1)}, u32[]{:S(2)}, u32[]{:S(2)}) collective-permute-start(bf16[4,112,128]{2,1,0:T(8,128)(2,1)S(1)} %get-tuple-element.22), channel_id=1, source_target_pairs={{0,48},{16,0},{32,16},{48,32},{1,49},{17,1},{33,17},{49,33},{2,50}... | collective-permute-start | bytes 344072 | tf_op jit(solution)/shard_map/ppermute | solution.py:36
  140.7 1.3 collective-permute-start.31
  142.5 4.3 %collective-permute-done.29 = bf16[4,112,128]{2,1,0:T(8,128)(2,1)S(1)} collective-permute-done((bf16[4,112,128]{2,1,0:T(8,128)(2,1)S(1)}, bf16[4,112,128]{2,1,0:T(8,128)(2,1)S(1)}, u32[]{:S(2)}, u32[]{:S(2)}) %collective-permute-start.29) | collective-permute-done | bytes 114720 | tf_op jit(solution)/shard_map/ppermute | solution.py:36
  146.9 4.6 %collective-permute-start.27 = (bf16[224,128]{1,0:T(8,128)(2,1)S(1)}, bf16[224,128]{1,0:T(8,128)(2,1)S(1)}, u32[]{:S(2)}, u32[]{:S(2)}) collective-permute-start(bf16[224,128]{1,0:T(8,128)(2,1)S(1)} %get-tuple-element.18), channel_id=1, source_target_pairs={{0,64},{64,0},{1,65},{65,1},{2,66},{66,2},{3,67},{67,3},{4,68},{68... | collective-permute-start | bytes 172040 | tf_op jit(solution)/shard_map/ppermute | solution.py:411
  151.5 1.1 collective-permute-start.36
  153.0 3.1 %collective-permute-start.37 = (bf16[4,112,128]{2,1,0:T(8,128)(2,1)S(1)}, bf16[4,112,128]{2,1,0:T(8,128)(2,1)S(1)}, u32[]{:S(2)}, u32[]{:S(2)}) collective-permute-start(bf16[4,112,128]{2,1,0:T(8,128)(2,1)S(1)} %get-tuple-element.21), channel_id=1, source_target_pairs={{0,2},{1,3},{2,0},{3,1},{4,6},{5,7},{6,4},{7,5},{8,10},{9,11},{10,... | collective-permute-start | bytes 344072 | tf_op jit(solution)/shard_map/ppermute | solution.py:36
  156.3 4.9 %collective-permute-done.36 = bf16[4,112,128]{2,1,0:T(8,128)(2,1)S(1)} collective-permute-done((bf16[4,112,128]{2,1,0:T(8,128)(2,1)S(1)}, bf16[4,112,128]{2,1,0:T(8,128)(2,1)S(1)}, u32[]{:S(2)}, u32[]{:S(2)}) %collective-permute-start.36) | collective-permute-done | bytes 114720 | tf_op jit(solution)/shard_map/ppermute | solution.py:36
  161.2 3.6 %collective-permute-start.33 = (bf16[4,4,112,128]{3,2,1,0:T(8,128)(2,1)S(1)}, bf16[4,4,112,128]{3,2,1,0:T(8,128)(2,1)S(1)}, u32[]{:S(2)}, u32[]{:S(2)}) collective-permute-start(bf16[4,4,112,128]{3,2,1,0:T(8,128)(2,1)S(1)} %pad_maximum_fusion.refs_0_), channel_id=1, source_target_pairs={{0,3},{1,0},{2,1},{3,2},{4,7},{5,4},{6,5},{7,6},{8,11},{9,8},{10,9... | collective-permute-start | bytes 1376264 | tf_op jit(solution)/shard_map/ppermute | solution.py:36
  164.8 1.6 collective-permute-start.40
  168.5 5.7 %collective-permute-done.33.refs_2_ = bf16[4,4,112,128]{3,2,1,0:T(8,128)(2,1)S(1)} collective-permute-done((bf16[4,4,112,128]{3,2,1,0:T(8,128)(2,1)S(1)}, bf16[4,4,112,128]{3,2,1,0:T(8,128)(2,1)S(1)}, u32[]{:S(2)}, u32[]{:S(2)}) %collective-permute-start.33) | collective-permute-done | bytes 458784 | tf_op jit(solution)/shard_map/ppermute | solution.py:36
  174.2 3.1 %collective-permute-done.32.refs_1_ = bf16[4,4,112,128]{3,2,1,0:T(8,128)(2,1)S(1)} collective-permute-done((bf16[4,4,112,128]{3,2,1,0:T(8,128)(2,1)S(1)}, bf16[4,4,112,128]{3,2,1,0:T(8,128)(2,1)S(1)}, u32[]{:S(2)}, u32[]{:S(2)}) %collective-permute-start.32) | collective-permute-done | bytes 458784 | tf_op jit(solution)/shard_map/ppermute | solution.py:36
  177.3 9.5 %collective-permute-done.39.refs_6_ = bf16[4,4,112,128]{3,2,1,0:T(8,128)(2,1)S(1)} collective-permute-done((bf16[4,4,112,128]{3,2,1,0:T(8,128)(2,1)S(1)}, bf16[4,4,112,128]{3,2,1,0:T(8,128)(2,1)S(1)}, u32[]{:S(2)}, u32[]{:S(2)}) %collective-permute-start.39) | collective-permute-done | bytes 458784 | tf_op jit(solution)/shard_map/ppermute | solution.py:36
  186.8 1.9 collective-permute-done.38.refs_5_
  188.7 6.6 %hessian.1 = f32[224,3584]{1,0:T(8,128)} custom-call(s32[4]{0:T(128)S(1)} %pad_add_fusion.1.from_ref, s32[4]{0:T(128)S(1)} %pad_add_fusion.group_ref, s32[1]{0:T(128)} %bitcast.place_ref, bf16[2,224,128]{2,1,0:T(8,128)(2,1)S(1)} %pad_maximum_fusion.4.near_ref, bf16[2,224,128]{2,1,0:T(8,128)(2,1)S(1)} %collective-permute-done.28.far_ref, ...), custom_call_target="tpu_custom_call" | custom-call | flops 822000000 | bytes 7100000 | tf_op jit(solution)/shard_map/hessian/pallas_call | solution.py:414
  (84 shorter events, 15.3 us)
Async XLA Ops:
  0.6 22.2 %copy-start = (f32[128,2048]{1,0:T(8,128)S(1)}, f32[128,2048]{1,0:T(8,128)}, u32[]{:S(2)}) copy-start(f32[128,2048]{1,0:T(8,128)} %factor_ref.1) | copy-start | bytes 3145732
  0.6 22.2 %copy-start.3 = (s32[128,128]{1,0:T(8,128)S(1)}, s32[128,128]{1,0:T(8,128)}, u32[]{:S(2)}) copy-start(s32[128,128]{1,0:T(8,128)} %mask_ref.1) | copy-start | bytes 196612
  2.3 23.2 %all-to-all-start = ((bf16[8,128,128]{2,1,0:T(8,128)(2,1)}), bf16[8,128,128]{2,1,0:T(8,128)(2,1)S(1)}, u32[]{:S(2)}, u32[]{:S(2)}) async-start(bf16[8,128,128]{2,1,0:T(8,128)(2,1)} %broadcast_in_dim.17), calls=%async_computation | async-start | bytes 524288 | tf_op jit(solution)/shard_map/all_to_all | solution.py:25
  15.0 2.7 %collective-permute-start.2 = (f32[128,128]{1,0:T(8,128)}, f32[128,128]{1,0:T(8,128)S(1)}, u32[]{:S(2)}, u32[]{:S(2)}) collective-permute-start(f32[128,128]{1,0:T(8,128)} %solve.1.solved_ref), channel_id=1, source_target_pairs={{0,192},{1,193},{2,194},{3,195},{4,196},{5,197},{6,198},{7,199},{8... | collective-permute-start | bytes 196616 | tf_op jit(solution)/shard_map/ppermute | solution.py:319
  15.7 2.0 %collective-permute-start.1 = (f32[128,128]{1,0:T(8,128)}, f32[128,128]{1,0:T(8,128)S(1)}, u32[]{:S(2)}, u32[]{:S(2)}) collective-permute-start(f32[128,128]{1,0:T(8,128)} %solve.1.solved_ref), channel_id=1, source_target_pairs={{0,128},{1,129},{2,130},{3,131},{4,132},{5,133},{6,134},{7,135},{8... | collective-permute-start | bytes 196616 | tf_op jit(solution)/shard_map/ppermute | solution.py:319
  16.4 6.5 %collective-permute-start = (f32[128,128]{1,0:T(8,128)}, f32[128,128]{1,0:T(8,128)S(1)}, u32[]{:S(2)}, u32[]{:S(2)}) collective-permute-start(f32[128,128]{1,0:T(8,128)} %solve.1.solved_ref), channel_id=1, source_target_pairs={{0,64},{1,65},{2,66},{3,67},{4,68},{5,69},{6,70},{7,71},{8,72},{9,... | collective-permute-start | bytes 196616 | tf_op jit(solution)/shard_map/ppermute | solution.py:319
  25.5 26.9 %copy-start.8 = (bf16[128]{0:T(256)(128)(2,1)S(1)}, bf16[128]{0:T(256)(128)(2,1)}, u32[]{:S(2)}) copy-start(bf16[128]{0:T(256)(128)(2,1)} %param.12) | copy-start | bytes 772
  25.5 26.9 %copy-start.7 = (bf16[128,128]{1,0:T(8,128)(2,1)S(1)}, bf16[128,128]{1,0:T(8,128)(2,1)}, u32[]{:S(2)}) copy-start(bf16[128,128]{1,0:T(8,128)(2,1)} %param.8) | copy-start | bytes 98308
  25.5 9.2 %collective-permute-start.5 = (bf16[8,128,128]{2,1,0:T(8,128)(2,1)S(1)}, bf16[8,128,128]{2,1,0:T(8,128)(2,1)S(1)}, u32[]{:S(2)}, u32[]{:S(2)}) collective-permute-start(bf16[8,128,128]{2,1,0:T(8,128)(2,1)S(1)} %all-to-all-done.refs_0_), channel_id=1, source_target_pairs={{0,2},{1,3},{2,0},{3,1},{4,6},{5,7},{6,4},{7,5},{8,10},{9,11},{10,... | collective-permute-start | bytes 786440 | tf_op jit(solution)/shard_map/ppermute | solution.py:36
  28.2 14.1 %collective-permute-start.10 = (bf16[128,2048]{1,0:T(8,128)(2,1)}, bf16[128,2048]{1,0:T(8,128)(2,1)S(1)}, u32[]{:S(2)}, u32[]{:S(2)}) collective-permute-start(bf16[128,2048]{1,0:T(8,128)(2,1)} %update.1), channel_id=1, source_target_pairs={{0,0},{16,64},{32,128},{48,192},{64,16},{80,80},{96,144},{112,208}... | collective-permute-start | bytes 1572872 | tf_op jit(solution)/shard_map/ppermute | solution.py:30
  31.7 8.7 %collective-permute-start.4 = (bf16[8,128,128]{2,1,0:T(8,128)(2,1)S(1)}, bf16[8,128,128]{2,1,0:T(8,128)(2,1)S(1)}, u32[]{:S(2)}, u32[]{:S(2)}) collective-permute-start(bf16[8,128,128]{2,1,0:T(8,128)(2,1)S(1)} %all-to-all-done.refs_0_), channel_id=1, source_target_pairs={{0,3},{1,0},{2,1},{3,2},{4,7},{5,4},{6,5},{7,6},{8,11},{9,8},{10,9... | collective-permute-start | bytes 786440 | tf_op jit(solution)/shard_map/ppermute | solution.py:36
  32.7 8.7 %collective-permute-start.3 = (bf16[8,128,128]{2,1,0:T(8,128)(2,1)S(1)}, bf16[8,128,128]{2,1,0:T(8,128)(2,1)S(1)}, u32[]{:S(2)}, u32[]{:S(2)}) collective-permute-start(bf16[8,128,128]{2,1,0:T(8,128)(2,1)S(1)} %all-to-all-done.refs_0_), channel_id=1, source_target_pairs={{0,1},{1,2},{2,3},{3,0},{4,5},{5,6},{6,7},{7,4},{8,9},{9,10},{10,1... | collective-permute-start | bytes 786440 | tf_op jit(solution)/shard_map/ppermute | solution.py:36
  33.3 9.1 %collective-permute-start.6 = (bf16[8,128,128]{2,1,0:T(8,128)(2,1)S(1)}, bf16[8,128,128]{2,1,0:T(8,128)(2,1)S(1)}, u32[]{:S(2)}, u32[]{:S(2)}) collective-permute-start(bf16[8,128,128]{2,1,0:T(8,128)(2,1)S(1)} %all-to-all-done.refs_0_), channel_id=1, source_target_pairs={{0,64},{64,0},{1,65},{65,1},{2,66},{66,2},{3,67},{67,3},{4,68},{68... | collective-permute-start | bytes 786440 | tf_op jit(solution)/shard_map/ppermute | solution.py:314
  34.7 7.7 %collective-permute-start.9 = (bf16[8,128,128]{2,1,0:T(8,128)(2,1)S(1)}, bf16[8,128,128]{2,1,0:T(8,128)(2,1)S(1)}, u32[]{:S(2)}, u32[]{:S(2)}) collective-permute-start(bf16[8,128,128]{2,1,0:T(8,128)(2,1)S(1)} %collective-permute-done.5.refs_3_), channel_id=1, source_target_pairs={{0,64},{64,0},{1,65},{65,1},{2,66},{66,2},{3,67},{67,3},{4,68},{68... | collective-permute-start | bytes 786440 | tf_op jit(solution)/shard_map/ppermute | solution.py:314
  40.4 2.2 %collective-permute-start.8 = (bf16[8,128,128]{2,1,0:T(8,128)(2,1)S(1)}, bf16[8,128,128]{2,1,0:T(8,128)(2,1)S(1)}, u32[]{:S(2)}, u32[]{:S(2)}) collective-permute-start(bf16[8,128,128]{2,1,0:T(8,128)(2,1)S(1)} %collective-permute-done.4.refs_2_), channel_id=1, source_target_pairs={{0,64},{64,0},{1,65},{65,1},{2,66},{66,2},{3,67},{67,3},{4,68},{68... | collective-permute-start | bytes 786440 | tf_op jit(solution)/shard_map/ppermute | solution.py:314
  41.4 1.5 collective-permute-start.7
  44.9 14.2 %all-to-all-start.1 = ((bf16[4,128,128]{2,1,0:T(8,128)(2,1)}), bf16[4,128,128]{2,1,0:T(8,128)(2,1)S(1)}, u32[]{:S(2)}, u32[]{:S(2)}) async-start(bf16[4,128,128]{2,1,0:T(8,128)(2,1)} %project.1), calls=%async_computation.1 | async-start | bytes 262144 | tf_op jit(solution)/shard_map/all_to_all | solution.py:332
  52.3 6.7 %collective-permute-start.11 = (bf16[144,128]{1,0:T(8,128)(2,1)S(1)}, bf16[144,128]{1,0:T(8,128)(2,1)S(1)}, u32[]{:S(2)}, u32[]{:S(2)}) collective-permute-start(bf16[144,128]{1,0:T(8,128)(2,1)S(1)} %pad_maximum_fusion.5), channel_id=1, source_target_pairs={{0,0},{16,64},{32,128},{48,192},{64,16},{80,80},{96,144},{112,208}... | collective-permute-start | bytes 110600 | tf_op jit(solution)/shard_map/ppermute | solution.py:30
  72.5 5.0 %collective-permute-start.13 = (bf16[4,64,128]{2,1,0:T(8,128)(2,1)S(1)}, bf16[4,64,128]{2,1,0:T(8,128)(2,1)S(1)}, u32[]{:S(2)}, u32[]{:S(2)}) collective-permute-start(bf16[4,64,128]{2,1,0:T(8,128)(2,1)S(1)} %get-tuple-element.26), channel_id=1, source_target_pairs={{0,48},{16,0},{32,16},{48,32},{1,49},{17,1},{33,17},{49,33},{2,50}... | collective-permute-start | bytes 196616 | tf_op jit(solution)/shard_map/ppermute | solution.py:36
  76.2 5.0 %collective-permute-start.12 = (bf16[4,64,128]{2,1,0:T(8,128)(2,1)S(1)}, bf16[4,64,128]{2,1,0:T(8,128)(2,1)S(1)}, u32[]{:S(2)}, u32[]{:S(2)}) collective-permute-start(bf16[4,64,128]{2,1,0:T(8,128)(2,1)S(1)} %get-tuple-element.26), channel_id=1, source_target_pairs={{0,16},{16,32},{32,48},{48,0},{1,17},{17,33},{33,49},{49,1},{2,18}... | collective-permute-start | bytes 196616 | tf_op jit(solution)/shard_map/ppermute | solution.py:36
  76.2 5.0 %collective-permute-start.14 = (bf16[4,64,128]{2,1,0:T(8,128)(2,1)S(1)}, bf16[4,64,128]{2,1,0:T(8,128)(2,1)S(1)}, u32[]{:S(2)}, u32[]{:S(2)}) collective-permute-start(bf16[4,64,128]{2,1,0:T(8,128)(2,1)S(1)} %get-tuple-element.26), channel_id=1, source_target_pairs={{0,32},{16,48},{32,0},{48,16},{1,33},{17,49},{33,1},{49,17},{2,34}... | collective-permute-start | bytes 196616 | tf_op jit(solution)/shard_map/ppermute | solution.py:36
  81.2 14.1 %collective-permute-start.17 = (bf16[4,4,64,128]{3,2,1,0:T(8,128)(2,1)S(1)}, bf16[4,4,64,128]{3,2,1,0:T(8,128)(2,1)S(1)}, u32[]{:S(2)}, u32[]{:S(2)}) collective-permute-start(bf16[4,4,64,128]{3,2,1,0:T(8,128)(2,1)S(1)} %pad_maximum_fusion.3.refs_0_), channel_id=1, source_target_pairs={{0,2},{1,3},{2,0},{3,1},{4,6},{5,7},{6,4},{7,5},{8,10},{9,11},{10,... | collective-permute-start | bytes 786440 | tf_op jit(solution)/shard_map/ppermute | solution.py:36
  81.6 5.7 %collective-permute-start.19 = (bf16[4,72,128]{2,1,0:T(8,128)(2,1)S(1)}, bf16[4,72,128]{2,1,0:T(8,128)(2,1)S(1)}, u32[]{:S(2)}, u32[]{:S(2)}) collective-permute-start(bf16[4,72,128]{2,1,0:T(8,128)(2,1)S(1)} %get-tuple-element.24), channel_id=1, source_target_pairs={{0,3},{1,0},{2,1},{3,2},{4,7},{5,4},{6,5},{7,6},{8,11},{9,8},{10,9... | collective-permute-start | bytes 221192 | tf_op jit(solution)/shard_map/ppermute | solution.py:36
  84.3 4.5 %collective-permute-start.18 = (bf16[4,72,128]{2,1,0:T(8,128)(2,1)S(1)}, bf16[4,72,128]{2,1,0:T(8,128)(2,1)S(1)}, u32[]{:S(2)}, u32[]{:S(2)}) collective-permute-start(bf16[4,72,128]{2,1,0:T(8,128)(2,1)S(1)} %get-tuple-element.24), channel_id=1, source_target_pairs={{0,1},{1,2},{2,3},{3,0},{4,5},{5,6},{6,7},{7,4},{8,9},{9,10},{10,1... | collective-permute-start | bytes 221192 | tf_op jit(solution)/shard_map/ppermute | solution.py:36
  84.3 5.3 %collective-permute-start.20 = (bf16[4,72,128]{2,1,0:T(8,128)(2,1)S(1)}, bf16[4,72,128]{2,1,0:T(8,128)(2,1)S(1)}, u32[]{:S(2)}, u32[]{:S(2)}) collective-permute-start(bf16[4,72,128]{2,1,0:T(8,128)(2,1)S(1)} %get-tuple-element.24), channel_id=1, source_target_pairs={{0,2},{1,3},{2,0},{3,1},{4,6},{5,7},{6,4},{7,5},{8,10},{9,11},{10,... | collective-permute-start | bytes 221192 | tf_op jit(solution)/shard_map/ppermute | solution.py:36
  89.7 12.4 %collective-permute-start.23 = (bf16[4,4,72,128]{3,2,1,0:T(8,128)(2,1)S(1)}, bf16[4,4,72,128]{3,2,1,0:T(8,128)(2,1)S(1)}, u32[]{:S(2)}, u32[]{:S(2)}) collective-permute-start(bf16[4,4,72,128]{3,2,1,0:T(8,128)(2,1)S(1)} %pad_maximum_fusion.2.refs_4_), channel_id=1, source_target_pairs={{0,32},{16,48},{32,0},{48,16},{1,33},{17,49},{33,1},{49,17},{2,34}... | collective-permute-start | bytes 884744 | tf_op jit(solution)/shard_map/ppermute | solution.py:36
  90.6 11.4 %collective-permute-start.22 = (bf16[4,4,72,128]{3,2,1,0:T(8,128)(2,1)S(1)}, bf16[4,4,72,128]{3,2,1,0:T(8,128)(2,1)S(1)}, u32[]{:S(2)}, u32[]{:S(2)}) collective-permute-start(bf16[4,4,72,128]{3,2,1,0:T(8,128)(2,1)S(1)} %pad_maximum_fusion.2.refs_4_), channel_id=1, source_target_pairs={{0,48},{16,0},{32,16},{48,32},{1,49},{17,1},{33,17},{49,33},{2,50}... | collective-permute-start | bytes 884744 | tf_op jit(solution)/shard_map/ppermute | solution.py:36
  92.1 9.9 %collective-permute-start.21 = (bf16[4,4,72,128]{3,2,1,0:T(8,128)(2,1)S(1)}, bf16[4,4,72,128]{3,2,1,0:T(8,128)(2,1)S(1)}, u32[]{:S(2)}, u32[]{:S(2)}) collective-permute-start(bf16[4,4,72,128]{3,2,1,0:T(8,128)(2,1)S(1)} %pad_maximum_fusion.2.refs_4_), channel_id=1, source_target_pairs={{0,16},{16,32},{32,48},{48,0},{1,17},{17,33},{33,49},{49,1},{2,18}... | collective-permute-start | bytes 884744 | tf_op jit(solution)/shard_map/ppermute | solution.py:36
  92.6 6.0 %collective-permute-start.16 = (bf16[4,4,64,128]{3,2,1,0:T(8,128)(2,1)S(1)}, bf16[4,4,64,128]{3,2,1,0:T(8,128)(2,1)}, u32[]{:S(2)}, u32[]{:S(2)}) collective-permute-start(bf16[4,4,64,128]{3,2,1,0:T(8,128)(2,1)S(1)} %pad_maximum_fusion.3.refs_0_), channel_id=1, source_target_pairs={{0,3},{1,0},{2,1},{3,2},{4,7},{5,4},{6,5},{7,6},{8,11},{9,8},{10,9... | collective-permute-start | bytes 786440 | tf_op jit(solution)/shard_map/ppermute | solution.py:36
  95.3 6.7 %collective-permute-start.15 = (bf16[4,4,64,128]{3,2,1,0:T(8,128)(2,1)S(1)}, bf16[4,4,64,128]{3,2,1,0:T(8,128)(2,1)}, u32[]{:S(2)}, u32[]{:S(2)}) collective-permute-start(bf16[4,4,64,128]{3,2,1,0:T(8,128)(2,1)S(1)} %pad_maximum_fusion.3.refs_0_), channel_id=1, source_target_pairs={{0,1},{1,2},{2,3},{3,0},{4,5},{5,6},{6,7},{7,4},{8,9},{9,10},{10,1... | collective-permute-start | bytes 786440 | tf_op jit(solution)/shard_map/ppermute | solution.py:36
  98.0 22.2 %copy-start.6 = (bf16[128,128]{1,0:T(8,128)(2,1)S(1)}, bf16[128,128]{1,0:T(8,128)(2,1)}, u32[]{:S(2)}) copy-start(bf16[128,128]{1,0:T(8,128)(2,1)} %copy-done.5) | copy-start | bytes 98308
  105.2 10.3 %collective-permute-start.24 = (bf16[2,464,128]{2,1,0:T(8,128)(2,1)S(1)}, bf16[2,464,128]{2,1,0:T(8,128)(2,1)S(1)}, u32[]{:S(2)}, u32[]{:S(2)}) collective-permute-start(bf16[2,464,128]{2,1,0:T(8,128)(2,1)S(1)} %get-tuple-element.13), channel_id=1, source_target_pairs={{0,64},{64,0},{1,65},{65,1},{2,66},{66,2},{3,67},{67,3},{4,68},{68... | collective-permute-start | bytes 712712 | tf_op jit(solution)/shard_map/ppermute | solution.py:372
  115.7 4.5 %collective-permute-start.25 = (bf16[464,128]{1,0:T(8,128)(2,1)S(1)}, bf16[464,128]{1,0:T(8,128)(2,1)S(1)}, u32[]{:S(2)}, u32[]{:S(2)}) collective-permute-start(bf16[464,128]{1,0:T(8,128)(2,1)S(1)} %get-tuple-element.15), channel_id=1, source_target_pairs={{0,128},{128,0},{1,129},{129,1},{2,130},{130,2},{3,131},{131,3},{4... | collective-permute-start | bytes 356360 | tf_op jit(solution)/shard_map/ppermute | solution.py:385
  120.2 7.2 %collective-permute-start.26 = (bf16[352,128]{1,0:T(8,128)(2,1)S(1)}, bf16[352,128]{1,0:T(8,128)(2,1)S(1)}, u32[]{:S(2)}, u32[]{:S(2)}) collective-permute-start(bf16[352,128]{1,0:T(8,128)(2,1)S(1)} %get-tuple-element.17), channel_id=1, source_target_pairs={{0,0},{16,64},{32,128},{48,192},{64,16},{80,80},{96,144},{112,208}... | collective-permute-start | bytes 270344 | tf_op jit(solution)/shard_map/ppermute | solution.py:30
  138.6 3.8 %collective-permute-start.30 = (bf16[4,112,128]{2,1,0:T(8,128)(2,1)S(1)}, bf16[4,112,128]{2,1,0:T(8,128)(2,1)S(1)}, u32[]{:S(2)}, u32[]{:S(2)}) collective-permute-start(bf16[4,112,128]{2,1,0:T(8,128)(2,1)S(1)} %get-tuple-element.22), channel_id=1, source_target_pairs={{0,48},{16,0},{32,16},{48,32},{1,49},{17,1},{33,17},{49,33},{2,50}... | collective-permute-start | bytes 344072 | tf_op jit(solution)/shard_map/ppermute | solution.py:36
  140.7 6.1 %collective-permute-start.29 = (bf16[4,112,128]{2,1,0:T(8,128)(2,1)S(1)}, bf16[4,112,128]{2,1,0:T(8,128)(2,1)S(1)}, u32[]{:S(2)}, u32[]{:S(2)}) collective-permute-start(bf16[4,112,128]{2,1,0:T(8,128)(2,1)S(1)} %get-tuple-element.22), channel_id=1, source_target_pairs={{0,16},{16,32},{32,48},{48,0},{1,17},{17,33},{33,49},{49,1},{2,18}... | collective-permute-start | bytes 344072 | tf_op jit(solution)/shard_map/ppermute | solution.py:36
  140.7 6.1 %collective-permute-start.31 = (bf16[4,112,128]{2,1,0:T(8,128)(2,1)S(1)}, bf16[4,112,128]{2,1,0:T(8,128)(2,1)S(1)}, u32[]{:S(2)}, u32[]{:S(2)}) collective-permute-start(bf16[4,112,128]{2,1,0:T(8,128)(2,1)S(1)} %get-tuple-element.22), channel_id=1, source_target_pairs={{0,32},{16,48},{32,0},{48,16},{1,33},{17,49},{33,1},{49,17},{2,34}... | collective-permute-start | bytes 344072 | tf_op jit(solution)/shard_map/ppermute | solution.py:36
  146.8 20.1 %collective-permute-start.34 = (bf16[4,4,112,128]{3,2,1,0:T(8,128)(2,1)S(1)}, bf16[4,4,112,128]{3,2,1,0:T(8,128)(2,1)S(1)}, u32[]{:S(2)}, u32[]{:S(2)}) collective-permute-start(bf16[4,4,112,128]{3,2,1,0:T(8,128)(2,1)S(1)} %pad_maximum_fusion.refs_0_), channel_id=1, source_target_pairs={{0,2},{1,3},{2,0},{3,1},{4,6},{5,7},{6,4},{7,5},{8,10},{9,11},{10,... | collective-permute-start | bytes 1376264 | tf_op jit(solution)/shard_map/ppermute | solution.py:36
  146.9 9.2 %collective-permute-start.27 = (bf16[224,128]{1,0:T(8,128)(2,1)S(1)}, bf16[224,128]{1,0:T(8,128)(2,1)S(1)}, u32[]{:S(2)}, u32[]{:S(2)}) collective-permute-start(bf16[224,128]{1,0:T(8,128)(2,1)S(1)} %get-tuple-element.18), channel_id=1, source_target_pairs={{0,64},{64,0},{1,65},{65,1},{2,66},{66,2},{3,67},{67,3},{4,68},{68... | collective-permute-start | bytes 172040 | tf_op jit(solution)/shard_map/ppermute | solution.py:411
  151.5 9.7 %collective-permute-start.36 = (bf16[4,112,128]{2,1,0:T(8,128)(2,1)S(1)}, bf16[4,112,128]{2,1,0:T(8,128)(2,1)S(1)}, u32[]{:S(2)}, u32[]{:S(2)}) collective-permute-start(bf16[4,112,128]{2,1,0:T(8,128)(2,1)S(1)} %get-tuple-element.21), channel_id=1, source_target_pairs={{0,3},{1,0},{2,1},{3,2},{4,7},{5,4},{6,5},{7,6},{8,11},{9,8},{10,9... | collective-permute-start | bytes 344072 | tf_op jit(solution)/shard_map/ppermute | solution.py:36
  152.6 12.2 %collective-permute-start.35 = (bf16[4,112,128]{2,1,0:T(8,128)(2,1)S(1)}, bf16[4,112,128]{2,1,0:T(8,128)(2,1)S(1)}, u32[]{:S(2)}, u32[]{:S(2)}) collective-permute-start(bf16[4,112,128]{2,1,0:T(8,128)(2,1)S(1)} %get-tuple-element.21), channel_id=1, source_target_pairs={{0,1},{1,2},{2,3},{3,0},{4,5},{5,6},{6,7},{7,4},{8,9},{9,10},{10,1... | collective-permute-start | bytes 344072 | tf_op jit(solution)/shard_map/ppermute | solution.py:36
  153.0 11.8 %collective-permute-start.37 = (bf16[4,112,128]{2,1,0:T(8,128)(2,1)S(1)}, bf16[4,112,128]{2,1,0:T(8,128)(2,1)S(1)}, u32[]{:S(2)}, u32[]{:S(2)}) collective-permute-start(bf16[4,112,128]{2,1,0:T(8,128)(2,1)S(1)} %get-tuple-element.21), channel_id=1, source_target_pairs={{0,2},{1,3},{2,0},{3,1},{4,6},{5,7},{6,4},{7,5},{8,10},{9,11},{10,... | collective-permute-start | bytes 344072 | tf_op jit(solution)/shard_map/ppermute | solution.py:36
  156.2 10.2 %collective-permute-start.28 = (bf16[2,224,128]{2,1,0:T(8,128)(2,1)S(1)}, bf16[2,224,128]{2,1,0:T(8,128)(2,1)S(1)}, u32[]{:S(2)}, u32[]{:S(2)}) collective-permute-start(bf16[2,224,128]{2,1,0:T(8,128)(2,1)S(1)} %pad_maximum_fusion.4.near_ref), channel_id=1, source_target_pairs={{0,128},{128,0},{1,129},{129,1},{2,130},{130,2},{3,131},{131,3},{4... | collective-permute-start | bytes 344072 | tf_op jit(solution)/shard_map/ppermute | solution.py:413
  161.2 13.0 %collective-permute-start.33 = (bf16[4,4,112,128]{3,2,1,0:T(8,128)(2,1)S(1)}, bf16[4,4,112,128]{3,2,1,0:T(8,128)(2,1)S(1)}, u32[]{:S(2)}, u32[]{:S(2)}) collective-permute-start(bf16[4,4,112,128]{3,2,1,0:T(8,128)(2,1)S(1)} %pad_maximum_fusion.refs_0_), channel_id=1, source_target_pairs={{0,3},{1,0},{2,1},{3,2},{4,7},{5,4},{6,5},{7,6},{8,11},{9,8},{10,9... | collective-permute-start | bytes 1376264 | tf_op jit(solution)/shard_map/ppermute | solution.py:36
  164.8 12.5 %collective-permute-start.32 = (bf16[4,4,112,128]{3,2,1,0:T(8,128)(2,1)S(1)}, bf16[4,4,112,128]{3,2,1,0:T(8,128)(2,1)S(1)}, u32[]{:S(2)}, u32[]{:S(2)}) collective-permute-start(bf16[4,4,112,128]{3,2,1,0:T(8,128)(2,1)S(1)} %pad_maximum_fusion.refs_0_), channel_id=1, source_target_pairs={{0,1},{1,2},{2,3},{3,0},{4,5},{5,6},{6,7},{7,4},{8,9},{9,10},{10,1... | collective-permute-start | bytes 1376264 | tf_op jit(solution)/shard_map/ppermute | solution.py:36
  164.8 12.5 %collective-permute-start.40 = (bf16[4,4,112,128]{3,2,1,0:T(8,128)(2,1)S(1)}, bf16[4,4,112,128]{3,2,1,0:T(8,128)(2,1)S(1)}, u32[]{:S(2)}, u32[]{:S(2)}) collective-permute-start(bf16[4,4,112,128]{3,2,1,0:T(8,128)(2,1)S(1)} %pad_maximum_fusion.1.refs_4_), channel_id=1, source_target_pairs={{0,32},{16,48},{32,0},{48,16},{1,33},{17,49},{33,1},{49,17},{2,34}... | collective-permute-start | bytes 1376264 | tf_op jit(solution)/shard_map/ppermute | solution.py:36
  166.4 20.4 %collective-permute-start.39 = (bf16[4,4,112,128]{3,2,1,0:T(8,128)(2,1)S(1)}, bf16[4,4,112,128]{3,2,1,0:T(8,128)(2,1)S(1)}, u32[]{:S(2)}, u32[]{:S(2)}) collective-permute-start(bf16[4,4,112,128]{3,2,1,0:T(8,128)(2,1)S(1)} %pad_maximum_fusion.1.refs_4_), channel_id=1, source_target_pairs={{0,48},{16,0},{32,16},{48,32},{1,49},{17,1},{33,17},{49,33},{2,50}... | collective-permute-start | bytes 1376264 | tf_op jit(solution)/shard_map/ppermute | solution.py:36
  166.9 21.8 %collective-permute-start.38 = (bf16[4,4,112,128]{3,2,1,0:T(8,128)(2,1)S(1)}, bf16[4,4,112,128]{3,2,1,0:T(8,128)(2,1)S(1)}, u32[]{:S(2)}, u32[]{:S(2)}) collective-permute-start(bf16[4,4,112,128]{3,2,1,0:T(8,128)(2,1)S(1)} %pad_maximum_fusion.1.refs_4_), channel_id=1, source_target_pairs={{0,16},{16,32},{32,48},{48,0},{1,17},{17,33},{33,49},{49,1},{2,18}... | collective-permute-start | bytes 1376264 | tf_op jit(solution)/shard_map/ppermute | solution.py:36
  (4 other events, 25.2 us)

commit v6 on v5

--- a/solution.py
+++ b/solution.py
@@ -37,11 +37,20 @@
     return blocks
 
 
-def over_y_and_x(x, half):
+def two_step_ring(x, axis):
+    up = [(k, (k + 1) % 4) for k in range(4)]
+    down = [(k, (k + 3) % 4) for k in range(4)]
+    half = x.shape[0] // 2
+    below, above = lax.ppermute(x, axis, up), lax.ppermute(x, axis, down)
+    far = [lax.ppermute(below[:half], axis, up), lax.ppermute(above[half:], axis, down)]
+    return [x, below, above, *far]
+
+
+def over_y_and_x(x, half, large=round_trip):
     lower = jnp.stack(round_trip(x[:, half:], "x"))
     upper = jnp.stack(round_trip(x[:, :half], "y"))
-    upper = round_trip(upper, "x")
-    lower = round_trip(lower, "y")
+    upper = large(upper, "x")
+    lower = large(lower, "y")
     return upper, lower
 
 
@@ -127,20 +136,16 @@
     )(weight, mask, factor)
 
 
-def update_kernel(
-    place_ref, solved_ref, e1, e2, e3, factor_ref, weight_ref, mask_ref, out_ref
-):
-    is_first = place_ref[0] == 0
-    errors = jnp.where(is_first, solved_ref[...], e1[...] + e2[...] + e3[...])
+def update_kernel(place_ref, errors_ref, factor_ref, weight_ref, mask_ref, out_ref):
     updated = weight_ref[...].astype(jnp.float32) - lax.dot_general(
-        errors,
+        errors_ref[0],
         factor_ref[...],
         (((1,), (0,)), ((), ())),
         precision=lax.Precision.HIGHEST,
         preferred_element_type=jnp.float32,
     )
     width = mask_ref.shape[1]
-    kept = jnp.where(is_first, mask_ref[...].astype(jnp.float32), 1.0)
+    kept = jnp.where(place_ref[0] == 0, mask_ref[...].astype(jnp.float32), 1.0)
     out_ref[:, :width] = (updated[:, :width] * kept).astype(jnp.bfloat16)
     out_ref[:, width:] = updated[:, width:].astype(jnp.bfloat16)
 
@@ -152,7 +157,7 @@
         out_shape=jax.ShapeDtypeStruct(weight.shape, jnp.bfloat16),
         in_specs=[
             SMEM,
-            *[corner(mask.shape)] * 4,
+            corner((1, *errors.shape[1:])),
             corner(factor.shape),
             corner(weight.shape),
             corner(mask.shape),
@@ -161,7 +166,7 @@
         name="update",
         compiler_params=params(12),
         cost_estimate=pl.CostEstimate(flops=400_000_000, bytes_accessed=2_200_000, transcendentals=0),
-    )(place, *errors, factor, weight, mask)
+    )(place, errors, factor, weight, mask)
 
 
 def columns_at(ref, block):
@@ -270,34 +275,34 @@
 
 
 def hessian_kernel(from_ref, group_ref, place_ref, near_ref, far_ref, *refs):
-    upper, lower, out_ref, left_ref, right_ref = refs[:4], refs[4:8], *refs[8:]
+    upper, lower, out_ref, left_ref, right_ref = refs[:5], refs[5:10], *refs[10:]
     units = near_ref.shape[1]
     half = units // 2
     z = pl.program_id(0)
-    part = pl.program_id(1)
 
     def lanes(group):
         return pl.ds(pl.multiple_of(group * LANES, LANES), LANES)
 
-    @pl.when((z == 0) & (part == 0))
+    def piece(blocks, large, small):
+        if large < 3:
+            return blocks[large][small, z]
+        return blocks[3 + small // 2][small % 2, z]
+
+    @pl.when(z == 0)
     def _():
         place = place_ref[0]
         for k in range(2):
             left_ref[:, lanes(jnp.bitwise_xor(place, k))] = near_ref[k]
             left_ref[:, lanes(jnp.bitwise_xor(place, 2 + k))] = far_ref[k]
 
-    @pl.when(part == 0)
-    def _():
-        for r in range(4):
-            base = from_ref[r] * units
-            for k in range(4):
-                group = lanes(group_ref[k])
-                right_ref[pl.ds(pl.multiple_of(base, 16), half), group] = upper[r][k, z]
-                right_ref[pl.ds(pl.multiple_of(base + half, 16), half), group] = lower[k][r, z]
-
-    rows = pl.ds(pl.multiple_of(part * half, 16), half)
+    for r in range(4):
+        base = from_ref[r] * units
+        for k in range(4):
+            group = lanes(group_ref[k])
+            right_ref[pl.ds(pl.multiple_of(base, 16), half), group] = piece(upper, r, k)
+            right_ref[pl.ds(pl.multiple_of(base + half, 16), half), group] = piece(lower, k, r)
     out_ref[...] = (2.0 / 512) * lax.dot_general(
-        left_ref[rows, :], right_ref[...], NT, preferred_element_type=jnp.float32
+        left_ref[...], right_ref[...], NT, preferred_element_type=jnp.float32
     )
 
 
@@ -316,7 +321,7 @@
     residual_turned = turned(jnp.concatenate([residual, gain_rows], axis=0))
 
     solved = solved_errors(output_weight, prune_mask, inverse_factor)
-    errors = [solved] + [lax.ppermute(solved, DP, [(0, k)]) for k in range(1, 4)]
+    errors = lax.all_gather(solved, DP)
     pruned_weight = updated_weight(place, errors, inverse_factor, output_weight, prune_mask)
     weight_turned = turned(pruned_weight)
 
@@ -407,16 +412,16 @@
         compiler_params=params(1),
     )(both)
     hidden_turned = both[:units]
-    upper, lower = over_y_and_x(over_z(hidden_turned), units // 2)
+    upper, lower = over_y_and_x(over_z(hidden_turned), units // 2, two_step_ring)
     other = lax.ppermute(hidden, "core", [(0, 1), (1, 0)])
     near = jnp.stack([hidden, other])
     far = lax.ppermute(near, "z_low", [(0, 1), (1, 0)])
     hessian = pl.pallas_call(
         hessian_kernel,
-        grid=(4, 2),
+        grid=(4,),
         out_shape=jax.ShapeDtypeStruct((units, 16 * units), jnp.float32),
-        in_specs=[SMEM] * 3 + [VMEM] * 10,
-        out_specs=pl.BlockSpec((units // 2, 4 * units), lambda z, part: (part, z)),
+        in_specs=[SMEM] * 3 + [VMEM] * 12,
+        out_specs=pl.BlockSpec((units, 4 * units), lambda z: (0, z)),
         scratch_shapes=[
             pltpu.VMEM((units, 4 * LANES), jnp.bfloat16),
             pltpu.VMEM((4 * units, 4 * LANES), jnp.bfloat16),

time: 196 us -> 177 us (0.903); the launches traced: 195 us -> 174 us
  waiting for transfers between devices: 64.6 us -> 37.8 us
  blocking collectives: 23.6 us -> 31.9 us
  Pallas kernels: 19.1 us -> 16.9 us
    ppermute x27 -> x21, waiting for transfers between devices: 47.4 us -> 21 us  [round_trip(): lax.ppermute(x, axis, [(k, (k + step) % 4) for k in range(4)])]
    ppermute x27 -> x21, starting transfers between devices: 34.2 us -> 24.1 us  [round_trip(): lax.ppermute(x, axis, [(k, (k + step) % 4) for k in range(4)])]
    all_gather x0 -> x1, blocking collectives: none -> 7.28 us  [body(): errors = lax.all_gather(solved, DP)]
    ppermute x3 -> x8, starting transfers between devices: 2.62 us -> 8.65 us  [the longest x4 4.95 us: two_step_ring(): below, above = (lax.ppermute(x, axis, up), lax.ppermute(x, axis, down))]
    pallas_call x1, Pallas kernels: 6.56 us -> 4.31 us  [body(): pl.pallas_call(hessian_kernel, grid=(4,), out_shape=jax.ShapeDtypeStruct(...]
    ppermute x3 -> x8, waiting for transfers between devices: 5.13 us -> 2.93 us  [the longest x2 2.13 us: two_step_ring(): lax.ppermute(below[:half], axis, up)]
    ppermute x1, starting transfers between devices: 0.09 us -> 2.26 us  [body(): far = lax.ppermute(near, 'z_low', [(0, 1), (1, 0)])]
  transfers between devices with their start and end apart: 43 -> 42, of which waited for: 24 -> 22; matrix products, arithmetic and copies ran while one was open for 0% -> 0% of each run, Pallas kernels for 4% -> 4%
where the time goes in v6:
time: 177 us; the launch traced here: 174 us
  starting transfers between devices  82.4 us (47%)
  waiting for transfers between devices  37.8 us (21%)
  blocking collectives  31.9 us (18%)
  Pallas kernels  16.9 us (10%)
  local copies, waits for them, and re-layouts  4 us (2%)
    all_to_all x2, blocking collectives, copy_for_each(): lax.all_to_all(jnp.broadcast_to(x[None], (size, *x.shape)), axis, 0, 0, t...  24.6 us
    ppermute x21, starting transfers between devices, round_trip(): lax.ppermute(x, axis, [(k, (k + step) % 4) for k in range(4)])  24.1 us
    ppermute x21, waiting for transfers between devices, round_trip(): lax.ppermute(x, axis, [(k, (k + step) % 4) for k in range(4)])  21 us
    ppermute x3, starting transfers between devices, turned(): return lax.ppermute(x, (*DP, 'y'), pairs)  12.4 us
    ppermute x1, starting transfers between devices, body(): got = lax.ppermute(send, 'core', [(0, 1), (1, 0)])  9.79 us
    all_to_all x1, starting transfers between devices, copy_for_each(): lax.all_to_all(jnp.broadcast_to(x[None], (size, *x.shape)), axis, 0, 0, t...  9 us
    all_to_all x1, starting transfers between devices, body(): parts = lax.all_to_all(parts, 'y', 0, 0, tiled=True)  7.46 us
    all_gather x1, blocking collectives, body(): errors = lax.all_gather(solved, DP)  7.28 us
  transfers between devices with their start and end apart: 42, of which 22 were waited for; matrix products, arithmetic and copies ran while one was open for 0% of the time, Pallas kernels for 4%

profile of v6, /device:TPU:1, one launch (start us, length us, event | category | flops | bytes accessed | tf_op | source)
XLA Modules:
  0.0 174.2 jit_solution(12496986107387957206)
XLA Ops:
  0.7 1.6 broadcast_in_dim.17
  2.3 9.0 %all-to-all-start = ((bf16[8,128,128]{2,1,0:T(8,128)(2,1)}), bf16[8,128,128]{2,1,0:T(8,128)(2,1)S(1)}, u32[]{:S(2)}, u32[]{:S(2)}) async-start(bf16[8,128,128]{2,1,0:T(8,128)(2,1)} %broadcast_in_dim.17), calls=%async_computation | async-start | bytes 524288 | tf_op jit(solution)/shard_map/all_to_all | solution.py:25
  11.3 3.7 %solve.1 = f32[128,128]{1,0:T(8,128)} custom-call(bf16[128,2048]{1,0:T(8,128)(2,1)} %weight_ref.1, s32[128,128]{1,0:T(8,128)} %mask_ref.1, f32[128,2048]{1,0:T(8,128)} %factor_ref.1), custom_call_target="tpu_custom_call" | custom-call | flops 20000000 | bytes 300000 | tf_op jit(solution)/shard_map/solve/pallas_call | solution.py:122
  15.0 7.3 %all-gather = f32[512,128]{1,0:T(8,128)S(1)} all-gather(f32[128,128]{1,0:T(8,128)} %solve.1), channel_id=2, replica_groups=mesh['z_low'=2,'core'=2,'y'=4,'z_high'=4,'x'=4] {'z_low','core'}, dimensions={0}, use_global_device_ids=true | all-gather | bytes 327680 | tf_op jit(solution)/shard_map/all_gather | solution.py:324
  22.3 1.8 %update.1 = bf16[128,2048]{1,0:T(8,128)(2,1)} custom-call(s32[1]{0:T(128)} %bitcast.place_ref, f32[4,128,128]{2,1,0:T(8,128)S(1)} %bitcast.38, f32[128,2048]{1,0:T(8,128)S(1)} %copy-done, bf16[128,2048]{1,0:T(8,128)(2,1)S(1)} %copy-done.1, s32[128,128]{1,0:T(8,128)S(1)} %copy-done.3), custom_call_target="tpu_custom_call" | custom-call | flops 400000000 | bytes 2200000 | tf_op jit(solution)/shard_map/update/pallas_call | solution.py:154
  24.1 2.7 %collective-permute-start.2 = (bf16[8,128,128]{2,1,0:T(8,128)(2,1)S(1)}, bf16[8,128,128]{2,1,0:T(8,128)(2,1)S(1)}, u32[]{:S(2)}, u32[]{:S(2)}) collective-permute-start(bf16[8,128,128]{2,1,0:T(8,128)(2,1)S(1)} %all-to-all-done.refs_0_), channel_id=1, source_target_pairs={{0,2},{1,3},{2,0},{3,1},{4,6},{5,7},{6,4},{7,5},{8,10},{9,11},{10,... | collective-permute-start | bytes 786440 | tf_op jit(solution)/shard_map/ppermute | solution.py:36
  26.9 3.5 %collective-permute-start.7 = (bf16[128,2048]{1,0:T(8,128)(2,1)}, bf16[128,2048]{1,0:T(8,128)(2,1)S(1)}, u32[]{:S(2)}, u32[]{:S(2)}) collective-permute-start(bf16[128,2048]{1,0:T(8,128)(2,1)} %update.1), channel_id=1, source_target_pairs={{0,0},{16,64},{32,128},{48,192},{64,16},{80,80},{96,144},{112,208}... | collective-permute-start | bytes 1572872 | tf_op jit(solution)/shard_map/ppermute | solution.py:30
  31.9 1.4 collective-permute-done.2.refs_3_
  33.3 1.1 collective-permute-start.6
  34.4 4.6 %collective-permute-done.1.refs_2_ = bf16[8,128,128]{2,1,0:T(8,128)(2,1)S(1)} collective-permute-done((bf16[8,128,128]{2,1,0:T(8,128)(2,1)S(1)}, bf16[8,128,128]{2,1,0:T(8,128)(2,1)S(1)}, u32[]{:S(2)}, u32[]{:S(2)}) %collective-permute-start.1) | collective-permute-done | bytes 262176 | tf_op jit(solution)/shard_map/ppermute | solution.py:36
  39.0 1.0 collective-permute-start.5
  41.6 1.9 %project.1 = bf16[4,128,128]{2,1,0:T(8,128)(2,1)} custom-call(s32[4]{0:T(128)S(1)} %pad_add_fusion.1.from_ref, s32[1]{0:T(128)} %bitcast.7.core_ref, bf16[8,128,128]{2,1,0:T(8,128)(2,1)S(1)} %all-to-all-done.refs_0_, bf16[8,128,128]{2,1,0:T(8,128)(2,1)S(1)} %collective-permute-done.refs_1_, bf16[8,128,128]{2,1,0:T(8,128)(2,1)S(1)} %collective-permute-done.1.refs_2_, ...), custom_call_target="tpu_custom_call" | custom-call | flops 268000000 | bytes 2700000 | tf_op jit(solution)/shard_map/project/pallas_call | solution.py:328
  43.5 7.5 %all-to-all-start.1 = ((bf16[4,128,128]{2,1,0:T(8,128)(2,1)}), bf16[4,128,128]{2,1,0:T(8,128)(2,1)S(1)}, u32[]{:S(2)}, u32[]{:S(2)}) async-start(bf16[4,128,128]{2,1,0:T(8,128)(2,1)} %project.1), calls=%async_computation.1 | async-start | bytes 262144 | tf_op jit(solution)/shard_map/all_to_all | solution.py:337
  51.0 4.8 %collective-permute-start.8 = (bf16[144,128]{1,0:T(8,128)(2,1)S(1)}, bf16[144,128]{1,0:T(8,128)(2,1)S(1)}, u32[]{:S(2)}, u32[]{:S(2)}) collective-permute-start(bf16[144,128]{1,0:T(8,128)(2,1)S(1)} %pad_maximum_fusion.5), channel_id=1, source_target_pairs={{0,0},{16,64},{32,128},{48,192},{64,16},{80,80},{96,144},{112,208}... | collective-permute-start | bytes 110600 | tf_op jit(solution)/shard_map/ppermute | solution.py:30
  55.8 1.9 %collective-permute-done.8.residual_ref = bf16[144,128]{1,0:T(8,128)(2,1)S(1)} collective-permute-done((bf16[144,128]{1,0:T(8,128)(2,1)S(1)}, bf16[144,128]{1,0:T(8,128)(2,1)S(1)}, u32[]{:S(2)}, u32[]{:S(2)}) %collective-permute-start.8) | collective-permute-done | bytes 36896 | tf_op jit(solution)/shard_map/ppermute | solution.py:30
  58.6 13.5 %all_to_all.20 = bf16[4,136,128]{2,1,0:T(8,128)(2,1)S(1)} all-to-all(bf16[4,136,128]{2,1,0:T(8,128)(2,1)S(1)} %broadcast_in_dim.38), channel_id=1, replica_groups=mesh['z_low'=2,'core'=2,'y'=4,'z_high'=4,'x'=4] {'z_high'}, dimensions={0} | all-to-all | bytes 278528 | tf_op jit(solution)/shard_map/all_to_all | solution.py:25
  72.1 3.5 %collective-permute-start.10 = (bf16[4,64,128]{2,1,0:T(8,128)(2,1)S(1)}, bf16[4,64,128]{2,1,0:T(8,128)(2,1)S(1)}, u32[]{:S(2)}, u32[]{:S(2)}) collective-permute-start(bf16[4,64,128]{2,1,0:T(8,128)(2,1)S(1)} %get-tuple-element.26), channel_id=1, source_target_pairs={{0,48},{16,0},{32,16},{48,32},{1,49},{17,1},{33,17},{49,33},{2,50}... | collective-permute-start | bytes 196616 | tf_op jit(solution)/shard_map/ppermute | solution.py:36
  75.6 1.3 collective-permute-start.11
  76.9 3.7 %collective-permute-done.9 = bf16[4,64,128]{2,1,0:T(8,128)(2,1)S(1)} collective-permute-done((bf16[4,64,128]{2,1,0:T(8,128)(2,1)S(1)}, bf16[4,64,128]{2,1,0:T(8,128)(2,1)S(1)}, u32[]{:S(2)}, u32[]{:S(2)}) %collective-permute-start.9) | collective-permute-done | bytes 65568 | tf_op jit(solution)/shard_map/ppermute | solution.py:36
  81.0 2.7 %collective-permute-start.16 = (bf16[4,72,128]{2,1,0:T(8,128)(2,1)S(1)}, bf16[4,72,128]{2,1,0:T(8,128)(2,1)S(1)}, u32[]{:S(2)}, u32[]{:S(2)}) collective-permute-start(bf16[4,72,128]{2,1,0:T(8,128)(2,1)S(1)} %get-tuple-element.24), channel_id=1, source_target_pairs={{0,3},{1,0},{2,1},{3,2},{4,7},{5,4},{6,5},{7,6},{8,11},{9,8},{10,9... | collective-permute-start | bytes 221192 | tf_op jit(solution)/shard_map/ppermute | solution.py:36
  83.8 1.7 collective-permute-start.17
  85.5 1.3 collective-permute-done.16
  86.8 1.5 collective-permute-done.15
  90.1 1.5 collective-permute-start.19
  92.1 2.5 %collective-permute-start.13 = (bf16[4,4,64,128]{3,2,1,0:T(8,128)(2,1)S(1)}, bf16[4,4,64,128]{3,2,1,0:T(8,128)(2,1)}, u32[]{:S(2)}, u32[]{:S(2)}) collective-permute-start(bf16[4,4,64,128]{3,2,1,0:T(8,128)(2,1)S(1)} %pad_maximum_fusion.3.refs_0_), channel_id=1, source_target_pairs={{0,3},{1,0},{2,1},{3,2},{4,7},{5,4},{6,5},{7,6},{8,11},{9,8},{10,9... | collective-permute-start | bytes 786440 | tf_op jit(solution)/shard_map/ppermute | solution.py:36
  94.6 1.5 copy-done.2
  96.1 1.0 order.1.refs_8_
  97.9 3.4 %collective-permute-done.12.refs_1_ = bf16[4,4,64,128]{3,2,1,0:T(8,128)(2,1)} collective-permute-done((bf16[4,4,64,128]{3,2,1,0:T(8,128)(2,1)S(1)}, bf16[4,4,64,128]{3,2,1,0:T(8,128)(2,1)}, u32[]{:S(2)}, u32[]{:S(2)}) %collective-permute-start.12) | collective-permute-done | bytes 262176 | tf_op jit(solution)/shard_map/ppermute | solution.py:36
  101.3 3.2 %gate_up.1 = (f32[2,464,128]{2,1,0:T(8,128)S(1)}, bf16[2,464,128]{2,1,0:T(8,128)(2,1)S(1)}) custom-call(s32[4]{0:T(128)S(1)} %pad_add_fusion.group_ref, s32[1]{0:T(128)} %bitcast.7.core_ref, bf16[4,4,64,128]{3,2,1,0:T(8,128)(2,1)S(1)} %pad_maximum_fusion.3.refs_0_, bf16[4,4,64,128]{3,2,1,0:T(8,128)(2,1)} %collective-permute-done.12.refs_1_, ...), custom_call_target="tpu_custom_call" | custom-call | flops 940000000 | bytes 4300000 | tf_op jit(solution)/shard_map/gate_up/pallas_call | solution.py:362
  104.5 9.8 %collective-permute-start.21 = (bf16[2,464,128]{2,1,0:T(8,128)(2,1)S(1)}, bf16[2,464,128]{2,1,0:T(8,128)(2,1)S(1)}, u32[]{:S(2)}, u32[]{:S(2)}) collective-permute-start(bf16[2,464,128]{2,1,0:T(8,128)(2,1)S(1)} %get-tuple-element.13), channel_id=1, source_target_pairs={{0,64},{64,0},{1,65},{65,1},{2,66},{66,2},{3,67},{67,3},{4,68},{68... | collective-permute-start | bytes 712712 | tf_op jit(solution)/shard_map/ppermute | solution.py:377
  114.3 1.1 collective-permute-done.21.got_ref
  115.6 4.4 %collective-permute-done.22.got_ref = bf16[464,128]{1,0:T(8,128)(2,1)S(1)} collective-permute-done((bf16[464,128]{1,0:T(8,128)(2,1)S(1)}, bf16[464,128]{1,0:T(8,128)(2,1)S(1)}, u32[]{:S(2)}, u32[]{:S(2)}) %collective-permute-start.22) | collective-permute-done | bytes 118816 | tf_op jit(solution)/shard_map/ppermute | solution.py:390
  120.1 4.0 %collective-permute-start.23 = (bf16[352,128]{1,0:T(8,128)(2,1)S(1)}, bf16[352,128]{1,0:T(8,128)(2,1)S(1)}, u32[]{:S(2)}, u32[]{:S(2)}) collective-permute-start(bf16[352,128]{1,0:T(8,128)(2,1)S(1)} %get-tuple-element.17), channel_id=1, source_target_pairs={{0,0},{16,64},{32,128},{48,192},{64,16},{80,80},{96,144},{112,208}... | collective-permute-start | bytes 270344 | tf_op jit(solution)/shard_map/ppermute | solution.py:30
  124.1 3.2 %collective-permute-done.23.in_ref = bf16[352,128]{1,0:T(8,128)(2,1)S(1)} collective-permute-done((bf16[352,128]{1,0:T(8,128)(2,1)S(1)}, bf16[352,128]{1,0:T(8,128)(2,1)S(1)}, u32[]{:S(2)}, u32[]{:S(2)}) %collective-permute-start.23) | collective-permute-done | bytes 90144 | tf_op jit(solution)/shard_map/ppermute | solution.py:30
  127.3 11.1 %all_to_all.21 = bf16[4,224,128]{2,1,0:T(8,128)(2,1)S(1)} all-to-all(bf16[4,224,128]{2,1,0:T(8,128)(2,1)S(1)} %broadcast_in_dim.39), channel_id=1, replica_groups=mesh['z_low'=2,'core'=2,'y'=4,'z_high'=4,'x'=4] {'z_high'}, dimensions={0} | all-to-all | bytes 458752 | tf_op jit(solution)/shard_map/all_to_all | solution.py:25
  138.5 2.0 %collective-permute-start.27 = (bf16[4,112,128]{2,1,0:T(8,128)(2,1)S(1)}, bf16[4,112,128]{2,1,0:T(8,128)(2,1)S(1)}, u32[]{:S(2)}, u32[]{:S(2)}) collective-permute-start(bf16[4,112,128]{2,1,0:T(8,128)(2,1)S(1)} %get-tuple-element.22), channel_id=1, source_target_pairs={{0,48},{16,0},{32,16},{48,32},{1,49},{17,1},{33,17},{49,33},{2,50}... | collective-permute-start | bytes 344072 | tf_op jit(solution)/shard_map/ppermute | solution.py:36
  140.5 1.3 collective-permute-start.28
  142.0 1.3 collective-permute-start.33
  143.2 3.3 %collective-permute-done.26 = bf16[4,112,128]{2,1,0:T(8,128)(2,1)S(1)} collective-permute-done((bf16[4,112,128]{2,1,0:T(8,128)(2,1)S(1)}, bf16[4,112,128]{2,1,0:T(8,128)(2,1)S(1)}, u32[]{:S(2)}, u32[]{:S(2)}) %collective-permute-start.26) | collective-permute-done | bytes 114720 | tf_op jit(solution)/shard_map/ppermute | solution.py:36
  146.9 1.3 collective-permute-start.29
  148.5 3.4 %collective-permute-start.37 = (bf16[4,4,112,128]{3,2,1,0:T(8,128)(2,1)S(1)}, bf16[4,4,112,128]{3,2,1,0:T(8,128)(2,1)S(1)}, u32[]{:S(2)}, u32[]{:S(2)}) collective-permute-start(bf16[4,4,112,128]{3,2,1,0:T(8,128)(2,1)S(1)} %pad_maximum_fusion.1.refs_5_), channel_id=1, source_target_pairs={{0,48},{16,0},{32,16},{48,32},{1,49},{17,1},{33,17},{49,33},{2,50}... | collective-permute-start | bytes 1376264 | tf_op jit(solution)/shard_map/ppermute | solution.py:44
  151.9 6.6 %collective-permute-start.24 = (bf16[224,128]{1,0:T(8,128)(2,1)S(1)}, bf16[224,128]{1,0:T(8,128)(2,1)S(1)}, u32[]{:S(2)}, u32[]{:S(2)}) collective-permute-start(bf16[224,128]{1,0:T(8,128)(2,1)S(1)} %get-tuple-element.18), channel_id=1, source_target_pairs={{0,64},{64,0},{1,65},{65,1},{2,66},{66,2},{3,67},{67,3},{4,68},{68... | collective-permute-start | bytes 172040 | tf_op jit(solution)/shard_map/ppermute | solution.py:416
  158.9 1.2 collective-permute-start.32
  160.6 2.3 %collective-permute-start.39 = (bf16[2,4,112,128]{3,2,1,0:T(8,128)(2,1)S(1)}, bf16[2,4,112,128]{3,2,1,0:T(8,128)(2,1)S(1)}, u32[]{:S(2)}, u32[]{:S(2)}) collective-permute-start(bf16[2,4,112,128]{3,2,1,0:T(8,128)(2,1)S(1)} %slice.44), channel_id=1, source_target_pairs={{0,48},{16,0},{32,16},{48,32},{1,49},{17,1},{33,17},{49,33},{2,50}... | collective-permute-start | bytes 688136 | tf_op jit(solution)/shard_map/ppermute | solution.py:45
  163.1 2.3 %collective-permute-start.25 = (bf16[2,224,128]{2,1,0:T(8,128)(2,1)S(1)}, bf16[2,224,128]{2,1,0:T(8,128)(2,1)S(1)}, u32[]{:S(2)}, u32[]{:S(2)}) collective-permute-start(bf16[2,224,128]{2,1,0:T(8,128)(2,1)S(1)} %pad_maximum_fusion.4.near_ref), channel_id=1, source_target_pairs={{0,128},{128,0},{1,129},{129,1},{2,130},{130,2},{3,131},{131,3},{4... | collective-permute-start | bytes 344072 | tf_op jit(solution)/shard_map/ppermute | solution.py:418
  165.9 1.9 %collective-permute-done.25.far_ref = bf16[2,224,128]{2,1,0:T(8,128)(2,1)S(1)} collective-permute-done((bf16[2,224,128]{2,1,0:T(8,128)(2,1)S(1)}, bf16[2,224,128]{2,1,0:T(8,128)(2,1)S(1)}, u32[]{:S(2)}, u32[]{:S(2)}) %collective-permute-start.25) | collective-permute-done | bytes 114720 | tf_op jit(solution)/shard_map/ppermute | solution.py:418
  167.8 2.1 %collective-permute-done.38.refs_8_ = bf16[2,4,112,128]{3,2,1,0:T(8,128)(2,1)S(1)} collective-permute-done((bf16[2,4,112,128]{3,2,1,0:T(8,128)(2,1)S(1)}, bf16[2,4,112,128]{3,2,1,0:T(8,128)(2,1)S(1)}, u32[]{:S(2)}, u32[]{:S(2)}) %collective-permute-start.38) | collective-permute-done | bytes 229408 | tf_op jit(solution)/shard_map/ppermute | solution.py:45
  169.9 4.3 %hessian.1 = f32[224,3584]{1,0:T(8,128)} custom-call(s32[4]{0:T(128)S(1)} %pad_add_fusion.1.from_ref, s32[4]{0:T(128)S(1)} %pad_add_fusion.group_ref, s32[1]{0:T(128)} %bitcast.place_ref, bf16[2,224,128]{2,1,0:T(8,128)(2,1)S(1)} %pad_maximum_fusion.4.near_ref, bf16[2,224,128]{2,1,0:T(8,128)(2,1)S(1)} %collective-permute-done.25.far_ref, ...), custom_call_target="tpu_custom_call" | custom-call | flops 822000000 | bytes 7100000 | tf_op jit(solution)/shard_map/hessian/pallas_call | solution.py:419
  (85 shorter events, 10.2 us)
Async XLA Ops:
  0.6 21.7 %copy-start = (f32[128,2048]{1,0:T(8,128)S(1)}, f32[128,2048]{1,0:T(8,128)}, u32[]{:S(2)}) copy-start(f32[128,2048]{1,0:T(8,128)} %factor_ref.1) | copy-start | bytes 3145732
  0.6 21.7 %copy-start.3 = (s32[128,128]{1,0:T(8,128)S(1)}, s32[128,128]{1,0:T(8,128)}, u32[]{:S(2)}) copy-start(s32[128,128]{1,0:T(8,128)} %mask_ref.1) | copy-start | bytes 196612
  0.7 21.6 %copy-start.1 = (bf16[128,2048]{1,0:T(8,128)(2,1)S(1)}, bf16[128,2048]{1,0:T(8,128)(2,1)}, u32[]{:S(2)}) copy-start(bf16[128,2048]{1,0:T(8,128)(2,1)} %weight_ref.1) | copy-start | bytes 1572868
  2.3 21.8 %all-to-all-start = ((bf16[8,128,128]{2,1,0:T(8,128)(2,1)}), bf16[8,128,128]{2,1,0:T(8,128)(2,1)S(1)}, u32[]{:S(2)}, u32[]{:S(2)}) async-start(bf16[8,128,128]{2,1,0:T(8,128)(2,1)} %broadcast_in_dim.17), calls=%async_computation | async-start | bytes 524288 | tf_op jit(solution)/shard_map/all_to_all | solution.py:25
  24.1 26.9 %copy-start.7 = (bf16[128]{0:T(256)(128)(2,1)S(1)}, bf16[128]{0:T(256)(128)(2,1)}, u32[]{:S(2)}) copy-start(bf16[128]{0:T(256)(128)(2,1)} %param.12) | copy-start | bytes 772
  24.1 26.9 %copy-start.6 = (bf16[128,128]{1,0:T(8,128)(2,1)S(1)}, bf16[128,128]{1,0:T(8,128)(2,1)}, u32[]{:S(2)}) copy-start(bf16[128,128]{1,0:T(8,128)(2,1)} %param.8) | copy-start | bytes 98308
  24.1 9.2 %collective-permute-start.2 = (bf16[8,128,128]{2,1,0:T(8,128)(2,1)S(1)}, bf16[8,128,128]{2,1,0:T(8,128)(2,1)S(1)}, u32[]{:S(2)}, u32[]{:S(2)}) collective-permute-start(bf16[8,128,128]{2,1,0:T(8,128)(2,1)S(1)} %all-to-all-done.refs_0_), channel_id=1, source_target_pairs={{0,2},{1,3},{2,0},{3,1},{4,6},{5,7},{6,4},{7,5},{8,10},{9,11},{10,... | collective-permute-start | bytes 786440 | tf_op jit(solution)/shard_map/ppermute | solution.py:36
  26.9 14.1 %collective-permute-start.7 = (bf16[128,2048]{1,0:T(8,128)(2,1)}, bf16[128,2048]{1,0:T(8,128)(2,1)S(1)}, u32[]{:S(2)}, u32[]{:S(2)}) collective-permute-start(bf16[128,2048]{1,0:T(8,128)(2,1)} %update.1), channel_id=1, source_target_pairs={{0,0},{16,64},{32,128},{48,192},{64,16},{80,80},{96,144},{112,208}... | collective-permute-start | bytes 1572872 | tf_op jit(solution)/shard_map/ppermute | solution.py:30
  30.4 8.6 %collective-permute-start.1 = (bf16[8,128,128]{2,1,0:T(8,128)(2,1)S(1)}, bf16[8,128,128]{2,1,0:T(8,128)(2,1)S(1)}, u32[]{:S(2)}, u32[]{:S(2)}) collective-permute-start(bf16[8,128,128]{2,1,0:T(8,128)(2,1)S(1)} %all-to-all-done.refs_0_), channel_id=1, source_target_pairs={{0,3},{1,0},{2,1},{3,2},{4,7},{5,4},{6,5},{7,6},{8,11},{9,8},{10,9... | collective-permute-start | bytes 786440 | tf_op jit(solution)/shard_map/ppermute | solution.py:36
  31.3 8.7 %collective-permute-start = (bf16[8,128,128]{2,1,0:T(8,128)(2,1)S(1)}, bf16[8,128,128]{2,1,0:T(8,128)(2,1)S(1)}, u32[]{:S(2)}, u32[]{:S(2)}) collective-permute-start(bf16[8,128,128]{2,1,0:T(8,128)(2,1)S(1)} %all-to-all-done.refs_0_), channel_id=1, source_target_pairs={{0,1},{1,2},{2,3},{3,0},{4,5},{5,6},{6,7},{7,4},{8,9},{9,10},{10,1... | collective-permute-start | bytes 786440 | tf_op jit(solution)/shard_map/ppermute | solution.py:36
  31.9 9.1 %collective-permute-start.3 = (bf16[8,128,128]{2,1,0:T(8,128)(2,1)S(1)}, bf16[8,128,128]{2,1,0:T(8,128)(2,1)S(1)}, u32[]{:S(2)}, u32[]{:S(2)}) collective-permute-start(bf16[8,128,128]{2,1,0:T(8,128)(2,1)S(1)} %all-to-all-done.refs_0_), channel_id=1, source_target_pairs={{0,64},{64,0},{1,65},{65,1},{2,66},{66,2},{3,67},{67,3},{4,68},{68... | collective-permute-start | bytes 786440 | tf_op jit(solution)/shard_map/ppermute | solution.py:319
  33.3 7.7 %collective-permute-start.6 = (bf16[8,128,128]{2,1,0:T(8,128)(2,1)S(1)}, bf16[8,128,128]{2,1,0:T(8,128)(2,1)S(1)}, u32[]{:S(2)}, u32[]{:S(2)}) collective-permute-start(bf16[8,128,128]{2,1,0:T(8,128)(2,1)S(1)} %collective-permute-done.2.refs_3_), channel_id=1, source_target_pairs={{0,64},{64,0},{1,65},{65,1},{2,66},{66,2},{3,67},{67,3},{4,68},{68... | collective-permute-start | bytes 786440 | tf_op jit(solution)/shard_map/ppermute | solution.py:319
  39.0 2.2 %collective-permute-start.5 = (bf16[8,128,128]{2,1,0:T(8,128)(2,1)S(1)}, bf16[8,128,128]{2,1,0:T(8,128)(2,1)S(1)}, u32[]{:S(2)}, u32[]{:S(2)}) collective-permute-start(bf16[8,128,128]{2,1,0:T(8,128)(2,1)S(1)} %collective-permute-done.1.refs_2_), channel_id=1, source_target_pairs={{0,64},{64,0},{1,65},{65,1},{2,66},{66,2},{3,67},{67,3},{4,68},{68... | collective-permute-start | bytes 786440 | tf_op jit(solution)/shard_map/ppermute | solution.py:319
  40.1 1.5 collective-permute-start.4
  43.5 14.2 %all-to-all-start.1 = ((bf16[4,128,128]{2,1,0:T(8,128)(2,1)}), bf16[4,128,128]{2,1,0:T(8,128)(2,1)S(1)}, u32[]{:S(2)}, u32[]{:S(2)}) async-start(bf16[4,128,128]{2,1,0:T(8,128)(2,1)} %project.1), calls=%async_computation.1 | async-start | bytes 262144 | tf_op jit(solution)/shard_map/all_to_all | solution.py:337
  51.0 6.7 %collective-permute-start.8 = (bf16[144,128]{1,0:T(8,128)(2,1)S(1)}, bf16[144,128]{1,0:T(8,128)(2,1)S(1)}, u32[]{:S(2)}, u32[]{:S(2)}) collective-permute-start(bf16[144,128]{1,0:T(8,128)(2,1)S(1)} %pad_maximum_fusion.5), channel_id=1, source_target_pairs={{0,0},{16,64},{32,128},{48,192},{64,16},{80,80},{96,144},{112,208}... | collective-permute-start | bytes 110600 | tf_op jit(solution)/shard_map/ppermute | solution.py:30
  72.1 4.8 %collective-permute-start.10 = (bf16[4,64,128]{2,1,0:T(8,128)(2,1)S(1)}, bf16[4,64,128]{2,1,0:T(8,128)(2,1)S(1)}, u32[]{:S(2)}, u32[]{:S(2)}) collective-permute-start(bf16[4,64,128]{2,1,0:T(8,128)(2,1)S(1)} %get-tuple-element.26), channel_id=1, source_target_pairs={{0,48},{16,0},{32,16},{48,32},{1,49},{17,1},{33,17},{49,33},{2,50}... | collective-permute-start | bytes 196616 | tf_op jit(solution)/shard_map/ppermute | solution.py:36
  75.6 5.0 %collective-permute-start.9 = (bf16[4,64,128]{2,1,0:T(8,128)(2,1)S(1)}, bf16[4,64,128]{2,1,0:T(8,128)(2,1)S(1)}, u32[]{:S(2)}, u32[]{:S(2)}) collective-permute-start(bf16[4,64,128]{2,1,0:T(8,128)(2,1)S(1)} %get-tuple-element.26), channel_id=1, source_target_pairs={{0,16},{16,32},{32,48},{48,0},{1,17},{17,33},{33,49},{49,1},{2,18}... | collective-permute-start | bytes 196616 | tf_op jit(solution)/shard_map/ppermute | solution.py:36
  75.6 5.0 %collective-permute-start.11 = (bf16[4,64,128]{2,1,0:T(8,128)(2,1)S(1)}, bf16[4,64,128]{2,1,0:T(8,128)(2,1)S(1)}, u32[]{:S(2)}, u32[]{:S(2)}) collective-permute-start(bf16[4,64,128]{2,1,0:T(8,128)(2,1)S(1)} %get-tuple-element.26), channel_id=1, source_target_pairs={{0,32},{16,48},{32,0},{48,16},{1,33},{17,49},{33,1},{49,17},{2,34}... | collective-permute-start | bytes 196616 | tf_op jit(solution)/shard_map/ppermute | solution.py:36
  80.7 13.9 %collective-permute-start.14 = (bf16[4,4,64,128]{3,2,1,0:T(8,128)(2,1)S(1)}, bf16[4,4,64,128]{3,2,1,0:T(8,128)(2,1)S(1)}, u32[]{:S(2)}, u32[]{:S(2)}) collective-permute-start(bf16[4,4,64,128]{3,2,1,0:T(8,128)(2,1)S(1)} %pad_maximum_fusion.3.refs_0_), channel_id=1, source_target_pairs={{0,2},{1,3},{2,0},{3,1},{4,6},{5,7},{6,4},{7,5},{8,10},{9,11},{10,... | collective-permute-start | bytes 786440 | tf_op jit(solution)/shard_map/ppermute | solution.py:36
  81.0 5.7 %collective-permute-start.16 = (bf16[4,72,128]{2,1,0:T(8,128)(2,1)S(1)}, bf16[4,72,128]{2,1,0:T(8,128)(2,1)S(1)}, u32[]{:S(2)}, u32[]{:S(2)}) collective-permute-start(bf16[4,72,128]{2,1,0:T(8,128)(2,1)S(1)} %get-tuple-element.24), channel_id=1, source_target_pairs={{0,3},{1,0},{2,1},{3,2},{4,7},{5,4},{6,5},{7,6},{8,11},{9,8},{10,9... | collective-permute-start | bytes 221192 | tf_op jit(solution)/shard_map/ppermute | solution.py:36
  83.8 4.5 %collective-permute-start.15 = (bf16[4,72,128]{2,1,0:T(8,128)(2,1)S(1)}, bf16[4,72,128]{2,1,0:T(8,128)(2,1)S(1)}, u32[]{:S(2)}, u32[]{:S(2)}) collective-permute-start(bf16[4,72,128]{2,1,0:T(8,128)(2,1)S(1)} %get-tuple-element.24), channel_id=1, source_target_pairs={{0,1},{1,2},{2,3},{3,0},{4,5},{5,6},{6,7},{7,4},{8,9},{9,10},{10,1... | collective-permute-start | bytes 221192 | tf_op jit(solution)/shard_map/ppermute | solution.py:36
  83.8 5.3 %collective-permute-start.17 = (bf16[4,72,128]{2,1,0:T(8,128)(2,1)S(1)}, bf16[4,72,128]{2,1,0:T(8,128)(2,1)S(1)}, u32[]{:S(2)}, u32[]{:S(2)}) collective-permute-start(bf16[4,72,128]{2,1,0:T(8,128)(2,1)S(1)} %get-tuple-element.24), channel_id=1, source_target_pairs={{0,2},{1,3},{2,0},{3,1},{4,6},{5,7},{6,4},{7,5},{8,10},{9,11},{10,... | collective-permute-start | bytes 221192 | tf_op jit(solution)/shard_map/ppermute | solution.py:36
  89.1 12.2 %collective-permute-start.20 = (bf16[4,4,72,128]{3,2,1,0:T(8,128)(2,1)S(1)}, bf16[4,4,72,128]{3,2,1,0:T(8,128)(2,1)S(1)}, u32[]{:S(2)}, u32[]{:S(2)}) collective-permute-start(bf16[4,4,72,128]{3,2,1,0:T(8,128)(2,1)S(1)} %pad_maximum_fusion.2.refs_4_), channel_id=1, source_target_pairs={{0,32},{16,48},{32,0},{48,16},{1,33},{17,49},{33,1},{49,17},{2,34}... | collective-permute-start | bytes 884744 | tf_op jit(solution)/shard_map/ppermute | solution.py:36
  90.1 11.2 %collective-permute-start.19 = (bf16[4,4,72,128]{3,2,1,0:T(8,128)(2,1)S(1)}, bf16[4,4,72,128]{3,2,1,0:T(8,128)(2,1)S(1)}, u32[]{:S(2)}, u32[]{:S(2)}) collective-permute-start(bf16[4,4,72,128]{3,2,1,0:T(8,128)(2,1)S(1)} %pad_maximum_fusion.2.refs_4_), channel_id=1, source_target_pairs={{0,48},{16,0},{32,16},{48,32},{1,49},{17,1},{33,17},{49,33},{2,50}... | collective-permute-start | bytes 884744 | tf_op jit(solution)/shard_map/ppermute | solution.py:36
  91.6 9.8 %collective-permute-start.18 = (bf16[4,4,72,128]{3,2,1,0:T(8,128)(2,1)S(1)}, bf16[4,4,72,128]{3,2,1,0:T(8,128)(2,1)S(1)}, u32[]{:S(2)}, u32[]{:S(2)}) collective-permute-start(bf16[4,4,72,128]{3,2,1,0:T(8,128)(2,1)S(1)} %pad_maximum_fusion.2.refs_4_), channel_id=1, source_target_pairs={{0,16},{16,32},{32,48},{48,0},{1,17},{17,33},{33,49},{49,1},{2,18}... | collective-permute-start | bytes 884744 | tf_op jit(solution)/shard_map/ppermute | solution.py:36
  92.1 5.8 %collective-permute-start.13 = (bf16[4,4,64,128]{3,2,1,0:T(8,128)(2,1)S(1)}, bf16[4,4,64,128]{3,2,1,0:T(8,128)(2,1)}, u32[]{:S(2)}, u32[]{:S(2)}) collective-permute-start(bf16[4,4,64,128]{3,2,1,0:T(8,128)(2,1)S(1)} %pad_maximum_fusion.3.refs_0_), channel_id=1, source_target_pairs={{0,3},{1,0},{2,1},{3,2},{4,7},{5,4},{6,5},{7,6},{8,11},{9,8},{10,9... | collective-permute-start | bytes 786440 | tf_op jit(solution)/shard_map/ppermute | solution.py:36
  94.6 6.7 %collective-permute-start.12 = (bf16[4,4,64,128]{3,2,1,0:T(8,128)(2,1)S(1)}, bf16[4,4,64,128]{3,2,1,0:T(8,128)(2,1)}, u32[]{:S(2)}, u32[]{:S(2)}) collective-permute-start(bf16[4,4,64,128]{3,2,1,0:T(8,128)(2,1)S(1)} %pad_maximum_fusion.3.refs_0_), channel_id=1, source_target_pairs={{0,1},{1,2},{2,3},{3,0},{4,5},{5,6},{6,7},{7,4},{8,9},{9,10},{10,1... | collective-permute-start | bytes 786440 | tf_op jit(solution)/shard_map/ppermute | solution.py:36
  97.2 22.8 %copy-start.5 = (bf16[128,128]{1,0:T(8,128)(2,1)S(1)}, bf16[128,128]{1,0:T(8,128)(2,1)}, u32[]{:S(2)}) copy-start(bf16[128,128]{1,0:T(8,128)(2,1)} %copy-done.4) | copy-start | bytes 98308
  104.5 10.9 %collective-permute-start.21 = (bf16[2,464,128]{2,1,0:T(8,128)(2,1)S(1)}, bf16[2,464,128]{2,1,0:T(8,128)(2,1)S(1)}, u32[]{:S(2)}, u32[]{:S(2)}) collective-permute-start(bf16[2,464,128]{2,1,0:T(8,128)(2,1)S(1)} %get-tuple-element.13), channel_id=1, source_target_pairs={{0,64},{64,0},{1,65},{65,1},{2,66},{66,2},{3,67},{67,3},{4,68},{68... | collective-permute-start | bytes 712712 | tf_op jit(solution)/shard_map/ppermute | solution.py:377
  115.5 4.5 %collective-permute-start.22 = (bf16[464,128]{1,0:T(8,128)(2,1)S(1)}, bf16[464,128]{1,0:T(8,128)(2,1)S(1)}, u32[]{:S(2)}, u32[]{:S(2)}) collective-permute-start(bf16[464,128]{1,0:T(8,128)(2,1)S(1)} %get-tuple-element.15), channel_id=1, source_target_pairs={{0,128},{128,0},{1,129},{129,1},{2,130},{130,2},{3,131},{131,3},{4... | collective-permute-start | bytes 356360 | tf_op jit(solution)/shard_map/ppermute | solution.py:390
  120.1 7.2 %collective-permute-start.23 = (bf16[352,128]{1,0:T(8,128)(2,1)S(1)}, bf16[352,128]{1,0:T(8,128)(2,1)S(1)}, u32[]{:S(2)}, u32[]{:S(2)}) collective-permute-start(bf16[352,128]{1,0:T(8,128)(2,1)S(1)} %get-tuple-element.17), channel_id=1, source_target_pairs={{0,0},{16,64},{32,128},{48,192},{64,16},{80,80},{96,144},{112,208}... | collective-permute-start | bytes 270344 | tf_op jit(solution)/shard_map/ppermute | solution.py:30
  138.5 4.8 %collective-permute-start.27 = (bf16[4,112,128]{2,1,0:T(8,128)(2,1)S(1)}, bf16[4,112,128]{2,1,0:T(8,128)(2,1)S(1)}, u32[]{:S(2)}, u32[]{:S(2)}) collective-permute-start(bf16[4,112,128]{2,1,0:T(8,128)(2,1)S(1)} %get-tuple-element.22), channel_id=1, source_target_pairs={{0,48},{16,0},{32,16},{48,32},{1,49},{17,1},{33,17},{49,33},{2,50}... | collective-permute-start | bytes 344072 | tf_op jit(solution)/shard_map/ppermute | solution.py:36
  140.5 6.1 %collective-permute-start.26 = (bf16[4,112,128]{2,1,0:T(8,128)(2,1)S(1)}, bf16[4,112,128]{2,1,0:T(8,128)(2,1)S(1)}, u32[]{:S(2)}, u32[]{:S(2)}) collective-permute-start(bf16[4,112,128]{2,1,0:T(8,128)(2,1)S(1)} %get-tuple-element.22), channel_id=1, source_target_pairs={{0,16},{16,32},{32,48},{48,0},{1,17},{17,33},{33,49},{49,1},{2,18}... | collective-permute-start | bytes 344072 | tf_op jit(solution)/shard_map/ppermute | solution.py:36
  140.5 6.1 %collective-permute-start.28 = (bf16[4,112,128]{2,1,0:T(8,128)(2,1)S(1)}, bf16[4,112,128]{2,1,0:T(8,128)(2,1)S(1)}, u32[]{:S(2)}, u32[]{:S(2)}) collective-permute-start(bf16[4,112,128]{2,1,0:T(8,128)(2,1)S(1)} %get-tuple-element.22), channel_id=1, source_target_pairs={{0,32},{16,48},{32,0},{48,16},{1,33},{17,49},{33,1},{49,17},{2,34}... | collective-permute-start | bytes 344072 | tf_op jit(solution)/shard_map/ppermute | solution.py:36
  141.8 6.4 %collective-permute-start.34 = (bf16[4,112,128]{2,1,0:T(8,128)(2,1)S(1)}, bf16[4,112,128]{2,1,0:T(8,128)(2,1)S(1)}, u32[]{:S(2)}, u32[]{:S(2)}) collective-permute-start(bf16[4,112,128]{2,1,0:T(8,128)(2,1)S(1)} %get-tuple-element.21), channel_id=1, source_target_pairs={{0,3},{1,0},{2,1},{3,2},{4,7},{5,4},{6,5},{7,6},{8,11},{9,8},{10,9... | collective-permute-start | bytes 344072 | tf_op jit(solution)/shard_map/ppermute | solution.py:36
  142.0 6.2 %collective-permute-start.33 = (bf16[4,112,128]{2,1,0:T(8,128)(2,1)S(1)}, bf16[4,112,128]{2,1,0:T(8,128)(2,1)S(1)}, u32[]{:S(2)}, u32[]{:S(2)}) collective-permute-start(bf16[4,112,128]{2,1,0:T(8,128)(2,1)S(1)} %get-tuple-element.21), channel_id=1, source_target_pairs={{0,1},{1,2},{2,3},{3,0},{4,5},{5,6},{6,7},{7,4},{8,9},{9,10},{10,1... | collective-permute-start | bytes 344072 | tf_op jit(solution)/shard_map/ppermute | solution.py:36
  143.2 5.1 %collective-permute-start.35 = (bf16[4,112,128]{2,1,0:T(8,128)(2,1)S(1)}, bf16[4,112,128]{2,1,0:T(8,128)(2,1)S(1)}, u32[]{:S(2)}, u32[]{:S(2)}) collective-permute-start(bf16[4,112,128]{2,1,0:T(8,128)(2,1)S(1)} %get-tuple-element.21), channel_id=1, source_target_pairs={{0,2},{1,3},{2,0},{3,1},{4,6},{5,7},{6,4},{7,5},{8,10},{9,11},{10,... | collective-permute-start | bytes 344072 | tf_op jit(solution)/shard_map/ppermute | solution.py:36
  146.6 12.2 %collective-permute-start.30 = (bf16[4,4,112,128]{3,2,1,0:T(8,128)(2,1)S(1)}, bf16[4,4,112,128]{3,2,1,0:T(8,128)(2,1)S(1)}, u32[]{:S(2)}, u32[]{:S(2)}) collective-permute-start(bf16[4,4,112,128]{3,2,1,0:T(8,128)(2,1)S(1)} %pad_maximum_fusion.refs_0_), channel_id=1, source_target_pairs={{0,3},{1,0},{2,1},{3,2},{4,7},{5,4},{6,5},{7,6},{8,11},{9,8},{10,9... | collective-permute-start | bytes 1376264 | tf_op jit(solution)/shard_map/ppermute | solution.py:44
  146.9 13.6 %collective-permute-start.29 = (bf16[4,4,112,128]{3,2,1,0:T(8,128)(2,1)S(1)}, bf16[4,4,112,128]{3,2,1,0:T(8,128)(2,1)S(1)}, u32[]{:S(2)}, u32[]{:S(2)}) collective-permute-start(bf16[4,4,112,128]{3,2,1,0:T(8,128)(2,1)S(1)} %pad_maximum_fusion.refs_0_), channel_id=1, source_target_pairs={{0,1},{1,2},{2,3},{3,0},{4,5},{5,6},{6,7},{7,4},{8,9},{9,10},{10,1... | collective-permute-start | bytes 1376264 | tf_op jit(solution)/shard_map/ppermute | solution.py:44
  148.5 12.1 %collective-permute-start.37 = (bf16[4,4,112,128]{3,2,1,0:T(8,128)(2,1)S(1)}, bf16[4,4,112,128]{3,2,1,0:T(8,128)(2,1)S(1)}, u32[]{:S(2)}, u32[]{:S(2)}) collective-permute-start(bf16[4,4,112,128]{3,2,1,0:T(8,128)(2,1)S(1)} %pad_maximum_fusion.1.refs_5_), channel_id=1, source_target_pairs={{0,48},{16,0},{32,16},{48,32},{1,49},{17,1},{33,17},{49,33},{2,50}... | collective-permute-start | bytes 1376264 | tf_op jit(solution)/shard_map/ppermute | solution.py:44
  151.9 11.1 %collective-permute-start.36 = (bf16[4,4,112,128]{3,2,1,0:T(8,128)(2,1)S(1)}, bf16[4,4,112,128]{3,2,1,0:T(8,128)(2,1)S(1)}, u32[]{:S(2)}, u32[]{:S(2)}) collective-permute-start(bf16[4,4,112,128]{3,2,1,0:T(8,128)(2,1)S(1)} %pad_maximum_fusion.1.refs_5_), channel_id=1, source_target_pairs={{0,16},{16,32},{32,48},{48,0},{1,17},{17,33},{33,49},{49,1},{2,18}... | collective-permute-start | bytes 1376264 | tf_op jit(solution)/shard_map/ppermute | solution.py:44
  151.9 11.2 %collective-permute-start.24 = (bf16[224,128]{1,0:T(8,128)(2,1)S(1)}, bf16[224,128]{1,0:T(8,128)(2,1)S(1)}, u32[]{:S(2)}, u32[]{:S(2)}) collective-permute-start(bf16[224,128]{1,0:T(8,128)(2,1)S(1)} %get-tuple-element.18), channel_id=1, source_target_pairs={{0,64},{64,0},{1,65},{65,1},{2,66},{66,2},{3,67},{67,3},{4,68},{68... | collective-permute-start | bytes 172040 | tf_op jit(solution)/shard_map/ppermute | solution.py:416
  158.9 8.9 %collective-permute-start.32 = (bf16[2,4,112,128]{3,2,1,0:T(8,128)(2,1)S(1)}, bf16[2,4,112,128]{3,2,1,0:T(8,128)(2,1)S(1)}, u32[]{:S(2)}, u32[]{:S(2)}) collective-permute-start(bf16[2,4,112,128]{3,2,1,0:T(8,128)(2,1)S(1)} %slice.41), channel_id=1, source_target_pairs={{0,3},{1,0},{2,1},{3,2},{4,7},{5,4},{6,5},{7,6},{8,11},{9,8},{10,9... | collective-permute-start | bytes 688136 | tf_op jit(solution)/shard_map/ppermute | solution.py:45
  160.5 7.3 %collective-permute-start.31 = (bf16[2,4,112,128]{3,2,1,0:T(8,128)(2,1)S(1)}, bf16[2,4,112,128]{3,2,1,0:T(8,128)(2,1)S(1)}, u32[]{:S(2)}, u32[]{:S(2)}) collective-permute-start(bf16[2,4,112,128]{3,2,1,0:T(8,128)(2,1)S(1)} %slice.40), channel_id=1, source_target_pairs={{0,1},{1,2},{2,3},{3,0},{4,5},{5,6},{6,7},{7,4},{8,9},{9,10},{10,1... | collective-permute-start | bytes 688136 | tf_op jit(solution)/shard_map/ppermute | solution.py:45
  160.6 7.2 %collective-permute-start.39 = (bf16[2,4,112,128]{3,2,1,0:T(8,128)(2,1)S(1)}, bf16[2,4,112,128]{3,2,1,0:T(8,128)(2,1)S(1)}, u32[]{:S(2)}, u32[]{:S(2)}) collective-permute-start(bf16[2,4,112,128]{3,2,1,0:T(8,128)(2,1)S(1)} %slice.44), channel_id=1, source_target_pairs={{0,48},{16,0},{32,16},{48,32},{1,49},{17,1},{33,17},{49,33},{2,50}... | collective-permute-start | bytes 688136 | tf_op jit(solution)/shard_map/ppermute | solution.py:45
  162.9 7.0 %collective-permute-start.38 = (bf16[2,4,112,128]{3,2,1,0:T(8,128)(2,1)S(1)}, bf16[2,4,112,128]{3,2,1,0:T(8,128)(2,1)S(1)}, u32[]{:S(2)}, u32[]{:S(2)}) collective-permute-start(bf16[2,4,112,128]{3,2,1,0:T(8,128)(2,1)S(1)} %slice.43), channel_id=1, source_target_pairs={{0,16},{16,32},{32,48},{48,0},{1,17},{17,33},{33,49},{49,1},{2,18}... | collective-permute-start | bytes 688136 | tf_op jit(solution)/shard_map/ppermute | solution.py:45
  163.1 4.7 %collective-permute-start.25 = (bf16[2,224,128]{2,1,0:T(8,128)(2,1)S(1)}, bf16[2,224,128]{2,1,0:T(8,128)(2,1)S(1)}, u32[]{:S(2)}, u32[]{:S(2)}) collective-permute-start(bf16[2,224,128]{2,1,0:T(8,128)(2,1)S(1)} %pad_maximum_fusion.4.near_ref), channel_id=1, source_target_pairs={{0,128},{128,0},{1,129},{129,1},{2,130},{130,2},{3,131},{131,3},{4... | collective-permute-start | bytes 344072 | tf_op jit(solution)/shard_map/ppermute | solution.py:418
  (2 other events, 2.1 us)

commit v7 on v6

--- a/solution.py
+++ b/solution.py
@@ -225,7 +225,7 @@
 
 def gate_up_kernel(group_ref, core_ref, *refs):
     upper, lower, weight_ref = refs[:4], refs[4:8], refs[8]
-    keep_ref, send_ref, part_ref = refs[9:]
+    keep_ref, send_ref = refs[9:]
     half = upper[0].shape[2]
     weight = weight_ref[...]
     units = weight.shape[0]
@@ -236,8 +236,7 @@
         square = jnp.zeros((8, LANES), jnp.float32)
         for r, z in places:
             square = square + lower[k][r, z, half:].astype(jnp.float32)
-        group = group_ref[k]
-        part_ref[group, :units, :] = lax.dot_general(
+        part = lax.dot_general(
             weight,
             jnp.concatenate([high, low], axis=0),
             NT,
@@ -245,10 +244,15 @@
         )
         total = jnp.broadcast_to(square[0:1] + square[1:2], square.shape)
         big = total.astype(jnp.bfloat16).astype(jnp.float32)
-        part_ref[group, units:, :] = jnp.concatenate([big, total - big], axis=0)
-    for low_z in range(2):
-        keep_ref[low_z] = part_ref[low_z * 2 + core_ref[0]]
-        send_ref[low_z] = part_ref[low_z * 2 + 1 - core_ref[0]].astype(jnp.bfloat16)
+        extra = jnp.concatenate([big, total - big], axis=0)
+        low_z = jnp.right_shift(group_ref[k], 1)
+        stays = jnp.bitwise_and(group_ref[k], 1) == core_ref[0]
+        for ref, mine in ((keep_ref, stays), (send_ref, jnp.logical_not(stays))):
+
+            @pl.when(mine)
+            def _():
+                ref[low_z, :units, :] = part.astype(ref.dtype)
+                ref[low_z, units:, :] = extra.astype(ref.dtype)
 
 
 def pair_kernel(low_ref, keep_ref, got_ref, next_keep_ref, next_send_ref):
@@ -275,35 +279,47 @@
 
 
 def hessian_kernel(from_ref, group_ref, place_ref, near_ref, far_ref, *refs):
-    upper, lower, out_ref, left_ref, right_ref = refs[:5], refs[5:10], *refs[10:]
+    upper, lower, out_hbm = refs[:5], refs[5:10], refs[10]
+    left_ref, right_ref, result_ref, sems = refs[11:]
     units = near_ref.shape[1]
     half = units // 2
-    z = pl.program_id(0)
+    wide = 4 * units
 
     def lanes(group):
         return pl.ds(pl.multiple_of(group * LANES, LANES), LANES)
 
-    def piece(blocks, large, small):
+    def piece(blocks, large, small, z):
         if large < 3:
             return blocks[large][small, z]
         return blocks[3 + small // 2][small % 2, z]
 
-    @pl.when(z == 0)
-    def _():
-        place = place_ref[0]
-        for k in range(2):
-            left_ref[:, lanes(jnp.bitwise_xor(place, k))] = near_ref[k]
-            left_ref[:, lanes(jnp.bitwise_xor(place, 2 + k))] = far_ref[k]
-
-    for r in range(4):
-        base = from_ref[r] * units
-        for k in range(4):
-            group = lanes(group_ref[k])
-            right_ref[pl.ds(pl.multiple_of(base, 16), half), group] = piece(upper, r, k)
-            right_ref[pl.ds(pl.multiple_of(base + half, 16), half), group] = piece(lower, k, r)
-    out_ref[...] = (2.0 / 512) * lax.dot_general(
-        left_ref[...], right_ref[...], NT, preferred_element_type=jnp.float32
-    )
+    place = place_ref[0]
+    for k in range(2):
+        left_ref[:, lanes(jnp.bitwise_xor(place, k))] = near_ref[k]
+        left_ref[:, lanes(jnp.bitwise_xor(place, 2 + k))] = far_ref[k]
+    copies = []
+    for z in range(4):
+        right = right_ref.at[z % 2]
+        for r in range(4):
+            base = from_ref[r] * units
+            for k in range(4):
+                group = lanes(group_ref[k])
+                right[pl.ds(pl.multiple_of(base, 16), half), group] = piece(upper, r, k, z)
+                right[pl.ds(pl.multiple_of(base + half, 16), half), group] = piece(lower, k, r, z)
+        result_ref[z] = (2.0 / 512) * lax.dot_general(
+            left_ref[...], right[...], NT, preferred_element_type=jnp.float32
+        )
+        for part in range(2):
+            rows = slice(part * half, (part + 1) * half)
+            copy = pltpu.make_async_copy(
+                result_ref.at[z, rows, :],
+                out_hbm.at[rows, z * wide : (z + 1) * wide],
+                sems.at[z * 2 + part],
+            )
+            copy.start()
+            copies.append(copy)
+    for copy in copies:
+        copy.wait()
 
 
 def body(attn_out, residual, output_weight, prune_mask, inverse_factor, norm_gain, gate_up_weight):
@@ -367,7 +383,6 @@
         ),
         in_specs=[SMEM] * 2 + [VMEM] * 9,
         out_specs=[VMEM] * 2,
-        scratch_shapes=[pltpu.VMEM((4, *sums[1:]), jnp.float32)],
         name="gate_up",
         compiler_params=params(14),
         cost_estimate=pl.CostEstimate(
@@ -418,13 +433,14 @@
     far = lax.ppermute(near, "z_low", [(0, 1), (1, 0)])
     hessian = pl.pallas_call(
         hessian_kernel,
-        grid=(4,),
         out_shape=jax.ShapeDtypeStruct((units, 16 * units), jnp.float32),
         in_specs=[SMEM] * 3 + [VMEM] * 12,
-        out_specs=pl.BlockSpec((units, 4 * units), lambda z: (0, z)),
+        out_specs=pl.BlockSpec(memory_space=pltpu.HBM),
         scratch_shapes=[
             pltpu.VMEM((units, 4 * LANES), jnp.bfloat16),
-            pltpu.VMEM((4 * units, 4 * LANES), jnp.bfloat16),
+            pltpu.VMEM((2, 4 * units, 4 * LANES), jnp.bfloat16),
+            pltpu.VMEM((4, units, 4 * units), jnp.float32),
+            pltpu.SemaphoreType.DMA((8,)),
         ],
         name="hessian",
         compiler_params=params(14),

time: 177 us -> 179 us (1.011)
    pallas_call x1, Pallas kernels: 3.17 us -> 5.44 us  [body(): pl.pallas_call(gate_up_kernel, out_shape=(jax.ShapeDtypeStruct(sums, jnp....]
where the time goes in v7:
time: 179 us; the launch traced here: 176 us
  starting transfers between devices  82.3 us (46%)
  waiting for transfers between devices  37.9 us (21%)
  blocking collectives  31.9 us (18%)
  Pallas kernels  18.2 us (10%)
  local copies, waits for them, and re-layouts  4 us (2%)
    all_to_all x2, blocking collectives, copy_for_each(): lax.all_to_all(jnp.broadcast_to(x[None], (size, *x.shape)), axis, 0, 0, t...  24.6 us
    ppermute x21, starting transfers between devices, round_trip(): lax.ppermute(x, axis, [(k, (k + step) % 4) for k in range(4)])  24.1 us
    ppermute x21, waiting for transfers between devices, round_trip(): lax.ppermute(x, axis, [(k, (k + step) % 4) for k in range(4)])  21 us
    ppermute x3, starting transfers between devices, turned(): return lax.ppermute(x, (*DP, 'y'), pairs)  12.4 us
    ppermute x1, starting transfers between devices, body(): got = lax.ppermute(send, 'core', [(0, 1), (1, 0)])  9.78 us
    all_to_all x1, starting transfers between devices, copy_for_each(): lax.all_to_all(jnp.broadcast_to(x[None], (size, *x.shape)), axis, 0, 0, t...  9 us
    all_to_all x1, starting transfers between devices, body(): parts = lax.all_to_all(parts, 'y', 0, 0, tiled=True)  7.46 us
    all_gather x1, blocking collectives, body(): errors = lax.all_gather(solved, DP)  7.28 us
  transfers between devices with their start and end apart: 42, of which 22 were waited for; matrix products, arithmetic and copies ran while one was open for 0% of the time, Pallas kernels for 4%

profile of v7, /device:TPU:1, one launch (start us, length us, event | category | flops | bytes accessed | tf_op | source)
XLA Modules:
  0.0 175.7 jit_solution(15205587748028105473)
XLA Ops:
  0.7 1.6 broadcast_in_dim.17
  2.3 9.0 %all-to-all-start = ((bf16[8,128,128]{2,1,0:T(8,128)(2,1)}), bf16[8,128,128]{2,1,0:T(8,128)(2,1)S(1)}, u32[]{:S(2)}, u32[]{:S(2)}) async-start(bf16[8,128,128]{2,1,0:T(8,128)(2,1)} %broadcast_in_dim.17), calls=%async_computation | async-start | bytes 524288 | tf_op jit(solution)/shard_map/all_to_all | solution.py:25
  11.3 3.7 %solve.1 = f32[128,128]{1,0:T(8,128)} custom-call(bf16[128,2048]{1,0:T(8,128)(2,1)} %weight_ref.1, s32[128,128]{1,0:T(8,128)} %mask_ref.1, f32[128,2048]{1,0:T(8,128)} %factor_ref.1), custom_call_target="tpu_custom_call" | custom-call | flops 20000000 | bytes 300000 | tf_op jit(solution)/shard_map/solve/pallas_call | solution.py:122
  15.0 7.3 %all-gather = f32[512,128]{1,0:T(8,128)S(1)} all-gather(f32[128,128]{1,0:T(8,128)} %solve.1), channel_id=2, replica_groups=mesh['z_low'=2,'core'=2,'y'=4,'z_high'=4,'x'=4] {'z_low','core'}, dimensions={0}, use_global_device_ids=true | all-gather | bytes 327680 | tf_op jit(solution)/shard_map/all_gather | solution.py:340
  22.3 1.8 %update.1 = bf16[128,2048]{1,0:T(8,128)(2,1)} custom-call(s32[1]{0:T(128)} %bitcast.place_ref, f32[4,128,128]{2,1,0:T(8,128)S(1)} %bitcast.38, f32[128,2048]{1,0:T(8,128)S(1)} %copy-done, bf16[128,2048]{1,0:T(8,128)(2,1)S(1)} %copy-done.1, s32[128,128]{1,0:T(8,128)S(1)} %copy-done.3), custom_call_target="tpu_custom_call" | custom-call | flops 400000000 | bytes 2200000 | tf_op jit(solution)/shard_map/update/pallas_call | solution.py:154
  24.1 2.7 %collective-permute-start.2 = (bf16[8,128,128]{2,1,0:T(8,128)(2,1)S(1)}, bf16[8,128,128]{2,1,0:T(8,128)(2,1)S(1)}, u32[]{:S(2)}, u32[]{:S(2)}) collective-permute-start(bf16[8,128,128]{2,1,0:T(8,128)(2,1)S(1)} %all-to-all-done.refs_0_), channel_id=1, source_target_pairs={{0,2},{1,3},{2,0},{3,1},{4,6},{5,7},{6,4},{7,5},{8,10},{9,11},{10,... | collective-permute-start | bytes 786440 | tf_op jit(solution)/shard_map/ppermute | solution.py:36
  26.9 3.5 %collective-permute-start.7 = (bf16[128,2048]{1,0:T(8,128)(2,1)}, bf16[128,2048]{1,0:T(8,128)(2,1)S(1)}, u32[]{:S(2)}, u32[]{:S(2)}) collective-permute-start(bf16[128,2048]{1,0:T(8,128)(2,1)} %update.1), channel_id=1, source_target_pairs={{0,0},{16,64},{32,128},{48,192},{64,16},{80,80},{96,144},{112,208}... | collective-permute-start | bytes 1572872 | tf_op jit(solution)/shard_map/ppermute | solution.py:30
  31.9 1.4 collective-permute-done.2.refs_3_
  33.3 1.1 collective-permute-start.6
  34.4 4.6 %collective-permute-done.1.refs_2_ = bf16[8,128,128]{2,1,0:T(8,128)(2,1)S(1)} collective-permute-done((bf16[8,128,128]{2,1,0:T(8,128)(2,1)S(1)}, bf16[8,128,128]{2,1,0:T(8,128)(2,1)S(1)}, u32[]{:S(2)}, u32[]{:S(2)}) %collective-permute-start.1) | collective-permute-done | bytes 262176 | tf_op jit(solution)/shard_map/ppermute | solution.py:36
  39.0 1.0 collective-permute-start.5
  41.6 1.9 %project.1 = bf16[4,128,128]{2,1,0:T(8,128)(2,1)} custom-call(s32[4]{0:T(128)S(1)} %pad_add_fusion.1.from_ref, s32[1]{0:T(128)} %bitcast.7.core_ref, bf16[8,128,128]{2,1,0:T(8,128)(2,1)S(1)} %all-to-all-done.refs_0_, bf16[8,128,128]{2,1,0:T(8,128)(2,1)S(1)} %collective-permute-done.refs_1_, bf16[8,128,128]{2,1,0:T(8,128)(2,1)S(1)} %collective-permute-done.1.refs_2_, ...), custom_call_target="tpu_custom_call" | custom-call | flops 268000000 | bytes 2700000 | tf_op jit(solution)/shard_map/project/pallas_call | solution.py:344
  43.5 7.5 %all-to-all-start.1 = ((bf16[4,128,128]{2,1,0:T(8,128)(2,1)}), bf16[4,128,128]{2,1,0:T(8,128)(2,1)S(1)}, u32[]{:S(2)}, u32[]{:S(2)}) async-start(bf16[4,128,128]{2,1,0:T(8,128)(2,1)} %project.1), calls=%async_computation.1 | async-start | bytes 262144 | tf_op jit(solution)/shard_map/all_to_all | solution.py:353
  51.0 4.8 %collective-permute-start.8 = (bf16[144,128]{1,0:T(8,128)(2,1)S(1)}, bf16[144,128]{1,0:T(8,128)(2,1)S(1)}, u32[]{:S(2)}, u32[]{:S(2)}) collective-permute-start(bf16[144,128]{1,0:T(8,128)(2,1)S(1)} %pad_maximum_fusion.5), channel_id=1, source_target_pairs={{0,0},{16,64},{32,128},{48,192},{64,16},{80,80},{96,144},{112,208}... | collective-permute-start | bytes 110600 | tf_op jit(solution)/shard_map/ppermute | solution.py:30
  55.8 1.9 %collective-permute-done.8.residual_ref = bf16[144,128]{1,0:T(8,128)(2,1)S(1)} collective-permute-done((bf16[144,128]{1,0:T(8,128)(2,1)S(1)}, bf16[144,128]{1,0:T(8,128)(2,1)S(1)}, u32[]{:S(2)}, u32[]{:S(2)}) %collective-permute-start.8) | collective-permute-done | bytes 36896 | tf_op jit(solution)/shard_map/ppermute | solution.py:30
  58.6 13.5 %all_to_all.20 = bf16[4,136,128]{2,1,0:T(8,128)(2,1)S(1)} all-to-all(bf16[4,136,128]{2,1,0:T(8,128)(2,1)S(1)} %broadcast_in_dim.38), channel_id=1, replica_groups=mesh['z_low'=2,'core'=2,'y'=4,'z_high'=4,'x'=4] {'z_high'}, dimensions={0} | all-to-all | bytes 278528 | tf_op jit(solution)/shard_map/all_to_all | solution.py:25
  72.1 3.5 %collective-permute-start.10 = (bf16[4,64,128]{2,1,0:T(8,128)(2,1)S(1)}, bf16[4,64,128]{2,1,0:T(8,128)(2,1)S(1)}, u32[]{:S(2)}, u32[]{:S(2)}) collective-permute-start(bf16[4,64,128]{2,1,0:T(8,128)(2,1)S(1)} %get-tuple-element.26), channel_id=1, source_target_pairs={{0,48},{16,0},{32,16},{48,32},{1,49},{17,1},{33,17},{49,33},{2,50}... | collective-permute-start | bytes 196616 | tf_op jit(solution)/shard_map/ppermute | solution.py:36
  75.6 1.3 collective-permute-start.11
  76.9 3.7 %collective-permute-done.9 = bf16[4,64,128]{2,1,0:T(8,128)(2,1)S(1)} collective-permute-done((bf16[4,64,128]{2,1,0:T(8,128)(2,1)S(1)}, bf16[4,64,128]{2,1,0:T(8,128)(2,1)S(1)}, u32[]{:S(2)}, u32[]{:S(2)}) %collective-permute-start.9) | collective-permute-done | bytes 65568 | tf_op jit(solution)/shard_map/ppermute | solution.py:36
  81.0 2.7 %collective-permute-start.16 = (bf16[4,72,128]{2,1,0:T(8,128)(2,1)S(1)}, bf16[4,72,128]{2,1,0:T(8,128)(2,1)S(1)}, u32[]{:S(2)}, u32[]{:S(2)}) collective-permute-start(bf16[4,72,128]{2,1,0:T(8,128)(2,1)S(1)} %get-tuple-element.24), channel_id=1, source_target_pairs={{0,3},{1,0},{2,1},{3,2},{4,7},{5,4},{6,5},{7,6},{8,11},{9,8},{10,9... | collective-permute-start | bytes 221192 | tf_op jit(solution)/shard_map/ppermute | solution.py:36
  83.8 1.7 collective-permute-start.17
  85.5 1.3 collective-permute-done.16
  86.8 1.5 collective-permute-done.15
  90.1 1.5 collective-permute-start.19
  92.1 2.5 %collective-permute-start.13 = (bf16[4,4,64,128]{3,2,1,0:T(8,128)(2,1)S(1)}, bf16[4,4,64,128]{3,2,1,0:T(8,128)(2,1)}, u32[]{:S(2)}, u32[]{:S(2)}) collective-permute-start(bf16[4,4,64,128]{3,2,1,0:T(8,128)(2,1)S(1)} %pad_maximum_fusion.3.refs_0_), channel_id=1, source_target_pairs={{0,3},{1,0},{2,1},{3,2},{4,7},{5,4},{6,5},{7,6},{8,11},{9,8},{10,9... | collective-permute-start | bytes 786440 | tf_op jit(solution)/shard_map/ppermute | solution.py:36
  94.6 1.5 copy-done.2
  96.1 1.0 order.1.refs_8_
  97.9 3.4 %collective-permute-done.12.refs_1_ = bf16[4,4,64,128]{3,2,1,0:T(8,128)(2,1)} collective-permute-done((bf16[4,4,64,128]{3,2,1,0:T(8,128)(2,1)S(1)}, bf16[4,4,64,128]{3,2,1,0:T(8,128)(2,1)}, u32[]{:S(2)}, u32[]{:S(2)}) %collective-permute-start.12) | collective-permute-done | bytes 262176 | tf_op jit(solution)/shard_map/ppermute | solution.py:36
  101.3 5.4 %gate_up.1 = (f32[2,464,128]{2,1,0:T(8,128)S(1)}, bf16[2,464,128]{2,1,0:T(8,128)(2,1)S(1)}) custom-call(s32[4]{0:T(128)S(1)} %pad_add_fusion.group_ref, s32[1]{0:T(128)} %bitcast.7.core_ref, bf16[4,4,64,128]{3,2,1,0:T(8,128)(2,1)S(1)} %pad_maximum_fusion.3.refs_0_, bf16[4,4,64,128]{3,2,1,0:T(8,128)(2,1)} %collective-permute-done.12.refs_1_, ...), custom_call_target="tpu_custom_call" | custom-call | flops 940000000 | bytes 4300000 | tf_op jit(solution)/shard_map/gate_up/pallas_call | solution.py:378
  106.8 9.8 %collective-permute-start.21 = (bf16[2,464,128]{2,1,0:T(8,128)(2,1)S(1)}, bf16[2,464,128]{2,1,0:T(8,128)(2,1)S(1)}, u32[]{:S(2)}, u32[]{:S(2)}) collective-permute-start(bf16[2,464,128]{2,1,0:T(8,128)(2,1)S(1)} %get-tuple-element.13), channel_id=1, source_target_pairs={{0,64},{64,0},{1,65},{65,1},{2,66},{66,2},{3,67},{67,3},{4,68},{68... | collective-permute-start | bytes 712712 | tf_op jit(solution)/shard_map/ppermute | solution.py:392
  116.6 1.1 collective-permute-done.21.got_ref
  117.8 4.4 %collective-permute-done.22.got_ref = bf16[464,128]{1,0:T(8,128)(2,1)S(1)} collective-permute-done((bf16[464,128]{1,0:T(8,128)(2,1)S(1)}, bf16[464,128]{1,0:T(8,128)(2,1)S(1)}, u32[]{:S(2)}, u32[]{:S(2)}) %collective-permute-start.22) | collective-permute-done | bytes 118816 | tf_op jit(solution)/shard_map/ppermute | solution.py:405
  122.3 4.0 %collective-permute-start.23 = (bf16[352,128]{1,0:T(8,128)(2,1)S(1)}, bf16[352,128]{1,0:T(8,128)(2,1)S(1)}, u32[]{:S(2)}, u32[]{:S(2)}) collective-permute-start(bf16[352,128]{1,0:T(8,128)(2,1)S(1)} %get-tuple-element.17), channel_id=1, source_target_pairs={{0,0},{16,64},{32,128},{48,192},{64,16},{80,80},{96,144},{112,208}... | collective-permute-start | bytes 270344 | tf_op jit(solution)/shard_map/ppermute | solution.py:30
  126.4 3.2 %collective-permute-done.23.in_ref = bf16[352,128]{1,0:T(8,128)(2,1)S(1)} collective-permute-done((bf16[352,128]{1,0:T(8,128)(2,1)S(1)}, bf16[352,128]{1,0:T(8,128)(2,1)S(1)}, u32[]{:S(2)}, u32[]{:S(2)}) %collective-permute-start.23) | collective-permute-done | bytes 90144 | tf_op jit(solution)/shard_map/ppermute | solution.py:30
  129.6 11.1 %all_to_all.21 = bf16[4,224,128]{2,1,0:T(8,128)(2,1)S(1)} all-to-all(bf16[4,224,128]{2,1,0:T(8,128)(2,1)S(1)} %broadcast_in_dim.39), channel_id=1, replica_groups=mesh['z_low'=2,'core'=2,'y'=4,'z_high'=4,'x'=4] {'z_high'}, dimensions={0} | all-to-all | bytes 458752 | tf_op jit(solution)/shard_map/all_to_all | solution.py:25
  140.7 2.0 %collective-permute-start.27 = (bf16[4,112,128]{2,1,0:T(8,128)(2,1)S(1)}, bf16[4,112,128]{2,1,0:T(8,128)(2,1)S(1)}, u32[]{:S(2)}, u32[]{:S(2)}) collective-permute-start(bf16[4,112,128]{2,1,0:T(8,128)(2,1)S(1)} %get-tuple-element.22), channel_id=1, source_target_pairs={{0,48},{16,0},{32,16},{48,32},{1,49},{17,1},{33,17},{49,33},{2,50}... | collective-permute-start | bytes 344072 | tf_op jit(solution)/shard_map/ppermute | solution.py:36
  142.8 1.3 collective-permute-start.28
  144.2 1.3 collective-permute-start.33
  145.5 3.3 %collective-permute-done.26 = bf16[4,112,128]{2,1,0:T(8,128)(2,1)S(1)} collective-permute-done((bf16[4,112,128]{2,1,0:T(8,128)(2,1)S(1)}, bf16[4,112,128]{2,1,0:T(8,128)(2,1)S(1)}, u32[]{:S(2)}, u32[]{:S(2)}) %collective-permute-start.26) | collective-permute-done | bytes 114720 | tf_op jit(solution)/shard_map/ppermute | solution.py:36
  149.2 1.3 collective-permute-start.29
  150.7 3.4 %collective-permute-start.37 = (bf16[4,4,112,128]{3,2,1,0:T(8,128)(2,1)S(1)}, bf16[4,4,112,128]{3,2,1,0:T(8,128)(2,1)S(1)}, u32[]{:S(2)}, u32[]{:S(2)}) collective-permute-start(bf16[4,4,112,128]{3,2,1,0:T(8,128)(2,1)S(1)} %pad_maximum_fusion.1.refs_5_), channel_id=1, source_target_pairs={{0,48},{16,0},{32,16},{48,32},{1,49},{17,1},{33,17},{49,33},{2,50}... | collective-permute-start | bytes 1376264 | tf_op jit(solution)/shard_map/ppermute | solution.py:44
  154.2 6.5 %collective-permute-start.24 = (bf16[224,128]{1,0:T(8,128)(2,1)S(1)}, bf16[224,128]{1,0:T(8,128)(2,1)S(1)}, u32[]{:S(2)}, u32[]{:S(2)}) collective-permute-start(bf16[224,128]{1,0:T(8,128)(2,1)S(1)} %get-tuple-element.18), channel_id=1, source_target_pairs={{0,64},{64,0},{1,65},{65,1},{2,66},{66,2},{3,67},{67,3},{4,68},{68... | collective-permute-start | bytes 172040 | tf_op jit(solution)/shard_map/ppermute | solution.py:431
  161.1 1.2 collective-permute-start.32
  162.9 2.3 %collective-permute-start.39 = (bf16[2,4,112,128]{3,2,1,0:T(8,128)(2,1)S(1)}, bf16[2,4,112,128]{3,2,1,0:T(8,128)(2,1)S(1)}, u32[]{:S(2)}, u32[]{:S(2)}) collective-permute-start(bf16[2,4,112,128]{3,2,1,0:T(8,128)(2,1)S(1)} %slice.44), channel_id=1, source_target_pairs={{0,48},{16,0},{32,16},{48,32},{1,49},{17,1},{33,17},{49,33},{2,50}... | collective-permute-start | bytes 688136 | tf_op jit(solution)/shard_map/ppermute | solution.py:45
  165.3 2.2 %collective-permute-start.25 = (bf16[2,224,128]{2,1,0:T(8,128)(2,1)S(1)}, bf16[2,224,128]{2,1,0:T(8,128)(2,1)S(1)}, u32[]{:S(2)}, u32[]{:S(2)}) collective-permute-start(bf16[2,224,128]{2,1,0:T(8,128)(2,1)S(1)} %pad_maximum_fusion.4.near_ref), channel_id=1, source_target_pairs={{0,128},{128,0},{1,129},{129,1},{2,130},{130,2},{3,131},{131,3},{4... | collective-permute-start | bytes 344072 | tf_op jit(solution)/shard_map/ppermute | solution.py:433
  168.2 1.9 %collective-permute-done.25.far_ref = bf16[2,224,128]{2,1,0:T(8,128)(2,1)S(1)} collective-permute-done((bf16[2,224,128]{2,1,0:T(8,128)(2,1)S(1)}, bf16[2,224,128]{2,1,0:T(8,128)(2,1)S(1)}, u32[]{:S(2)}, u32[]{:S(2)}) %collective-permute-start.25) | collective-permute-done | bytes 114720 | tf_op jit(solution)/shard_map/ppermute | solution.py:433
  170.1 2.2 %collective-permute-done.38.refs_8_ = bf16[2,4,112,128]{3,2,1,0:T(8,128)(2,1)S(1)} collective-permute-done((bf16[2,4,112,128]{3,2,1,0:T(8,128)(2,1)S(1)}, bf16[2,4,112,128]{3,2,1,0:T(8,128)(2,1)S(1)}, u32[]{:S(2)}, u32[]{:S(2)}) %collective-permute-start.38) | collective-permute-done | bytes 229408 | tf_op jit(solution)/shard_map/ppermute | solution.py:45
  172.2 3.3 %hessian.1 = f32[224,3584]{1,0:T(8,128)} custom-call(s32[4]{0:T(128)S(1)} %pad_add_fusion.1.from_ref, s32[4]{0:T(128)S(1)} %pad_add_fusion.group_ref, s32[1]{0:T(128)} %bitcast.place_ref, bf16[2,224,128]{2,1,0:T(8,128)(2,1)S(1)} %pad_maximum_fusion.4.near_ref, bf16[2,224,128]{2,1,0:T(8,128)(2,1)S(1)} %collective-permute-done.25.far_ref, ...), custom_call_target="tpu_custom_call" | custom-call | flops 822000000 | bytes 7100000 | tf_op jit(solution)/shard_map/hessian/pallas_call | solution.py:434
  (85 shorter events, 10.3 us)
Async XLA Ops:
  0.6 21.7 %copy-start = (f32[128,2048]{1,0:T(8,128)S(1)}, f32[128,2048]{1,0:T(8,128)}, u32[]{:S(2)}) copy-start(f32[128,2048]{1,0:T(8,128)} %factor_ref.1) | copy-start | bytes 3145732
  0.6 21.7 %copy-start.3 = (s32[128,128]{1,0:T(8,128)S(1)}, s32[128,128]{1,0:T(8,128)}, u32[]{:S(2)}) copy-start(s32[128,128]{1,0:T(8,128)} %mask_ref.1) | copy-start | bytes 196612
  0.7 21.6 %copy-start.1 = (bf16[128,2048]{1,0:T(8,128)(2,1)S(1)}, bf16[128,2048]{1,0:T(8,128)(2,1)}, u32[]{:S(2)}) copy-start(bf16[128,2048]{1,0:T(8,128)(2,1)} %weight_ref.1) | copy-start | bytes 1572868
  2.3 21.8 %all-to-all-start = ((bf16[8,128,128]{2,1,0:T(8,128)(2,1)}), bf16[8,128,128]{2,1,0:T(8,128)(2,1)S(1)}, u32[]{:S(2)}, u32[]{:S(2)}) async-start(bf16[8,128,128]{2,1,0:T(8,128)(2,1)} %broadcast_in_dim.17), calls=%async_computation | async-start | bytes 524288 | tf_op jit(solution)/shard_map/all_to_all | solution.py:25
  24.1 26.9 %copy-start.7 = (bf16[128]{0:T(256)(128)(2,1)S(1)}, bf16[128]{0:T(256)(128)(2,1)}, u32[]{:S(2)}) copy-start(bf16[128]{0:T(256)(128)(2,1)} %param.12) | copy-start | bytes 772
  24.1 26.9 %copy-start.6 = (bf16[128,128]{1,0:T(8,128)(2,1)S(1)}, bf16[128,128]{1,0:T(8,128)(2,1)}, u32[]{:S(2)}) copy-start(bf16[128,128]{1,0:T(8,128)(2,1)} %param.8) | copy-start | bytes 98308
  24.1 9.2 %collective-permute-start.2 = (bf16[8,128,128]{2,1,0:T(8,128)(2,1)S(1)}, bf16[8,128,128]{2,1,0:T(8,128)(2,1)S(1)}, u32[]{:S(2)}, u32[]{:S(2)}) collective-permute-start(bf16[8,128,128]{2,1,0:T(8,128)(2,1)S(1)} %all-to-all-done.refs_0_), channel_id=1, source_target_pairs={{0,2},{1,3},{2,0},{3,1},{4,6},{5,7},{6,4},{7,5},{8,10},{9,11},{10,... | collective-permute-start | bytes 786440 | tf_op jit(solution)/shard_map/ppermute | solution.py:36
  26.9 14.1 %collective-permute-start.7 = (bf16[128,2048]{1,0:T(8,128)(2,1)}, bf16[128,2048]{1,0:T(8,128)(2,1)S(1)}, u32[]{:S(2)}, u32[]{:S(2)}) collective-permute-start(bf16[128,2048]{1,0:T(8,128)(2,1)} %update.1), channel_id=1, source_target_pairs={{0,0},{16,64},{32,128},{48,192},{64,16},{80,80},{96,144},{112,208}... | collective-permute-start | bytes 1572872 | tf_op jit(solution)/shard_map/ppermute | solution.py:30
  30.4 8.6 %collective-permute-start.1 = (bf16[8,128,128]{2,1,0:T(8,128)(2,1)S(1)}, bf16[8,128,128]{2,1,0:T(8,128)(2,1)S(1)}, u32[]{:S(2)}, u32[]{:S(2)}) collective-permute-start(bf16[8,128,128]{2,1,0:T(8,128)(2,1)S(1)} %all-to-all-done.refs_0_), channel_id=1, source_target_pairs={{0,3},{1,0},{2,1},{3,2},{4,7},{5,4},{6,5},{7,6},{8,11},{9,8},{10,9... | collective-permute-start | bytes 786440 | tf_op jit(solution)/shard_map/ppermute | solution.py:36
  31.3 8.7 %collective-permute-start = (bf16[8,128,128]{2,1,0:T(8,128)(2,1)S(1)}, bf16[8,128,128]{2,1,0:T(8,128)(2,1)S(1)}, u32[]{:S(2)}, u32[]{:S(2)}) collective-permute-start(bf16[8,128,128]{2,1,0:T(8,128)(2,1)S(1)} %all-to-all-done.refs_0_), channel_id=1, source_target_pairs={{0,1},{1,2},{2,3},{3,0},{4,5},{5,6},{6,7},{7,4},{8,9},{9,10},{10,1... | collective-permute-start | bytes 786440 | tf_op jit(solution)/shard_map/ppermute | solution.py:36
  31.9 9.1 %collective-permute-start.3 = (bf16[8,128,128]{2,1,0:T(8,128)(2,1)S(1)}, bf16[8,128,128]{2,1,0:T(8,128)(2,1)S(1)}, u32[]{:S(2)}, u32[]{:S(2)}) collective-permute-start(bf16[8,128,128]{2,1,0:T(8,128)(2,1)S(1)} %all-to-all-done.refs_0_), channel_id=1, source_target_pairs={{0,64},{64,0},{1,65},{65,1},{2,66},{66,2},{3,67},{67,3},{4,68},{68... | collective-permute-start | bytes 786440 | tf_op jit(solution)/shard_map/ppermute | solution.py:335
  33.3 7.7 %collective-permute-start.6 = (bf16[8,128,128]{2,1,0:T(8,128)(2,1)S(1)}, bf16[8,128,128]{2,1,0:T(8,128)(2,1)S(1)}, u32[]{:S(2)}, u32[]{:S(2)}) collective-permute-start(bf16[8,128,128]{2,1,0:T(8,128)(2,1)S(1)} %collective-permute-done.2.refs_3_), channel_id=1, source_target_pairs={{0,64},{64,0},{1,65},{65,1},{2,66},{66,2},{3,67},{67,3},{4,68},{68... | collective-permute-start | bytes 786440 | tf_op jit(solution)/shard_map/ppermute | solution.py:335
  39.0 2.2 %collective-permute-start.5 = (bf16[8,128,128]{2,1,0:T(8,128)(2,1)S(1)}, bf16[8,128,128]{2,1,0:T(8,128)(2,1)S(1)}, u32[]{:S(2)}, u32[]{:S(2)}) collective-permute-start(bf16[8,128,128]{2,1,0:T(8,128)(2,1)S(1)} %collective-permute-done.1.refs_2_), channel_id=1, source_target_pairs={{0,64},{64,0},{1,65},{65,1},{2,66},{66,2},{3,67},{67,3},{4,68},{68... | collective-permute-start | bytes 786440 | tf_op jit(solution)/shard_map/ppermute | solution.py:335
  40.1 1.5 collective-permute-start.4
  43.5 14.2 %all-to-all-start.1 = ((bf16[4,128,128]{2,1,0:T(8,128)(2,1)}), bf16[4,128,128]{2,1,0:T(8,128)(2,1)S(1)}, u32[]{:S(2)}, u32[]{:S(2)}) async-start(bf16[4,128,128]{2,1,0:T(8,128)(2,1)} %project.1), calls=%async_computation.1 | async-start | bytes 262144 | tf_op jit(solution)/shard_map/all_to_all | solution.py:353
  51.0 6.7 %collective-permute-start.8 = (bf16[144,128]{1,0:T(8,128)(2,1)S(1)}, bf16[144,128]{1,0:T(8,128)(2,1)S(1)}, u32[]{:S(2)}, u32[]{:S(2)}) collective-permute-start(bf16[144,128]{1,0:T(8,128)(2,1)S(1)} %pad_maximum_fusion.5), channel_id=1, source_target_pairs={{0,0},{16,64},{32,128},{48,192},{64,16},{80,80},{96,144},{112,208}... | collective-permute-start | bytes 110600 | tf_op jit(solution)/shard_map/ppermute | solution.py:30
  72.1 4.8 %collective-permute-start.10 = (bf16[4,64,128]{2,1,0:T(8,128)(2,1)S(1)}, bf16[4,64,128]{2,1,0:T(8,128)(2,1)S(1)}, u32[]{:S(2)}, u32[]{:S(2)}) collective-permute-start(bf16[4,64,128]{2,1,0:T(8,128)(2,1)S(1)} %get-tuple-element.26), channel_id=1, source_target_pairs={{0,48},{16,0},{32,16},{48,32},{1,49},{17,1},{33,17},{49,33},{2,50}... | collective-permute-start | bytes 196616 | tf_op jit(solution)/shard_map/ppermute | solution.py:36
  75.6 5.0 %collective-permute-start.9 = (bf16[4,64,128]{2,1,0:T(8,128)(2,1)S(1)}, bf16[4,64,128]{2,1,0:T(8,128)(2,1)S(1)}, u32[]{:S(2)}, u32[]{:S(2)}) collective-permute-start(bf16[4,64,128]{2,1,0:T(8,128)(2,1)S(1)} %get-tuple-element.26), channel_id=1, source_target_pairs={{0,16},{16,32},{32,48},{48,0},{1,17},{17,33},{33,49},{49,1},{2,18}... | collective-permute-start | bytes 196616 | tf_op jit(solution)/shard_map/ppermute | solution.py:36
  75.6 5.0 %collective-permute-start.11 = (bf16[4,64,128]{2,1,0:T(8,128)(2,1)S(1)}, bf16[4,64,128]{2,1,0:T(8,128)(2,1)S(1)}, u32[]{:S(2)}, u32[]{:S(2)}) collective-permute-start(bf16[4,64,128]{2,1,0:T(8,128)(2,1)S(1)} %get-tuple-element.26), channel_id=1, source_target_pairs={{0,32},{16,48},{32,0},{48,16},{1,33},{17,49},{33,1},{49,17},{2,34}... | collective-permute-start | bytes 196616 | tf_op jit(solution)/shard_map/ppermute | solution.py:36
  80.7 13.9 %collective-permute-start.14 = (bf16[4,4,64,128]{3,2,1,0:T(8,128)(2,1)S(1)}, bf16[4,4,64,128]{3,2,1,0:T(8,128)(2,1)S(1)}, u32[]{:S(2)}, u32[]{:S(2)}) collective-permute-start(bf16[4,4,64,128]{3,2,1,0:T(8,128)(2,1)S(1)} %pad_maximum_fusion.3.refs_0_), channel_id=1, source_target_pairs={{0,2},{1,3},{2,0},{3,1},{4,6},{5,7},{6,4},{7,5},{8,10},{9,11},{10,... | collective-permute-start | bytes 786440 | tf_op jit(solution)/shard_map/ppermute | solution.py:36
  81.0 5.7 %collective-permute-start.16 = (bf16[4,72,128]{2,1,0:T(8,128)(2,1)S(1)}, bf16[4,72,128]{2,1,0:T(8,128)(2,1)S(1)}, u32[]{:S(2)}, u32[]{:S(2)}) collective-permute-start(bf16[4,72,128]{2,1,0:T(8,128)(2,1)S(1)} %get-tuple-element.24), channel_id=1, source_target_pairs={{0,3},{1,0},{2,1},{3,2},{4,7},{5,4},{6,5},{7,6},{8,11},{9,8},{10,9... | collective-permute-start | bytes 221192 | tf_op jit(solution)/shard_map/ppermute | solution.py:36
  83.8 4.5 %collective-permute-start.15 = (bf16[4,72,128]{2,1,0:T(8,128)(2,1)S(1)}, bf16[4,72,128]{2,1,0:T(8,128)(2,1)S(1)}, u32[]{:S(2)}, u32[]{:S(2)}) collective-permute-start(bf16[4,72,128]{2,1,0:T(8,128)(2,1)S(1)} %get-tuple-element.24), channel_id=1, source_target_pairs={{0,1},{1,2},{2,3},{3,0},{4,5},{5,6},{6,7},{7,4},{8,9},{9,10},{10,1... | collective-permute-start | bytes 221192 | tf_op jit(solution)/shard_map/ppermute | solution.py:36
  83.8 5.3 %collective-permute-start.17 = (bf16[4,72,128]{2,1,0:T(8,128)(2,1)S(1)}, bf16[4,72,128]{2,1,0:T(8,128)(2,1)S(1)}, u32[]{:S(2)}, u32[]{:S(2)}) collective-permute-start(bf16[4,72,128]{2,1,0:T(8,128)(2,1)S(1)} %get-tuple-element.24), channel_id=1, source_target_pairs={{0,2},{1,3},{2,0},{3,1},{4,6},{5,7},{6,4},{7,5},{8,10},{9,11},{10,... | collective-permute-start | bytes 221192 | tf_op jit(solution)/shard_map/ppermute | solution.py:36
  89.1 12.2 %collective-permute-start.20 = (bf16[4,4,72,128]{3,2,1,0:T(8,128)(2,1)S(1)}, bf16[4,4,72,128]{3,2,1,0:T(8,128)(2,1)S(1)}, u32[]{:S(2)}, u32[]{:S(2)}) collective-permute-start(bf16[4,4,72,128]{3,2,1,0:T(8,128)(2,1)S(1)} %pad_maximum_fusion.2.refs_4_), channel_id=1, source_target_pairs={{0,32},{16,48},{32,0},{48,16},{1,33},{17,49},{33,1},{49,17},{2,34}... | collective-permute-start | bytes 884744 | tf_op jit(solution)/shard_map/ppermute | solution.py:36
  90.1 11.2 %collective-permute-start.19 = (bf16[4,4,72,128]{3,2,1,0:T(8,128)(2,1)S(1)}, bf16[4,4,72,128]{3,2,1,0:T(8,128)(2,1)S(1)}, u32[]{:S(2)}, u32[]{:S(2)}) collective-permute-start(bf16[4,4,72,128]{3,2,1,0:T(8,128)(2,1)S(1)} %pad_maximum_fusion.2.refs_4_), channel_id=1, source_target_pairs={{0,48},{16,0},{32,16},{48,32},{1,49},{17,1},{33,17},{49,33},{2,50}... | collective-permute-start | bytes 884744 | tf_op jit(solution)/shard_map/ppermute | solution.py:36
  91.6 9.8 %collective-permute-start.18 = (bf16[4,4,72,128]{3,2,1,0:T(8,128)(2,1)S(1)}, bf16[4,4,72,128]{3,2,1,0:T(8,128)(2,1)S(1)}, u32[]{:S(2)}, u32[]{:S(2)}) collective-permute-start(bf16[4,4,72,128]{3,2,1,0:T(8,128)(2,1)S(1)} %pad_maximum_fusion.2.refs_4_), channel_id=1, source_target_pairs={{0,16},{16,32},{32,48},{48,0},{1,17},{17,33},{33,49},{49,1},{2,18}... | collective-permute-start | bytes 884744 | tf_op jit(solution)/shard_map/ppermute | solution.py:36
  92.1 5.8 %collective-permute-start.13 = (bf16[4,4,64,128]{3,2,1,0:T(8,128)(2,1)S(1)}, bf16[4,4,64,128]{3,2,1,0:T(8,128)(2,1)}, u32[]{:S(2)}, u32[]{:S(2)}) collective-permute-start(bf16[4,4,64,128]{3,2,1,0:T(8,128)(2,1)S(1)} %pad_maximum_fusion.3.refs_0_), channel_id=1, source_target_pairs={{0,3},{1,0},{2,1},{3,2},{4,7},{5,4},{6,5},{7,6},{8,11},{9,8},{10,9... | collective-permute-start | bytes 786440 | tf_op jit(solution)/shard_map/ppermute | solution.py:36
  94.6 6.7 %collective-permute-start.12 = (bf16[4,4,64,128]{3,2,1,0:T(8,128)(2,1)S(1)}, bf16[4,4,64,128]{3,2,1,0:T(8,128)(2,1)}, u32[]{:S(2)}, u32[]{:S(2)}) collective-permute-start(bf16[4,4,64,128]{3,2,1,0:T(8,128)(2,1)S(1)} %pad_maximum_fusion.3.refs_0_), channel_id=1, source_target_pairs={{0,1},{1,2},{2,3},{3,0},{4,5},{5,6},{6,7},{7,4},{8,9},{9,10},{10,1... | collective-permute-start | bytes 786440 | tf_op jit(solution)/shard_map/ppermute | solution.py:36
  97.2 25.0 %copy-start.5 = (bf16[128,128]{1,0:T(8,128)(2,1)S(1)}, bf16[128,128]{1,0:T(8,128)(2,1)}, u32[]{:S(2)}) copy-start(bf16[128,128]{1,0:T(8,128)(2,1)} %copy-done.4) | copy-start | bytes 98308
  106.8 10.9 %collective-permute-start.21 = (bf16[2,464,128]{2,1,0:T(8,128)(2,1)S(1)}, bf16[2,464,128]{2,1,0:T(8,128)(2,1)S(1)}, u32[]{:S(2)}, u32[]{:S(2)}) collective-permute-start(bf16[2,464,128]{2,1,0:T(8,128)(2,1)S(1)} %get-tuple-element.13), channel_id=1, source_target_pairs={{0,64},{64,0},{1,65},{65,1},{2,66},{66,2},{3,67},{67,3},{4,68},{68... | collective-permute-start | bytes 712712 | tf_op jit(solution)/shard_map/ppermute | solution.py:392
  117.7 4.5 %collective-permute-start.22 = (bf16[464,128]{1,0:T(8,128)(2,1)S(1)}, bf16[464,128]{1,0:T(8,128)(2,1)S(1)}, u32[]{:S(2)}, u32[]{:S(2)}) collective-permute-start(bf16[464,128]{1,0:T(8,128)(2,1)S(1)} %get-tuple-element.15), channel_id=1, source_target_pairs={{0,128},{128,0},{1,129},{129,1},{2,130},{130,2},{3,131},{131,3},{4... | collective-permute-start | bytes 356360 | tf_op jit(solution)/shard_map/ppermute | solution.py:405
  122.3 7.2 %collective-permute-start.23 = (bf16[352,128]{1,0:T(8,128)(2,1)S(1)}, bf16[352,128]{1,0:T(8,128)(2,1)S(1)}, u32[]{:S(2)}, u32[]{:S(2)}) collective-permute-start(bf16[352,128]{1,0:T(8,128)(2,1)S(1)} %get-tuple-element.17), channel_id=1, source_target_pairs={{0,0},{16,64},{32,128},{48,192},{64,16},{80,80},{96,144},{112,208}... | collective-permute-start | bytes 270344 | tf_op jit(solution)/shard_map/ppermute | solution.py:30
  140.7 4.8 %collective-permute-start.27 = (bf16[4,112,128]{2,1,0:T(8,128)(2,1)S(1)}, bf16[4,112,128]{2,1,0:T(8,128)(2,1)S(1)}, u32[]{:S(2)}, u32[]{:S(2)}) collective-permute-start(bf16[4,112,128]{2,1,0:T(8,128)(2,1)S(1)} %get-tuple-element.22), channel_id=1, source_target_pairs={{0,48},{16,0},{32,16},{48,32},{1,49},{17,1},{33,17},{49,33},{2,50}... | collective-permute-start | bytes 344072 | tf_op jit(solution)/shard_map/ppermute | solution.py:36
  142.8 6.1 %collective-permute-start.26 = (bf16[4,112,128]{2,1,0:T(8,128)(2,1)S(1)}, bf16[4,112,128]{2,1,0:T(8,128)(2,1)S(1)}, u32[]{:S(2)}, u32[]{:S(2)}) collective-permute-start(bf16[4,112,128]{2,1,0:T(8,128)(2,1)S(1)} %get-tuple-element.22), channel_id=1, source_target_pairs={{0,16},{16,32},{32,48},{48,0},{1,17},{17,33},{33,49},{49,1},{2,18}... | collective-permute-start | bytes 344072 | tf_op jit(solution)/shard_map/ppermute | solution.py:36
  142.8 6.1 %collective-permute-start.28 = (bf16[4,112,128]{2,1,0:T(8,128)(2,1)S(1)}, bf16[4,112,128]{2,1,0:T(8,128)(2,1)S(1)}, u32[]{:S(2)}, u32[]{:S(2)}) collective-permute-start(bf16[4,112,128]{2,1,0:T(8,128)(2,1)S(1)} %get-tuple-element.22), channel_id=1, source_target_pairs={{0,32},{16,48},{32,0},{48,16},{1,33},{17,49},{33,1},{49,17},{2,34}... | collective-permute-start | bytes 344072 | tf_op jit(solution)/shard_map/ppermute | solution.py:36
  144.0 6.4 %collective-permute-start.34 = (bf16[4,112,128]{2,1,0:T(8,128)(2,1)S(1)}, bf16[4,112,128]{2,1,0:T(8,128)(2,1)S(1)}, u32[]{:S(2)}, u32[]{:S(2)}) collective-permute-start(bf16[4,112,128]{2,1,0:T(8,128)(2,1)S(1)} %get-tuple-element.21), channel_id=1, source_target_pairs={{0,3},{1,0},{2,1},{3,2},{4,7},{5,4},{6,5},{7,6},{8,11},{9,8},{10,9... | collective-permute-start | bytes 344072 | tf_op jit(solution)/shard_map/ppermute | solution.py:36
  144.2 6.2 %collective-permute-start.33 = (bf16[4,112,128]{2,1,0:T(8,128)(2,1)S(1)}, bf16[4,112,128]{2,1,0:T(8,128)(2,1)S(1)}, u32[]{:S(2)}, u32[]{:S(2)}) collective-permute-start(bf16[4,112,128]{2,1,0:T(8,128)(2,1)S(1)} %get-tuple-element.21), channel_id=1, source_target_pairs={{0,1},{1,2},{2,3},{3,0},{4,5},{5,6},{6,7},{7,4},{8,9},{9,10},{10,1... | collective-permute-start | bytes 344072 | tf_op jit(solution)/shard_map/ppermute | solution.py:36
  145.5 5.1 %collective-permute-start.35 = (bf16[4,112,128]{2,1,0:T(8,128)(2,1)S(1)}, bf16[4,112,128]{2,1,0:T(8,128)(2,1)S(1)}, u32[]{:S(2)}, u32[]{:S(2)}) collective-permute-start(bf16[4,112,128]{2,1,0:T(8,128)(2,1)S(1)} %get-tuple-element.21), channel_id=1, source_target_pairs={{0,2},{1,3},{2,0},{3,1},{4,6},{5,7},{6,4},{7,5},{8,10},{9,11},{10,... | collective-permute-start | bytes 344072 | tf_op jit(solution)/shard_map/ppermute | solution.py:36
  148.9 12.2 %collective-permute-start.30 = (bf16[4,4,112,128]{3,2,1,0:T(8,128)(2,1)S(1)}, bf16[4,4,112,128]{3,2,1,0:T(8,128)(2,1)S(1)}, u32[]{:S(2)}, u32[]{:S(2)}) collective-permute-start(bf16[4,4,112,128]{3,2,1,0:T(8,128)(2,1)S(1)} %pad_maximum_fusion.refs_0_), channel_id=1, source_target_pairs={{0,3},{1,0},{2,1},{3,2},{4,7},{5,4},{6,5},{7,6},{8,11},{9,8},{10,9... | collective-permute-start | bytes 1376264 | tf_op jit(solution)/shard_map/ppermute | solution.py:44
  149.2 13.6 %collective-permute-start.29 = (bf16[4,4,112,128]{3,2,1,0:T(8,128)(2,1)S(1)}, bf16[4,4,112,128]{3,2,1,0:T(8,128)(2,1)S(1)}, u32[]{:S(2)}, u32[]{:S(2)}) collective-permute-start(bf16[4,4,112,128]{3,2,1,0:T(8,128)(2,1)S(1)} %pad_maximum_fusion.refs_0_), channel_id=1, source_target_pairs={{0,1},{1,2},{2,3},{3,0},{4,5},{5,6},{6,7},{7,4},{8,9},{9,10},{10,1... | collective-permute-start | bytes 1376264 | tf_op jit(solution)/shard_map/ppermute | solution.py:44
  150.7 12.1 %collective-permute-start.37 = (bf16[4,4,112,128]{3,2,1,0:T(8,128)(2,1)S(1)}, bf16[4,4,112,128]{3,2,1,0:T(8,128)(2,1)S(1)}, u32[]{:S(2)}, u32[]{:S(2)}) collective-permute-start(bf16[4,4,112,128]{3,2,1,0:T(8,128)(2,1)S(1)} %pad_maximum_fusion.1.refs_5_), channel_id=1, source_target_pairs={{0,48},{16,0},{32,16},{48,32},{1,49},{17,1},{33,17},{49,33},{2,50}... | collective-permute-start | bytes 1376264 | tf_op jit(solution)/shard_map/ppermute | solution.py:44
  154.1 11.0 %collective-permute-start.36 = (bf16[4,4,112,128]{3,2,1,0:T(8,128)(2,1)S(1)}, bf16[4,4,112,128]{3,2,1,0:T(8,128)(2,1)S(1)}, u32[]{:S(2)}, u32[]{:S(2)}) collective-permute-start(bf16[4,4,112,128]{3,2,1,0:T(8,128)(2,1)S(1)} %pad_maximum_fusion.1.refs_5_), channel_id=1, source_target_pairs={{0,16},{16,32},{32,48},{48,0},{1,17},{17,33},{33,49},{49,1},{2,18}... | collective-permute-start | bytes 1376264 | tf_op jit(solution)/shard_map/ppermute | solution.py:44
  154.2 11.2 %collective-permute-start.24 = (bf16[224,128]{1,0:T(8,128)(2,1)S(1)}, bf16[224,128]{1,0:T(8,128)(2,1)S(1)}, u32[]{:S(2)}, u32[]{:S(2)}) collective-permute-start(bf16[224,128]{1,0:T(8,128)(2,1)S(1)} %get-tuple-element.18), channel_id=1, source_target_pairs={{0,64},{64,0},{1,65},{65,1},{2,66},{66,2},{3,67},{67,3},{4,68},{68... | collective-permute-start | bytes 172040 | tf_op jit(solution)/shard_map/ppermute | solution.py:431
  161.1 8.9 %collective-permute-start.32 = (bf16[2,4,112,128]{3,2,1,0:T(8,128)(2,1)S(1)}, bf16[2,4,112,128]{3,2,1,0:T(8,128)(2,1)S(1)}, u32[]{:S(2)}, u32[]{:S(2)}) collective-permute-start(bf16[2,4,112,128]{3,2,1,0:T(8,128)(2,1)S(1)} %slice.41), channel_id=1, source_target_pairs={{0,3},{1,0},{2,1},{3,2},{4,7},{5,4},{6,5},{7,6},{8,11},{9,8},{10,9... | collective-permute-start | bytes 688136 | tf_op jit(solution)/shard_map/ppermute | solution.py:45
  162.8 7.3 %collective-permute-start.31 = (bf16[2,4,112,128]{3,2,1,0:T(8,128)(2,1)S(1)}, bf16[2,4,112,128]{3,2,1,0:T(8,128)(2,1)S(1)}, u32[]{:S(2)}, u32[]{:S(2)}) collective-permute-start(bf16[2,4,112,128]{3,2,1,0:T(8,128)(2,1)S(1)} %slice.40), channel_id=1, source_target_pairs={{0,1},{1,2},{2,3},{3,0},{4,5},{5,6},{6,7},{7,4},{8,9},{9,10},{10,1... | collective-permute-start | bytes 688136 | tf_op jit(solution)/shard_map/ppermute | solution.py:45
  162.9 7.1 %collective-permute-start.39 = (bf16[2,4,112,128]{3,2,1,0:T(8,128)(2,1)S(1)}, bf16[2,4,112,128]{3,2,1,0:T(8,128)(2,1)S(1)}, u32[]{:S(2)}, u32[]{:S(2)}) collective-permute-start(bf16[2,4,112,128]{3,2,1,0:T(8,128)(2,1)S(1)} %slice.44), channel_id=1, source_target_pairs={{0,48},{16,0},{32,16},{48,32},{1,49},{17,1},{33,17},{49,33},{2,50}... | collective-permute-start | bytes 688136 | tf_op jit(solution)/shard_map/ppermute | solution.py:45
  165.2 7.0 %collective-permute-start.38 = (bf16[2,4,112,128]{3,2,1,0:T(8,128)(2,1)S(1)}, bf16[2,4,112,128]{3,2,1,0:T(8,128)(2,1)S(1)}, u32[]{:S(2)}, u32[]{:S(2)}) collective-permute-start(bf16[2,4,112,128]{3,2,1,0:T(8,128)(2,1)S(1)} %slice.43), channel_id=1, source_target_pairs={{0,16},{16,32},{32,48},{48,0},{1,17},{17,33},{33,49},{49,1},{2,18}... | collective-permute-start | bytes 688136 | tf_op jit(solution)/shard_map/ppermute | solution.py:45
  165.3 4.7 %collective-permute-start.25 = (bf16[2,224,128]{2,1,0:T(8,128)(2,1)S(1)}, bf16[2,224,128]{2,1,0:T(8,128)(2,1)S(1)}, u32[]{:S(2)}, u32[]{:S(2)}) collective-permute-start(bf16[2,224,128]{2,1,0:T(8,128)(2,1)S(1)} %pad_maximum_fusion.4.near_ref), channel_id=1, source_target_pairs={{0,128},{128,0},{1,129},{129,1},{2,130},{130,2},{3,131},{131,3},{4... | collective-permute-start | bytes 344072 | tf_op jit(solution)/shard_map/ppermute | solution.py:433
  (2 other events, 2.1 us)

commit v8 on v7

--- a/solution.py
+++ b/solution.py
@@ -55,7 +55,10 @@
 
 
 def over_z(x):
-    return copy_for_each(x, "z_high")
+    pair = jnp.stack([x, lax.ppermute(x, "z_high", [(k, k ^ 1) for k in range(4)])])
+    return jnp.concatenate(
+        [pair, lax.ppermute(pair, "z_high", [(k, k ^ 2) for k in range(4)])]
+    )
 
 
 def senders(axis):
@@ -173,15 +176,20 @@
     return ref[:, pl.ds(pl.multiple_of(block * LANES, LANES), LANES)]
 
 
-def ordered_columns(ref, from_ref):
+def ordered_columns(ref, from_ref, z_here):
     return jnp.concatenate(
-        [columns_at(ref, z * 4 + from_ref[r]) for r in range(4) for z in range(4)], axis=1
+        [
+            columns_at(ref, jnp.bitwise_xor(z_here, z) * 4 + from_ref[r])
+            for r in range(4)
+            for z in range(4)
+        ],
+        axis=1,
     )
 
 
 def project_kernel(from_ref, core_ref, *refs):
     mine, other, weight_ref, out_ref = refs[:4], refs[4:8], refs[8], refs[9]
-    weight = ordered_columns(weight_ref, from_ref)
+    weight = ordered_columns(weight_ref, from_ref, 0)
     for low in range(2):
         for source, core in ((mine, core_ref[0]), (other, 1 - core_ref[0])):
             tokens = jnp.concatenate(
@@ -219,13 +227,13 @@
     out_ref[...] = in_ref[in_ref.shape[0] - rows :]
 
 
-def order_kernel(from_ref, weight_ref, out_ref):
-    out_ref[...] = ordered_columns(weight_ref, from_ref)
+def order_kernel(from_ref, high_ref, weight_ref, out_ref):
+    out_ref[...] = ordered_columns(weight_ref, from_ref, high_ref[0])
 
 
 def gate_up_kernel(group_ref, core_ref, *refs):
     upper, lower, weight_ref = refs[:4], refs[4:8], refs[8]
-    keep_ref, send_ref = refs[9:]
+    keep_ref, send_ref, part_ref = refs[9:]
     half = upper[0].shape[2]
     weight = weight_ref[...]
     units = weight.shape[0]
@@ -236,7 +244,8 @@
         square = jnp.zeros((8, LANES), jnp.float32)
         for r, z in places:
             square = square + lower[k][r, z, half:].astype(jnp.float32)
-        part = lax.dot_general(
+        group = group_ref[k]
+        part_ref[group, :units, :] = lax.dot_general(
             weight,
             jnp.concatenate([high, low], axis=0),
             NT,
@@ -244,15 +253,10 @@
         )
         total = jnp.broadcast_to(square[0:1] + square[1:2], square.shape)
         big = total.astype(jnp.bfloat16).astype(jnp.float32)
-        extra = jnp.concatenate([big, total - big], axis=0)
-        low_z = jnp.right_shift(group_ref[k], 1)
-        stays = jnp.bitwise_and(group_ref[k], 1) == core_ref[0]
-        for ref, mine in ((keep_ref, stays), (send_ref, jnp.logical_not(stays))):
-
-            @pl.when(mine)
-            def _():
-                ref[low_z, :units, :] = part.astype(ref.dtype)
-                ref[low_z, units:, :] = extra.astype(ref.dtype)
+        part_ref[group, units:, :] = jnp.concatenate([big, total - big], axis=0)
+    for low_z in range(2):
+        keep_ref[low_z] = part_ref[low_z * 2 + core_ref[0]]
+        send_ref[low_z] = part_ref[low_z * 2 + 1 - core_ref[0]].astype(jnp.bfloat16)
 
 
 def pair_kernel(low_ref, keep_ref, got_ref, next_keep_ref, next_send_ref):
@@ -278,7 +282,7 @@
     both_ref[units:] = stream_ref[...]
 
 
-def hessian_kernel(from_ref, group_ref, place_ref, near_ref, far_ref, *refs):
+def hessian_kernel(from_ref, group_ref, high_ref, place_ref, near_ref, far_ref, *refs):
     upper, lower, out_hbm = refs[:5], refs[5:10], refs[10]
     left_ref, right_ref, result_ref, sems = refs[11:]
     units = near_ref.shape[1]
@@ -297,8 +301,18 @@
     for k in range(2):
         left_ref[:, lanes(jnp.bitwise_xor(place, k))] = near_ref[k]
         left_ref[:, lanes(jnp.bitwise_xor(place, 2 + k))] = far_ref[k]
-    copies = []
-    for z in range(4):
+
+    def written(z, part):
+        rows = pl.ds(part * half, half)
+        base = pl.multiple_of(jnp.bitwise_xor(high_ref[0], z) * wide, LANES)
+        return pltpu.make_async_copy(
+            result_ref.at[z, rows, :],
+            out_hbm.at[rows, pl.ds(base, wide)],
+            sems.at[z * 2 + part],
+        )
+
+    @pl.loop(0, 4)
+    def _(z):
         right = right_ref.at[z % 2]
         for r in range(4):
             base = from_ref[r] * units
@@ -310,16 +324,11 @@
             left_ref[...], right[...], NT, preferred_element_type=jnp.float32
         )
         for part in range(2):
-            rows = slice(part * half, (part + 1) * half)
-            copy = pltpu.make_async_copy(
-                result_ref.at[z, rows, :],
-                out_hbm.at[rows, z * wide : (z + 1) * wide],
-                sems.at[z * 2 + part],
-            )
-            copy.start()
-            copies.append(copy)
-    for copy in copies:
-        copy.wait()
+            written(z, part).start()
+
+    for z in range(4):
+        for part in range(2):
+            written(z, part).wait()
 
 
 def body(attn_out, residual, output_weight, prune_mask, inverse_factor, norm_gain, gate_up_weight):
@@ -329,6 +338,7 @@
     groups = senders("y")
     core = lax.axis_index("core").astype(jnp.int32)[None]
     low_z = lax.axis_index("z_low").astype(jnp.int32)[None]
+    high_z = lax.axis_index("z_high").astype(jnp.int32)[None]
 
     mine = copy_for_each(attn_out, ("z_high", "z_low"))
     mine = round_trip(mine, "x")
@@ -367,12 +377,12 @@
     flat_weight = pl.pallas_call(
         order_kernel,
         out_shape=jax.ShapeDtypeStruct(flat_weight.shape, jnp.bfloat16),
-        in_specs=[SMEM, VMEM],
+        in_specs=[SMEM, SMEM, VMEM],
         out_specs=VMEM,
         name="order",
         compiler_params=params(8),
         cost_estimate=pl.CostEstimate(flops=0, bytes_accessed=3_700_000, transcendentals=0),
-    )(order, flat_weight)
+    )(order, high_z, flat_weight)
     upper, lower = over_y_and_x(over_z(block), 64)
     sums = (2, 2 * units + 16, 128)
     keep, send = pl.pallas_call(
@@ -383,6 +393,7 @@
         ),
         in_specs=[SMEM] * 2 + [VMEM] * 9,
         out_specs=[VMEM] * 2,
+        scratch_shapes=[pltpu.VMEM((4, *sums[1:]), jnp.float32)],
         name="gate_up",
         compiler_params=params(14),
         cost_estimate=pl.CostEstimate(
@@ -434,7 +445,7 @@
     hessian = pl.pallas_call(
         hessian_kernel,
         out_shape=jax.ShapeDtypeStruct((units, 16 * units), jnp.float32),
-        in_specs=[SMEM] * 3 + [VMEM] * 12,
+        in_specs=[SMEM] * 4 + [VMEM] * 12,
         out_specs=pl.BlockSpec(memory_space=pltpu.HBM),
         scratch_shapes=[
             pltpu.VMEM((units, 4 * LANES), jnp.bfloat16),
@@ -445,7 +456,7 @@
         name="hessian",
         compiler_params=params(14),
         cost_estimate=pl.CostEstimate(flops=822_000_000, bytes_accessed=7_100_000, transcendentals=0),
-    )(order, groups, place, near, far, *upper, *lower)
+    )(order, groups, high_z, place, near, far, *upper, *lower)
     return (pruned_weight, stream, hessian)
 
 

time: 179 us -> 177 us (0.989)
  the two profiles are of different devices: /device:TPU:1 before, /device:TPU:2 now
where the time goes in v8:
time: 177 us
  starting transfers between devices  96.1 us (54%)
  waiting for transfers between devices  53.7 us (30%)
  Pallas kernels  16.6 us (9%)
  blocking collectives  6.49 us (4%)
  local copies, waits for them, and re-layouts  2.43 us (1%)
    ppermute x21, starting transfers between devices, round_trip(): lax.ppermute(x, axis, [(k, (k + step) % 4) for k in range(4)])  45.3 us
    ppermute x21, waiting for transfers between devices, round_trip(): lax.ppermute(x, axis, [(k, (k + step) % 4) for k in range(4)])  18.5 us
    ppermute x2, starting transfers between devices, over_z(): lax.ppermute(pair, 'z_high', [(k, k ^ 2) for k in range(4)])  11.1 us
    all_to_all x1, starting transfers between devices, copy_for_each(): lax.all_to_all(jnp.broadcast_to(x[None], (size, *x.shape)), axis, 0, 0, t...  8.47 us
    all_to_all x1, starting transfers between devices, body(): parts = lax.all_to_all(parts, 'y', 0, 0, tiled=True)  7.8 us
    ppermute x2, waiting for transfers between devices, over_z(): lax.ppermute(pair, 'z_high', [(k, k ^ 2) for k in range(4)])  6.91 us
    all_gather x1, blocking collectives, body(): errors = lax.all_gather(solved, DP)  6.49 us
    ppermute x2, starting transfers between devices, over_z(): lax.ppermute(x, 'z_high', [(k, k ^ 1) for k in range(4)])  6.28 us
  transfers between devices with their start and end apart: 46, of which 23 were waited for; matrix products, arithmetic and copies ran while one was open for 0% of the time, Pallas kernels for 4%

profile of v8, /device:TPU:2, one launch (start us, length us, event | category | flops | bytes accessed | tf_op | source)
XLA Modules:
  0.0 176.9 jit_solution(10975982926313165118)
XLA Ops:
  0.7 1.6 broadcast_in_dim.27
  2.3 8.5 %all-to-all-start = ((bf16[8,128,128]{2,1,0:T(8,128)(2,1)}), bf16[8,128,128]{2,1,0:T(8,128)(2,1)S(1)}, u32[]{:S(2)}, u32[]{:S(2)}) async-start(bf16[8,128,128]{2,1,0:T(8,128)(2,1)} %broadcast_in_dim.27), calls=%async_computation | async-start | bytes 524288 | tf_op jit(solution)/shard_map/all_to_all | solution.py:25
  10.7 3.7 %solve.1 = f32[128,128]{1,0:T(8,128)} custom-call(bf16[128,2048]{1,0:T(8,128)(2,1)} %weight_ref.1, s32[128,128]{1,0:T(8,128)} %mask_ref.1, f32[128,2048]{1,0:T(8,128)} %factor_ref.1), custom_call_target="tpu_custom_call" | custom-call | flops 20000000 | bytes 300000 | tf_op jit(solution)/shard_map/solve/pallas_call | solution.py:125
  14.5 6.5 %all-gather = f32[512,128]{1,0:T(8,128)S(1)} all-gather(f32[128,128]{1,0:T(8,128)} %solve.1), channel_id=2, replica_groups=mesh['z_low'=2,'core'=2,'y'=4,'z_high'=4,'x'=4] {'z_low','core'}, dimensions={0}, use_global_device_ids=true | all-gather | bytes 327680 | tf_op jit(solution)/shard_map/all_gather | solution.py:350
  21.0 1.8 %update.1 = bf16[128,2048]{1,0:T(8,128)(2,1)} custom-call(s32[1]{0:T(128)} %bitcast.place_ref, f32[4,128,128]{2,1,0:T(8,128)S(1)} %bitcast.44, f32[128,2048]{1,0:T(8,128)S(1)} %copy-done, bf16[128,2048]{1,0:T(8,128)(2,1)S(1)} %copy-done.1, s32[128,128]{1,0:T(8,128)S(1)} %copy-done.3), custom_call_target="tpu_custom_call" | custom-call | flops 400000000 | bytes 2200000 | tf_op jit(solution)/shard_map/update/pallas_call | solution.py:157
  22.8 2.1 %collective-permute-start.2 = (bf16[8,128,128]{2,1,0:T(8,128)(2,1)S(1)}, bf16[8,128,128]{2,1,0:T(8,128)(2,1)S(1)}, u32[]{:S(2)}, u32[]{:S(2)}) collective-permute-start(bf16[8,128,128]{2,1,0:T(8,128)(2,1)S(1)} %all-to-all-done.refs_0_), channel_id=1, source_target_pairs={{0,2},{1,3},{2,0},{3,1},{4,6},{5,7},{6,4},{7,5},{8,10},{9,11},{10,... | collective-permute-start | bytes 786440 | tf_op jit(solution)/shard_map/ppermute | solution.py:36
  24.9 1.7 collective-permute-start.7
  26.6 1.4 collective-permute-start.1
  28.6 1.4 collective-permute-start.3
  30.0 3.5 %collective-permute-done.2.refs_3_ = bf16[8,128,128]{2,1,0:T(8,128)(2,1)S(1)} collective-permute-done((bf16[8,128,128]{2,1,0:T(8,128)(2,1)S(1)}, bf16[8,128,128]{2,1,0:T(8,128)(2,1)S(1)}, u32[]{:S(2)}, u32[]{:S(2)}) %collective-permute-start.2) | collective-permute-done | bytes 262176 | tf_op jit(solution)/shard_map/ppermute | solution.py:36
  33.5 4.9 %collective-permute-done.1.refs_2_ = bf16[8,128,128]{2,1,0:T(8,128)(2,1)S(1)} collective-permute-done((bf16[8,128,128]{2,1,0:T(8,128)(2,1)S(1)}, bf16[8,128,128]{2,1,0:T(8,128)(2,1)S(1)}, u32[]{:S(2)}, u32[]{:S(2)}) %collective-permute-start.1) | collective-permute-done | bytes 262176 | tf_op jit(solution)/shard_map/ppermute | solution.py:36
  40.3 1.9 %project.1 = bf16[4,128,128]{2,1,0:T(8,128)(2,1)} custom-call(s32[4]{0:T(128)S(1)} %pad_add_fusion.1.from_ref, s32[1]{0:T(128)} %bitcast.7.core_ref, bf16[8,128,128]{2,1,0:T(8,128)(2,1)S(1)} %all-to-all-done.refs_0_, bf16[8,128,128]{2,1,0:T(8,128)(2,1)S(1)} %collective-permute-done.refs_1_, bf16[8,128,128]{2,1,0:T(8,128)(2,1)S(1)} %collective-permute-done.1.refs_2_, ...), custom_call_target="tpu_custom_call" | custom-call | flops 268000000 | bytes 2700000 | tf_op jit(solution)/shard_map/project/pallas_call | solution.py:354
  42.2 7.8 %all-to-all-start.1 = ((bf16[4,128,128]{2,1,0:T(8,128)(2,1)}), bf16[4,128,128]{2,1,0:T(8,128)(2,1)S(1)}, u32[]{:S(2)}, u32[]{:S(2)}) async-start(bf16[4,128,128]{2,1,0:T(8,128)(2,1)} %project.1), calls=%async_computation.1 | async-start | bytes 262144 | tf_op jit(solution)/shard_map/all_to_all | solution.py:363
  50.7 5.3 %all-to-all-done.1.parts_ref = bf16[4,128,128]{2,1,0:T(8,128)(2,1)S(1)} async-done(((bf16[4,128,128]{2,1,0:T(8,128)(2,1)}), bf16[4,128,128]{2,1,0:T(8,128)(2,1)S(1)}, u32[]{:S(2)}, u32[]{:S(2)}) %all-to-all-start.1) | async-done | bytes 131104 | tf_op jit(solution)/shard_map/all_to_all | solution.py:363
  56.8 3.4 %collective-permute-start.9 = (bf16[136,128]{1,0:T(8,128)(2,1)S(1)}, bf16[136,128]{1,0:T(8,128)(2,1)S(1)}, u32[]{:S(2)}, u32[]{:S(2)}) collective-permute-start(bf16[136,128]{1,0:T(8,128)(2,1)S(1)} %get-tuple-element.11), channel_id=1, source_target_pairs={{0,4},{4,0},{8,12},{12,8},{1,5},{5,1},{9,13},{13,9},{2,6},{6,2},{1... | collective-permute-start | bytes 104456 | tf_op jit(solution)/shard_map/ppermute | solution.py:58
  60.2 1.9 %collective-permute-done.9 = bf16[136,128]{1,0:T(8,128)(2,1)S(1)} collective-permute-done((bf16[136,128]{1,0:T(8,128)(2,1)S(1)}, bf16[136,128]{1,0:T(8,128)(2,1)S(1)}, u32[]{:S(2)}, u32[]{:S(2)}) %collective-permute-start.9) | collective-permute-done | bytes 34848 | tf_op jit(solution)/shard_map/ppermute | solution.py:58
  62.2 5.0 %collective-permute-start.10 = (bf16[2,136,128]{2,1,0:T(8,128)(2,1)S(1)}, bf16[2,136,128]{2,1,0:T(8,128)(2,1)S(1)}, u32[]{:S(2)}, u32[]{:S(2)}) collective-permute-start(bf16[2,136,128]{2,1,0:T(8,128)(2,1)S(1)} %pad_maximum_fusion.9), channel_id=1, source_target_pairs={{0,8},{4,12},{8,0},{12,4},{1,9},{5,13},{9,1},{13,5},{2,10},{6,14},... | collective-permute-start | bytes 208904 | tf_op jit(solution)/shard_map/ppermute | solution.py:60
  67.2 4.0 %collective-permute-done.10 = bf16[2,136,128]{2,1,0:T(8,128)(2,1)S(1)} collective-permute-done((bf16[2,136,128]{2,1,0:T(8,128)(2,1)S(1)}, bf16[2,136,128]{2,1,0:T(8,128)(2,1)S(1)}, u32[]{:S(2)}, u32[]{:S(2)}) %collective-permute-start.10) | collective-permute-done | bytes 69664 | tf_op jit(solution)/shard_map/ppermute | solution.py:60
  71.2 5.0 %collective-permute-start.12 = (bf16[4,64,128]{2,1,0:T(8,128)(2,1)S(1)}, bf16[4,64,128]{2,1,0:T(8,128)(2,1)S(1)}, u32[]{:S(2)}, u32[]{:S(2)}) collective-permute-start(bf16[4,64,128]{2,1,0:T(8,128)(2,1)S(1)} %pad_maximum_fusion.10), channel_id=1, source_target_pairs={{0,48},{16,0},{32,16},{48,32},{1,49},{17,1},{33,17},{49,33},{2,50}... | collective-permute-start | bytes 196616 | tf_op jit(solution)/shard_map/ppermute | solution.py:36
  76.3 2.4 %collective-permute-start.13 = (bf16[4,64,128]{2,1,0:T(8,128)(2,1)S(1)}, bf16[4,64,128]{2,1,0:T(8,128)(2,1)S(1)}, u32[]{:S(2)}, u32[]{:S(2)}) collective-permute-start(bf16[4,64,128]{2,1,0:T(8,128)(2,1)S(1)} %pad_maximum_fusion.10), channel_id=1, source_target_pairs={{0,32},{16,48},{32,0},{48,16},{1,33},{17,49},{33,1},{49,17},{2,34}... | collective-permute-start | bytes 196616 | tf_op jit(solution)/shard_map/ppermute | solution.py:36
  78.7 2.0 %collective-permute-start.18 = (bf16[4,72,128]{2,1,0:T(8,128)(2,1)S(1)}, bf16[4,72,128]{2,1,0:T(8,128)(2,1)S(1)}, u32[]{:S(2)}, u32[]{:S(2)}) collective-permute-start(bf16[4,72,128]{2,1,0:T(8,128)(2,1)S(1)} %pad_maximum_fusion.7), channel_id=1, source_target_pairs={{0,3},{1,0},{2,1},{3,2},{4,7},{5,4},{6,5},{7,6},{8,11},{9,8},{10,9... | collective-permute-start | bytes 221192 | tf_op jit(solution)/shard_map/ppermute | solution.py:36
  80.8 1.6 collective-permute-start.19
  82.5 2.0 %collective-permute-start.16 = (bf16[4,4,64,128]{3,2,1,0:T(8,128)(2,1)S(1)}, bf16[4,4,64,128]{3,2,1,0:T(8,128)(2,1)S(1)}, u32[]{:S(2)}, u32[]{:S(2)}) collective-permute-start(bf16[4,4,64,128]{3,2,1,0:T(8,128)(2,1)S(1)} %pad_maximum_fusion.3.refs_0_), channel_id=1, source_target_pairs={{0,2},{1,3},{2,0},{3,1},{4,6},{5,7},{6,4},{7,5},{8,10},{9,11},{10,... | collective-permute-start | bytes 786440 | tf_op jit(solution)/shard_map/ppermute | solution.py:36
  84.8 1.9 %collective-permute-done.19 = bf16[4,72,128]{2,1,0:T(8,128)(2,1)S(1)} collective-permute-done((bf16[4,72,128]{2,1,0:T(8,128)(2,1)S(1)}, bf16[4,72,128]{2,1,0:T(8,128)(2,1)S(1)}, u32[]{:S(2)}, u32[]{:S(2)}) %collective-permute-start.19) | collective-permute-done | bytes 73760 | tf_op jit(solution)/shard_map/ppermute | solution.py:36
  86.7 1.2 collective-permute-start.22
  87.9 4.0 %collective-permute-start.21 = (bf16[4,4,72,128]{3,2,1,0:T(8,128)(2,1)S(1)}, bf16[4,4,72,128]{3,2,1,0:T(8,128)(2,1)S(1)}, u32[]{:S(2)}, u32[]{:S(2)}) collective-permute-start(bf16[4,4,72,128]{3,2,1,0:T(8,128)(2,1)S(1)} %pad_maximum_fusion.2.refs_4_), channel_id=1, source_target_pairs={{0,48},{16,0},{32,16},{48,32},{1,49},{17,1},{33,17},{49,33},{2,50}... | collective-permute-start | bytes 884744 | tf_op jit(solution)/shard_map/ppermute | solution.py:36
  93.1 2.4 %collective-permute-start.14 = (bf16[4,4,64,128]{3,2,1,0:T(8,128)(2,1)S(1)}, bf16[4,4,64,128]{3,2,1,0:T(8,128)(2,1)}, u32[]{:S(2)}, u32[]{:S(2)}) collective-permute-start(bf16[4,4,64,128]{3,2,1,0:T(8,128)(2,1)S(1)} %pad_maximum_fusion.3.refs_0_), channel_id=1, source_target_pairs={{0,1},{1,2},{2,3},{3,0},{4,5},{5,6},{6,7},{7,4},{8,9},{9,10},{10,1... | collective-permute-start | bytes 786440 | tf_op jit(solution)/shard_map/ppermute | solution.py:36
  96.6 1.8 %collective-permute-done.15.refs_2_ = bf16[4,4,64,128]{3,2,1,0:T(8,128)(2,1)} collective-permute-done((bf16[4,4,64,128]{3,2,1,0:T(8,128)(2,1)S(1)}, bf16[4,4,64,128]{3,2,1,0:T(8,128)(2,1)}, u32[]{:S(2)}, u32[]{:S(2)}) %collective-permute-start.15) | collective-permute-done | bytes 262176 | tf_op jit(solution)/shard_map/ppermute | solution.py:36
  99.9 3.2 %gate_up.1 = (f32[2,464,128]{2,1,0:T(8,128)S(1)}, bf16[2,464,128]{2,1,0:T(8,128)(2,1)S(1)}) custom-call(s32[4]{0:T(128)S(1)} %pad_add_fusion.group_ref, s32[1]{0:T(128)} %bitcast.7.core_ref, bf16[4,4,64,128]{3,2,1,0:T(8,128)(2,1)S(1)} %pad_maximum_fusion.3.refs_0_, bf16[4,4,64,128]{3,2,1,0:T(8,128)(2,1)} %collective-permute-done.14.refs_1_, ...), custom_call_target="tpu_custom_call" | custom-call | flops 940000000 | bytes 4300000 | tf_op jit(solution)/shard_map/gate_up/pallas_call | solution.py:388
  103.1 1.5 collective-permute-done.23.got_ref
  104.8 5.3 %collective-permute-done.24.got_ref = bf16[464,128]{1,0:T(8,128)(2,1)S(1)} collective-permute-done((bf16[464,128]{1,0:T(8,128)(2,1)S(1)}, bf16[464,128]{1,0:T(8,128)(2,1)S(1)}, u32[]{:S(2)}, u32[]{:S(2)}) %collective-permute-start.24) | collective-permute-done | bytes 118816 | tf_op jit(solution)/shard_map/ppermute | solution.py:416
  110.8 2.9 %collective-permute-start.28 = (bf16[224,128]{1,0:T(8,128)(2,1)S(1)}, bf16[224,128]{1,0:T(8,128)(2,1)S(1)}, u32[]{:S(2)}, u32[]{:S(2)}) collective-permute-start(bf16[224,128]{1,0:T(8,128)(2,1)S(1)} %get-tuple-element.24), channel_id=1, source_target_pairs={{0,4},{4,0},{8,12},{12,8},{1,5},{5,1},{9,13},{13,9},{2,6},{6,2},{1... | collective-permute-start | bytes 172040 | tf_op jit(solution)/shard_map/ppermute | solution.py:58
  113.7 2.3 %collective-permute-done.28 = bf16[224,128]{1,0:T(8,128)(2,1)S(1)} collective-permute-done((bf16[224,128]{1,0:T(8,128)(2,1)S(1)}, bf16[224,128]{1,0:T(8,128)(2,1)S(1)}, u32[]{:S(2)}, u32[]{:S(2)}) %collective-permute-start.28) | collective-permute-done | bytes 57376 | tf_op jit(solution)/shard_map/ppermute | solution.py:58
  116.0 6.1 %collective-permute-start.29 = (bf16[2,224,128]{2,1,0:T(8,128)(2,1)S(1)}, bf16[2,224,128]{2,1,0:T(8,128)(2,1)S(1)}, u32[]{:S(2)}, u32[]{:S(2)}) collective-permute-start(bf16[2,224,128]{2,1,0:T(8,128)(2,1)S(1)} %pad_maximum_fusion.6), channel_id=1, source_target_pairs={{0,8},{4,12},{8,0},{12,4},{1,9},{5,13},{9,1},{13,5},{2,10},{6,14},... | collective-permute-start | bytes 344072 | tf_op jit(solution)/shard_map/ppermute | solution.py:60
  122.1 2.9 %collective-permute-done.29 = bf16[2,224,128]{2,1,0:T(8,128)(2,1)S(1)} collective-permute-done((bf16[2,224,128]{2,1,0:T(8,128)(2,1)S(1)}, bf16[2,224,128]{2,1,0:T(8,128)(2,1)S(1)}, u32[]{:S(2)}, u32[]{:S(2)}) %collective-permute-start.29) | collective-permute-done | bytes 114720 | tf_op jit(solution)/shard_map/ppermute | solution.py:60
  125.1 15.0 %collective-permute-start.31 = (bf16[4,112,128]{2,1,0:T(8,128)(2,1)S(1)}, bf16[4,112,128]{2,1,0:T(8,128)(2,1)S(1)}, u32[]{:S(2)}, u32[]{:S(2)}) collective-permute-start(bf16[4,112,128]{2,1,0:T(8,128)(2,1)S(1)} %get-tuple-element.22), channel_id=1, source_target_pairs={{0,48},{16,0},{32,16},{48,32},{1,49},{17,1},{33,17},{49,33},{2,50}... | collective-permute-start | bytes 344072 | tf_op jit(solution)/shard_map/ppermute | solution.py:36
  140.1 1.6 collective-permute-start.32
  142.4 1.4 collective-permute-start.37
  144.4 3.2 %collective-permute-done.30 = bf16[4,112,128]{2,1,0:T(8,128)(2,1)S(1)} collective-permute-done((bf16[4,112,128]{2,1,0:T(8,128)(2,1)S(1)}, bf16[4,112,128]{2,1,0:T(8,128)(2,1)S(1)}, u32[]{:S(2)}, u32[]{:S(2)}) %collective-permute-start.30) | collective-permute-done | bytes 114720 | tf_op jit(solution)/shard_map/ppermute | solution.py:36
  147.8 2.0 %collective-permute-start.33 = (bf16[4,4,112,128]{3,2,1,0:T(8,128)(2,1)S(1)}, bf16[4,4,112,128]{3,2,1,0:T(8,128)(2,1)S(1)}, u32[]{:S(2)}, u32[]{:S(2)}) collective-permute-start(bf16[4,4,112,128]{3,2,1,0:T(8,128)(2,1)S(1)} %pad_maximum_fusion.refs_0_), channel_id=1, source_target_pairs={{0,1},{1,2},{2,3},{3,0},{4,5},{5,6},{6,7},{7,4},{8,9},{9,10},{10,1... | collective-permute-start | bytes 1376264 | tf_op jit(solution)/shard_map/ppermute | solution.py:44
  149.9 1.4 collective-permute-done.39
  151.3 3.7 %collective-permute-start.41 = (bf16[4,4,112,128]{3,2,1,0:T(8,128)(2,1)S(1)}, bf16[4,4,112,128]{3,2,1,0:T(8,128)(2,1)S(1)}, u32[]{:S(2)}, u32[]{:S(2)}) collective-permute-start(bf16[4,4,112,128]{3,2,1,0:T(8,128)(2,1)S(1)} %pad_maximum_fusion.1.refs_5_), channel_id=1, source_target_pairs={{0,48},{16,0},{32,16},{48,32},{1,49},{17,1},{33,17},{49,33},{2,50}... | collective-permute-start | bytes 1376264 | tf_op jit(solution)/shard_map/ppermute | solution.py:44
  155.1 4.1 %collective-permute-done.34.refs_2_ = bf16[4,4,112,128]{3,2,1,0:T(8,128)(2,1)S(1)} collective-permute-done((bf16[4,4,112,128]{3,2,1,0:T(8,128)(2,1)S(1)}, bf16[4,4,112,128]{3,2,1,0:T(8,128)(2,1)S(1)}, u32[]{:S(2)}, u32[]{:S(2)}) %collective-permute-start.34) | collective-permute-done | bytes 458784 | tf_op jit(solution)/shard_map/ppermute | solution.py:44
  159.3 2.1 %collective-permute-start.35 = (bf16[2,4,112,128]{3,2,1,0:T(8,128)(2,1)S(1)}, bf16[2,4,112,128]{3,2,1,0:T(8,128)(2,1)S(1)}, u32[]{:S(2)}, u32[]{:S(2)}) collective-permute-start(bf16[2,4,112,128]{3,2,1,0:T(8,128)(2,1)S(1)} %slice.38), channel_id=1, source_target_pairs={{0,1},{1,2},{2,3},{3,0},{4,5},{5,6},{6,7},{7,4},{8,9},{9,10},{10,1... | collective-permute-start | bytes 688136 | tf_op jit(solution)/shard_map/ppermute | solution.py:45
  161.4 3.8 %collective-permute-start.43 = (bf16[2,4,112,128]{3,2,1,0:T(8,128)(2,1)S(1)}, bf16[2,4,112,128]{3,2,1,0:T(8,128)(2,1)S(1)}, u32[]{:S(2)}, u32[]{:S(2)}) collective-permute-start(bf16[2,4,112,128]{3,2,1,0:T(8,128)(2,1)S(1)} %slice.42), channel_id=1, source_target_pairs={{0,48},{16,0},{32,16},{48,32},{1,49},{17,1},{33,17},{49,33},{2,50}... | collective-permute-start | bytes 688136 | tf_op jit(solution)/shard_map/ppermute | solution.py:45
  166.1 4.2 %collective-permute-done.27.far_ref = bf16[2,224,128]{2,1,0:T(8,128)(2,1)S(1)} collective-permute-done((bf16[2,224,128]{2,1,0:T(8,128)(2,1)S(1)}, bf16[2,224,128]{2,1,0:T(8,128)(2,1)S(1)}, u32[]{:S(2)}, u32[]{:S(2)}) %collective-permute-start.27) | collective-permute-done | bytes 114720 | tf_op jit(solution)/shard_map/ppermute | solution.py:444
  170.3 2.3 %collective-permute-done.42.refs_8_ = bf16[2,4,112,128]{3,2,1,0:T(8,128)(2,1)S(1)} collective-permute-done((bf16[2,4,112,128]{3,2,1,0:T(8,128)(2,1)S(1)}, bf16[2,4,112,128]{3,2,1,0:T(8,128)(2,1)S(1)}, u32[]{:S(2)}, u32[]{:S(2)}) %collective-permute-start.42) | collective-permute-done | bytes 229408 | tf_op jit(solution)/shard_map/ppermute | solution.py:45
  172.6 4.1 %hessian.1 = f32[224,3584]{1,0:T(8,128)} custom-call(s32[4]{0:T(128)S(1)} %pad_add_fusion.1.from_ref, s32[4]{0:T(128)S(1)} %pad_add_fusion.group_ref, s32[1]{0:T(128)} %bitcast.22.high_ref, s32[1]{0:T(128)} %bitcast.place_ref, bf16[2,224,128]{2,1,0:T(8,128)(2,1)S(1)} %pad_maximum_fusion.5.near_ref, bf16[2,224,128]{2,1,0:T(8,128)(2,1)S(1)} %collective-permute-done.27.far_ref, ...), custom_call_target="tpu_custom_call" | custom-call | flops 822000000 | bytes 7100000 | tf_op jit(solution)/shard_map/hessian/pallas_call | solution.py:445
  (94 shorter events, 12.0 us)
Async XLA Ops:
  2.3 20.5 %all-to-all-start = ((bf16[8,128,128]{2,1,0:T(8,128)(2,1)}), bf16[8,128,128]{2,1,0:T(8,128)(2,1)S(1)}, u32[]{:S(2)}, u32[]{:S(2)}) async-start(bf16[8,128,128]{2,1,0:T(8,128)(2,1)} %broadcast_in_dim.27), calls=%async_computation | async-start | bytes 524288 | tf_op jit(solution)/shard_map/all_to_all | solution.py:25
  22.8 27.2 %copy-start.6 = (bf16[128,128]{1,0:T(8,128)(2,1)S(1)}, bf16[128,128]{1,0:T(8,128)(2,1)}, u32[]{:S(2)}) copy-start(bf16[128,128]{1,0:T(8,128)(2,1)} %param.8) | copy-start | bytes 98308
  22.8 10.7 %collective-permute-start.2 = (bf16[8,128,128]{2,1,0:T(8,128)(2,1)S(1)}, bf16[8,128,128]{2,1,0:T(8,128)(2,1)S(1)}, u32[]{:S(2)}, u32[]{:S(2)}) collective-permute-start(bf16[8,128,128]{2,1,0:T(8,128)(2,1)S(1)} %all-to-all-done.refs_0_), channel_id=1, source_target_pairs={{0,2},{1,3},{2,0},{3,1},{4,6},{5,7},{6,4},{7,5},{8,10},{9,11},{10,... | collective-permute-start | bytes 786440 | tf_op jit(solution)/shard_map/ppermute | solution.py:36
  24.9 14.1 %collective-permute-start.7 = (bf16[128,2048]{1,0:T(8,128)(2,1)}, bf16[128,2048]{1,0:T(8,128)(2,1)S(1)}, u32[]{:S(2)}, u32[]{:S(2)}) collective-permute-start(bf16[128,2048]{1,0:T(8,128)(2,1)} %update.1), channel_id=1, source_target_pairs={{0,0},{16,64},{32,128},{48,192},{64,16},{80,80},{96,144},{112,208}... | collective-permute-start | bytes 1572872 | tf_op jit(solution)/shard_map/ppermute | solution.py:30
  26.6 11.8 %collective-permute-start.1 = (bf16[8,128,128]{2,1,0:T(8,128)(2,1)S(1)}, bf16[8,128,128]{2,1,0:T(8,128)(2,1)S(1)}, u32[]{:S(2)}, u32[]{:S(2)}) collective-permute-start(bf16[8,128,128]{2,1,0:T(8,128)(2,1)S(1)} %all-to-all-done.refs_0_), channel_id=1, source_target_pairs={{0,3},{1,0},{2,1},{3,2},{4,7},{5,4},{6,5},{7,6},{8,11},{9,8},{10,9... | collective-permute-start | bytes 786440 | tf_op jit(solution)/shard_map/ppermute | solution.py:36
  28.0 10.5 %collective-permute-start = (bf16[8,128,128]{2,1,0:T(8,128)(2,1)S(1)}, bf16[8,128,128]{2,1,0:T(8,128)(2,1)S(1)}, u32[]{:S(2)}, u32[]{:S(2)}) collective-permute-start(bf16[8,128,128]{2,1,0:T(8,128)(2,1)S(1)} %all-to-all-done.refs_0_), channel_id=1, source_target_pairs={{0,1},{1,2},{2,3},{3,0},{4,5},{5,6},{6,7},{7,4},{8,9},{9,10},{10,1... | collective-permute-start | bytes 786440 | tf_op jit(solution)/shard_map/ppermute | solution.py:36
  28.6 10.3 %collective-permute-start.3 = (bf16[8,128,128]{2,1,0:T(8,128)(2,1)S(1)}, bf16[8,128,128]{2,1,0:T(8,128)(2,1)S(1)}, u32[]{:S(2)}, u32[]{:S(2)}) collective-permute-start(bf16[8,128,128]{2,1,0:T(8,128)(2,1)S(1)} %all-to-all-done.refs_0_), channel_id=1, source_target_pairs={{0,64},{64,0},{1,65},{65,1},{2,66},{66,2},{3,67},{67,3},{4,68},{68... | collective-permute-start | bytes 786440 | tf_op jit(solution)/shard_map/ppermute | solution.py:345
  33.5 5.5 %collective-permute-start.6 = (bf16[8,128,128]{2,1,0:T(8,128)(2,1)S(1)}, bf16[8,128,128]{2,1,0:T(8,128)(2,1)S(1)}, u32[]{:S(2)}, u32[]{:S(2)}) collective-permute-start(bf16[8,128,128]{2,1,0:T(8,128)(2,1)S(1)} %collective-permute-done.2.refs_3_), channel_id=1, source_target_pairs={{0,64},{64,0},{1,65},{65,1},{2,66},{66,2},{3,67},{67,3},{4,68},{68... | collective-permute-start | bytes 786440 | tf_op jit(solution)/shard_map/ppermute | solution.py:345
  38.4 1.5 collective-permute-start.5
  38.6 1.7 collective-permute-start.4
  42.2 53.3 %copy-start.2 = (bf16[2048,2,224]{0,2,1:T(8,128)(2,1)S(1)}, bf16[2048,2,224]{0,2,1:T(8,128)(2,1)}, u32[]{:S(2)}) copy-start(bf16[2048,2,224]{0,2,1:T(8,128)(2,1)} %param.13) | copy-start | bytes 5505028
  42.2 13.8 %all-to-all-start.1 = ((bf16[4,128,128]{2,1,0:T(8,128)(2,1)}), bf16[4,128,128]{2,1,0:T(8,128)(2,1)S(1)}, u32[]{:S(2)}, u32[]{:S(2)}) async-start(bf16[4,128,128]{2,1,0:T(8,128)(2,1)} %project.1), calls=%async_computation.1 | async-start | bytes 262144 | tf_op jit(solution)/shard_map/all_to_all | solution.py:363
  50.0 0.7 collective-permute-start.8
  56.8 5.3 %collective-permute-start.9 = (bf16[136,128]{1,0:T(8,128)(2,1)S(1)}, bf16[136,128]{1,0:T(8,128)(2,1)S(1)}, u32[]{:S(2)}, u32[]{:S(2)}) collective-permute-start(bf16[136,128]{1,0:T(8,128)(2,1)S(1)} %get-tuple-element.11), channel_id=1, source_target_pairs={{0,4},{4,0},{8,12},{12,8},{1,5},{5,1},{9,13},{13,9},{2,6},{6,2},{1... | collective-permute-start | bytes 104456 | tf_op jit(solution)/shard_map/ppermute | solution.py:58
  62.2 9.1 %collective-permute-start.10 = (bf16[2,136,128]{2,1,0:T(8,128)(2,1)S(1)}, bf16[2,136,128]{2,1,0:T(8,128)(2,1)S(1)}, u32[]{:S(2)}, u32[]{:S(2)}) collective-permute-start(bf16[2,136,128]{2,1,0:T(8,128)(2,1)S(1)} %pad_maximum_fusion.9), channel_id=1, source_target_pairs={{0,8},{4,12},{8,0},{12,4},{1,9},{5,13},{9,1},{13,5},{2,10},{6,14},... | collective-permute-start | bytes 208904 | tf_op jit(solution)/shard_map/ppermute | solution.py:60
  71.2 9.5 %collective-permute-start.12 = (bf16[4,64,128]{2,1,0:T(8,128)(2,1)S(1)}, bf16[4,64,128]{2,1,0:T(8,128)(2,1)S(1)}, u32[]{:S(2)}, u32[]{:S(2)}) collective-permute-start(bf16[4,64,128]{2,1,0:T(8,128)(2,1)S(1)} %pad_maximum_fusion.10), channel_id=1, source_target_pairs={{0,48},{16,0},{32,16},{48,32},{1,49},{17,1},{33,17},{49,33},{2,50}... | collective-permute-start | bytes 196616 | tf_op jit(solution)/shard_map/ppermute | solution.py:36
  76.3 6.2 %collective-permute-start.11 = (bf16[4,64,128]{2,1,0:T(8,128)(2,1)S(1)}, bf16[4,64,128]{2,1,0:T(8,128)(2,1)S(1)}, u32[]{:S(2)}, u32[]{:S(2)}) collective-permute-start(bf16[4,64,128]{2,1,0:T(8,128)(2,1)S(1)} %pad_maximum_fusion.10), channel_id=1, source_target_pairs={{0,16},{16,32},{32,48},{48,0},{1,17},{17,33},{33,49},{49,1},{2,18}... | collective-permute-start | bytes 196616 | tf_op jit(solution)/shard_map/ppermute | solution.py:36
  76.3 6.2 %collective-permute-start.13 = (bf16[4,64,128]{2,1,0:T(8,128)(2,1)S(1)}, bf16[4,64,128]{2,1,0:T(8,128)(2,1)S(1)}, u32[]{:S(2)}, u32[]{:S(2)}) collective-permute-start(bf16[4,64,128]{2,1,0:T(8,128)(2,1)S(1)} %pad_maximum_fusion.10), channel_id=1, source_target_pairs={{0,32},{16,48},{32,0},{48,16},{1,33},{17,49},{33,1},{49,17},{2,34}... | collective-permute-start | bytes 196616 | tf_op jit(solution)/shard_map/ppermute | solution.py:36
  78.7 5.8 %collective-permute-start.17 = (bf16[4,72,128]{2,1,0:T(8,128)(2,1)S(1)}, bf16[4,72,128]{2,1,0:T(8,128)(2,1)S(1)}, u32[]{:S(2)}, u32[]{:S(2)}) collective-permute-start(bf16[4,72,128]{2,1,0:T(8,128)(2,1)S(1)} %pad_maximum_fusion.7), channel_id=1, source_target_pairs={{0,1},{1,2},{2,3},{3,0},{4,5},{5,6},{6,7},{7,4},{8,9},{9,10},{10,1... | collective-permute-start | bytes 221192 | tf_op jit(solution)/shard_map/ppermute | solution.py:36
  78.7 6.1 %collective-permute-start.18 = (bf16[4,72,128]{2,1,0:T(8,128)(2,1)S(1)}, bf16[4,72,128]{2,1,0:T(8,128)(2,1)S(1)}, u32[]{:S(2)}, u32[]{:S(2)}) collective-permute-start(bf16[4,72,128]{2,1,0:T(8,128)(2,1)S(1)} %pad_maximum_fusion.7), channel_id=1, source_target_pairs={{0,3},{1,0},{2,1},{3,2},{4,7},{5,4},{6,5},{7,6},{8,11},{9,8},{10,9... | collective-permute-start | bytes 221192 | tf_op jit(solution)/shard_map/ppermute | solution.py:36
  80.8 5.9 %collective-permute-start.19 = (bf16[4,72,128]{2,1,0:T(8,128)(2,1)S(1)}, bf16[4,72,128]{2,1,0:T(8,128)(2,1)S(1)}, u32[]{:S(2)}, u32[]{:S(2)}) collective-permute-start(bf16[4,72,128]{2,1,0:T(8,128)(2,1)S(1)} %pad_maximum_fusion.7), channel_id=1, source_target_pairs={{0,2},{1,3},{2,0},{3,1},{4,6},{5,7},{6,4},{7,5},{8,10},{9,11},{10,... | collective-permute-start | bytes 221192 | tf_op jit(solution)/shard_map/ppermute | solution.py:36
  82.5 10.6 %collective-permute-start.16 = (bf16[4,4,64,128]{3,2,1,0:T(8,128)(2,1)S(1)}, bf16[4,4,64,128]{3,2,1,0:T(8,128)(2,1)S(1)}, u32[]{:S(2)}, u32[]{:S(2)}) collective-permute-start(bf16[4,4,64,128]{3,2,1,0:T(8,128)(2,1)S(1)} %pad_maximum_fusion.3.refs_0_), channel_id=1, source_target_pairs={{0,2},{1,3},{2,0},{3,1},{4,6},{5,7},{6,4},{7,5},{8,10},{9,11},{10,... | collective-permute-start | bytes 786440 | tf_op jit(solution)/shard_map/ppermute | solution.py:36
  86.7 12.8 %collective-permute-start.22 = (bf16[4,4,72,128]{3,2,1,0:T(8,128)(2,1)S(1)}, bf16[4,4,72,128]{3,2,1,0:T(8,128)(2,1)S(1)}, u32[]{:S(2)}, u32[]{:S(2)}) collective-permute-start(bf16[4,4,72,128]{3,2,1,0:T(8,128)(2,1)S(1)} %pad_maximum_fusion.2.refs_4_), channel_id=1, source_target_pairs={{0,32},{16,48},{32,0},{48,16},{1,33},{17,49},{33,1},{49,17},{2,34}... | collective-permute-start | bytes 884744 | tf_op jit(solution)/shard_map/ppermute | solution.py:36
  87.9 11.7 %collective-permute-start.21 = (bf16[4,4,72,128]{3,2,1,0:T(8,128)(2,1)S(1)}, bf16[4,4,72,128]{3,2,1,0:T(8,128)(2,1)S(1)}, u32[]{:S(2)}, u32[]{:S(2)}) collective-permute-start(bf16[4,4,72,128]{3,2,1,0:T(8,128)(2,1)S(1)} %pad_maximum_fusion.2.refs_4_), channel_id=1, source_target_pairs={{0,48},{16,0},{32,16},{48,32},{1,49},{17,1},{33,17},{49,33},{2,50}... | collective-permute-start | bytes 884744 | tf_op jit(solution)/shard_map/ppermute | solution.py:36
  91.9 7.9 %collective-permute-start.20 = (bf16[4,4,72,128]{3,2,1,0:T(8,128)(2,1)S(1)}, bf16[4,4,72,128]{3,2,1,0:T(8,128)(2,1)S(1)}, u32[]{:S(2)}, u32[]{:S(2)}) collective-permute-start(bf16[4,4,72,128]{3,2,1,0:T(8,128)(2,1)S(1)} %pad_maximum_fusion.2.refs_4_), channel_id=1, source_target_pairs={{0,16},{16,32},{32,48},{48,0},{1,17},{17,33},{33,49},{49,1},{2,18}... | collective-permute-start | bytes 884744 | tf_op jit(solution)/shard_map/ppermute | solution.py:36
  91.9 6.5 %collective-permute-start.15 = (bf16[4,4,64,128]{3,2,1,0:T(8,128)(2,1)S(1)}, bf16[4,4,64,128]{3,2,1,0:T(8,128)(2,1)}, u32[]{:S(2)}, u32[]{:S(2)}) collective-permute-start(bf16[4,4,64,128]{3,2,1,0:T(8,128)(2,1)S(1)} %pad_maximum_fusion.3.refs_0_), channel_id=1, source_target_pairs={{0,3},{1,0},{2,1},{3,2},{4,7},{5,4},{6,5},{7,6},{8,11},{9,8},{10,9... | collective-permute-start | bytes 786440 | tf_op jit(solution)/shard_map/ppermute | solution.py:36
  93.1 6.5 %collective-permute-start.14 = (bf16[4,4,64,128]{3,2,1,0:T(8,128)(2,1)S(1)}, bf16[4,4,64,128]{3,2,1,0:T(8,128)(2,1)}, u32[]{:S(2)}, u32[]{:S(2)}) collective-permute-start(bf16[4,4,64,128]{3,2,1,0:T(8,128)(2,1)S(1)} %pad_maximum_fusion.3.refs_0_), channel_id=1, source_target_pairs={{0,1},{1,2},{2,3},{3,0},{4,5},{5,6},{6,7},{7,4},{8,9},{9,10},{10,1... | collective-permute-start | bytes 786440 | tf_op jit(solution)/shard_map/ppermute | solution.py:36
  103.0 1.6 collective-permute-start.23
  104.7 5.4 %collective-permute-start.24 = (bf16[464,128]{1,0:T(8,128)(2,1)S(1)}, bf16[464,128]{1,0:T(8,128)(2,1)S(1)}, u32[]{:S(2)}, u32[]{:S(2)}) collective-permute-start(bf16[464,128]{1,0:T(8,128)(2,1)S(1)} %get-tuple-element.15), channel_id=1, source_target_pairs={{0,128},{128,0},{1,129},{129,1},{2,130},{130,2},{3,131},{131,3},{4... | collective-permute-start | bytes 356360 | tf_op jit(solution)/shard_map/ppermute | solution.py:416
  110.1 0.7 collective-permute-start.25
  110.8 5.2 %collective-permute-start.28 = (bf16[224,128]{1,0:T(8,128)(2,1)S(1)}, bf16[224,128]{1,0:T(8,128)(2,1)S(1)}, u32[]{:S(2)}, u32[]{:S(2)}) collective-permute-start(bf16[224,128]{1,0:T(8,128)(2,1)S(1)} %get-tuple-element.24), channel_id=1, source_target_pairs={{0,4},{4,0},{8,12},{12,8},{1,5},{5,1},{9,13},{13,9},{2,6},{6,2},{1... | collective-permute-start | bytes 172040 | tf_op jit(solution)/shard_map/ppermute | solution.py:58
  116.0 9.0 %collective-permute-start.29 = (bf16[2,224,128]{2,1,0:T(8,128)(2,1)S(1)}, bf16[2,224,128]{2,1,0:T(8,128)(2,1)S(1)}, u32[]{:S(2)}, u32[]{:S(2)}) collective-permute-start(bf16[2,224,128]{2,1,0:T(8,128)(2,1)S(1)} %pad_maximum_fusion.6), channel_id=1, source_target_pairs={{0,8},{4,12},{8,0},{12,4},{1,9},{5,13},{9,1},{13,5},{2,10},{6,14},... | collective-permute-start | bytes 344072 | tf_op jit(solution)/shard_map/ppermute | solution.py:60
  125.1 18.6 %collective-permute-start.31 = (bf16[4,112,128]{2,1,0:T(8,128)(2,1)S(1)}, bf16[4,112,128]{2,1,0:T(8,128)(2,1)S(1)}, u32[]{:S(2)}, u32[]{:S(2)}) collective-permute-start(bf16[4,112,128]{2,1,0:T(8,128)(2,1)S(1)} %get-tuple-element.22), channel_id=1, source_target_pairs={{0,48},{16,0},{32,16},{48,32},{1,49},{17,1},{33,17},{49,33},{2,50}... | collective-permute-start | bytes 344072 | tf_op jit(solution)/shard_map/ppermute | solution.py:36
  140.1 7.5 %collective-permute-start.30 = (bf16[4,112,128]{2,1,0:T(8,128)(2,1)S(1)}, bf16[4,112,128]{2,1,0:T(8,128)(2,1)S(1)}, u32[]{:S(2)}, u32[]{:S(2)}) collective-permute-start(bf16[4,112,128]{2,1,0:T(8,128)(2,1)S(1)} %get-tuple-element.22), channel_id=1, source_target_pairs={{0,16},{16,32},{32,48},{48,0},{1,17},{17,33},{33,49},{49,1},{2,18}... | collective-permute-start | bytes 344072 | tf_op jit(solution)/shard_map/ppermute | solution.py:36
  140.1 7.5 %collective-permute-start.32 = (bf16[4,112,128]{2,1,0:T(8,128)(2,1)S(1)}, bf16[4,112,128]{2,1,0:T(8,128)(2,1)S(1)}, u32[]{:S(2)}, u32[]{:S(2)}) collective-permute-start(bf16[4,112,128]{2,1,0:T(8,128)(2,1)S(1)} %get-tuple-element.22), channel_id=1, source_target_pairs={{0,32},{16,48},{32,0},{48,16},{1,33},{17,49},{33,1},{49,17},{2,34}... | collective-permute-start | bytes 344072 | tf_op jit(solution)/shard_map/ppermute | solution.py:36
  141.7 8.2 %collective-permute-start.38 = (bf16[4,112,128]{2,1,0:T(8,128)(2,1)S(1)}, bf16[4,112,128]{2,1,0:T(8,128)(2,1)S(1)}, u32[]{:S(2)}, u32[]{:S(2)}) collective-permute-start(bf16[4,112,128]{2,1,0:T(8,128)(2,1)S(1)} %get-tuple-element.21), channel_id=1, source_target_pairs={{0,3},{1,0},{2,1},{3,2},{4,7},{5,4},{6,5},{7,6},{8,11},{9,8},{10,9... | collective-permute-start | bytes 344072 | tf_op jit(solution)/shard_map/ppermute | solution.py:36
  142.4 7.5 %collective-permute-start.37 = (bf16[4,112,128]{2,1,0:T(8,128)(2,1)S(1)}, bf16[4,112,128]{2,1,0:T(8,128)(2,1)S(1)}, u32[]{:S(2)}, u32[]{:S(2)}) collective-permute-start(bf16[4,112,128]{2,1,0:T(8,128)(2,1)S(1)} %get-tuple-element.21), channel_id=1, source_target_pairs={{0,1},{1,2},{2,3},{3,0},{4,5},{5,6},{6,7},{7,4},{8,9},{9,10},{10,1... | collective-permute-start | bytes 344072 | tf_op jit(solution)/shard_map/ppermute | solution.py:36
  143.7 7.5 %collective-permute-start.39 = (bf16[4,112,128]{2,1,0:T(8,128)(2,1)S(1)}, bf16[4,112,128]{2,1,0:T(8,128)(2,1)S(1)}, u32[]{:S(2)}, u32[]{:S(2)}) collective-permute-start(bf16[4,112,128]{2,1,0:T(8,128)(2,1)S(1)} %get-tuple-element.21), channel_id=1, source_target_pairs={{0,2},{1,3},{2,0},{3,1},{4,6},{5,7},{6,4},{7,5},{8,10},{9,11},{10,... | collective-permute-start | bytes 344072 | tf_op jit(solution)/shard_map/ppermute | solution.py:36
  147.7 11.4 %collective-permute-start.34 = (bf16[4,4,112,128]{3,2,1,0:T(8,128)(2,1)S(1)}, bf16[4,4,112,128]{3,2,1,0:T(8,128)(2,1)S(1)}, u32[]{:S(2)}, u32[]{:S(2)}) collective-permute-start(bf16[4,4,112,128]{3,2,1,0:T(8,128)(2,1)S(1)} %pad_maximum_fusion.refs_0_), channel_id=1, source_target_pairs={{0,3},{1,0},{2,1},{3,2},{4,7},{5,4},{6,5},{7,6},{8,11},{9,8},{10,9... | collective-permute-start | bytes 1376264 | tf_op jit(solution)/shard_map/ppermute | solution.py:44
  147.8 11.5 %collective-permute-start.33 = (bf16[4,4,112,128]{3,2,1,0:T(8,128)(2,1)S(1)}, bf16[4,4,112,128]{3,2,1,0:T(8,128)(2,1)S(1)}, u32[]{:S(2)}, u32[]{:S(2)}) collective-permute-start(bf16[4,4,112,128]{3,2,1,0:T(8,128)(2,1)S(1)} %pad_maximum_fusion.refs_0_), channel_id=1, source_target_pairs={{0,1},{1,2},{2,3},{3,0},{4,5},{5,6},{6,7},{7,4},{8,9},{9,10},{10,1... | collective-permute-start | bytes 1376264 | tf_op jit(solution)/shard_map/ppermute | solution.py:44
  151.3 10.1 %collective-permute-start.41 = (bf16[4,4,112,128]{3,2,1,0:T(8,128)(2,1)S(1)}, bf16[4,4,112,128]{3,2,1,0:T(8,128)(2,1)S(1)}, u32[]{:S(2)}, u32[]{:S(2)}) collective-permute-start(bf16[4,4,112,128]{3,2,1,0:T(8,128)(2,1)S(1)} %pad_maximum_fusion.1.refs_5_), channel_id=1, source_target_pairs={{0,48},{16,0},{32,16},{48,32},{1,49},{17,1},{33,17},{49,33},{2,50}... | collective-permute-start | bytes 1376264 | tf_op jit(solution)/shard_map/ppermute | solution.py:44
  155.0 10.2 %collective-permute-start.40 = (bf16[4,4,112,128]{3,2,1,0:T(8,128)(2,1)S(1)}, bf16[4,4,112,128]{3,2,1,0:T(8,128)(2,1)S(1)}, u32[]{:S(2)}, u32[]{:S(2)}) collective-permute-start(bf16[4,4,112,128]{3,2,1,0:T(8,128)(2,1)S(1)} %pad_maximum_fusion.1.refs_5_), channel_id=1, source_target_pairs={{0,16},{16,32},{32,48},{48,0},{1,17},{17,33},{33,49},{49,1},{2,18}... | collective-permute-start | bytes 1376264 | tf_op jit(solution)/shard_map/ppermute | solution.py:44
  155.1 10.3 %collective-permute-start.26 = (bf16[224,128]{1,0:T(8,128)(2,1)S(1)}, bf16[224,128]{1,0:T(8,128)(2,1)S(1)}, u32[]{:S(2)}, u32[]{:S(2)}) collective-permute-start(bf16[224,128]{1,0:T(8,128)(2,1)S(1)} %get-tuple-element.18), channel_id=1, source_target_pairs={{0,64},{64,0},{1,65},{65,1},{2,66},{66,2},{3,67},{67,3},{4,68},{68... | collective-permute-start | bytes 172040 | tf_op jit(solution)/shard_map/ppermute | solution.py:442
  159.2 11.1 %collective-permute-start.36 = (bf16[2,4,112,128]{3,2,1,0:T(8,128)(2,1)S(1)}, bf16[2,4,112,128]{3,2,1,0:T(8,128)(2,1)S(1)}, u32[]{:S(2)}, u32[]{:S(2)}) collective-permute-start(bf16[2,4,112,128]{3,2,1,0:T(8,128)(2,1)S(1)} %slice.39), channel_id=1, source_target_pairs={{0,3},{1,0},{2,1},{3,2},{4,7},{5,4},{6,5},{7,6},{8,11},{9,8},{10,9... | collective-permute-start | bytes 688136 | tf_op jit(solution)/shard_map/ppermute | solution.py:45
  159.3 11.0 %collective-permute-start.35 = (bf16[2,4,112,128]{3,2,1,0:T(8,128)(2,1)S(1)}, bf16[2,4,112,128]{3,2,1,0:T(8,128)(2,1)S(1)}, u32[]{:S(2)}, u32[]{:S(2)}) collective-permute-start(bf16[2,4,112,128]{3,2,1,0:T(8,128)(2,1)S(1)} %slice.38), channel_id=1, source_target_pairs={{0,1},{1,2},{2,3},{3,0},{4,5},{5,6},{6,7},{7,4},{8,9},{9,10},{10,1... | collective-permute-start | bytes 688136 | tf_op jit(solution)/shard_map/ppermute | solution.py:45
  161.4 8.9 %collective-permute-start.43 = (bf16[2,4,112,128]{3,2,1,0:T(8,128)(2,1)S(1)}, bf16[2,4,112,128]{3,2,1,0:T(8,128)(2,1)S(1)}, u32[]{:S(2)}, u32[]{:S(2)}) collective-permute-start(bf16[2,4,112,128]{3,2,1,0:T(8,128)(2,1)S(1)} %slice.42), channel_id=1, source_target_pairs={{0,48},{16,0},{32,16},{48,32},{1,49},{17,1},{33,17},{49,33},{2,50}... | collective-permute-start | bytes 688136 | tf_op jit(solution)/shard_map/ppermute | solution.py:45
  165.3 7.3 %collective-permute-start.42 = (bf16[2,4,112,128]{3,2,1,0:T(8,128)(2,1)S(1)}, bf16[2,4,112,128]{3,2,1,0:T(8,128)(2,1)S(1)}, u32[]{:S(2)}, u32[]{:S(2)}) collective-permute-start(bf16[2,4,112,128]{3,2,1,0:T(8,128)(2,1)S(1)} %slice.41), channel_id=1, source_target_pairs={{0,16},{16,32},{32,48},{48,0},{1,17},{17,33},{33,49},{49,1},{2,18}... | collective-permute-start | bytes 688136 | tf_op jit(solution)/shard_map/ppermute | solution.py:45
  165.4 4.9 %collective-permute-start.27 = (bf16[2,224,128]{2,1,0:T(8,128)(2,1)S(1)}, bf16[2,224,128]{2,1,0:T(8,128)(2,1)S(1)}, u32[]{:S(2)}, u32[]{:S(2)}) collective-permute-start(bf16[2,224,128]{2,1,0:T(8,128)(2,1)S(1)} %pad_maximum_fusion.5.near_ref), channel_id=1, source_target_pairs={{0,128},{128,0},{1,129},{129,1},{2,130},{130,2},{3,131},{131,3},{4... | collective-permute-start | bytes 344072 | tf_op jit(solution)/shard_map/ppermute | solution.py:444
  (6 other events, 102.3 us)

commit v9 on v7

--- a/solution.py
+++ b/solution.py
@@ -225,7 +225,7 @@
 
 def gate_up_kernel(group_ref, core_ref, *refs):
     upper, lower, weight_ref = refs[:4], refs[4:8], refs[8]
-    keep_ref, send_ref = refs[9:]
+    keep_ref, send_ref, part_ref = refs[9:]
     half = upper[0].shape[2]
     weight = weight_ref[...]
     units = weight.shape[0]
@@ -236,7 +236,8 @@
         square = jnp.zeros((8, LANES), jnp.float32)
         for r, z in places:
             square = square + lower[k][r, z, half:].astype(jnp.float32)
-        part = lax.dot_general(
+        group = group_ref[k]
+        part_ref[group, :units, :] = lax.dot_general(
             weight,
             jnp.concatenate([high, low], axis=0),
             NT,
@@ -244,15 +245,10 @@
         )
         total = jnp.broadcast_to(square[0:1] + square[1:2], square.shape)
         big = total.astype(jnp.bfloat16).astype(jnp.float32)
-        extra = jnp.concatenate([big, total - big], axis=0)
-        low_z = jnp.right_shift(group_ref[k], 1)
-        stays = jnp.bitwise_and(group_ref[k], 1) == core_ref[0]
-        for ref, mine in ((keep_ref, stays), (send_ref, jnp.logical_not(stays))):
-
-            @pl.when(mine)
-            def _():
-                ref[low_z, :units, :] = part.astype(ref.dtype)
-                ref[low_z, units:, :] = extra.astype(ref.dtype)
+        part_ref[group, units:, :] = jnp.concatenate([big, total - big], axis=0)
+    for low_z in range(2):
+        keep_ref[low_z] = part_ref[low_z * 2 + core_ref[0]]
+        send_ref[low_z] = part_ref[low_z * 2 + 1 - core_ref[0]].astype(jnp.bfloat16)
 
 
 def pair_kernel(low_ref, keep_ref, got_ref, next_keep_ref, next_send_ref):
@@ -383,6 +379,7 @@
         ),
         in_specs=[SMEM] * 2 + [VMEM] * 9,
         out_specs=[VMEM] * 2,
+        scratch_shapes=[pltpu.VMEM((4, *sums[1:]), jnp.float32)],
         name="gate_up",
         compiler_params=params(14),
         cost_estimate=pl.CostEstimate(

time: 179 us -> 177 us (0.989)
  Pallas kernels: 18.2 us -> 15.9 us
    pallas_call x1, Pallas kernels: 5.44 us -> 3.17 us  [body(): pl.pallas_call(gate_up_kernel, out_shape=(jax.ShapeDtypeStruct(sums, jnp....]
where the time goes in v9:
time: 177 us; the launch traced here: 173 us
  starting transfers between devices  82.4 us (47%)
  waiting for transfers between devices  37.8 us (21%)
  blocking collectives  31.9 us (18%)
  Pallas kernels  15.9 us (9%)
  local copies, waits for them, and re-layouts  4 us (2%)
    all_to_all x2, blocking collectives, copy_for_each(): lax.all_to_all(jnp.broadcast_to(x[None], (size, *x.shape)), axis, 0, 0, t...  24.6 us
    ppermute x21, starting transfers between devices, round_trip(): lax.ppermute(x, axis, [(k, (k + step) % 4) for k in range(4)])  24.1 us
    ppermute x21, waiting for transfers between devices, round_trip(): lax.ppermute(x, axis, [(k, (k + step) % 4) for k in range(4)])  21 us
    ppermute x3, starting transfers between devices, turned(): return lax.ppermute(x, (*DP, 'y'), pairs)  12.4 us
    ppermute x1, starting transfers between devices, body(): got = lax.ppermute(send, 'core', [(0, 1), (1, 0)])  9.79 us
    all_to_all x1, starting transfers between devices, copy_for_each(): lax.all_to_all(jnp.broadcast_to(x[None], (size, *x.shape)), axis, 0, 0, t...  9 us
    all_to_all x1, starting transfers between devices, body(): parts = lax.all_to_all(parts, 'y', 0, 0, tiled=True)  7.46 us
    all_gather x1, blocking collectives, body(): errors = lax.all_gather(solved, DP)  7.28 us
  transfers between devices with their start and end apart: 42, of which 22 were waited for; matrix products, arithmetic and copies ran while one was open for 0% of the time, Pallas kernels for 4%

profile of v9, /device:TPU:1, one launch (start us, length us, event | category | flops | bytes accessed | tf_op | source)
XLA Modules:
  0.0 173.4 jit_solution(216620061365911828)
XLA Ops:
  0.7 1.6 broadcast_in_dim.17
  2.3 9.0 %all-to-all-start = ((bf16[8,128,128]{2,1,0:T(8,128)(2,1)}), bf16[8,128,128]{2,1,0:T(8,128)(2,1)S(1)}, u32[]{:S(2)}, u32[]{:S(2)}) async-start(bf16[8,128,128]{2,1,0:T(8,128)(2,1)} %broadcast_in_dim.17), calls=%async_computation | async-start | bytes 524288 | tf_op jit(solution)/shard_map/all_to_all | solution.py:25
  11.3 3.7 %solve.1 = f32[128,128]{1,0:T(8,128)} custom-call(bf16[128,2048]{1,0:T(8,128)(2,1)} %weight_ref.1, s32[128,128]{1,0:T(8,128)} %mask_ref.1, f32[128,2048]{1,0:T(8,128)} %factor_ref.1), custom_call_target="tpu_custom_call" | custom-call | flops 20000000 | bytes 300000 | tf_op jit(solution)/shard_map/solve/pallas_call | solution.py:122
  15.0 7.3 %all-gather = f32[512,128]{1,0:T(8,128)S(1)} all-gather(f32[128,128]{1,0:T(8,128)} %solve.1), channel_id=2, replica_groups=mesh['z_low'=2,'core'=2,'y'=4,'z_high'=4,'x'=4] {'z_low','core'}, dimensions={0}, use_global_device_ids=true | all-gather | bytes 327680 | tf_op jit(solution)/shard_map/all_gather | solution.py:336
  22.3 1.8 %update.1 = bf16[128,2048]{1,0:T(8,128)(2,1)} custom-call(s32[1]{0:T(128)} %bitcast.place_ref, f32[4,128,128]{2,1,0:T(8,128)S(1)} %bitcast.38, f32[128,2048]{1,0:T(8,128)S(1)} %copy-done, bf16[128,2048]{1,0:T(8,128)(2,1)S(1)} %copy-done.1, s32[128,128]{1,0:T(8,128)S(1)} %copy-done.3), custom_call_target="tpu_custom_call" | custom-call | flops 400000000 | bytes 2200000 | tf_op jit(solution)/shard_map/update/pallas_call | solution.py:154
  24.1 2.7 %collective-permute-start.2 = (bf16[8,128,128]{2,1,0:T(8,128)(2,1)S(1)}, bf16[8,128,128]{2,1,0:T(8,128)(2,1)S(1)}, u32[]{:S(2)}, u32[]{:S(2)}) collective-permute-start(bf16[8,128,128]{2,1,0:T(8,128)(2,1)S(1)} %all-to-all-done.refs_0_), channel_id=1, source_target_pairs={{0,2},{1,3},{2,0},{3,1},{4,6},{5,7},{6,4},{7,5},{8,10},{9,11},{10,... | collective-permute-start | bytes 786440 | tf_op jit(solution)/shard_map/ppermute | solution.py:36
  26.9 3.5 %collective-permute-start.7 = (bf16[128,2048]{1,0:T(8,128)(2,1)}, bf16[128,2048]{1,0:T(8,128)(2,1)S(1)}, u32[]{:S(2)}, u32[]{:S(2)}) collective-permute-start(bf16[128,2048]{1,0:T(8,128)(2,1)} %update.1), channel_id=1, source_target_pairs={{0,0},{16,64},{32,128},{48,192},{64,16},{80,80},{96,144},{112,208}... | collective-permute-start | bytes 1572872 | tf_op jit(solution)/shard_map/ppermute | solution.py:30
  31.9 1.4 collective-permute-done.2.refs_3_
  33.3 1.1 collective-permute-start.6
  34.4 4.6 %collective-permute-done.1.refs_2_ = bf16[8,128,128]{2,1,0:T(8,128)(2,1)S(1)} collective-permute-done((bf16[8,128,128]{2,1,0:T(8,128)(2,1)S(1)}, bf16[8,128,128]{2,1,0:T(8,128)(2,1)S(1)}, u32[]{:S(2)}, u32[]{:S(2)}) %collective-permute-start.1) | collective-permute-done | bytes 262176 | tf_op jit(solution)/shard_map/ppermute | solution.py:36
  39.0 1.0 collective-permute-start.5
  41.6 1.9 %project.1 = bf16[4,128,128]{2,1,0:T(8,128)(2,1)} custom-call(s32[4]{0:T(128)S(1)} %pad_add_fusion.1.from_ref, s32[1]{0:T(128)} %bitcast.7.core_ref, bf16[8,128,128]{2,1,0:T(8,128)(2,1)S(1)} %all-to-all-done.refs_0_, bf16[8,128,128]{2,1,0:T(8,128)(2,1)S(1)} %collective-permute-done.refs_1_, bf16[8,128,128]{2,1,0:T(8,128)(2,1)S(1)} %collective-permute-done.1.refs_2_, ...), custom_call_target="tpu_custom_call" | custom-call | flops 268000000 | bytes 2700000 | tf_op jit(solution)/shard_map/project/pallas_call | solution.py:340
  43.5 7.5 %all-to-all-start.1 = ((bf16[4,128,128]{2,1,0:T(8,128)(2,1)}), bf16[4,128,128]{2,1,0:T(8,128)(2,1)S(1)}, u32[]{:S(2)}, u32[]{:S(2)}) async-start(bf16[4,128,128]{2,1,0:T(8,128)(2,1)} %project.1), calls=%async_computation.1 | async-start | bytes 262144 | tf_op jit(solution)/shard_map/all_to_all | solution.py:349
  51.0 4.8 %collective-permute-start.8 = (bf16[144,128]{1,0:T(8,128)(2,1)S(1)}, bf16[144,128]{1,0:T(8,128)(2,1)S(1)}, u32[]{:S(2)}, u32[]{:S(2)}) collective-permute-start(bf16[144,128]{1,0:T(8,128)(2,1)S(1)} %pad_maximum_fusion.5), channel_id=1, source_target_pairs={{0,0},{16,64},{32,128},{48,192},{64,16},{80,80},{96,144},{112,208}... | collective-permute-start | bytes 110600 | tf_op jit(solution)/shard_map/ppermute | solution.py:30
  55.8 1.9 %collective-permute-done.8.residual_ref = bf16[144,128]{1,0:T(8,128)(2,1)S(1)} collective-permute-done((bf16[144,128]{1,0:T(8,128)(2,1)S(1)}, bf16[144,128]{1,0:T(8,128)(2,1)S(1)}, u32[]{:S(2)}, u32[]{:S(2)}) %collective-permute-start.8) | collective-permute-done | bytes 36896 | tf_op jit(solution)/shard_map/ppermute | solution.py:30
  58.6 13.5 %all_to_all.20 = bf16[4,136,128]{2,1,0:T(8,128)(2,1)S(1)} all-to-all(bf16[4,136,128]{2,1,0:T(8,128)(2,1)S(1)} %broadcast_in_dim.38), channel_id=1, replica_groups=mesh['z_low'=2,'core'=2,'y'=4,'z_high'=4,'x'=4] {'z_high'}, dimensions={0} | all-to-all | bytes 278528 | tf_op jit(solution)/shard_map/all_to_all | solution.py:25
  72.1 3.5 %collective-permute-start.10 = (bf16[4,64,128]{2,1,0:T(8,128)(2,1)S(1)}, bf16[4,64,128]{2,1,0:T(8,128)(2,1)S(1)}, u32[]{:S(2)}, u32[]{:S(2)}) collective-permute-start(bf16[4,64,128]{2,1,0:T(8,128)(2,1)S(1)} %get-tuple-element.26), channel_id=1, source_target_pairs={{0,48},{16,0},{32,16},{48,32},{1,49},{17,1},{33,17},{49,33},{2,50}... | collective-permute-start | bytes 196616 | tf_op jit(solution)/shard_map/ppermute | solution.py:36
  75.6 1.3 collective-permute-start.11
  76.9 3.7 %collective-permute-done.9 = bf16[4,64,128]{2,1,0:T(8,128)(2,1)S(1)} collective-permute-done((bf16[4,64,128]{2,1,0:T(8,128)(2,1)S(1)}, bf16[4,64,128]{2,1,0:T(8,128)(2,1)S(1)}, u32[]{:S(2)}, u32[]{:S(2)}) %collective-permute-start.9) | collective-permute-done | bytes 65568 | tf_op jit(solution)/shard_map/ppermute | solution.py:36
  81.0 2.7 %collective-permute-start.16 = (bf16[4,72,128]{2,1,0:T(8,128)(2,1)S(1)}, bf16[4,72,128]{2,1,0:T(8,128)(2,1)S(1)}, u32[]{:S(2)}, u32[]{:S(2)}) collective-permute-start(bf16[4,72,128]{2,1,0:T(8,128)(2,1)S(1)} %get-tuple-element.24), channel_id=1, source_target_pairs={{0,3},{1,0},{2,1},{3,2},{4,7},{5,4},{6,5},{7,6},{8,11},{9,8},{10,9... | collective-permute-start | bytes 221192 | tf_op jit(solution)/shard_map/ppermute | solution.py:36
  83.8 1.7 collective-permute-start.17
  85.5 1.3 collective-permute-done.16
  86.8 1.5 collective-permute-done.15
  90.1 1.5 collective-permute-start.19
  92.1 2.5 %collective-permute-start.13 = (bf16[4,4,64,128]{3,2,1,0:T(8,128)(2,1)S(1)}, bf16[4,4,64,128]{3,2,1,0:T(8,128)(2,1)}, u32[]{:S(2)}, u32[]{:S(2)}) collective-permute-start(bf16[4,4,64,128]{3,2,1,0:T(8,128)(2,1)S(1)} %pad_maximum_fusion.3.refs_0_), channel_id=1, source_target_pairs={{0,3},{1,0},{2,1},{3,2},{4,7},{5,4},{6,5},{7,6},{8,11},{9,8},{10,9... | collective-permute-start | bytes 786440 | tf_op jit(solution)/shard_map/ppermute | solution.py:36
  94.6 1.5 copy-done.2
  96.1 1.0 order.1.refs_8_
  97.9 3.4 %collective-permute-done.12.refs_1_ = bf16[4,4,64,128]{3,2,1,0:T(8,128)(2,1)} collective-permute-done((bf16[4,4,64,128]{3,2,1,0:T(8,128)(2,1)S(1)}, bf16[4,4,64,128]{3,2,1,0:T(8,128)(2,1)}, u32[]{:S(2)}, u32[]{:S(2)}) %collective-permute-start.12) | collective-permute-done | bytes 262176 | tf_op jit(solution)/shard_map/ppermute | solution.py:36
  101.3 3.2 %gate_up.1 = (f32[2,464,128]{2,1,0:T(8,128)S(1)}, bf16[2,464,128]{2,1,0:T(8,128)(2,1)S(1)}) custom-call(s32[4]{0:T(128)S(1)} %pad_add_fusion.group_ref, s32[1]{0:T(128)} %bitcast.7.core_ref, bf16[4,4,64,128]{3,2,1,0:T(8,128)(2,1)S(1)} %pad_maximum_fusion.3.refs_0_, bf16[4,4,64,128]{3,2,1,0:T(8,128)(2,1)} %collective-permute-done.12.refs_1_, ...), custom_call_target="tpu_custom_call" | custom-call | flops 940000000 | bytes 4300000 | tf_op jit(solution)/shard_map/gate_up/pallas_call | solution.py:374
  104.5 9.8 %collective-permute-start.21 = (bf16[2,464,128]{2,1,0:T(8,128)(2,1)S(1)}, bf16[2,464,128]{2,1,0:T(8,128)(2,1)S(1)}, u32[]{:S(2)}, u32[]{:S(2)}) collective-permute-start(bf16[2,464,128]{2,1,0:T(8,128)(2,1)S(1)} %get-tuple-element.13), channel_id=1, source_target_pairs={{0,64},{64,0},{1,65},{65,1},{2,66},{66,2},{3,67},{67,3},{4,68},{68... | collective-permute-start | bytes 712712 | tf_op jit(solution)/shard_map/ppermute | solution.py:389
  114.3 1.1 collective-permute-done.21.got_ref
  115.6 4.4 %collective-permute-done.22.got_ref = bf16[464,128]{1,0:T(8,128)(2,1)S(1)} collective-permute-done((bf16[464,128]{1,0:T(8,128)(2,1)S(1)}, bf16[464,128]{1,0:T(8,128)(2,1)S(1)}, u32[]{:S(2)}, u32[]{:S(2)}) %collective-permute-start.22) | collective-permute-done | bytes 118816 | tf_op jit(solution)/shard_map/ppermute | solution.py:402
  120.1 4.0 %collective-permute-start.23 = (bf16[352,128]{1,0:T(8,128)(2,1)S(1)}, bf16[352,128]{1,0:T(8,128)(2,1)S(1)}, u32[]{:S(2)}, u32[]{:S(2)}) collective-permute-start(bf16[352,128]{1,0:T(8,128)(2,1)S(1)} %get-tuple-element.17), channel_id=1, source_target_pairs={{0,0},{16,64},{32,128},{48,192},{64,16},{80,80},{96,144},{112,208}... | collective-permute-start | bytes 270344 | tf_op jit(solution)/shard_map/ppermute | solution.py:30
  124.1 3.2 %collective-permute-done.23.in_ref = bf16[352,128]{1,0:T(8,128)(2,1)S(1)} collective-permute-done((bf16[352,128]{1,0:T(8,128)(2,1)S(1)}, bf16[352,128]{1,0:T(8,128)(2,1)S(1)}, u32[]{:S(2)}, u32[]{:S(2)}) %collective-permute-start.23) | collective-permute-done | bytes 90144 | tf_op jit(solution)/shard_map/ppermute | solution.py:30
  127.3 11.1 %all_to_all.21 = bf16[4,224,128]{2,1,0:T(8,128)(2,1)S(1)} all-to-all(bf16[4,224,128]{2,1,0:T(8,128)(2,1)S(1)} %broadcast_in_dim.39), channel_id=1, replica_groups=mesh['z_low'=2,'core'=2,'y'=4,'z_high'=4,'x'=4] {'z_high'}, dimensions={0} | all-to-all | bytes 458752 | tf_op jit(solution)/shard_map/all_to_all | solution.py:25
  138.5 2.0 %collective-permute-start.27 = (bf16[4,112,128]{2,1,0:T(8,128)(2,1)S(1)}, bf16[4,112,128]{2,1,0:T(8,128)(2,1)S(1)}, u32[]{:S(2)}, u32[]{:S(2)}) collective-permute-start(bf16[4,112,128]{2,1,0:T(8,128)(2,1)S(1)} %get-tuple-element.22), channel_id=1, source_target_pairs={{0,48},{16,0},{32,16},{48,32},{1,49},{17,1},{33,17},{49,33},{2,50}... | collective-permute-start | bytes 344072 | tf_op jit(solution)/shard_map/ppermute | solution.py:36
  140.5 1.3 collective-permute-start.28
  142.0 1.3 collective-permute-start.33
  143.2 3.3 %collective-permute-done.26 = bf16[4,112,128]{2,1,0:T(8,128)(2,1)S(1)} collective-permute-done((bf16[4,112,128]{2,1,0:T(8,128)(2,1)S(1)}, bf16[4,112,128]{2,1,0:T(8,128)(2,1)S(1)}, u32[]{:S(2)}, u32[]{:S(2)}) %collective-permute-start.26) | collective-permute-done | bytes 114720 | tf_op jit(solution)/shard_map/ppermute | solution.py:36
  146.9 1.3 collective-permute-start.29
  148.5 3.4 %collective-permute-start.37 = (bf16[4,4,112,128]{3,2,1,0:T(8,128)(2,1)S(1)}, bf16[4,4,112,128]{3,2,1,0:T(8,128)(2,1)S(1)}, u32[]{:S(2)}, u32[]{:S(2)}) collective-permute-start(bf16[4,4,112,128]{3,2,1,0:T(8,128)(2,1)S(1)} %pad_maximum_fusion.1.refs_5_), channel_id=1, source_target_pairs={{0,48},{16,0},{32,16},{48,32},{1,49},{17,1},{33,17},{49,33},{2,50}... | collective-permute-start | bytes 1376264 | tf_op jit(solution)/shard_map/ppermute | solution.py:44
  151.9 6.6 %collective-permute-start.24 = (bf16[224,128]{1,0:T(8,128)(2,1)S(1)}, bf16[224,128]{1,0:T(8,128)(2,1)S(1)}, u32[]{:S(2)}, u32[]{:S(2)}) collective-permute-start(bf16[224,128]{1,0:T(8,128)(2,1)S(1)} %get-tuple-element.18), channel_id=1, source_target_pairs={{0,64},{64,0},{1,65},{65,1},{2,66},{66,2},{3,67},{67,3},{4,68},{68... | collective-permute-start | bytes 172040 | tf_op jit(solution)/shard_map/ppermute | solution.py:428
  158.9 1.2 collective-permute-start.32
  160.6 2.3 %collective-permute-start.39 = (bf16[2,4,112,128]{3,2,1,0:T(8,128)(2,1)S(1)}, bf16[2,4,112,128]{3,2,1,0:T(8,128)(2,1)S(1)}, u32[]{:S(2)}, u32[]{:S(2)}) collective-permute-start(bf16[2,4,112,128]{3,2,1,0:T(8,128)(2,1)S(1)} %slice.44), channel_id=1, source_target_pairs={{0,48},{16,0},{32,16},{48,32},{1,49},{17,1},{33,17},{49,33},{2,50}... | collective-permute-start | bytes 688136 | tf_op jit(solution)/shard_map/ppermute | solution.py:45
  163.1 2.3 %collective-permute-start.25 = (bf16[2,224,128]{2,1,0:T(8,128)(2,1)S(1)}, bf16[2,224,128]{2,1,0:T(8,128)(2,1)S(1)}, u32[]{:S(2)}, u32[]{:S(2)}) collective-permute-start(bf16[2,224,128]{2,1,0:T(8,128)(2,1)S(1)} %pad_maximum_fusion.4.near_ref), channel_id=1, source_target_pairs={{0,128},{128,0},{1,129},{129,1},{2,130},{130,2},{3,131},{131,3},{4... | collective-permute-start | bytes 344072 | tf_op jit(solution)/shard_map/ppermute | solution.py:430
  165.9 1.9 %collective-permute-done.25.far_ref = bf16[2,224,128]{2,1,0:T(8,128)(2,1)S(1)} collective-permute-done((bf16[2,224,128]{2,1,0:T(8,128)(2,1)S(1)}, bf16[2,224,128]{2,1,0:T(8,128)(2,1)S(1)}, u32[]{:S(2)}, u32[]{:S(2)}) %collective-permute-start.25) | collective-permute-done | bytes 114720 | tf_op jit(solution)/shard_map/ppermute | solution.py:430
  167.8 2.1 %collective-permute-done.38.refs_8_ = bf16[2,4,112,128]{3,2,1,0:T(8,128)(2,1)S(1)} collective-permute-done((bf16[2,4,112,128]{3,2,1,0:T(8,128)(2,1)S(1)}, bf16[2,4,112,128]{3,2,1,0:T(8,128)(2,1)S(1)}, u32[]{:S(2)}, u32[]{:S(2)}) %collective-permute-start.38) | collective-permute-done | bytes 229408 | tf_op jit(solution)/shard_map/ppermute | solution.py:45
  169.9 3.3 %hessian.1 = f32[224,3584]{1,0:T(8,128)} custom-call(s32[4]{0:T(128)S(1)} %pad_add_fusion.1.from_ref, s32[4]{0:T(128)S(1)} %pad_add_fusion.group_ref, s32[1]{0:T(128)} %bitcast.place_ref, bf16[2,224,128]{2,1,0:T(8,128)(2,1)S(1)} %pad_maximum_fusion.4.near_ref, bf16[2,224,128]{2,1,0:T(8,128)(2,1)S(1)} %collective-permute-done.25.far_ref, ...), custom_call_target="tpu_custom_call" | custom-call | flops 822000000 | bytes 7100000 | tf_op jit(solution)/shard_map/hessian/pallas_call | solution.py:431
  (85 shorter events, 10.2 us)
Async XLA Ops:
  0.6 21.7 %copy-start = (f32[128,2048]{1,0:T(8,128)S(1)}, f32[128,2048]{1,0:T(8,128)}, u32[]{:S(2)}) copy-start(f32[128,2048]{1,0:T(8,128)} %factor_ref.1) | copy-start | bytes 3145732
  0.6 21.7 %copy-start.3 = (s32[128,128]{1,0:T(8,128)S(1)}, s32[128,128]{1,0:T(8,128)}, u32[]{:S(2)}) copy-start(s32[128,128]{1,0:T(8,128)} %mask_ref.1) | copy-start | bytes 196612
  0.7 21.6 %copy-start.1 = (bf16[128,2048]{1,0:T(8,128)(2,1)S(1)}, bf16[128,2048]{1,0:T(8,128)(2,1)}, u32[]{:S(2)}) copy-start(bf16[128,2048]{1,0:T(8,128)(2,1)} %weight_ref.1) | copy-start | bytes 1572868
  2.3 21.8 %all-to-all-start = ((bf16[8,128,128]{2,1,0:T(8,128)(2,1)}), bf16[8,128,128]{2,1,0:T(8,128)(2,1)S(1)}, u32[]{:S(2)}, u32[]{:S(2)}) async-start(bf16[8,128,128]{2,1,0:T(8,128)(2,1)} %broadcast_in_dim.17), calls=%async_computation | async-start | bytes 524288 | tf_op jit(solution)/shard_map/all_to_all | solution.py:25
  24.1 26.9 %copy-start.7 = (bf16[128]{0:T(256)(128)(2,1)S(1)}, bf16[128]{0:T(256)(128)(2,1)}, u32[]{:S(2)}) copy-start(bf16[128]{0:T(256)(128)(2,1)} %param.12) | copy-start | bytes 772
  24.1 26.9 %copy-start.6 = (bf16[128,128]{1,0:T(8,128)(2,1)S(1)}, bf16[128,128]{1,0:T(8,128)(2,1)}, u32[]{:S(2)}) copy-start(bf16[128,128]{1,0:T(8,128)(2,1)} %param.8) | copy-start | bytes 98308
  24.1 9.2 %collective-permute-start.2 = (bf16[8,128,128]{2,1,0:T(8,128)(2,1)S(1)}, bf16[8,128,128]{2,1,0:T(8,128)(2,1)S(1)}, u32[]{:S(2)}, u32[]{:S(2)}) collective-permute-start(bf16[8,128,128]{2,1,0:T(8,128)(2,1)S(1)} %all-to-all-done.refs_0_), channel_id=1, source_target_pairs={{0,2},{1,3},{2,0},{3,1},{4,6},{5,7},{6,4},{7,5},{8,10},{9,11},{10,... | collective-permute-start | bytes 786440 | tf_op jit(solution)/shard_map/ppermute | solution.py:36
  26.9 14.1 %collective-permute-start.7 = (bf16[128,2048]{1,0:T(8,128)(2,1)}, bf16[128,2048]{1,0:T(8,128)(2,1)S(1)}, u32[]{:S(2)}, u32[]{:S(2)}) collective-permute-start(bf16[128,2048]{1,0:T(8,128)(2,1)} %update.1), channel_id=1, source_target_pairs={{0,0},{16,64},{32,128},{48,192},{64,16},{80,80},{96,144},{112,208}... | collective-permute-start | bytes 1572872 | tf_op jit(solution)/shard_map/ppermute | solution.py:30
  30.4 8.6 %collective-permute-start.1 = (bf16[8,128,128]{2,1,0:T(8,128)(2,1)S(1)}, bf16[8,128,128]{2,1,0:T(8,128)(2,1)S(1)}, u32[]{:S(2)}, u32[]{:S(2)}) collective-permute-start(bf16[8,128,128]{2,1,0:T(8,128)(2,1)S(1)} %all-to-all-done.refs_0_), channel_id=1, source_target_pairs={{0,3},{1,0},{2,1},{3,2},{4,7},{5,4},{6,5},{7,6},{8,11},{9,8},{10,9... | collective-permute-start | bytes 786440 | tf_op jit(solution)/shard_map/ppermute | solution.py:36
  31.3 8.7 %collective-permute-start = (bf16[8,128,128]{2,1,0:T(8,128)(2,1)S(1)}, bf16[8,128,128]{2,1,0:T(8,128)(2,1)S(1)}, u32[]{:S(2)}, u32[]{:S(2)}) collective-permute-start(bf16[8,128,128]{2,1,0:T(8,128)(2,1)S(1)} %all-to-all-done.refs_0_), channel_id=1, source_target_pairs={{0,1},{1,2},{2,3},{3,0},{4,5},{5,6},{6,7},{7,4},{8,9},{9,10},{10,1... | collective-permute-start | bytes 786440 | tf_op jit(solution)/shard_map/ppermute | solution.py:36
  31.9 9.1 %collective-permute-start.3 = (bf16[8,128,128]{2,1,0:T(8,128)(2,1)S(1)}, bf16[8,128,128]{2,1,0:T(8,128)(2,1)S(1)}, u32[]{:S(2)}, u32[]{:S(2)}) collective-permute-start(bf16[8,128,128]{2,1,0:T(8,128)(2,1)S(1)} %all-to-all-done.refs_0_), channel_id=1, source_target_pairs={{0,64},{64,0},{1,65},{65,1},{2,66},{66,2},{3,67},{67,3},{4,68},{68... | collective-permute-start | bytes 786440 | tf_op jit(solution)/shard_map/ppermute | solution.py:331
  33.3 7.7 %collective-permute-start.6 = (bf16[8,128,128]{2,1,0:T(8,128)(2,1)S(1)}, bf16[8,128,128]{2,1,0:T(8,128)(2,1)S(1)}, u32[]{:S(2)}, u32[]{:S(2)}) collective-permute-start(bf16[8,128,128]{2,1,0:T(8,128)(2,1)S(1)} %collective-permute-done.2.refs_3_), channel_id=1, source_target_pairs={{0,64},{64,0},{1,65},{65,1},{2,66},{66,2},{3,67},{67,3},{4,68},{68... | collective-permute-start | bytes 786440 | tf_op jit(solution)/shard_map/ppermute | solution.py:331
  39.0 2.2 %collective-permute-start.5 = (bf16[8,128,128]{2,1,0:T(8,128)(2,1)S(1)}, bf16[8,128,128]{2,1,0:T(8,128)(2,1)S(1)}, u32[]{:S(2)}, u32[]{:S(2)}) collective-permute-start(bf16[8,128,128]{2,1,0:T(8,128)(2,1)S(1)} %collective-permute-done.1.refs_2_), channel_id=1, source_target_pairs={{0,64},{64,0},{1,65},{65,1},{2,66},{66,2},{3,67},{67,3},{4,68},{68... | collective-permute-start | bytes 786440 | tf_op jit(solution)/shard_map/ppermute | solution.py:331
  40.1 1.5 collective-permute-start.4
  43.5 14.2 %all-to-all-start.1 = ((bf16[4,128,128]{2,1,0:T(8,128)(2,1)}), bf16[4,128,128]{2,1,0:T(8,128)(2,1)S(1)}, u32[]{:S(2)}, u32[]{:S(2)}) async-start(bf16[4,128,128]{2,1,0:T(8,128)(2,1)} %project.1), calls=%async_computation.1 | async-start | bytes 262144 | tf_op jit(solution)/shard_map/all_to_all | solution.py:349
  51.0 6.7 %collective-permute-start.8 = (bf16[144,128]{1,0:T(8,128)(2,1)S(1)}, bf16[144,128]{1,0:T(8,128)(2,1)S(1)}, u32[]{:S(2)}, u32[]{:S(2)}) collective-permute-start(bf16[144,128]{1,0:T(8,128)(2,1)S(1)} %pad_maximum_fusion.5), channel_id=1, source_target_pairs={{0,0},{16,64},{32,128},{48,192},{64,16},{80,80},{96,144},{112,208}... | collective-permute-start | bytes 110600 | tf_op jit(solution)/shard_map/ppermute | solution.py:30
  72.1 4.8 %collective-permute-start.10 = (bf16[4,64,128]{2,1,0:T(8,128)(2,1)S(1)}, bf16[4,64,128]{2,1,0:T(8,128)(2,1)S(1)}, u32[]{:S(2)}, u32[]{:S(2)}) collective-permute-start(bf16[4,64,128]{2,1,0:T(8,128)(2,1)S(1)} %get-tuple-element.26), channel_id=1, source_target_pairs={{0,48},{16,0},{32,16},{48,32},{1,49},{17,1},{33,17},{49,33},{2,50}... | collective-permute-start | bytes 196616 | tf_op jit(solution)/shard_map/ppermute | solution.py:36
  75.6 5.0 %collective-permute-start.9 = (bf16[4,64,128]{2,1,0:T(8,128)(2,1)S(1)}, bf16[4,64,128]{2,1,0:T(8,128)(2,1)S(1)}, u32[]{:S(2)}, u32[]{:S(2)}) collective-permute-start(bf16[4,64,128]{2,1,0:T(8,128)(2,1)S(1)} %get-tuple-element.26), channel_id=1, source_target_pairs={{0,16},{16,32},{32,48},{48,0},{1,17},{17,33},{33,49},{49,1},{2,18}... | collective-permute-start | bytes 196616 | tf_op jit(solution)/shard_map/ppermute | solution.py:36
  75.6 5.0 %collective-permute-start.11 = (bf16[4,64,128]{2,1,0:T(8,128)(2,1)S(1)}, bf16[4,64,128]{2,1,0:T(8,128)(2,1)S(1)}, u32[]{:S(2)}, u32[]{:S(2)}) collective-permute-start(bf16[4,64,128]{2,1,0:T(8,128)(2,1)S(1)} %get-tuple-element.26), channel_id=1, source_target_pairs={{0,32},{16,48},{32,0},{48,16},{1,33},{17,49},{33,1},{49,17},{2,34}... | collective-permute-start | bytes 196616 | tf_op jit(solution)/shard_map/ppermute | solution.py:36
  80.7 13.9 %collective-permute-start.14 = (bf16[4,4,64,128]{3,2,1,0:T(8,128)(2,1)S(1)}, bf16[4,4,64,128]{3,2,1,0:T(8,128)(2,1)S(1)}, u32[]{:S(2)}, u32[]{:S(2)}) collective-permute-start(bf16[4,4,64,128]{3,2,1,0:T(8,128)(2,1)S(1)} %pad_maximum_fusion.3.refs_0_), channel_id=1, source_target_pairs={{0,2},{1,3},{2,0},{3,1},{4,6},{5,7},{6,4},{7,5},{8,10},{9,11},{10,... | collective-permute-start | bytes 786440 | tf_op jit(solution)/shard_map/ppermute | solution.py:36
  81.0 5.7 %collective-permute-start.16 = (bf16[4,72,128]{2,1,0:T(8,128)(2,1)S(1)}, bf16[4,72,128]{2,1,0:T(8,128)(2,1)S(1)}, u32[]{:S(2)}, u32[]{:S(2)}) collective-permute-start(bf16[4,72,128]{2,1,0:T(8,128)(2,1)S(1)} %get-tuple-element.24), channel_id=1, source_target_pairs={{0,3},{1,0},{2,1},{3,2},{4,7},{5,4},{6,5},{7,6},{8,11},{9,8},{10,9... | collective-permute-start | bytes 221192 | tf_op jit(solution)/shard_map/ppermute | solution.py:36
  83.8 4.5 %collective-permute-start.15 = (bf16[4,72,128]{2,1,0:T(8,128)(2,1)S(1)}, bf16[4,72,128]{2,1,0:T(8,128)(2,1)S(1)}, u32[]{:S(2)}, u32[]{:S(2)}) collective-permute-start(bf16[4,72,128]{2,1,0:T(8,128)(2,1)S(1)} %get-tuple-element.24), channel_id=1, source_target_pairs={{0,1},{1,2},{2,3},{3,0},{4,5},{5,6},{6,7},{7,4},{8,9},{9,10},{10,1... | collective-permute-start | bytes 221192 | tf_op jit(solution)/shard_map/ppermute | solution.py:36
  83.8 5.3 %collective-permute-start.17 = (bf16[4,72,128]{2,1,0:T(8,128)(2,1)S(1)}, bf16[4,72,128]{2,1,0:T(8,128)(2,1)S(1)}, u32[]{:S(2)}, u32[]{:S(2)}) collective-permute-start(bf16[4,72,128]{2,1,0:T(8,128)(2,1)S(1)} %get-tuple-element.24), channel_id=1, source_target_pairs={{0,2},{1,3},{2,0},{3,1},{4,6},{5,7},{6,4},{7,5},{8,10},{9,11},{10,... | collective-permute-start | bytes 221192 | tf_op jit(solution)/shard_map/ppermute | solution.py:36
  89.1 12.2 %collective-permute-start.20 = (bf16[4,4,72,128]{3,2,1,0:T(8,128)(2,1)S(1)}, bf16[4,4,72,128]{3,2,1,0:T(8,128)(2,1)S(1)}, u32[]{:S(2)}, u32[]{:S(2)}) collective-permute-start(bf16[4,4,72,128]{3,2,1,0:T(8,128)(2,1)S(1)} %pad_maximum_fusion.2.refs_4_), channel_id=1, source_target_pairs={{0,32},{16,48},{32,0},{48,16},{1,33},{17,49},{33,1},{49,17},{2,34}... | collective-permute-start | bytes 884744 | tf_op jit(solution)/shard_map/ppermute | solution.py:36
  90.1 11.2 %collective-permute-start.19 = (bf16[4,4,72,128]{3,2,1,0:T(8,128)(2,1)S(1)}, bf16[4,4,72,128]{3,2,1,0:T(8,128)(2,1)S(1)}, u32[]{:S(2)}, u32[]{:S(2)}) collective-permute-start(bf16[4,4,72,128]{3,2,1,0:T(8,128)(2,1)S(1)} %pad_maximum_fusion.2.refs_4_), channel_id=1, source_target_pairs={{0,48},{16,0},{32,16},{48,32},{1,49},{17,1},{33,17},{49,33},{2,50}... | collective-permute-start | bytes 884744 | tf_op jit(solution)/shard_map/ppermute | solution.py:36
  91.6 9.8 %collective-permute-start.18 = (bf16[4,4,72,128]{3,2,1,0:T(8,128)(2,1)S(1)}, bf16[4,4,72,128]{3,2,1,0:T(8,128)(2,1)S(1)}, u32[]{:S(2)}, u32[]{:S(2)}) collective-permute-start(bf16[4,4,72,128]{3,2,1,0:T(8,128)(2,1)S(1)} %pad_maximum_fusion.2.refs_4_), channel_id=1, source_target_pairs={{0,16},{16,32},{32,48},{48,0},{1,17},{17,33},{33,49},{49,1},{2,18}... | collective-permute-start | bytes 884744 | tf_op jit(solution)/shard_map/ppermute | solution.py:36
  92.1 5.8 %collective-permute-start.13 = (bf16[4,4,64,128]{3,2,1,0:T(8,128)(2,1)S(1)}, bf16[4,4,64,128]{3,2,1,0:T(8,128)(2,1)}, u32[]{:S(2)}, u32[]{:S(2)}) collective-permute-start(bf16[4,4,64,128]{3,2,1,0:T(8,128)(2,1)S(1)} %pad_maximum_fusion.3.refs_0_), channel_id=1, source_target_pairs={{0,3},{1,0},{2,1},{3,2},{4,7},{5,4},{6,5},{7,6},{8,11},{9,8},{10,9... | collective-permute-start | bytes 786440 | tf_op jit(solution)/shard_map/ppermute | solution.py:36
  94.6 6.7 %collective-permute-start.12 = (bf16[4,4,64,128]{3,2,1,0:T(8,128)(2,1)S(1)}, bf16[4,4,64,128]{3,2,1,0:T(8,128)(2,1)}, u32[]{:S(2)}, u32[]{:S(2)}) collective-permute-start(bf16[4,4,64,128]{3,2,1,0:T(8,128)(2,1)S(1)} %pad_maximum_fusion.3.refs_0_), channel_id=1, source_target_pairs={{0,1},{1,2},{2,3},{3,0},{4,5},{5,6},{6,7},{7,4},{8,9},{9,10},{10,1... | collective-permute-start | bytes 786440 | tf_op jit(solution)/shard_map/ppermute | solution.py:36
  97.2 22.8 %copy-start.5 = (bf16[128,128]{1,0:T(8,128)(2,1)S(1)}, bf16[128,128]{1,0:T(8,128)(2,1)}, u32[]{:S(2)}) copy-start(bf16[128,128]{1,0:T(8,128)(2,1)} %copy-done.4) | copy-start | bytes 98308
  104.5 10.9 %collective-permute-start.21 = (bf16[2,464,128]{2,1,0:T(8,128)(2,1)S(1)}, bf16[2,464,128]{2,1,0:T(8,128)(2,1)S(1)}, u32[]{:S(2)}, u32[]{:S(2)}) collective-permute-start(bf16[2,464,128]{2,1,0:T(8,128)(2,1)S(1)} %get-tuple-element.13), channel_id=1, source_target_pairs={{0,64},{64,0},{1,65},{65,1},{2,66},{66,2},{3,67},{67,3},{4,68},{68... | collective-permute-start | bytes 712712 | tf_op jit(solution)/shard_map/ppermute | solution.py:389
  115.5 4.5 %collective-permute-start.22 = (bf16[464,128]{1,0:T(8,128)(2,1)S(1)}, bf16[464,128]{1,0:T(8,128)(2,1)S(1)}, u32[]{:S(2)}, u32[]{:S(2)}) collective-permute-start(bf16[464,128]{1,0:T(8,128)(2,1)S(1)} %get-tuple-element.15), channel_id=1, source_target_pairs={{0,128},{128,0},{1,129},{129,1},{2,130},{130,2},{3,131},{131,3},{4... | collective-permute-start | bytes 356360 | tf_op jit(solution)/shard_map/ppermute | solution.py:402
  120.1 7.2 %collective-permute-start.23 = (bf16[352,128]{1,0:T(8,128)(2,1)S(1)}, bf16[352,128]{1,0:T(8,128)(2,1)S(1)}, u32[]{:S(2)}, u32[]{:S(2)}) collective-permute-start(bf16[352,128]{1,0:T(8,128)(2,1)S(1)} %get-tuple-element.17), channel_id=1, source_target_pairs={{0,0},{16,64},{32,128},{48,192},{64,16},{80,80},{96,144},{112,208}... | collective-permute-start | bytes 270344 | tf_op jit(solution)/shard_map/ppermute | solution.py:30
  138.5 4.8 %collective-permute-start.27 = (bf16[4,112,128]{2,1,0:T(8,128)(2,1)S(1)}, bf16[4,112,128]{2,1,0:T(8,128)(2,1)S(1)}, u32[]{:S(2)}, u32[]{:S(2)}) collective-permute-start(bf16[4,112,128]{2,1,0:T(8,128)(2,1)S(1)} %get-tuple-element.22), channel_id=1, source_target_pairs={{0,48},{16,0},{32,16},{48,32},{1,49},{17,1},{33,17},{49,33},{2,50}... | collective-permute-start | bytes 344072 | tf_op jit(solution)/shard_map/ppermute | solution.py:36
  140.5 6.1 %collective-permute-start.26 = (bf16[4,112,128]{2,1,0:T(8,128)(2,1)S(1)}, bf16[4,112,128]{2,1,0:T(8,128)(2,1)S(1)}, u32[]{:S(2)}, u32[]{:S(2)}) collective-permute-start(bf16[4,112,128]{2,1,0:T(8,128)(2,1)S(1)} %get-tuple-element.22), channel_id=1, source_target_pairs={{0,16},{16,32},{32,48},{48,0},{1,17},{17,33},{33,49},{49,1},{2,18}... | collective-permute-start | bytes 344072 | tf_op jit(solution)/shard_map/ppermute | solution.py:36
  140.5 6.1 %collective-permute-start.28 = (bf16[4,112,128]{2,1,0:T(8,128)(2,1)S(1)}, bf16[4,112,128]{2,1,0:T(8,128)(2,1)S(1)}, u32[]{:S(2)}, u32[]{:S(2)}) collective-permute-start(bf16[4,112,128]{2,1,0:T(8,128)(2,1)S(1)} %get-tuple-element.22), channel_id=1, source_target_pairs={{0,32},{16,48},{32,0},{48,16},{1,33},{17,49},{33,1},{49,17},{2,34}... | collective-permute-start | bytes 344072 | tf_op jit(solution)/shard_map/ppermute | solution.py:36
  141.8 6.4 %collective-permute-start.34 = (bf16[4,112,128]{2,1,0:T(8,128)(2,1)S(1)}, bf16[4,112,128]{2,1,0:T(8,128)(2,1)S(1)}, u32[]{:S(2)}, u32[]{:S(2)}) collective-permute-start(bf16[4,112,128]{2,1,0:T(8,128)(2,1)S(1)} %get-tuple-element.21), channel_id=1, source_target_pairs={{0,3},{1,0},{2,1},{3,2},{4,7},{5,4},{6,5},{7,6},{8,11},{9,8},{10,9... | collective-permute-start | bytes 344072 | tf_op jit(solution)/shard_map/ppermute | solution.py:36
  142.0 6.2 %collective-permute-start.33 = (bf16[4,112,128]{2,1,0:T(8,128)(2,1)S(1)}, bf16[4,112,128]{2,1,0:T(8,128)(2,1)S(1)}, u32[]{:S(2)}, u32[]{:S(2)}) collective-permute-start(bf16[4,112,128]{2,1,0:T(8,128)(2,1)S(1)} %get-tuple-element.21), channel_id=1, source_target_pairs={{0,1},{1,2},{2,3},{3,0},{4,5},{5,6},{6,7},{7,4},{8,9},{9,10},{10,1... | collective-permute-start | bytes 344072 | tf_op jit(solution)/shard_map/ppermute | solution.py:36
  143.2 5.1 %collective-permute-start.35 = (bf16[4,112,128]{2,1,0:T(8,128)(2,1)S(1)}, bf16[4,112,128]{2,1,0:T(8,128)(2,1)S(1)}, u32[]{:S(2)}, u32[]{:S(2)}) collective-permute-start(bf16[4,112,128]{2,1,0:T(8,128)(2,1)S(1)} %get-tuple-element.21), channel_id=1, source_target_pairs={{0,2},{1,3},{2,0},{3,1},{4,6},{5,7},{6,4},{7,5},{8,10},{9,11},{10,... | collective-permute-start | bytes 344072 | tf_op jit(solution)/shard_map/ppermute | solution.py:36
  146.6 12.2 %collective-permute-start.30 = (bf16[4,4,112,128]{3,2,1,0:T(8,128)(2,1)S(1)}, bf16[4,4,112,128]{3,2,1,0:T(8,128)(2,1)S(1)}, u32[]{:S(2)}, u32[]{:S(2)}) collective-permute-start(bf16[4,4,112,128]{3,2,1,0:T(8,128)(2,1)S(1)} %pad_maximum_fusion.refs_0_), channel_id=1, source_target_pairs={{0,3},{1,0},{2,1},{3,2},{4,7},{5,4},{6,5},{7,6},{8,11},{9,8},{10,9... | collective-permute-start | bytes 1376264 | tf_op jit(solution)/shard_map/ppermute | solution.py:44
  146.9 13.6 %collective-permute-start.29 = (bf16[4,4,112,128]{3,2,1,0:T(8,128)(2,1)S(1)}, bf16[4,4,112,128]{3,2,1,0:T(8,128)(2,1)S(1)}, u32[]{:S(2)}, u32[]{:S(2)}) collective-permute-start(bf16[4,4,112,128]{3,2,1,0:T(8,128)(2,1)S(1)} %pad_maximum_fusion.refs_0_), channel_id=1, source_target_pairs={{0,1},{1,2},{2,3},{3,0},{4,5},{5,6},{6,7},{7,4},{8,9},{9,10},{10,1... | collective-permute-start | bytes 1376264 | tf_op jit(solution)/shard_map/ppermute | solution.py:44
  148.5 12.1 %collective-permute-start.37 = (bf16[4,4,112,128]{3,2,1,0:T(8,128)(2,1)S(1)}, bf16[4,4,112,128]{3,2,1,0:T(8,128)(2,1)S(1)}, u32[]{:S(2)}, u32[]{:S(2)}) collective-permute-start(bf16[4,4,112,128]{3,2,1,0:T(8,128)(2,1)S(1)} %pad_maximum_fusion.1.refs_5_), channel_id=1, source_target_pairs={{0,48},{16,0},{32,16},{48,32},{1,49},{17,1},{33,17},{49,33},{2,50}... | collective-permute-start | bytes 1376264 | tf_op jit(solution)/shard_map/ppermute | solution.py:44
  151.9 11.1 %collective-permute-start.36 = (bf16[4,4,112,128]{3,2,1,0:T(8,128)(2,1)S(1)}, bf16[4,4,112,128]{3,2,1,0:T(8,128)(2,1)S(1)}, u32[]{:S(2)}, u32[]{:S(2)}) collective-permute-start(bf16[4,4,112,128]{3,2,1,0:T(8,128)(2,1)S(1)} %pad_maximum_fusion.1.refs_5_), channel_id=1, source_target_pairs={{0,16},{16,32},{32,48},{48,0},{1,17},{17,33},{33,49},{49,1},{2,18}... | collective-permute-start | bytes 1376264 | tf_op jit(solution)/shard_map/ppermute | solution.py:44
  151.9 11.2 %collective-permute-start.24 = (bf16[224,128]{1,0:T(8,128)(2,1)S(1)}, bf16[224,128]{1,0:T(8,128)(2,1)S(1)}, u32[]{:S(2)}, u32[]{:S(2)}) collective-permute-start(bf16[224,128]{1,0:T(8,128)(2,1)S(1)} %get-tuple-element.18), channel_id=1, source_target_pairs={{0,64},{64,0},{1,65},{65,1},{2,66},{66,2},{3,67},{67,3},{4,68},{68... | collective-permute-start | bytes 172040 | tf_op jit(solution)/shard_map/ppermute | solution.py:428
  158.9 8.9 %collective-permute-start.32 = (bf16[2,4,112,128]{3,2,1,0:T(8,128)(2,1)S(1)}, bf16[2,4,112,128]{3,2,1,0:T(8,128)(2,1)S(1)}, u32[]{:S(2)}, u32[]{:S(2)}) collective-permute-start(bf16[2,4,112,128]{3,2,1,0:T(8,128)(2,1)S(1)} %slice.41), channel_id=1, source_target_pairs={{0,3},{1,0},{2,1},{3,2},{4,7},{5,4},{6,5},{7,6},{8,11},{9,8},{10,9... | collective-permute-start | bytes 688136 | tf_op jit(solution)/shard_map/ppermute | solution.py:45
  160.5 7.3 %collective-permute-start.31 = (bf16[2,4,112,128]{3,2,1,0:T(8,128)(2,1)S(1)}, bf16[2,4,112,128]{3,2,1,0:T(8,128)(2,1)S(1)}, u32[]{:S(2)}, u32[]{:S(2)}) collective-permute-start(bf16[2,4,112,128]{3,2,1,0:T(8,128)(2,1)S(1)} %slice.40), channel_id=1, source_target_pairs={{0,1},{1,2},{2,3},{3,0},{4,5},{5,6},{6,7},{7,4},{8,9},{9,10},{10,1... | collective-permute-start | bytes 688136 | tf_op jit(solution)/shard_map/ppermute | solution.py:45
  160.6 7.2 %collective-permute-start.39 = (bf16[2,4,112,128]{3,2,1,0:T(8,128)(2,1)S(1)}, bf16[2,4,112,128]{3,2,1,0:T(8,128)(2,1)S(1)}, u32[]{:S(2)}, u32[]{:S(2)}) collective-permute-start(bf16[2,4,112,128]{3,2,1,0:T(8,128)(2,1)S(1)} %slice.44), channel_id=1, source_target_pairs={{0,48},{16,0},{32,16},{48,32},{1,49},{17,1},{33,17},{49,33},{2,50}... | collective-permute-start | bytes 688136 | tf_op jit(solution)/shard_map/ppermute | solution.py:45
  162.9 7.0 %collective-permute-start.38 = (bf16[2,4,112,128]{3,2,1,0:T(8,128)(2,1)S(1)}, bf16[2,4,112,128]{3,2,1,0:T(8,128)(2,1)S(1)}, u32[]{:S(2)}, u32[]{:S(2)}) collective-permute-start(bf16[2,4,112,128]{3,2,1,0:T(8,128)(2,1)S(1)} %slice.43), channel_id=1, source_target_pairs={{0,16},{16,32},{32,48},{48,0},{1,17},{17,33},{33,49},{49,1},{2,18}... | collective-permute-start | bytes 688136 | tf_op jit(solution)/shard_map/ppermute | solution.py:45
  163.1 4.7 %collective-permute-start.25 = (bf16[2,224,128]{2,1,0:T(8,128)(2,1)S(1)}, bf16[2,224,128]{2,1,0:T(8,128)(2,1)S(1)}, u32[]{:S(2)}, u32[]{:S(2)}) collective-permute-start(bf16[2,224,128]{2,1,0:T(8,128)(2,1)S(1)} %pad_maximum_fusion.4.near_ref), channel_id=1, source_target_pairs={{0,128},{128,0},{1,129},{129,1},{2,130},{130,2},{3,131},{131,3},{4... | collective-permute-start | bytes 344072 | tf_op jit(solution)/shard_map/ppermute | solution.py:430
  (2 other events, 2.1 us)

commit v10 on v9

--- a/solution.py
+++ b/solution.py
@@ -136,7 +136,7 @@
     )(weight, mask, factor)
 
 
-def update_kernel(place_ref, errors_ref, factor_ref, weight_ref, mask_ref, out_ref):
+def update_kernel(place_ref, errors_ref, factor_ref, weight_ref, mask_ref, out_ref, copy_ref):
     updated = weight_ref[...].astype(jnp.float32) - lax.dot_general(
         errors_ref[0],
         factor_ref[...],
@@ -146,15 +146,16 @@
     )
     width = mask_ref.shape[1]
     kept = jnp.where(place_ref[0] == 0, mask_ref[...].astype(jnp.float32), 1.0)
-    out_ref[:, :width] = (updated[:, :width] * kept).astype(jnp.bfloat16)
-    out_ref[:, width:] = updated[:, width:].astype(jnp.bfloat16)
+    for ref in (out_ref, copy_ref):
+        ref[:, :width] = (updated[:, :width] * kept).astype(jnp.bfloat16)
+        ref[:, width:] = updated[:, width:].astype(jnp.bfloat16)
 
 
 def updated_weight(place, errors, factor, weight, mask):
     return pl.pallas_call(
         update_kernel,
         grid=(1,),
-        out_shape=jax.ShapeDtypeStruct(weight.shape, jnp.bfloat16),
+        out_shape=(jax.ShapeDtypeStruct(weight.shape, jnp.bfloat16),) * 2,
         in_specs=[
             SMEM,
             corner((1, *errors.shape[1:])),
@@ -162,7 +163,7 @@
             corner(weight.shape),
             corner(mask.shape),
         ],
-        out_specs=corner(weight.shape),
+        out_specs=(corner(weight.shape),) * 2,
         name="update",
         compiler_params=params(12),
         cost_estimate=pl.CostEstimate(flops=400_000_000, bytes_accessed=2_200_000, transcendentals=0),
@@ -334,8 +335,8 @@
 
     solved = solved_errors(output_weight, prune_mask, inverse_factor)
     errors = lax.all_gather(solved, DP)
-    pruned_weight = updated_weight(place, errors, inverse_factor, output_weight, prune_mask)
-    weight_turned = turned(pruned_weight)
+    pruned_weight, weight_copy = updated_weight(place, errors, inverse_factor, output_weight, prune_mask)
+    weight_turned = turned(weight_copy)
 
     parts = pl.pallas_call(
         project_kernel,

time: 177 us -> 176 us (level)
  no operation moved by 1% of the time
where the time goes in v10:
time: 176 us; the launch traced here: 173 us
  starting transfers between devices  82.1 us (47%)
  waiting for transfers between devices  37.9 us (22%)
  blocking collectives  31.9 us (18%)
  Pallas kernels  15.9 us (9%)
  local copies, waits for them, and re-layouts  4 us (2%)
    all_to_all x2, blocking collectives, copy_for_each(): lax.all_to_all(jnp.broadcast_to(x[None], (size, *x.shape)), axis, 0, 0, t...  24.6 us
    ppermute x21, starting transfers between devices, round_trip(): lax.ppermute(x, axis, [(k, (k + step) % 4) for k in range(4)])  24.1 us
    ppermute x21, waiting for transfers between devices, round_trip(): lax.ppermute(x, axis, [(k, (k + step) % 4) for k in range(4)])  21 us
    ppermute x3, starting transfers between devices, turned(): return lax.ppermute(x, (*DP, 'y'), pairs)  12.4 us
    ppermute x1, starting transfers between devices, body(): got = lax.ppermute(send, 'core', [(0, 1), (1, 0)])  9.76 us
    all_to_all x1, starting transfers between devices, copy_for_each(): lax.all_to_all(jnp.broadcast_to(x[None], (size, *x.shape)), axis, 0, 0, t...  9 us
    all_gather x1, blocking collectives, body(): errors = lax.all_gather(solved, DP)  7.28 us
    all_to_all x1, starting transfers between devices, body(): parts = lax.all_to_all(parts, 'y', 0, 0, tiled=True)  7.21 us
  transfers between devices with their start and end apart: 42, of which 22 were waited for; matrix products, arithmetic and copies ran while one was open for 0% of the time, Pallas kernels for 4%

profile of v10, /device:TPU:1, one launch (start us, length us, event | category | flops | bytes accessed | tf_op | source)
XLA Modules:
  0.0 173.2 jit_solution(13131436392363335246)
XLA Ops:
  0.7 1.6 broadcast_in_dim.17
  2.3 9.0 %all-to-all-start = ((bf16[8,128,128]{2,1,0:T(8,128)(2,1)}), bf16[8,128,128]{2,1,0:T(8,128)(2,1)S(1)}, u32[]{:S(2)}, u32[]{:S(2)}) async-start(bf16[8,128,128]{2,1,0:T(8,128)(2,1)} %broadcast_in_dim.17), calls=%async_computation | async-start | bytes 524288 | tf_op jit(solution)/shard_map/all_to_all | solution.py:25
  11.3 3.7 %solve.1 = f32[128,128]{1,0:T(8,128)} custom-call(bf16[128,2048]{1,0:T(8,128)(2,1)} %weight_ref.1, s32[128,128]{1,0:T(8,128)} %mask_ref.1, f32[128,2048]{1,0:T(8,128)} %factor_ref.1), custom_call_target="tpu_custom_call" | custom-call | flops 20000000 | bytes 300000 | tf_op jit(solution)/shard_map/solve/pallas_call | solution.py:122
  15.0 7.3 %all-gather = f32[512,128]{1,0:T(8,128)S(1)} all-gather(f32[128,128]{1,0:T(8,128)} %solve.1), channel_id=2, replica_groups=mesh['z_low'=2,'core'=2,'y'=4,'z_high'=4,'x'=4] {'z_low','core'}, dimensions={0}, use_global_device_ids=true | all-gather | bytes 327680 | tf_op jit(solution)/shard_map/all_gather | solution.py:337
  22.3 1.8 %update.1 = (bf16[128,2048]{1,0:T(8,128)(2,1)}, bf16[128,2048]{1,0:T(8,128)(2,1)S(1)}) custom-call(s32[1]{0:T(128)} %bitcast.place_ref, f32[4,128,128]{2,1,0:T(8,128)S(1)} %bitcast.38, f32[128,2048]{1,0:T(8,128)S(1)} %copy-done, bf16[128,2048]{1,0:T(8,128)(2,1)S(1)} %copy-done.1, s32[128,128]{1,0:T(8,128)S(1)} %copy-done.3), custom_call_target="tpu_custom_call" | custom-call | flops 400000000 | bytes 2200000 | tf_op jit(solution)/shard_map/update/pallas_call | solution.py:155
  24.1 2.7 %collective-permute-start.2 = (bf16[8,128,128]{2,1,0:T(8,128)(2,1)S(1)}, bf16[8,128,128]{2,1,0:T(8,128)(2,1)S(1)}, u32[]{:S(2)}, u32[]{:S(2)}) collective-permute-start(bf16[8,128,128]{2,1,0:T(8,128)(2,1)S(1)} %all-to-all-done.refs_0_), channel_id=1, source_target_pairs={{0,2},{1,3},{2,0},{3,1},{4,6},{5,7},{6,4},{7,5},{8,10},{9,11},{10,... | collective-permute-start | bytes 786440 | tf_op jit(solution)/shard_map/ppermute | solution.py:36
  26.9 3.5 %collective-permute-start.7 = (bf16[128,2048]{1,0:T(8,128)(2,1)S(1)}, bf16[128,2048]{1,0:T(8,128)(2,1)S(1)}, u32[]{:S(2)}, u32[]{:S(2)}) collective-permute-start(bf16[128,2048]{1,0:T(8,128)(2,1)S(1)} %get-tuple-element.14), channel_id=1, source_target_pairs={{0,0},{16,64},{32,128},{48,192},{64,16},{80,80},{96,144},{112,208}... | collective-permute-start | bytes 1572872 | tf_op jit(solution)/shard_map/ppermute | solution.py:30
  31.9 1.4 collective-permute-done.2.refs_3_
  33.3 1.1 collective-permute-start.6
  34.4 4.6 %collective-permute-done.1.refs_2_ = bf16[8,128,128]{2,1,0:T(8,128)(2,1)S(1)} collective-permute-done((bf16[8,128,128]{2,1,0:T(8,128)(2,1)S(1)}, bf16[8,128,128]{2,1,0:T(8,128)(2,1)S(1)}, u32[]{:S(2)}, u32[]{:S(2)}) %collective-permute-start.1) | collective-permute-done | bytes 262176 | tf_op jit(solution)/shard_map/ppermute | solution.py:36
  39.1 1.0 collective-permute-start.5
  41.6 1.9 %project.1 = bf16[4,128,128]{2,1,0:T(8,128)(2,1)} custom-call(s32[4]{0:T(128)S(1)} %pad_add_fusion.1.from_ref, s32[1]{0:T(128)} %bitcast.7.core_ref, bf16[8,128,128]{2,1,0:T(8,128)(2,1)S(1)} %all-to-all-done.refs_0_, bf16[8,128,128]{2,1,0:T(8,128)(2,1)S(1)} %collective-permute-done.refs_1_, bf16[8,128,128]{2,1,0:T(8,128)(2,1)S(1)} %collective-permute-done.1.refs_2_, ...), custom_call_target="tpu_custom_call" | custom-call | flops 268000000 | bytes 2700000 | tf_op jit(solution)/shard_map/project/pallas_call | solution.py:341
  43.5 7.2 %all-to-all-start.1 = ((bf16[4,128,128]{2,1,0:T(8,128)(2,1)}), bf16[4,128,128]{2,1,0:T(8,128)(2,1)S(1)}, u32[]{:S(2)}, u32[]{:S(2)}) async-start(bf16[4,128,128]{2,1,0:T(8,128)(2,1)} %project.1), calls=%async_computation.1 | async-start | bytes 262144 | tf_op jit(solution)/shard_map/all_to_all | solution.py:350
  50.8 4.8 %collective-permute-start.8 = (bf16[144,128]{1,0:T(8,128)(2,1)S(1)}, bf16[144,128]{1,0:T(8,128)(2,1)S(1)}, u32[]{:S(2)}, u32[]{:S(2)}) collective-permute-start(bf16[144,128]{1,0:T(8,128)(2,1)S(1)} %pad_maximum_fusion.5), channel_id=1, source_target_pairs={{0,0},{16,64},{32,128},{48,192},{64,16},{80,80},{96,144},{112,208}... | collective-permute-start | bytes 110600 | tf_op jit(solution)/shard_map/ppermute | solution.py:30
  55.6 1.9 %collective-permute-done.8.residual_ref = bf16[144,128]{1,0:T(8,128)(2,1)S(1)} collective-permute-done((bf16[144,128]{1,0:T(8,128)(2,1)S(1)}, bf16[144,128]{1,0:T(8,128)(2,1)S(1)}, u32[]{:S(2)}, u32[]{:S(2)}) %collective-permute-start.8) | collective-permute-done | bytes 36896 | tf_op jit(solution)/shard_map/ppermute | solution.py:30
  58.4 13.5 %all_to_all.20 = bf16[4,136,128]{2,1,0:T(8,128)(2,1)S(1)} all-to-all(bf16[4,136,128]{2,1,0:T(8,128)(2,1)S(1)} %broadcast_in_dim.38), channel_id=1, replica_groups=mesh['z_low'=2,'core'=2,'y'=4,'z_high'=4,'x'=4] {'z_high'}, dimensions={0} | all-to-all | bytes 278528 | tf_op jit(solution)/shard_map/all_to_all | solution.py:25
  71.9 3.5 %collective-permute-start.10 = (bf16[4,64,128]{2,1,0:T(8,128)(2,1)S(1)}, bf16[4,64,128]{2,1,0:T(8,128)(2,1)S(1)}, u32[]{:S(2)}, u32[]{:S(2)}) collective-permute-start(bf16[4,64,128]{2,1,0:T(8,128)(2,1)S(1)} %get-tuple-element.30), channel_id=1, source_target_pairs={{0,48},{16,0},{32,16},{48,32},{1,49},{17,1},{33,17},{49,33},{2,50}... | collective-permute-start | bytes 196616 | tf_op jit(solution)/shard_map/ppermute | solution.py:36
  75.4 1.3 collective-permute-start.11
  76.7 3.7 %collective-permute-done.9 = bf16[4,64,128]{2,1,0:T(8,128)(2,1)S(1)} collective-permute-done((bf16[4,64,128]{2,1,0:T(8,128)(2,1)S(1)}, bf16[4,64,128]{2,1,0:T(8,128)(2,1)S(1)}, u32[]{:S(2)}, u32[]{:S(2)}) %collective-permute-start.9) | collective-permute-done | bytes 65568 | tf_op jit(solution)/shard_map/ppermute | solution.py:36
  80.8 2.7 %collective-permute-start.16 = (bf16[4,72,128]{2,1,0:T(8,128)(2,1)S(1)}, bf16[4,72,128]{2,1,0:T(8,128)(2,1)S(1)}, u32[]{:S(2)}, u32[]{:S(2)}) collective-permute-start(bf16[4,72,128]{2,1,0:T(8,128)(2,1)S(1)} %get-tuple-element.28), channel_id=1, source_target_pairs={{0,3},{1,0},{2,1},{3,2},{4,7},{5,4},{6,5},{7,6},{8,11},{9,8},{10,9... | collective-permute-start | bytes 221192 | tf_op jit(solution)/shard_map/ppermute | solution.py:36
  83.6 1.7 collective-permute-start.17
  85.3 1.3 collective-permute-done.16
  86.6 1.5 collective-permute-done.15
  89.9 1.5 collective-permute-start.19
  91.8 2.5 %collective-permute-start.13 = (bf16[4,4,64,128]{3,2,1,0:T(8,128)(2,1)S(1)}, bf16[4,4,64,128]{3,2,1,0:T(8,128)(2,1)}, u32[]{:S(2)}, u32[]{:S(2)}) collective-permute-start(bf16[4,4,64,128]{3,2,1,0:T(8,128)(2,1)S(1)} %pad_maximum_fusion.3.refs_0_), channel_id=1, source_target_pairs={{0,3},{1,0},{2,1},{3,2},{4,7},{5,4},{6,5},{7,6},{8,11},{9,8},{10,9... | collective-permute-start | bytes 786440 | tf_op jit(solution)/shard_map/ppermute | solution.py:36
  94.4 1.5 copy-done.2
  95.9 1.0 order.1.refs_8_
  97.7 3.4 %collective-permute-done.12.refs_1_ = bf16[4,4,64,128]{3,2,1,0:T(8,128)(2,1)} collective-permute-done((bf16[4,4,64,128]{3,2,1,0:T(8,128)(2,1)S(1)}, bf16[4,4,64,128]{3,2,1,0:T(8,128)(2,1)}, u32[]{:S(2)}, u32[]{:S(2)}) %collective-permute-start.12) | collective-permute-done | bytes 262176 | tf_op jit(solution)/shard_map/ppermute | solution.py:36
  101.1 3.2 %gate_up.1 = (f32[2,464,128]{2,1,0:T(8,128)S(1)}, bf16[2,464,128]{2,1,0:T(8,128)(2,1)S(1)}) custom-call(s32[4]{0:T(128)S(1)} %pad_add_fusion.group_ref, s32[1]{0:T(128)} %bitcast.7.core_ref, bf16[4,4,64,128]{3,2,1,0:T(8,128)(2,1)S(1)} %pad_maximum_fusion.3.refs_0_, bf16[4,4,64,128]{3,2,1,0:T(8,128)(2,1)} %collective-permute-done.12.refs_1_, ...), custom_call_target="tpu_custom_call" | custom-call | flops 940000000 | bytes 4300000 | tf_op jit(solution)/shard_map/gate_up/pallas_call | solution.py:375
  104.3 9.8 %collective-permute-start.21 = (bf16[2,464,128]{2,1,0:T(8,128)(2,1)S(1)}, bf16[2,464,128]{2,1,0:T(8,128)(2,1)S(1)}, u32[]{:S(2)}, u32[]{:S(2)}) collective-permute-start(bf16[2,464,128]{2,1,0:T(8,128)(2,1)S(1)} %get-tuple-element.17), channel_id=1, source_target_pairs={{0,64},{64,0},{1,65},{65,1},{2,66},{66,2},{3,67},{67,3},{4,68},{68... | collective-permute-start | bytes 712712 | tf_op jit(solution)/shard_map/ppermute | solution.py:390
  114.1 1.1 collective-permute-done.21.got_ref
  115.3 4.4 %collective-permute-done.22.got_ref = bf16[464,128]{1,0:T(8,128)(2,1)S(1)} collective-permute-done((bf16[464,128]{1,0:T(8,128)(2,1)S(1)}, bf16[464,128]{1,0:T(8,128)(2,1)S(1)}, u32[]{:S(2)}, u32[]{:S(2)}) %collective-permute-start.22) | collective-permute-done | bytes 118816 | tf_op jit(solution)/shard_map/ppermute | solution.py:403
  119.8 4.0 %collective-permute-start.23 = (bf16[352,128]{1,0:T(8,128)(2,1)S(1)}, bf16[352,128]{1,0:T(8,128)(2,1)S(1)}, u32[]{:S(2)}, u32[]{:S(2)}) collective-permute-start(bf16[352,128]{1,0:T(8,128)(2,1)S(1)} %get-tuple-element.21), channel_id=1, source_target_pairs={{0,0},{16,64},{32,128},{48,192},{64,16},{80,80},{96,144},{112,208}... | collective-permute-start | bytes 270344 | tf_op jit(solution)/shard_map/ppermute | solution.py:30
  123.9 3.2 %collective-permute-done.23.in_ref = bf16[352,128]{1,0:T(8,128)(2,1)S(1)} collective-permute-done((bf16[352,128]{1,0:T(8,128)(2,1)S(1)}, bf16[352,128]{1,0:T(8,128)(2,1)S(1)}, u32[]{:S(2)}, u32[]{:S(2)}) %collective-permute-start.23) | collective-permute-done | bytes 90144 | tf_op jit(solution)/shard_map/ppermute | solution.py:30
  127.1 11.1 %all_to_all.21 = bf16[4,224,128]{2,1,0:T(8,128)(2,1)S(1)} all-to-all(bf16[4,224,128]{2,1,0:T(8,128)(2,1)S(1)} %broadcast_in_dim.39), channel_id=1, replica_groups=mesh['z_low'=2,'core'=2,'y'=4,'z_high'=4,'x'=4] {'z_high'}, dimensions={0} | all-to-all | bytes 458752 | tf_op jit(solution)/shard_map/all_to_all | solution.py:25
  138.2 2.1 %collective-permute-start.27 = (bf16[4,112,128]{2,1,0:T(8,128)(2,1)S(1)}, bf16[4,112,128]{2,1,0:T(8,128)(2,1)S(1)}, u32[]{:S(2)}, u32[]{:S(2)}) collective-permute-start(bf16[4,112,128]{2,1,0:T(8,128)(2,1)S(1)} %get-tuple-element.26), channel_id=1, source_target_pairs={{0,48},{16,0},{32,16},{48,32},{1,49},{17,1},{33,17},{49,33},{2,50}... | collective-permute-start | bytes 344072 | tf_op jit(solution)/shard_map/ppermute | solution.py:36
  140.3 1.3 collective-permute-start.28
  141.7 1.3 collective-permute-start.33
  143.0 3.3 %collective-permute-done.26 = bf16[4,112,128]{2,1,0:T(8,128)(2,1)S(1)} collective-permute-done((bf16[4,112,128]{2,1,0:T(8,128)(2,1)S(1)}, bf16[4,112,128]{2,1,0:T(8,128)(2,1)S(1)}, u32[]{:S(2)}, u32[]{:S(2)}) %collective-permute-start.26) | collective-permute-done | bytes 114720 | tf_op jit(solution)/shard_map/ppermute | solution.py:36
  146.7 1.3 collective-permute-start.29
  148.2 3.4 %collective-permute-start.37 = (bf16[4,4,112,128]{3,2,1,0:T(8,128)(2,1)S(1)}, bf16[4,4,112,128]{3,2,1,0:T(8,128)(2,1)S(1)}, u32[]{:S(2)}, u32[]{:S(2)}) collective-permute-start(bf16[4,4,112,128]{3,2,1,0:T(8,128)(2,1)S(1)} %pad_maximum_fusion.1.refs_5_), channel_id=1, source_target_pairs={{0,48},{16,0},{32,16},{48,32},{1,49},{17,1},{33,17},{49,33},{2,50}... | collective-permute-start | bytes 1376264 | tf_op jit(solution)/shard_map/ppermute | solution.py:44
  151.7 6.5 %collective-permute-start.24 = (bf16[224,128]{1,0:T(8,128)(2,1)S(1)}, bf16[224,128]{1,0:T(8,128)(2,1)S(1)}, u32[]{:S(2)}, u32[]{:S(2)}) collective-permute-start(bf16[224,128]{1,0:T(8,128)(2,1)S(1)} %get-tuple-element.22), channel_id=1, source_target_pairs={{0,64},{64,0},{1,65},{65,1},{2,66},{66,2},{3,67},{67,3},{4,68},{68... | collective-permute-start | bytes 172040 | tf_op jit(solution)/shard_map/ppermute | solution.py:429
  158.7 1.2 collective-permute-start.32
  160.4 2.3 %collective-permute-start.39 = (bf16[2,4,112,128]{3,2,1,0:T(8,128)(2,1)S(1)}, bf16[2,4,112,128]{3,2,1,0:T(8,128)(2,1)S(1)}, u32[]{:S(2)}, u32[]{:S(2)}) collective-permute-start(bf16[2,4,112,128]{3,2,1,0:T(8,128)(2,1)S(1)} %slice.44), channel_id=1, source_target_pairs={{0,48},{16,0},{32,16},{48,32},{1,49},{17,1},{33,17},{49,33},{2,50}... | collective-permute-start | bytes 688136 | tf_op jit(solution)/shard_map/ppermute | solution.py:45
  162.9 2.3 %collective-permute-start.25 = (bf16[2,224,128]{2,1,0:T(8,128)(2,1)S(1)}, bf16[2,224,128]{2,1,0:T(8,128)(2,1)S(1)}, u32[]{:S(2)}, u32[]{:S(2)}) collective-permute-start(bf16[2,224,128]{2,1,0:T(8,128)(2,1)S(1)} %pad_maximum_fusion.4.near_ref), channel_id=1, source_target_pairs={{0,128},{128,0},{1,129},{129,1},{2,130},{130,2},{3,131},{131,3},{4... | collective-permute-start | bytes 344072 | tf_op jit(solution)/shard_map/ppermute | solution.py:431
  165.8 1.9 %collective-permute-done.25.far_ref = bf16[2,224,128]{2,1,0:T(8,128)(2,1)S(1)} collective-permute-done((bf16[2,224,128]{2,1,0:T(8,128)(2,1)S(1)}, bf16[2,224,128]{2,1,0:T(8,128)(2,1)S(1)}, u32[]{:S(2)}, u32[]{:S(2)}) %collective-permute-start.25) | collective-permute-done | bytes 114720 | tf_op jit(solution)/shard_map/ppermute | solution.py:431
  167.6 2.1 %collective-permute-done.38.refs_8_ = bf16[2,4,112,128]{3,2,1,0:T(8,128)(2,1)S(1)} collective-permute-done((bf16[2,4,112,128]{3,2,1,0:T(8,128)(2,1)S(1)}, bf16[2,4,112,128]{3,2,1,0:T(8,128)(2,1)S(1)}, u32[]{:S(2)}, u32[]{:S(2)}) %collective-permute-start.38) | collective-permute-done | bytes 229408 | tf_op jit(solution)/shard_map/ppermute | solution.py:45
  169.7 3.3 %hessian.1 = f32[224,3584]{1,0:T(8,128)} custom-call(s32[4]{0:T(128)S(1)} %pad_add_fusion.1.from_ref, s32[4]{0:T(128)S(1)} %pad_add_fusion.group_ref, s32[1]{0:T(128)} %bitcast.place_ref, bf16[2,224,128]{2,1,0:T(8,128)(2,1)S(1)} %pad_maximum_fusion.4.near_ref, bf16[2,224,128]{2,1,0:T(8,128)(2,1)S(1)} %collective-permute-done.25.far_ref, ...), custom_call_target="tpu_custom_call" | custom-call | flops 822000000 | bytes 7100000 | tf_op jit(solution)/shard_map/hessian/pallas_call | solution.py:432
  (85 shorter events, 10.3 us)
Async XLA Ops:
  0.6 21.7 %copy-start = (f32[128,2048]{1,0:T(8,128)S(1)}, f32[128,2048]{1,0:T(8,128)}, u32[]{:S(2)}) copy-start(f32[128,2048]{1,0:T(8,128)} %factor_ref.1) | copy-start | bytes 3145732
  0.6 21.7 %copy-start.3 = (s32[128,128]{1,0:T(8,128)S(1)}, s32[128,128]{1,0:T(8,128)}, u32[]{:S(2)}) copy-start(s32[128,128]{1,0:T(8,128)} %mask_ref.1) | copy-start | bytes 196612
  0.7 21.6 %copy-start.1 = (bf16[128,2048]{1,0:T(8,128)(2,1)S(1)}, bf16[128,2048]{1,0:T(8,128)(2,1)}, u32[]{:S(2)}) copy-start(bf16[128,2048]{1,0:T(8,128)(2,1)} %weight_ref.1) | copy-start | bytes 1572868
  2.3 21.8 %all-to-all-start = ((bf16[8,128,128]{2,1,0:T(8,128)(2,1)}), bf16[8,128,128]{2,1,0:T(8,128)(2,1)S(1)}, u32[]{:S(2)}, u32[]{:S(2)}) async-start(bf16[8,128,128]{2,1,0:T(8,128)(2,1)} %broadcast_in_dim.17), calls=%async_computation | async-start | bytes 524288 | tf_op jit(solution)/shard_map/all_to_all | solution.py:25
  24.1 26.7 %copy-start.7 = (bf16[128]{0:T(256)(128)(2,1)S(1)}, bf16[128]{0:T(256)(128)(2,1)}, u32[]{:S(2)}) copy-start(bf16[128]{0:T(256)(128)(2,1)} %param.12) | copy-start | bytes 772
  24.1 26.7 %copy-start.6 = (bf16[128,128]{1,0:T(8,128)(2,1)S(1)}, bf16[128,128]{1,0:T(8,128)(2,1)}, u32[]{:S(2)}) copy-start(bf16[128,128]{1,0:T(8,128)(2,1)} %param.8) | copy-start | bytes 98308
  24.1 9.2 %collective-permute-start.2 = (bf16[8,128,128]{2,1,0:T(8,128)(2,1)S(1)}, bf16[8,128,128]{2,1,0:T(8,128)(2,1)S(1)}, u32[]{:S(2)}, u32[]{:S(2)}) collective-permute-start(bf16[8,128,128]{2,1,0:T(8,128)(2,1)S(1)} %all-to-all-done.refs_0_), channel_id=1, source_target_pairs={{0,2},{1,3},{2,0},{3,1},{4,6},{5,7},{6,4},{7,5},{8,10},{9,11},{10,... | collective-permute-start | bytes 786440 | tf_op jit(solution)/shard_map/ppermute | solution.py:36
  26.9 13.9 %collective-permute-start.7 = (bf16[128,2048]{1,0:T(8,128)(2,1)S(1)}, bf16[128,2048]{1,0:T(8,128)(2,1)S(1)}, u32[]{:S(2)}, u32[]{:S(2)}) collective-permute-start(bf16[128,2048]{1,0:T(8,128)(2,1)S(1)} %get-tuple-element.14), channel_id=1, source_target_pairs={{0,0},{16,64},{32,128},{48,192},{64,16},{80,80},{96,144},{112,208}... | collective-permute-start | bytes 1572872 | tf_op jit(solution)/shard_map/ppermute | solution.py:30
  30.4 8.7 %collective-permute-start.1 = (bf16[8,128,128]{2,1,0:T(8,128)(2,1)S(1)}, bf16[8,128,128]{2,1,0:T(8,128)(2,1)S(1)}, u32[]{:S(2)}, u32[]{:S(2)}) collective-permute-start(bf16[8,128,128]{2,1,0:T(8,128)(2,1)S(1)} %all-to-all-done.refs_0_), channel_id=1, source_target_pairs={{0,3},{1,0},{2,1},{3,2},{4,7},{5,4},{6,5},{7,6},{8,11},{9,8},{10,9... | collective-permute-start | bytes 786440 | tf_op jit(solution)/shard_map/ppermute | solution.py:36
  31.3 8.8 %collective-permute-start = (bf16[8,128,128]{2,1,0:T(8,128)(2,1)S(1)}, bf16[8,128,128]{2,1,0:T(8,128)(2,1)S(1)}, u32[]{:S(2)}, u32[]{:S(2)}) collective-permute-start(bf16[8,128,128]{2,1,0:T(8,128)(2,1)S(1)} %all-to-all-done.refs_0_), channel_id=1, source_target_pairs={{0,1},{1,2},{2,3},{3,0},{4,5},{5,6},{6,7},{7,4},{8,9},{9,10},{10,1... | collective-permute-start | bytes 786440 | tf_op jit(solution)/shard_map/ppermute | solution.py:36
  31.9 8.9 %collective-permute-start.3 = (bf16[8,128,128]{2,1,0:T(8,128)(2,1)S(1)}, bf16[8,128,128]{2,1,0:T(8,128)(2,1)S(1)}, u32[]{:S(2)}, u32[]{:S(2)}) collective-permute-start(bf16[8,128,128]{2,1,0:T(8,128)(2,1)S(1)} %all-to-all-done.refs_0_), channel_id=1, source_target_pairs={{0,64},{64,0},{1,65},{65,1},{2,66},{66,2},{3,67},{67,3},{4,68},{68... | collective-permute-start | bytes 786440 | tf_op jit(solution)/shard_map/ppermute | solution.py:332
  33.3 7.5 %collective-permute-start.6 = (bf16[8,128,128]{2,1,0:T(8,128)(2,1)S(1)}, bf16[8,128,128]{2,1,0:T(8,128)(2,1)S(1)}, u32[]{:S(2)}, u32[]{:S(2)}) collective-permute-start(bf16[8,128,128]{2,1,0:T(8,128)(2,1)S(1)} %collective-permute-done.2.refs_3_), channel_id=1, source_target_pairs={{0,64},{64,0},{1,65},{65,1},{2,66},{66,2},{3,67},{67,3},{4,68},{68... | collective-permute-start | bytes 786440 | tf_op jit(solution)/shard_map/ppermute | solution.py:332
  39.1 2.2 %collective-permute-start.5 = (bf16[8,128,128]{2,1,0:T(8,128)(2,1)S(1)}, bf16[8,128,128]{2,1,0:T(8,128)(2,1)S(1)}, u32[]{:S(2)}, u32[]{:S(2)}) collective-permute-start(bf16[8,128,128]{2,1,0:T(8,128)(2,1)S(1)} %collective-permute-done.1.refs_2_), channel_id=1, source_target_pairs={{0,64},{64,0},{1,65},{65,1},{2,66},{66,2},{3,67},{67,3},{4,68},{68... | collective-permute-start | bytes 786440 | tf_op jit(solution)/shard_map/ppermute | solution.py:332
  40.1 1.5 collective-permute-start.4
  43.5 14.0 %all-to-all-start.1 = ((bf16[4,128,128]{2,1,0:T(8,128)(2,1)}), bf16[4,128,128]{2,1,0:T(8,128)(2,1)S(1)}, u32[]{:S(2)}, u32[]{:S(2)}) async-start(bf16[4,128,128]{2,1,0:T(8,128)(2,1)} %project.1), calls=%async_computation.1 | async-start | bytes 262144 | tf_op jit(solution)/shard_map/all_to_all | solution.py:350
  50.8 6.7 %collective-permute-start.8 = (bf16[144,128]{1,0:T(8,128)(2,1)S(1)}, bf16[144,128]{1,0:T(8,128)(2,1)S(1)}, u32[]{:S(2)}, u32[]{:S(2)}) collective-permute-start(bf16[144,128]{1,0:T(8,128)(2,1)S(1)} %pad_maximum_fusion.5), channel_id=1, source_target_pairs={{0,0},{16,64},{32,128},{48,192},{64,16},{80,80},{96,144},{112,208}... | collective-permute-start | bytes 110600 | tf_op jit(solution)/shard_map/ppermute | solution.py:30
  71.9 4.8 %collective-permute-start.10 = (bf16[4,64,128]{2,1,0:T(8,128)(2,1)S(1)}, bf16[4,64,128]{2,1,0:T(8,128)(2,1)S(1)}, u32[]{:S(2)}, u32[]{:S(2)}) collective-permute-start(bf16[4,64,128]{2,1,0:T(8,128)(2,1)S(1)} %get-tuple-element.30), channel_id=1, source_target_pairs={{0,48},{16,0},{32,16},{48,32},{1,49},{17,1},{33,17},{49,33},{2,50}... | collective-permute-start | bytes 196616 | tf_op jit(solution)/shard_map/ppermute | solution.py:36
  75.4 5.0 %collective-permute-start.9 = (bf16[4,64,128]{2,1,0:T(8,128)(2,1)S(1)}, bf16[4,64,128]{2,1,0:T(8,128)(2,1)S(1)}, u32[]{:S(2)}, u32[]{:S(2)}) collective-permute-start(bf16[4,64,128]{2,1,0:T(8,128)(2,1)S(1)} %get-tuple-element.30), channel_id=1, source_target_pairs={{0,16},{16,32},{32,48},{48,0},{1,17},{17,33},{33,49},{49,1},{2,18}... | collective-permute-start | bytes 196616 | tf_op jit(solution)/shard_map/ppermute | solution.py:36
  75.4 5.0 %collective-permute-start.11 = (bf16[4,64,128]{2,1,0:T(8,128)(2,1)S(1)}, bf16[4,64,128]{2,1,0:T(8,128)(2,1)S(1)}, u32[]{:S(2)}, u32[]{:S(2)}) collective-permute-start(bf16[4,64,128]{2,1,0:T(8,128)(2,1)S(1)} %get-tuple-element.30), channel_id=1, source_target_pairs={{0,32},{16,48},{32,0},{48,16},{1,33},{17,49},{33,1},{49,17},{2,34}... | collective-permute-start | bytes 196616 | tf_op jit(solution)/shard_map/ppermute | solution.py:36
  80.5 13.9 %collective-permute-start.14 = (bf16[4,4,64,128]{3,2,1,0:T(8,128)(2,1)S(1)}, bf16[4,4,64,128]{3,2,1,0:T(8,128)(2,1)S(1)}, u32[]{:S(2)}, u32[]{:S(2)}) collective-permute-start(bf16[4,4,64,128]{3,2,1,0:T(8,128)(2,1)S(1)} %pad_maximum_fusion.3.refs_0_), channel_id=1, source_target_pairs={{0,2},{1,3},{2,0},{3,1},{4,6},{5,7},{6,4},{7,5},{8,10},{9,11},{10,... | collective-permute-start | bytes 786440 | tf_op jit(solution)/shard_map/ppermute | solution.py:36
  80.8 5.7 %collective-permute-start.16 = (bf16[4,72,128]{2,1,0:T(8,128)(2,1)S(1)}, bf16[4,72,128]{2,1,0:T(8,128)(2,1)S(1)}, u32[]{:S(2)}, u32[]{:S(2)}) collective-permute-start(bf16[4,72,128]{2,1,0:T(8,128)(2,1)S(1)} %get-tuple-element.28), channel_id=1, source_target_pairs={{0,3},{1,0},{2,1},{3,2},{4,7},{5,4},{6,5},{7,6},{8,11},{9,8},{10,9... | collective-permute-start | bytes 221192 | tf_op jit(solution)/shard_map/ppermute | solution.py:36
  83.6 4.5 %collective-permute-start.15 = (bf16[4,72,128]{2,1,0:T(8,128)(2,1)S(1)}, bf16[4,72,128]{2,1,0:T(8,128)(2,1)S(1)}, u32[]{:S(2)}, u32[]{:S(2)}) collective-permute-start(bf16[4,72,128]{2,1,0:T(8,128)(2,1)S(1)} %get-tuple-element.28), channel_id=1, source_target_pairs={{0,1},{1,2},{2,3},{3,0},{4,5},{5,6},{6,7},{7,4},{8,9},{9,10},{10,1... | collective-permute-start | bytes 221192 | tf_op jit(solution)/shard_map/ppermute | solution.py:36
  83.6 5.3 %collective-permute-start.17 = (bf16[4,72,128]{2,1,0:T(8,128)(2,1)S(1)}, bf16[4,72,128]{2,1,0:T(8,128)(2,1)S(1)}, u32[]{:S(2)}, u32[]{:S(2)}) collective-permute-start(bf16[4,72,128]{2,1,0:T(8,128)(2,1)S(1)} %get-tuple-element.28), channel_id=1, source_target_pairs={{0,2},{1,3},{2,0},{3,1},{4,6},{5,7},{6,4},{7,5},{8,10},{9,11},{10,... | collective-permute-start | bytes 221192 | tf_op jit(solution)/shard_map/ppermute | solution.py:36
  88.9 12.2 %collective-permute-start.20 = (bf16[4,4,72,128]{3,2,1,0:T(8,128)(2,1)S(1)}, bf16[4,4,72,128]{3,2,1,0:T(8,128)(2,1)S(1)}, u32[]{:S(2)}, u32[]{:S(2)}) collective-permute-start(bf16[4,4,72,128]{3,2,1,0:T(8,128)(2,1)S(1)} %pad_maximum_fusion.2.refs_4_), channel_id=1, source_target_pairs={{0,32},{16,48},{32,0},{48,16},{1,33},{17,49},{33,1},{49,17},{2,34}... | collective-permute-start | bytes 884744 | tf_op jit(solution)/shard_map/ppermute | solution.py:36
  89.9 11.2 %collective-permute-start.19 = (bf16[4,4,72,128]{3,2,1,0:T(8,128)(2,1)S(1)}, bf16[4,4,72,128]{3,2,1,0:T(8,128)(2,1)S(1)}, u32[]{:S(2)}, u32[]{:S(2)}) collective-permute-start(bf16[4,4,72,128]{3,2,1,0:T(8,128)(2,1)S(1)} %pad_maximum_fusion.2.refs_4_), channel_id=1, source_target_pairs={{0,48},{16,0},{32,16},{48,32},{1,49},{17,1},{33,17},{49,33},{2,50}... | collective-permute-start | bytes 884744 | tf_op jit(solution)/shard_map/ppermute | solution.py:36
  91.4 9.7 %collective-permute-start.18 = (bf16[4,4,72,128]{3,2,1,0:T(8,128)(2,1)S(1)}, bf16[4,4,72,128]{3,2,1,0:T(8,128)(2,1)S(1)}, u32[]{:S(2)}, u32[]{:S(2)}) collective-permute-start(bf16[4,4,72,128]{3,2,1,0:T(8,128)(2,1)S(1)} %pad_maximum_fusion.2.refs_4_), channel_id=1, source_target_pairs={{0,16},{16,32},{32,48},{48,0},{1,17},{17,33},{33,49},{49,1},{2,18}... | collective-permute-start | bytes 884744 | tf_op jit(solution)/shard_map/ppermute | solution.py:36
  91.8 5.8 %collective-permute-start.13 = (bf16[4,4,64,128]{3,2,1,0:T(8,128)(2,1)S(1)}, bf16[4,4,64,128]{3,2,1,0:T(8,128)(2,1)}, u32[]{:S(2)}, u32[]{:S(2)}) collective-permute-start(bf16[4,4,64,128]{3,2,1,0:T(8,128)(2,1)S(1)} %pad_maximum_fusion.3.refs_0_), channel_id=1, source_target_pairs={{0,3},{1,0},{2,1},{3,2},{4,7},{5,4},{6,5},{7,6},{8,11},{9,8},{10,9... | collective-permute-start | bytes 786440 | tf_op jit(solution)/shard_map/ppermute | solution.py:36
  94.4 6.7 %collective-permute-start.12 = (bf16[4,4,64,128]{3,2,1,0:T(8,128)(2,1)S(1)}, bf16[4,4,64,128]{3,2,1,0:T(8,128)(2,1)}, u32[]{:S(2)}, u32[]{:S(2)}) collective-permute-start(bf16[4,4,64,128]{3,2,1,0:T(8,128)(2,1)S(1)} %pad_maximum_fusion.3.refs_0_), channel_id=1, source_target_pairs={{0,1},{1,2},{2,3},{3,0},{4,5},{5,6},{6,7},{7,4},{8,9},{9,10},{10,1... | collective-permute-start | bytes 786440 | tf_op jit(solution)/shard_map/ppermute | solution.py:36
  97.0 22.8 %copy-start.5 = (bf16[128,128]{1,0:T(8,128)(2,1)S(1)}, bf16[128,128]{1,0:T(8,128)(2,1)}, u32[]{:S(2)}) copy-start(bf16[128,128]{1,0:T(8,128)(2,1)} %copy-done.4) | copy-start | bytes 98308
  104.3 10.9 %collective-permute-start.21 = (bf16[2,464,128]{2,1,0:T(8,128)(2,1)S(1)}, bf16[2,464,128]{2,1,0:T(8,128)(2,1)S(1)}, u32[]{:S(2)}, u32[]{:S(2)}) collective-permute-start(bf16[2,464,128]{2,1,0:T(8,128)(2,1)S(1)} %get-tuple-element.17), channel_id=1, source_target_pairs={{0,64},{64,0},{1,65},{65,1},{2,66},{66,2},{3,67},{67,3},{4,68},{68... | collective-permute-start | bytes 712712 | tf_op jit(solution)/shard_map/ppermute | solution.py:390
  115.2 4.5 %collective-permute-start.22 = (bf16[464,128]{1,0:T(8,128)(2,1)S(1)}, bf16[464,128]{1,0:T(8,128)(2,1)S(1)}, u32[]{:S(2)}, u32[]{:S(2)}) collective-permute-start(bf16[464,128]{1,0:T(8,128)(2,1)S(1)} %get-tuple-element.19), channel_id=1, source_target_pairs={{0,128},{128,0},{1,129},{129,1},{2,130},{130,2},{3,131},{131,3},{4... | collective-permute-start | bytes 356360 | tf_op jit(solution)/shard_map/ppermute | solution.py:403
  119.8 7.2 %collective-permute-start.23 = (bf16[352,128]{1,0:T(8,128)(2,1)S(1)}, bf16[352,128]{1,0:T(8,128)(2,1)S(1)}, u32[]{:S(2)}, u32[]{:S(2)}) collective-permute-start(bf16[352,128]{1,0:T(8,128)(2,1)S(1)} %get-tuple-element.21), channel_id=1, source_target_pairs={{0,0},{16,64},{32,128},{48,192},{64,16},{80,80},{96,144},{112,208}... | collective-permute-start | bytes 270344 | tf_op jit(solution)/shard_map/ppermute | solution.py:30
  138.2 4.8 %collective-permute-start.27 = (bf16[4,112,128]{2,1,0:T(8,128)(2,1)S(1)}, bf16[4,112,128]{2,1,0:T(8,128)(2,1)S(1)}, u32[]{:S(2)}, u32[]{:S(2)}) collective-permute-start(bf16[4,112,128]{2,1,0:T(8,128)(2,1)S(1)} %get-tuple-element.26), channel_id=1, source_target_pairs={{0,48},{16,0},{32,16},{48,32},{1,49},{17,1},{33,17},{49,33},{2,50}... | collective-permute-start | bytes 344072 | tf_op jit(solution)/shard_map/ppermute | solution.py:36
  140.3 6.1 %collective-permute-start.26 = (bf16[4,112,128]{2,1,0:T(8,128)(2,1)S(1)}, bf16[4,112,128]{2,1,0:T(8,128)(2,1)S(1)}, u32[]{:S(2)}, u32[]{:S(2)}) collective-permute-start(bf16[4,112,128]{2,1,0:T(8,128)(2,1)S(1)} %get-tuple-element.26), channel_id=1, source_target_pairs={{0,16},{16,32},{32,48},{48,0},{1,17},{17,33},{33,49},{49,1},{2,18}... | collective-permute-start | bytes 344072 | tf_op jit(solution)/shard_map/ppermute | solution.py:36
  140.3 6.1 %collective-permute-start.28 = (bf16[4,112,128]{2,1,0:T(8,128)(2,1)S(1)}, bf16[4,112,128]{2,1,0:T(8,128)(2,1)S(1)}, u32[]{:S(2)}, u32[]{:S(2)}) collective-permute-start(bf16[4,112,128]{2,1,0:T(8,128)(2,1)S(1)} %get-tuple-element.26), channel_id=1, source_target_pairs={{0,32},{16,48},{32,0},{48,16},{1,33},{17,49},{33,1},{49,17},{2,34}... | collective-permute-start | bytes 344072 | tf_op jit(solution)/shard_map/ppermute | solution.py:36
  141.6 6.4 %collective-permute-start.34 = (bf16[4,112,128]{2,1,0:T(8,128)(2,1)S(1)}, bf16[4,112,128]{2,1,0:T(8,128)(2,1)S(1)}, u32[]{:S(2)}, u32[]{:S(2)}) collective-permute-start(bf16[4,112,128]{2,1,0:T(8,128)(2,1)S(1)} %get-tuple-element.25), channel_id=1, source_target_pairs={{0,3},{1,0},{2,1},{3,2},{4,7},{5,4},{6,5},{7,6},{8,11},{9,8},{10,9... | collective-permute-start | bytes 344072 | tf_op jit(solution)/shard_map/ppermute | solution.py:36
  141.7 6.2 %collective-permute-start.33 = (bf16[4,112,128]{2,1,0:T(8,128)(2,1)S(1)}, bf16[4,112,128]{2,1,0:T(8,128)(2,1)S(1)}, u32[]{:S(2)}, u32[]{:S(2)}) collective-permute-start(bf16[4,112,128]{2,1,0:T(8,128)(2,1)S(1)} %get-tuple-element.25), channel_id=1, source_target_pairs={{0,1},{1,2},{2,3},{3,0},{4,5},{5,6},{6,7},{7,4},{8,9},{9,10},{10,1... | collective-permute-start | bytes 344072 | tf_op jit(solution)/shard_map/ppermute | solution.py:36
  143.0 5.1 %collective-permute-start.35 = (bf16[4,112,128]{2,1,0:T(8,128)(2,1)S(1)}, bf16[4,112,128]{2,1,0:T(8,128)(2,1)S(1)}, u32[]{:S(2)}, u32[]{:S(2)}) collective-permute-start(bf16[4,112,128]{2,1,0:T(8,128)(2,1)S(1)} %get-tuple-element.25), channel_id=1, source_target_pairs={{0,2},{1,3},{2,0},{3,1},{4,6},{5,7},{6,4},{7,5},{8,10},{9,11},{10,... | collective-permute-start | bytes 344072 | tf_op jit(solution)/shard_map/ppermute | solution.py:36
  146.4 12.2 %collective-permute-start.30 = (bf16[4,4,112,128]{3,2,1,0:T(8,128)(2,1)S(1)}, bf16[4,4,112,128]{3,2,1,0:T(8,128)(2,1)S(1)}, u32[]{:S(2)}, u32[]{:S(2)}) collective-permute-start(bf16[4,4,112,128]{3,2,1,0:T(8,128)(2,1)S(1)} %pad_maximum_fusion.refs_0_), channel_id=1, source_target_pairs={{0,3},{1,0},{2,1},{3,2},{4,7},{5,4},{6,5},{7,6},{8,11},{9,8},{10,9... | collective-permute-start | bytes 1376264 | tf_op jit(solution)/shard_map/ppermute | solution.py:44
  146.7 13.6 %collective-permute-start.29 = (bf16[4,4,112,128]{3,2,1,0:T(8,128)(2,1)S(1)}, bf16[4,4,112,128]{3,2,1,0:T(8,128)(2,1)S(1)}, u32[]{:S(2)}, u32[]{:S(2)}) collective-permute-start(bf16[4,4,112,128]{3,2,1,0:T(8,128)(2,1)S(1)} %pad_maximum_fusion.refs_0_), channel_id=1, source_target_pairs={{0,1},{1,2},{2,3},{3,0},{4,5},{5,6},{6,7},{7,4},{8,9},{9,10},{10,1... | collective-permute-start | bytes 1376264 | tf_op jit(solution)/shard_map/ppermute | solution.py:44
  148.2 12.1 %collective-permute-start.37 = (bf16[4,4,112,128]{3,2,1,0:T(8,128)(2,1)S(1)}, bf16[4,4,112,128]{3,2,1,0:T(8,128)(2,1)S(1)}, u32[]{:S(2)}, u32[]{:S(2)}) collective-permute-start(bf16[4,4,112,128]{3,2,1,0:T(8,128)(2,1)S(1)} %pad_maximum_fusion.1.refs_5_), channel_id=1, source_target_pairs={{0,48},{16,0},{32,16},{48,32},{1,49},{17,1},{33,17},{49,33},{2,50}... | collective-permute-start | bytes 1376264 | tf_op jit(solution)/shard_map/ppermute | solution.py:44
  151.7 11.1 %collective-permute-start.36 = (bf16[4,4,112,128]{3,2,1,0:T(8,128)(2,1)S(1)}, bf16[4,4,112,128]{3,2,1,0:T(8,128)(2,1)S(1)}, u32[]{:S(2)}, u32[]{:S(2)}) collective-permute-start(bf16[4,4,112,128]{3,2,1,0:T(8,128)(2,1)S(1)} %pad_maximum_fusion.1.refs_5_), channel_id=1, source_target_pairs={{0,16},{16,32},{32,48},{48,0},{1,17},{17,33},{33,49},{49,1},{2,18}... | collective-permute-start | bytes 1376264 | tf_op jit(solution)/shard_map/ppermute | solution.py:44
  151.7 11.2 %collective-permute-start.24 = (bf16[224,128]{1,0:T(8,128)(2,1)S(1)}, bf16[224,128]{1,0:T(8,128)(2,1)S(1)}, u32[]{:S(2)}, u32[]{:S(2)}) collective-permute-start(bf16[224,128]{1,0:T(8,128)(2,1)S(1)} %get-tuple-element.22), channel_id=1, source_target_pairs={{0,64},{64,0},{1,65},{65,1},{2,66},{66,2},{3,67},{67,3},{4,68},{68... | collective-permute-start | bytes 172040 | tf_op jit(solution)/shard_map/ppermute | solution.py:429
  158.7 9.0 %collective-permute-start.32 = (bf16[2,4,112,128]{3,2,1,0:T(8,128)(2,1)S(1)}, bf16[2,4,112,128]{3,2,1,0:T(8,128)(2,1)S(1)}, u32[]{:S(2)}, u32[]{:S(2)}) collective-permute-start(bf16[2,4,112,128]{3,2,1,0:T(8,128)(2,1)S(1)} %slice.41), channel_id=1, source_target_pairs={{0,3},{1,0},{2,1},{3,2},{4,7},{5,4},{6,5},{7,6},{8,11},{9,8},{10,9... | collective-permute-start | bytes 688136 | tf_op jit(solution)/shard_map/ppermute | solution.py:45
  160.3 7.3 %collective-permute-start.31 = (bf16[2,4,112,128]{3,2,1,0:T(8,128)(2,1)S(1)}, bf16[2,4,112,128]{3,2,1,0:T(8,128)(2,1)S(1)}, u32[]{:S(2)}, u32[]{:S(2)}) collective-permute-start(bf16[2,4,112,128]{3,2,1,0:T(8,128)(2,1)S(1)} %slice.40), channel_id=1, source_target_pairs={{0,1},{1,2},{2,3},{3,0},{4,5},{5,6},{6,7},{7,4},{8,9},{9,10},{10,1... | collective-permute-start | bytes 688136 | tf_op jit(solution)/shard_map/ppermute | solution.py:45
  160.4 7.2 %collective-permute-start.39 = (bf16[2,4,112,128]{3,2,1,0:T(8,128)(2,1)S(1)}, bf16[2,4,112,128]{3,2,1,0:T(8,128)(2,1)S(1)}, u32[]{:S(2)}, u32[]{:S(2)}) collective-permute-start(bf16[2,4,112,128]{3,2,1,0:T(8,128)(2,1)S(1)} %slice.44), channel_id=1, source_target_pairs={{0,48},{16,0},{32,16},{48,32},{1,49},{17,1},{33,17},{49,33},{2,50}... | collective-permute-start | bytes 688136 | tf_op jit(solution)/shard_map/ppermute | solution.py:45
  162.7 7.0 %collective-permute-start.38 = (bf16[2,4,112,128]{3,2,1,0:T(8,128)(2,1)S(1)}, bf16[2,4,112,128]{3,2,1,0:T(8,128)(2,1)S(1)}, u32[]{:S(2)}, u32[]{:S(2)}) collective-permute-start(bf16[2,4,112,128]{3,2,1,0:T(8,128)(2,1)S(1)} %slice.43), channel_id=1, source_target_pairs={{0,16},{16,32},{32,48},{48,0},{1,17},{17,33},{33,49},{49,1},{2,18}... | collective-permute-start | bytes 688136 | tf_op jit(solution)/shard_map/ppermute | solution.py:45
  162.9 4.8 %collective-permute-start.25 = (bf16[2,224,128]{2,1,0:T(8,128)(2,1)S(1)}, bf16[2,224,128]{2,1,0:T(8,128)(2,1)S(1)}, u32[]{:S(2)}, u32[]{:S(2)}) collective-permute-start(bf16[2,224,128]{2,1,0:T(8,128)(2,1)S(1)} %pad_maximum_fusion.4.near_ref), channel_id=1, source_target_pairs={{0,128},{128,0},{1,129},{129,1},{2,130},{130,2},{3,131},{131,3},{4... | collective-permute-start | bytes 344072 | tf_op jit(solution)/shard_map/ppermute | solution.py:431
  (2 other events, 2.1 us)

commit v11 on v10

--- a/solution.py
+++ b/solution.py
@@ -231,22 +231,24 @@
     weight = weight_ref[...]
     units = weight.shape[0]
     places = [(r, z) for r in range(4) for z in range(4)]
-    for k in range(4):
-        high = jnp.concatenate([upper[r][k, z] for r, z in places], axis=1)
-        low = jnp.concatenate([lower[k][r, z, :half] for r, z in places], axis=1)
-        square = jnp.zeros((8, LANES), jnp.float32)
-        for r, z in places:
-            square = square + lower[k][r, z, half:].astype(jnp.float32)
-        group = group_ref[k]
-        part_ref[group, :units, :] = lax.dot_general(
-            weight,
-            jnp.concatenate([high, low], axis=0),
-            NT,
-            preferred_element_type=jnp.float32,
+    for first in (0, 2):
+        tokens = []
+        for k in (first, first + 1):
+            tokens.append(jnp.concatenate([upper[r][k, z] for r, z in places], axis=1))
+            tokens.append(jnp.concatenate([lower[k][r, z, :half] for r, z in places], axis=1))
+        both = lax.dot_general(
+            weight, jnp.concatenate(tokens, axis=0), NT, preferred_element_type=jnp.float32
         )
-        total = jnp.broadcast_to(square[0:1] + square[1:2], square.shape)
-        big = total.astype(jnp.bfloat16).astype(jnp.float32)
-        part_ref[group, units:, :] = jnp.concatenate([big, total - big], axis=0)
+        for k in (first, first + 1):
+            square = jnp.zeros((8, LANES), jnp.float32)
+            for r, z in places:
+                square = square + lower[k][r, z, half:].astype(jnp.float32)
+            group = group_ref[k]
+            at = (k - first) * LANES
+            part_ref[group, :units, :] = both[:, at : at + LANES]
+            total = jnp.broadcast_to(square[0:1] + square[1:2], square.shape)
+            big = total.astype(jnp.bfloat16).astype(jnp.float32)
+            part_ref[group, units:, :] = jnp.concatenate([big, total - big], axis=0)
     for low_z in range(2):
         keep_ref[low_z] = part_ref[low_z * 2 + core_ref[0]]
         send_ref[low_z] = part_ref[low_z * 2 + 1 - core_ref[0]].astype(jnp.bfloat16)

time: 176 us -> 176 us (level)
  transfers between devices with their start and end apart: 42 -> 42, of which waited for: 22 -> 21; matrix products, arithmetic and copies ran while one was open for 0% -> 0% of each run, Pallas kernels for 4% -> 4%
where the time goes in v11:
time: 176 us; the launch traced here: 172 us
  starting transfers between devices  81.8 us (46%)
  waiting for transfers between devices  38.2 us (22%)
  blocking collectives  31.9 us (18%)
  Pallas kernels  15 us (9%)
  local copies, waits for them, and re-layouts  4 us (2%)
    all_to_all x2, blocking collectives, copy_for_each(): lax.all_to_all(jnp.broadcast_to(x[None], (size, *x.shape)), axis, 0, 0, t...  24.6 us
    ppermute x21, starting transfers between devices, round_trip(): lax.ppermute(x, axis, [(k, (k + step) % 4) for k in range(4)])  24 us
    ppermute x21, waiting for transfers between devices, round_trip(): lax.ppermute(x, axis, [(k, (k + step) % 4) for k in range(4)])  20.8 us
    ppermute x3, starting transfers between devices, turned(): return lax.ppermute(x, (*DP, 'y'), pairs)  12.4 us
    ppermute x1, starting transfers between devices, body(): got = lax.ppermute(send, 'core', [(0, 1), (1, 0)])  9.77 us
    all_to_all x1, starting transfers between devices, copy_for_each(): lax.all_to_all(jnp.broadcast_to(x[None], (size, *x.shape)), axis, 0, 0, t...  9 us
    all_gather x1, blocking collectives, body(): errors = lax.all_gather(solved, DP)  7.28 us
    all_to_all x1, starting transfers between devices, body(): parts = lax.all_to_all(parts, 'y', 0, 0, tiled=True)  7.21 us
  transfers between devices with their start and end apart: 42, of which 21 were waited for; matrix products, arithmetic and copies ran while one was open for 0% of the time, Pallas kernels for 4%

profile of v11, /device:TPU:1, one launch (start us, length us, event | category | flops | bytes accessed | tf_op | source)
XLA Modules:
  0.0 172.3 jit_solution(5860321260217248114)
XLA Ops:
  0.7 1.6 broadcast_in_dim.17
  2.3 9.0 %all-to-all-start = ((bf16[8,128,128]{2,1,0:T(8,128)(2,1)}), bf16[8,128,128]{2,1,0:T(8,128)(2,1)S(1)}, u32[]{:S(2)}, u32[]{:S(2)}) async-start(bf16[8,128,128]{2,1,0:T(8,128)(2,1)} %broadcast_in_dim.17), calls=%async_computation | async-start | bytes 524288 | tf_op jit(solution)/shard_map/all_to_all | solution.py:25
  11.3 3.7 %solve.1 = f32[128,128]{1,0:T(8,128)} custom-call(bf16[128,2048]{1,0:T(8,128)(2,1)} %weight_ref.1, s32[128,128]{1,0:T(8,128)} %mask_ref.1, f32[128,2048]{1,0:T(8,128)} %factor_ref.1), custom_call_target="tpu_custom_call" | custom-call | flops 20000000 | bytes 300000 | tf_op jit(solution)/shard_map/solve/pallas_call | solution.py:122
  15.0 7.3 %all-gather = f32[512,128]{1,0:T(8,128)S(1)} all-gather(f32[128,128]{1,0:T(8,128)} %solve.1), channel_id=2, replica_groups=mesh['z_low'=2,'core'=2,'y'=4,'z_high'=4,'x'=4] {'z_low','core'}, dimensions={0}, use_global_device_ids=true | all-gather | bytes 327680 | tf_op jit(solution)/shard_map/all_gather | solution.py:339
  22.3 1.8 %update.1 = (bf16[128,2048]{1,0:T(8,128)(2,1)}, bf16[128,2048]{1,0:T(8,128)(2,1)S(1)}) custom-call(s32[1]{0:T(128)} %bitcast.place_ref, f32[4,128,128]{2,1,0:T(8,128)S(1)} %bitcast.38, f32[128,2048]{1,0:T(8,128)S(1)} %copy-done, bf16[128,2048]{1,0:T(8,128)(2,1)S(1)} %copy-done.1, s32[128,128]{1,0:T(8,128)S(1)} %copy-done.3), custom_call_target="tpu_custom_call" | custom-call | flops 400000000 | bytes 2200000 | tf_op jit(solution)/shard_map/update/pallas_call | solution.py:155
  24.1 2.7 %collective-permute-start.2 = (bf16[8,128,128]{2,1,0:T(8,128)(2,1)S(1)}, bf16[8,128,128]{2,1,0:T(8,128)(2,1)S(1)}, u32[]{:S(2)}, u32[]{:S(2)}) collective-permute-start(bf16[8,128,128]{2,1,0:T(8,128)(2,1)S(1)} %all-to-all-done.refs_0_), channel_id=1, source_target_pairs={{0,2},{1,3},{2,0},{3,1},{4,6},{5,7},{6,4},{7,5},{8,10},{9,11},{10,... | collective-permute-start | bytes 786440 | tf_op jit(solution)/shard_map/ppermute | solution.py:36
  26.9 3.5 %collective-permute-start.7 = (bf16[128,2048]{1,0:T(8,128)(2,1)S(1)}, bf16[128,2048]{1,0:T(8,128)(2,1)S(1)}, u32[]{:S(2)}, u32[]{:S(2)}) collective-permute-start(bf16[128,2048]{1,0:T(8,128)(2,1)S(1)} %get-tuple-element.14), channel_id=1, source_target_pairs={{0,0},{16,64},{32,128},{48,192},{64,16},{80,80},{96,144},{112,208}... | collective-permute-start | bytes 1572872 | tf_op jit(solution)/shard_map/ppermute | solution.py:30
  31.9 1.4 collective-permute-done.2.refs_3_
  33.3 1.1 collective-permute-start.6
  34.4 4.6 %collective-permute-done.1.refs_2_ = bf16[8,128,128]{2,1,0:T(8,128)(2,1)S(1)} collective-permute-done((bf16[8,128,128]{2,1,0:T(8,128)(2,1)S(1)}, bf16[8,128,128]{2,1,0:T(8,128)(2,1)S(1)}, u32[]{:S(2)}, u32[]{:S(2)}) %collective-permute-start.1) | collective-permute-done | bytes 262176 | tf_op jit(solution)/shard_map/ppermute | solution.py:36
  39.1 1.0 collective-permute-start.5
  41.6 1.9 %project.1 = bf16[4,128,128]{2,1,0:T(8,128)(2,1)} custom-call(s32[4]{0:T(128)S(1)} %pad_add_fusion.1.from_ref, s32[1]{0:T(128)} %bitcast.7.core_ref, bf16[8,128,128]{2,1,0:T(8,128)(2,1)S(1)} %all-to-all-done.refs_0_, bf16[8,128,128]{2,1,0:T(8,128)(2,1)S(1)} %collective-permute-done.refs_1_, bf16[8,128,128]{2,1,0:T(8,128)(2,1)S(1)} %collective-permute-done.1.refs_2_, ...), custom_call_target="tpu_custom_call" | custom-call | flops 268000000 | bytes 2700000 | tf_op jit(solution)/shard_map/project/pallas_call | solution.py:343
  43.5 7.2 %all-to-all-start.1 = ((bf16[4,128,128]{2,1,0:T(8,128)(2,1)}), bf16[4,128,128]{2,1,0:T(8,128)(2,1)S(1)}, u32[]{:S(2)}, u32[]{:S(2)}) async-start(bf16[4,128,128]{2,1,0:T(8,128)(2,1)} %project.1), calls=%async_computation.1 | async-start | bytes 262144 | tf_op jit(solution)/shard_map/all_to_all | solution.py:352
  50.8 4.8 %collective-permute-start.8 = (bf16[144,128]{1,0:T(8,128)(2,1)S(1)}, bf16[144,128]{1,0:T(8,128)(2,1)S(1)}, u32[]{:S(2)}, u32[]{:S(2)}) collective-permute-start(bf16[144,128]{1,0:T(8,128)(2,1)S(1)} %pad_maximum_fusion.5), channel_id=1, source_target_pairs={{0,0},{16,64},{32,128},{48,192},{64,16},{80,80},{96,144},{112,208}... | collective-permute-start | bytes 110600 | tf_op jit(solution)/shard_map/ppermute | solution.py:30
  55.6 1.9 %collective-permute-done.8.residual_ref = bf16[144,128]{1,0:T(8,128)(2,1)S(1)} collective-permute-done((bf16[144,128]{1,0:T(8,128)(2,1)S(1)}, bf16[144,128]{1,0:T(8,128)(2,1)S(1)}, u32[]{:S(2)}, u32[]{:S(2)}) %collective-permute-start.8) | collective-permute-done | bytes 36896 | tf_op jit(solution)/shard_map/ppermute | solution.py:30
  58.4 13.5 %all_to_all.20 = bf16[4,136,128]{2,1,0:T(8,128)(2,1)S(1)} all-to-all(bf16[4,136,128]{2,1,0:T(8,128)(2,1)S(1)} %broadcast_in_dim.38), channel_id=1, replica_groups=mesh['z_low'=2,'core'=2,'y'=4,'z_high'=4,'x'=4] {'z_high'}, dimensions={0} | all-to-all | bytes 278528 | tf_op jit(solution)/shard_map/all_to_all | solution.py:25
  71.9 3.5 %collective-permute-start.10 = (bf16[4,64,128]{2,1,0:T(8,128)(2,1)S(1)}, bf16[4,64,128]{2,1,0:T(8,128)(2,1)S(1)}, u32[]{:S(2)}, u32[]{:S(2)}) collective-permute-start(bf16[4,64,128]{2,1,0:T(8,128)(2,1)S(1)} %get-tuple-element.30), channel_id=1, source_target_pairs={{0,48},{16,0},{32,16},{48,32},{1,49},{17,1},{33,17},{49,33},{2,50}... | collective-permute-start | bytes 196616 | tf_op jit(solution)/shard_map/ppermute | solution.py:36
  75.4 1.3 collective-permute-start.11
  76.7 3.7 %collective-permute-done.9 = bf16[4,64,128]{2,1,0:T(8,128)(2,1)S(1)} collective-permute-done((bf16[4,64,128]{2,1,0:T(8,128)(2,1)S(1)}, bf16[4,64,128]{2,1,0:T(8,128)(2,1)S(1)}, u32[]{:S(2)}, u32[]{:S(2)}) %collective-permute-start.9) | collective-permute-done | bytes 65568 | tf_op jit(solution)/shard_map/ppermute | solution.py:36
  80.8 2.7 %collective-permute-start.16 = (bf16[4,72,128]{2,1,0:T(8,128)(2,1)S(1)}, bf16[4,72,128]{2,1,0:T(8,128)(2,1)S(1)}, u32[]{:S(2)}, u32[]{:S(2)}) collective-permute-start(bf16[4,72,128]{2,1,0:T(8,128)(2,1)S(1)} %get-tuple-element.28), channel_id=1, source_target_pairs={{0,3},{1,0},{2,1},{3,2},{4,7},{5,4},{6,5},{7,6},{8,11},{9,8},{10,9... | collective-permute-start | bytes 221192 | tf_op jit(solution)/shard_map/ppermute | solution.py:36
  83.6 1.7 %collective-permute-start.17 = (bf16[4,72,128]{2,1,0:T(8,128)(2,1)S(1)}, bf16[4,72,128]{2,1,0:T(8,128)(2,1)S(1)}, u32[]{:S(2)}, u32[]{:S(2)}) collective-permute-start(bf16[4,72,128]{2,1,0:T(8,128)(2,1)S(1)} %get-tuple-element.28), channel_id=1, source_target_pairs={{0,2},{1,3},{2,0},{3,1},{4,6},{5,7},{6,4},{7,5},{8,10},{9,11},{10,... | collective-permute-start | bytes 221192 | tf_op jit(solution)/shard_map/ppermute | solution.py:36
  85.3 1.3 collective-permute-done.16
  86.6 1.5 collective-permute-done.15
  88.9 0.9 collective-permute-start.20
  89.9 1.5 collective-permute-start.19
  91.8 2.5 %collective-permute-start.13 = (bf16[4,4,64,128]{3,2,1,0:T(8,128)(2,1)S(1)}, bf16[4,4,64,128]{3,2,1,0:T(8,128)(2,1)}, u32[]{:S(2)}, u32[]{:S(2)}) collective-permute-start(bf16[4,4,64,128]{3,2,1,0:T(8,128)(2,1)S(1)} %pad_maximum_fusion.3.refs_0_), channel_id=1, source_target_pairs={{0,3},{1,0},{2,1},{3,2},{4,7},{5,4},{6,5},{7,6},{8,11},{9,8},{10,9... | collective-permute-start | bytes 786440 | tf_op jit(solution)/shard_map/ppermute | solution.py:36
  94.4 1.5 copy-done.2
  95.9 1.0 order.1.refs_8_
  97.7 3.4 %collective-permute-done.12.refs_1_ = bf16[4,4,64,128]{3,2,1,0:T(8,128)(2,1)} collective-permute-done((bf16[4,4,64,128]{3,2,1,0:T(8,128)(2,1)S(1)}, bf16[4,4,64,128]{3,2,1,0:T(8,128)(2,1)}, u32[]{:S(2)}, u32[]{:S(2)}) %collective-permute-start.12) | collective-permute-done | bytes 262176 | tf_op jit(solution)/shard_map/ppermute | solution.py:36
  101.1 2.3 %gate_up.1 = (f32[2,464,128]{2,1,0:T(8,128)S(1)}, bf16[2,464,128]{2,1,0:T(8,128)(2,1)S(1)}) custom-call(s32[4]{0:T(128)S(1)} %pad_add_fusion.group_ref, s32[1]{0:T(128)} %bitcast.7.core_ref, bf16[4,4,64,128]{3,2,1,0:T(8,128)(2,1)S(1)} %pad_maximum_fusion.3.refs_0_, bf16[4,4,64,128]{3,2,1,0:T(8,128)(2,1)} %collective-permute-done.12.refs_1_, ...), custom_call_target="tpu_custom_call" | custom-call | flops 940000000 | bytes 4300000 | tf_op jit(solution)/shard_map/gate_up/pallas_call | solution.py:377
  103.4 9.8 %collective-permute-start.21 = (bf16[2,464,128]{2,1,0:T(8,128)(2,1)S(1)}, bf16[2,464,128]{2,1,0:T(8,128)(2,1)S(1)}, u32[]{:S(2)}, u32[]{:S(2)}) collective-permute-start(bf16[2,464,128]{2,1,0:T(8,128)(2,1)S(1)} %get-tuple-element.17), channel_id=1, source_target_pairs={{0,64},{64,0},{1,65},{65,1},{2,66},{66,2},{3,67},{67,3},{4,68},{68... | collective-permute-start | bytes 712712 | tf_op jit(solution)/shard_map/ppermute | solution.py:392
  113.2 1.1 collective-permute-done.21.got_ref
  114.5 4.4 %collective-permute-done.22.got_ref = bf16[464,128]{1,0:T(8,128)(2,1)S(1)} collective-permute-done((bf16[464,128]{1,0:T(8,128)(2,1)S(1)}, bf16[464,128]{1,0:T(8,128)(2,1)S(1)}, u32[]{:S(2)}, u32[]{:S(2)}) %collective-permute-start.22) | collective-permute-done | bytes 118816 | tf_op jit(solution)/shard_map/ppermute | solution.py:405
  119.0 4.0 %collective-permute-start.23 = (bf16[352,128]{1,0:T(8,128)(2,1)S(1)}, bf16[352,128]{1,0:T(8,128)(2,1)S(1)}, u32[]{:S(2)}, u32[]{:S(2)}) collective-permute-start(bf16[352,128]{1,0:T(8,128)(2,1)S(1)} %get-tuple-element.21), channel_id=1, source_target_pairs={{0,0},{16,64},{32,128},{48,192},{64,16},{80,80},{96,144},{112,208}... | collective-permute-start | bytes 270344 | tf_op jit(solution)/shard_map/ppermute | solution.py:30
  123.0 3.2 %collective-permute-done.23.in_ref = bf16[352,128]{1,0:T(8,128)(2,1)S(1)} collective-permute-done((bf16[352,128]{1,0:T(8,128)(2,1)S(1)}, bf16[352,128]{1,0:T(8,128)(2,1)S(1)}, u32[]{:S(2)}, u32[]{:S(2)}) %collective-permute-start.23) | collective-permute-done | bytes 90144 | tf_op jit(solution)/shard_map/ppermute | solution.py:30
  126.2 11.1 %all_to_all.21 = bf16[4,224,128]{2,1,0:T(8,128)(2,1)S(1)} all-to-all(bf16[4,224,128]{2,1,0:T(8,128)(2,1)S(1)} %broadcast_in_dim.39), channel_id=1, replica_groups=mesh['z_low'=2,'core'=2,'y'=4,'z_high'=4,'x'=4] {'z_high'}, dimensions={0} | all-to-all | bytes 458752 | tf_op jit(solution)/shard_map/all_to_all | solution.py:25
  137.3 2.0 %collective-permute-start.27 = (bf16[4,112,128]{2,1,0:T(8,128)(2,1)S(1)}, bf16[4,112,128]{2,1,0:T(8,128)(2,1)S(1)}, u32[]{:S(2)}, u32[]{:S(2)}) collective-permute-start(bf16[4,112,128]{2,1,0:T(8,128)(2,1)S(1)} %get-tuple-element.26), channel_id=1, source_target_pairs={{0,48},{16,0},{32,16},{48,32},{1,49},{17,1},{33,17},{49,33},{2,50}... | collective-permute-start | bytes 344072 | tf_op jit(solution)/shard_map/ppermute | solution.py:36
  139.4 1.3 collective-permute-start.28
  140.9 1.3 collective-permute-start.33
  142.1 3.3 %collective-permute-done.26 = bf16[4,112,128]{2,1,0:T(8,128)(2,1)S(1)} collective-permute-done((bf16[4,112,128]{2,1,0:T(8,128)(2,1)S(1)}, bf16[4,112,128]{2,1,0:T(8,128)(2,1)S(1)}, u32[]{:S(2)}, u32[]{:S(2)}) %collective-permute-start.26) | collective-permute-done | bytes 114720 | tf_op jit(solution)/shard_map/ppermute | solution.py:36
  146.0 1.3 collective-permute-start.29
  147.4 3.4 %collective-permute-start.37 = (bf16[4,4,112,128]{3,2,1,0:T(8,128)(2,1)S(1)}, bf16[4,4,112,128]{3,2,1,0:T(8,128)(2,1)S(1)}, u32[]{:S(2)}, u32[]{:S(2)}) collective-permute-start(bf16[4,4,112,128]{3,2,1,0:T(8,128)(2,1)S(1)} %pad_maximum_fusion.1.refs_5_), channel_id=1, source_target_pairs={{0,48},{16,0},{32,16},{48,32},{1,49},{17,1},{33,17},{49,33},{2,50}... | collective-permute-start | bytes 1376264 | tf_op jit(solution)/shard_map/ppermute | solution.py:44
  150.8 6.5 %collective-permute-start.24 = (bf16[224,128]{1,0:T(8,128)(2,1)S(1)}, bf16[224,128]{1,0:T(8,128)(2,1)S(1)}, u32[]{:S(2)}, u32[]{:S(2)}) collective-permute-start(bf16[224,128]{1,0:T(8,128)(2,1)S(1)} %get-tuple-element.22), channel_id=1, source_target_pairs={{0,64},{64,0},{1,65},{65,1},{2,66},{66,2},{3,67},{67,3},{4,68},{68... | collective-permute-start | bytes 172040 | tf_op jit(solution)/shard_map/ppermute | solution.py:431
  159.9 1.9 %collective-permute-start.39 = (bf16[2,4,112,128]{3,2,1,0:T(8,128)(2,1)S(1)}, bf16[2,4,112,128]{3,2,1,0:T(8,128)(2,1)S(1)}, u32[]{:S(2)}, u32[]{:S(2)}) collective-permute-start(bf16[2,4,112,128]{3,2,1,0:T(8,128)(2,1)S(1)} %slice.44), channel_id=1, source_target_pairs={{0,48},{16,0},{32,16},{48,32},{1,49},{17,1},{33,17},{49,33},{2,50}... | collective-permute-start | bytes 688136 | tf_op jit(solution)/shard_map/ppermute | solution.py:45
  162.0 2.3 %collective-permute-start.25 = (bf16[2,224,128]{2,1,0:T(8,128)(2,1)S(1)}, bf16[2,224,128]{2,1,0:T(8,128)(2,1)S(1)}, u32[]{:S(2)}, u32[]{:S(2)}) collective-permute-start(bf16[2,224,128]{2,1,0:T(8,128)(2,1)S(1)} %pad_maximum_fusion.4.near_ref), channel_id=1, source_target_pairs={{0,128},{128,0},{1,129},{129,1},{2,130},{130,2},{3,131},{131,3},{4... | collective-permute-start | bytes 344072 | tf_op jit(solution)/shard_map/ppermute | solution.py:433
  164.9 1.9 %collective-permute-done.25.far_ref = bf16[2,224,128]{2,1,0:T(8,128)(2,1)S(1)} collective-permute-done((bf16[2,224,128]{2,1,0:T(8,128)(2,1)S(1)}, bf16[2,224,128]{2,1,0:T(8,128)(2,1)S(1)}, u32[]{:S(2)}, u32[]{:S(2)}) %collective-permute-start.25) | collective-permute-done | bytes 114720 | tf_op jit(solution)/shard_map/ppermute | solution.py:433
  166.8 2.1 %collective-permute-done.38.refs_8_ = bf16[2,4,112,128]{3,2,1,0:T(8,128)(2,1)S(1)} collective-permute-done((bf16[2,4,112,128]{3,2,1,0:T(8,128)(2,1)S(1)}, bf16[2,4,112,128]{3,2,1,0:T(8,128)(2,1)S(1)}, u32[]{:S(2)}, u32[]{:S(2)}) %collective-permute-start.38) | collective-permute-done | bytes 229408 | tf_op jit(solution)/shard_map/ppermute | solution.py:45
  168.8 3.3 %hessian.1 = f32[224,3584]{1,0:T(8,128)} custom-call(s32[4]{0:T(128)S(1)} %pad_add_fusion.1.from_ref, s32[4]{0:T(128)S(1)} %pad_add_fusion.group_ref, s32[1]{0:T(128)} %bitcast.place_ref, bf16[2,224,128]{2,1,0:T(8,128)(2,1)S(1)} %pad_maximum_fusion.4.near_ref, bf16[2,224,128]{2,1,0:T(8,128)(2,1)S(1)} %collective-permute-done.25.far_ref, ...), custom_call_target="tpu_custom_call" | custom-call | flops 822000000 | bytes 7100000 | tf_op jit(solution)/shard_map/hessian/pallas_call | solution.py:434
  (85 shorter events, 11.0 us)
Async XLA Ops:
  0.6 21.7 %copy-start = (f32[128,2048]{1,0:T(8,128)S(1)}, f32[128,2048]{1,0:T(8,128)}, u32[]{:S(2)}) copy-start(f32[128,2048]{1,0:T(8,128)} %factor_ref.1) | copy-start | bytes 3145732
  0.6 21.7 %copy-start.3 = (s32[128,128]{1,0:T(8,128)S(1)}, s32[128,128]{1,0:T(8,128)}, u32[]{:S(2)}) copy-start(s32[128,128]{1,0:T(8,128)} %mask_ref.1) | copy-start | bytes 196612
  0.7 21.6 %copy-start.1 = (bf16[128,2048]{1,0:T(8,128)(2,1)S(1)}, bf16[128,2048]{1,0:T(8,128)(2,1)}, u32[]{:S(2)}) copy-start(bf16[128,2048]{1,0:T(8,128)(2,1)} %weight_ref.1) | copy-start | bytes 1572868
  2.3 21.8 %all-to-all-start = ((bf16[8,128,128]{2,1,0:T(8,128)(2,1)}), bf16[8,128,128]{2,1,0:T(8,128)(2,1)S(1)}, u32[]{:S(2)}, u32[]{:S(2)}) async-start(bf16[8,128,128]{2,1,0:T(8,128)(2,1)} %broadcast_in_dim.17), calls=%async_computation | async-start | bytes 524288 | tf_op jit(solution)/shard_map/all_to_all | solution.py:25
  24.1 26.7 %copy-start.7 = (bf16[128]{0:T(256)(128)(2,1)S(1)}, bf16[128]{0:T(256)(128)(2,1)}, u32[]{:S(2)}) copy-start(bf16[128]{0:T(256)(128)(2,1)} %param.12) | copy-start | bytes 772
  24.1 26.7 %copy-start.6 = (bf16[128,128]{1,0:T(8,128)(2,1)S(1)}, bf16[128,128]{1,0:T(8,128)(2,1)}, u32[]{:S(2)}) copy-start(bf16[128,128]{1,0:T(8,128)(2,1)} %param.8) | copy-start | bytes 98308
  24.1 9.2 %collective-permute-start.2 = (bf16[8,128,128]{2,1,0:T(8,128)(2,1)S(1)}, bf16[8,128,128]{2,1,0:T(8,128)(2,1)S(1)}, u32[]{:S(2)}, u32[]{:S(2)}) collective-permute-start(bf16[8,128,128]{2,1,0:T(8,128)(2,1)S(1)} %all-to-all-done.refs_0_), channel_id=1, source_target_pairs={{0,2},{1,3},{2,0},{3,1},{4,6},{5,7},{6,4},{7,5},{8,10},{9,11},{10,... | collective-permute-start | bytes 786440 | tf_op jit(solution)/shard_map/ppermute | solution.py:36
  26.9 13.9 %collective-permute-start.7 = (bf16[128,2048]{1,0:T(8,128)(2,1)S(1)}, bf16[128,2048]{1,0:T(8,128)(2,1)S(1)}, u32[]{:S(2)}, u32[]{:S(2)}) collective-permute-start(bf16[128,2048]{1,0:T(8,128)(2,1)S(1)} %get-tuple-element.14), channel_id=1, source_target_pairs={{0,0},{16,64},{32,128},{48,192},{64,16},{80,80},{96,144},{112,208}... | collective-permute-start | bytes 1572872 | tf_op jit(solution)/shard_map/ppermute | solution.py:30
  30.4 8.7 %collective-permute-start.1 = (bf16[8,128,128]{2,1,0:T(8,128)(2,1)S(1)}, bf16[8,128,128]{2,1,0:T(8,128)(2,1)S(1)}, u32[]{:S(2)}, u32[]{:S(2)}) collective-permute-start(bf16[8,128,128]{2,1,0:T(8,128)(2,1)S(1)} %all-to-all-done.refs_0_), channel_id=1, source_target_pairs={{0,3},{1,0},{2,1},{3,2},{4,7},{5,4},{6,5},{7,6},{8,11},{9,8},{10,9... | collective-permute-start | bytes 786440 | tf_op jit(solution)/shard_map/ppermute | solution.py:36
  31.3 8.8 %collective-permute-start = (bf16[8,128,128]{2,1,0:T(8,128)(2,1)S(1)}, bf16[8,128,128]{2,1,0:T(8,128)(2,1)S(1)}, u32[]{:S(2)}, u32[]{:S(2)}) collective-permute-start(bf16[8,128,128]{2,1,0:T(8,128)(2,1)S(1)} %all-to-all-done.refs_0_), channel_id=1, source_target_pairs={{0,1},{1,2},{2,3},{3,0},{4,5},{5,6},{6,7},{7,4},{8,9},{9,10},{10,1... | collective-permute-start | bytes 786440 | tf_op jit(solution)/shard_map/ppermute | solution.py:36
  31.9 8.9 %collective-permute-start.3 = (bf16[8,128,128]{2,1,0:T(8,128)(2,1)S(1)}, bf16[8,128,128]{2,1,0:T(8,128)(2,1)S(1)}, u32[]{:S(2)}, u32[]{:S(2)}) collective-permute-start(bf16[8,128,128]{2,1,0:T(8,128)(2,1)S(1)} %all-to-all-done.refs_0_), channel_id=1, source_target_pairs={{0,64},{64,0},{1,65},{65,1},{2,66},{66,2},{3,67},{67,3},{4,68},{68... | collective-permute-start | bytes 786440 | tf_op jit(solution)/shard_map/ppermute | solution.py:334
  33.3 7.5 %collective-permute-start.6 = (bf16[8,128,128]{2,1,0:T(8,128)(2,1)S(1)}, bf16[8,128,128]{2,1,0:T(8,128)(2,1)S(1)}, u32[]{:S(2)}, u32[]{:S(2)}) collective-permute-start(bf16[8,128,128]{2,1,0:T(8,128)(2,1)S(1)} %collective-permute-done.2.refs_3_), channel_id=1, source_target_pairs={{0,64},{64,0},{1,65},{65,1},{2,66},{66,2},{3,67},{67,3},{4,68},{68... | collective-permute-start | bytes 786440 | tf_op jit(solution)/shard_map/ppermute | solution.py:334
  39.1 2.2 %collective-permute-start.5 = (bf16[8,128,128]{2,1,0:T(8,128)(2,1)S(1)}, bf16[8,128,128]{2,1,0:T(8,128)(2,1)S(1)}, u32[]{:S(2)}, u32[]{:S(2)}) collective-permute-start(bf16[8,128,128]{2,1,0:T(8,128)(2,1)S(1)} %collective-permute-done.1.refs_2_), channel_id=1, source_target_pairs={{0,64},{64,0},{1,65},{65,1},{2,66},{66,2},{3,67},{67,3},{4,68},{68... | collective-permute-start | bytes 786440 | tf_op jit(solution)/shard_map/ppermute | solution.py:334
  40.1 1.5 collective-permute-start.4
  43.5 14.0 %all-to-all-start.1 = ((bf16[4,128,128]{2,1,0:T(8,128)(2,1)}), bf16[4,128,128]{2,1,0:T(8,128)(2,1)S(1)}, u32[]{:S(2)}, u32[]{:S(2)}) async-start(bf16[4,128,128]{2,1,0:T(8,128)(2,1)} %project.1), calls=%async_computation.1 | async-start | bytes 262144 | tf_op jit(solution)/shard_map/all_to_all | solution.py:352
  50.8 6.7 %collective-permute-start.8 = (bf16[144,128]{1,0:T(8,128)(2,1)S(1)}, bf16[144,128]{1,0:T(8,128)(2,1)S(1)}, u32[]{:S(2)}, u32[]{:S(2)}) collective-permute-start(bf16[144,128]{1,0:T(8,128)(2,1)S(1)} %pad_maximum_fusion.5), channel_id=1, source_target_pairs={{0,0},{16,64},{32,128},{48,192},{64,16},{80,80},{96,144},{112,208}... | collective-permute-start | bytes 110600 | tf_op jit(solution)/shard_map/ppermute | solution.py:30
  71.9 4.8 %collective-permute-start.10 = (bf16[4,64,128]{2,1,0:T(8,128)(2,1)S(1)}, bf16[4,64,128]{2,1,0:T(8,128)(2,1)S(1)}, u32[]{:S(2)}, u32[]{:S(2)}) collective-permute-start(bf16[4,64,128]{2,1,0:T(8,128)(2,1)S(1)} %get-tuple-element.30), channel_id=1, source_target_pairs={{0,48},{16,0},{32,16},{48,32},{1,49},{17,1},{33,17},{49,33},{2,50}... | collective-permute-start | bytes 196616 | tf_op jit(solution)/shard_map/ppermute | solution.py:36
  75.4 5.0 %collective-permute-start.9 = (bf16[4,64,128]{2,1,0:T(8,128)(2,1)S(1)}, bf16[4,64,128]{2,1,0:T(8,128)(2,1)S(1)}, u32[]{:S(2)}, u32[]{:S(2)}) collective-permute-start(bf16[4,64,128]{2,1,0:T(8,128)(2,1)S(1)} %get-tuple-element.30), channel_id=1, source_target_pairs={{0,16},{16,32},{32,48},{48,0},{1,17},{17,33},{33,49},{49,1},{2,18}... | collective-permute-start | bytes 196616 | tf_op jit(solution)/shard_map/ppermute | solution.py:36
  75.4 5.0 %collective-permute-start.11 = (bf16[4,64,128]{2,1,0:T(8,128)(2,1)S(1)}, bf16[4,64,128]{2,1,0:T(8,128)(2,1)S(1)}, u32[]{:S(2)}, u32[]{:S(2)}) collective-permute-start(bf16[4,64,128]{2,1,0:T(8,128)(2,1)S(1)} %get-tuple-element.30), channel_id=1, source_target_pairs={{0,32},{16,48},{32,0},{48,16},{1,33},{17,49},{33,1},{49,17},{2,34}... | collective-permute-start | bytes 196616 | tf_op jit(solution)/shard_map/ppermute | solution.py:36
  80.5 13.9 %collective-permute-start.14 = (bf16[4,4,64,128]{3,2,1,0:T(8,128)(2,1)S(1)}, bf16[4,4,64,128]{3,2,1,0:T(8,128)(2,1)S(1)}, u32[]{:S(2)}, u32[]{:S(2)}) collective-permute-start(bf16[4,4,64,128]{3,2,1,0:T(8,128)(2,1)S(1)} %pad_maximum_fusion.3.refs_0_), channel_id=1, source_target_pairs={{0,2},{1,3},{2,0},{3,1},{4,6},{5,7},{6,4},{7,5},{8,10},{9,11},{10,... | collective-permute-start | bytes 786440 | tf_op jit(solution)/shard_map/ppermute | solution.py:36
  80.8 5.7 %collective-permute-start.16 = (bf16[4,72,128]{2,1,0:T(8,128)(2,1)S(1)}, bf16[4,72,128]{2,1,0:T(8,128)(2,1)S(1)}, u32[]{:S(2)}, u32[]{:S(2)}) collective-permute-start(bf16[4,72,128]{2,1,0:T(8,128)(2,1)S(1)} %get-tuple-element.28), channel_id=1, source_target_pairs={{0,3},{1,0},{2,1},{3,2},{4,7},{5,4},{6,5},{7,6},{8,11},{9,8},{10,9... | collective-permute-start | bytes 221192 | tf_op jit(solution)/shard_map/ppermute | solution.py:36
  83.6 4.5 %collective-permute-start.15 = (bf16[4,72,128]{2,1,0:T(8,128)(2,1)S(1)}, bf16[4,72,128]{2,1,0:T(8,128)(2,1)S(1)}, u32[]{:S(2)}, u32[]{:S(2)}) collective-permute-start(bf16[4,72,128]{2,1,0:T(8,128)(2,1)S(1)} %get-tuple-element.28), channel_id=1, source_target_pairs={{0,1},{1,2},{2,3},{3,0},{4,5},{5,6},{6,7},{7,4},{8,9},{9,10},{10,1... | collective-permute-start | bytes 221192 | tf_op jit(solution)/shard_map/ppermute | solution.py:36
  83.6 5.3 %collective-permute-start.17 = (bf16[4,72,128]{2,1,0:T(8,128)(2,1)S(1)}, bf16[4,72,128]{2,1,0:T(8,128)(2,1)S(1)}, u32[]{:S(2)}, u32[]{:S(2)}) collective-permute-start(bf16[4,72,128]{2,1,0:T(8,128)(2,1)S(1)} %get-tuple-element.28), channel_id=1, source_target_pairs={{0,2},{1,3},{2,0},{3,1},{4,6},{5,7},{6,4},{7,5},{8,10},{9,11},{10,... | collective-permute-start | bytes 221192 | tf_op jit(solution)/shard_map/ppermute | solution.py:36
  88.9 12.2 %collective-permute-start.20 = (bf16[4,4,72,128]{3,2,1,0:T(8,128)(2,1)S(1)}, bf16[4,4,72,128]{3,2,1,0:T(8,128)(2,1)S(1)}, u32[]{:S(2)}, u32[]{:S(2)}) collective-permute-start(bf16[4,4,72,128]{3,2,1,0:T(8,128)(2,1)S(1)} %pad_maximum_fusion.2.refs_4_), channel_id=1, source_target_pairs={{0,32},{16,48},{32,0},{48,16},{1,33},{17,49},{33,1},{49,17},{2,34}... | collective-permute-start | bytes 884744 | tf_op jit(solution)/shard_map/ppermute | solution.py:36
  89.9 11.2 %collective-permute-start.19 = (bf16[4,4,72,128]{3,2,1,0:T(8,128)(2,1)S(1)}, bf16[4,4,72,128]{3,2,1,0:T(8,128)(2,1)S(1)}, u32[]{:S(2)}, u32[]{:S(2)}) collective-permute-start(bf16[4,4,72,128]{3,2,1,0:T(8,128)(2,1)S(1)} %pad_maximum_fusion.2.refs_4_), channel_id=1, source_target_pairs={{0,48},{16,0},{32,16},{48,32},{1,49},{17,1},{33,17},{49,33},{2,50}... | collective-permute-start | bytes 884744 | tf_op jit(solution)/shard_map/ppermute | solution.py:36
  91.4 9.7 %collective-permute-start.18 = (bf16[4,4,72,128]{3,2,1,0:T(8,128)(2,1)S(1)}, bf16[4,4,72,128]{3,2,1,0:T(8,128)(2,1)S(1)}, u32[]{:S(2)}, u32[]{:S(2)}) collective-permute-start(bf16[4,4,72,128]{3,2,1,0:T(8,128)(2,1)S(1)} %pad_maximum_fusion.2.refs_4_), channel_id=1, source_target_pairs={{0,16},{16,32},{32,48},{48,0},{1,17},{17,33},{33,49},{49,1},{2,18}... | collective-permute-start | bytes 884744 | tf_op jit(solution)/shard_map/ppermute | solution.py:36
  91.8 5.8 %collective-permute-start.13 = (bf16[4,4,64,128]{3,2,1,0:T(8,128)(2,1)S(1)}, bf16[4,4,64,128]{3,2,1,0:T(8,128)(2,1)}, u32[]{:S(2)}, u32[]{:S(2)}) collective-permute-start(bf16[4,4,64,128]{3,2,1,0:T(8,128)(2,1)S(1)} %pad_maximum_fusion.3.refs_0_), channel_id=1, source_target_pairs={{0,3},{1,0},{2,1},{3,2},{4,7},{5,4},{6,5},{7,6},{8,11},{9,8},{10,9... | collective-permute-start | bytes 786440 | tf_op jit(solution)/shard_map/ppermute | solution.py:36
  94.4 6.7 %collective-permute-start.12 = (bf16[4,4,64,128]{3,2,1,0:T(8,128)(2,1)S(1)}, bf16[4,4,64,128]{3,2,1,0:T(8,128)(2,1)}, u32[]{:S(2)}, u32[]{:S(2)}) collective-permute-start(bf16[4,4,64,128]{3,2,1,0:T(8,128)(2,1)S(1)} %pad_maximum_fusion.3.refs_0_), channel_id=1, source_target_pairs={{0,1},{1,2},{2,3},{3,0},{4,5},{5,6},{6,7},{7,4},{8,9},{9,10},{10,1... | collective-permute-start | bytes 786440 | tf_op jit(solution)/shard_map/ppermute | solution.py:36
  97.0 21.9 %copy-start.5 = (bf16[128,128]{1,0:T(8,128)(2,1)S(1)}, bf16[128,128]{1,0:T(8,128)(2,1)}, u32[]{:S(2)}) copy-start(bf16[128,128]{1,0:T(8,128)(2,1)} %copy-done.4) | copy-start | bytes 98308
  103.4 10.9 %collective-permute-start.21 = (bf16[2,464,128]{2,1,0:T(8,128)(2,1)S(1)}, bf16[2,464,128]{2,1,0:T(8,128)(2,1)S(1)}, u32[]{:S(2)}, u32[]{:S(2)}) collective-permute-start(bf16[2,464,128]{2,1,0:T(8,128)(2,1)S(1)} %get-tuple-element.17), channel_id=1, source_target_pairs={{0,64},{64,0},{1,65},{65,1},{2,66},{66,2},{3,67},{67,3},{4,68},{68... | collective-permute-start | bytes 712712 | tf_op jit(solution)/shard_map/ppermute | solution.py:392
  114.4 4.5 %collective-permute-start.22 = (bf16[464,128]{1,0:T(8,128)(2,1)S(1)}, bf16[464,128]{1,0:T(8,128)(2,1)S(1)}, u32[]{:S(2)}, u32[]{:S(2)}) collective-permute-start(bf16[464,128]{1,0:T(8,128)(2,1)S(1)} %get-tuple-element.19), channel_id=1, source_target_pairs={{0,128},{128,0},{1,129},{129,1},{2,130},{130,2},{3,131},{131,3},{4... | collective-permute-start | bytes 356360 | tf_op jit(solution)/shard_map/ppermute | solution.py:405
  119.0 7.2 %collective-permute-start.23 = (bf16[352,128]{1,0:T(8,128)(2,1)S(1)}, bf16[352,128]{1,0:T(8,128)(2,1)S(1)}, u32[]{:S(2)}, u32[]{:S(2)}) collective-permute-start(bf16[352,128]{1,0:T(8,128)(2,1)S(1)} %get-tuple-element.21), channel_id=1, source_target_pairs={{0,0},{16,64},{32,128},{48,192},{64,16},{80,80},{96,144},{112,208}... | collective-permute-start | bytes 270344 | tf_op jit(solution)/shard_map/ppermute | solution.py:30
  137.3 4.8 %collective-permute-start.27 = (bf16[4,112,128]{2,1,0:T(8,128)(2,1)S(1)}, bf16[4,112,128]{2,1,0:T(8,128)(2,1)S(1)}, u32[]{:S(2)}, u32[]{:S(2)}) collective-permute-start(bf16[4,112,128]{2,1,0:T(8,128)(2,1)S(1)} %get-tuple-element.26), channel_id=1, source_target_pairs={{0,48},{16,0},{32,16},{48,32},{1,49},{17,1},{33,17},{49,33},{2,50}... | collective-permute-start | bytes 344072 | tf_op jit(solution)/shard_map/ppermute | solution.py:36
  139.4 6.1 %collective-permute-start.26 = (bf16[4,112,128]{2,1,0:T(8,128)(2,1)S(1)}, bf16[4,112,128]{2,1,0:T(8,128)(2,1)S(1)}, u32[]{:S(2)}, u32[]{:S(2)}) collective-permute-start(bf16[4,112,128]{2,1,0:T(8,128)(2,1)S(1)} %get-tuple-element.26), channel_id=1, source_target_pairs={{0,16},{16,32},{32,48},{48,0},{1,17},{17,33},{33,49},{49,1},{2,18}... | collective-permute-start | bytes 344072 | tf_op jit(solution)/shard_map/ppermute | solution.py:36
  139.4 6.1 %collective-permute-start.28 = (bf16[4,112,128]{2,1,0:T(8,128)(2,1)S(1)}, bf16[4,112,128]{2,1,0:T(8,128)(2,1)S(1)}, u32[]{:S(2)}, u32[]{:S(2)}) collective-permute-start(bf16[4,112,128]{2,1,0:T(8,128)(2,1)S(1)} %get-tuple-element.26), channel_id=1, source_target_pairs={{0,32},{16,48},{32,0},{48,16},{1,33},{17,49},{33,1},{49,17},{2,34}... | collective-permute-start | bytes 344072 | tf_op jit(solution)/shard_map/ppermute | solution.py:36
  140.7 6.6 %collective-permute-start.34 = (bf16[4,112,128]{2,1,0:T(8,128)(2,1)S(1)}, bf16[4,112,128]{2,1,0:T(8,128)(2,1)S(1)}, u32[]{:S(2)}, u32[]{:S(2)}) collective-permute-start(bf16[4,112,128]{2,1,0:T(8,128)(2,1)S(1)} %get-tuple-element.25), channel_id=1, source_target_pairs={{0,3},{1,0},{2,1},{3,2},{4,7},{5,4},{6,5},{7,6},{8,11},{9,8},{10,9... | collective-permute-start | bytes 344072 | tf_op jit(solution)/shard_map/ppermute | solution.py:36
  140.9 6.5 %collective-permute-start.33 = (bf16[4,112,128]{2,1,0:T(8,128)(2,1)S(1)}, bf16[4,112,128]{2,1,0:T(8,128)(2,1)S(1)}, u32[]{:S(2)}, u32[]{:S(2)}) collective-permute-start(bf16[4,112,128]{2,1,0:T(8,128)(2,1)S(1)} %get-tuple-element.25), channel_id=1, source_target_pairs={{0,1},{1,2},{2,3},{3,0},{4,5},{5,6},{6,7},{7,4},{8,9},{9,10},{10,1... | collective-permute-start | bytes 344072 | tf_op jit(solution)/shard_map/ppermute | solution.py:36
  142.1 5.2 %collective-permute-start.35 = (bf16[4,112,128]{2,1,0:T(8,128)(2,1)S(1)}, bf16[4,112,128]{2,1,0:T(8,128)(2,1)S(1)}, u32[]{:S(2)}, u32[]{:S(2)}) collective-permute-start(bf16[4,112,128]{2,1,0:T(8,128)(2,1)S(1)} %get-tuple-element.25), channel_id=1, source_target_pairs={{0,2},{1,3},{2,0},{3,1},{4,6},{5,7},{6,4},{7,5},{8,10},{9,11},{10,... | collective-permute-start | bytes 344072 | tf_op jit(solution)/shard_map/ppermute | solution.py:36
  145.5 12.6 %collective-permute-start.30 = (bf16[4,4,112,128]{3,2,1,0:T(8,128)(2,1)S(1)}, bf16[4,4,112,128]{3,2,1,0:T(8,128)(2,1)S(1)}, u32[]{:S(2)}, u32[]{:S(2)}) collective-permute-start(bf16[4,4,112,128]{3,2,1,0:T(8,128)(2,1)S(1)} %pad_maximum_fusion.refs_0_), channel_id=1, source_target_pairs={{0,3},{1,0},{2,1},{3,2},{4,7},{5,4},{6,5},{7,6},{8,11},{9,8},{10,9... | collective-permute-start | bytes 1376264 | tf_op jit(solution)/shard_map/ppermute | solution.py:44
  146.0 13.6 %collective-permute-start.29 = (bf16[4,4,112,128]{3,2,1,0:T(8,128)(2,1)S(1)}, bf16[4,4,112,128]{3,2,1,0:T(8,128)(2,1)S(1)}, u32[]{:S(2)}, u32[]{:S(2)}) collective-permute-start(bf16[4,4,112,128]{3,2,1,0:T(8,128)(2,1)S(1)} %pad_maximum_fusion.refs_0_), channel_id=1, source_target_pairs={{0,1},{1,2},{2,3},{3,0},{4,5},{5,6},{6,7},{7,4},{8,9},{9,10},{10,1... | collective-permute-start | bytes 1376264 | tf_op jit(solution)/shard_map/ppermute | solution.py:44
  147.4 12.5 %collective-permute-start.37 = (bf16[4,4,112,128]{3,2,1,0:T(8,128)(2,1)S(1)}, bf16[4,4,112,128]{3,2,1,0:T(8,128)(2,1)S(1)}, u32[]{:S(2)}, u32[]{:S(2)}) collective-permute-start(bf16[4,4,112,128]{3,2,1,0:T(8,128)(2,1)S(1)} %pad_maximum_fusion.1.refs_5_), channel_id=1, source_target_pairs={{0,48},{16,0},{32,16},{48,32},{1,49},{17,1},{33,17},{49,33},{2,50}... | collective-permute-start | bytes 1376264 | tf_op jit(solution)/shard_map/ppermute | solution.py:44
  150.8 11.1 %collective-permute-start.36 = (bf16[4,4,112,128]{3,2,1,0:T(8,128)(2,1)S(1)}, bf16[4,4,112,128]{3,2,1,0:T(8,128)(2,1)S(1)}, u32[]{:S(2)}, u32[]{:S(2)}) collective-permute-start(bf16[4,4,112,128]{3,2,1,0:T(8,128)(2,1)S(1)} %pad_maximum_fusion.1.refs_5_), channel_id=1, source_target_pairs={{0,16},{16,32},{32,48},{48,0},{1,17},{17,33},{33,49},{49,1},{2,18}... | collective-permute-start | bytes 1376264 | tf_op jit(solution)/shard_map/ppermute | solution.py:44
  150.8 11.2 %collective-permute-start.24 = (bf16[224,128]{1,0:T(8,128)(2,1)S(1)}, bf16[224,128]{1,0:T(8,128)(2,1)S(1)}, u32[]{:S(2)}, u32[]{:S(2)}) collective-permute-start(bf16[224,128]{1,0:T(8,128)(2,1)S(1)} %get-tuple-element.22), channel_id=1, source_target_pairs={{0,64},{64,0},{1,65},{65,1},{2,66},{66,2},{3,67},{67,3},{4,68},{68... | collective-permute-start | bytes 172040 | tf_op jit(solution)/shard_map/ppermute | solution.py:431
  158.2 8.6 %collective-permute-start.32 = (bf16[2,4,112,128]{3,2,1,0:T(8,128)(2,1)S(1)}, bf16[2,4,112,128]{3,2,1,0:T(8,128)(2,1)S(1)}, u32[]{:S(2)}, u32[]{:S(2)}) collective-permute-start(bf16[2,4,112,128]{3,2,1,0:T(8,128)(2,1)S(1)} %slice.41), channel_id=1, source_target_pairs={{0,3},{1,0},{2,1},{3,2},{4,7},{5,4},{6,5},{7,6},{8,11},{9,8},{10,9... | collective-permute-start | bytes 688136 | tf_op jit(solution)/shard_map/ppermute | solution.py:45
  159.6 7.2 %collective-permute-start.31 = (bf16[2,4,112,128]{3,2,1,0:T(8,128)(2,1)S(1)}, bf16[2,4,112,128]{3,2,1,0:T(8,128)(2,1)S(1)}, u32[]{:S(2)}, u32[]{:S(2)}) collective-permute-start(bf16[2,4,112,128]{3,2,1,0:T(8,128)(2,1)S(1)} %slice.40), channel_id=1, source_target_pairs={{0,1},{1,2},{2,3},{3,0},{4,5},{5,6},{6,7},{7,4},{8,9},{9,10},{10,1... | collective-permute-start | bytes 688136 | tf_op jit(solution)/shard_map/ppermute | solution.py:45
  159.9 6.9 %collective-permute-start.39 = (bf16[2,4,112,128]{3,2,1,0:T(8,128)(2,1)S(1)}, bf16[2,4,112,128]{3,2,1,0:T(8,128)(2,1)S(1)}, u32[]{:S(2)}, u32[]{:S(2)}) collective-permute-start(bf16[2,4,112,128]{3,2,1,0:T(8,128)(2,1)S(1)} %slice.44), channel_id=1, source_target_pairs={{0,48},{16,0},{32,16},{48,32},{1,49},{17,1},{33,17},{49,33},{2,50}... | collective-permute-start | bytes 688136 | tf_op jit(solution)/shard_map/ppermute | solution.py:45
  161.8 7.0 %collective-permute-start.38 = (bf16[2,4,112,128]{3,2,1,0:T(8,128)(2,1)S(1)}, bf16[2,4,112,128]{3,2,1,0:T(8,128)(2,1)S(1)}, u32[]{:S(2)}, u32[]{:S(2)}) collective-permute-start(bf16[2,4,112,128]{3,2,1,0:T(8,128)(2,1)S(1)} %slice.43), channel_id=1, source_target_pairs={{0,16},{16,32},{32,48},{48,0},{1,17},{17,33},{33,49},{49,1},{2,18}... | collective-permute-start | bytes 688136 | tf_op jit(solution)/shard_map/ppermute | solution.py:45
  162.0 4.8 %collective-permute-start.25 = (bf16[2,224,128]{2,1,0:T(8,128)(2,1)S(1)}, bf16[2,224,128]{2,1,0:T(8,128)(2,1)S(1)}, u32[]{:S(2)}, u32[]{:S(2)}) collective-permute-start(bf16[2,224,128]{2,1,0:T(8,128)(2,1)S(1)} %pad_maximum_fusion.4.near_ref), channel_id=1, source_target_pairs={{0,128},{128,0},{1,129},{129,1},{2,130},{130,2},{3,131},{131,3},{4... | collective-permute-start | bytes 344072 | tf_op jit(solution)/shard_map/ppermute | solution.py:433
  (2 other events, 2.1 us)
